TPU v7x, 512 devices: a whole 4x4x16 slice. The times are simulated.
512 devices in a mesh: dp: 8 (over z_lo), lat: 16 (over y, z_hi, core), lon: 4 (over x).
Axes of the slice: x: 4, y: 4, z: 16 (z_hi: 2, z_lo: 8; z = z_hi * 8 + z_lo), core: 2. Of those that a mesh axis runs over, the one named last changes fastest.
Arguments:
- hidden_in: bfloat16 [8, 256, 512, 128], P('dp', 'lat', 'lon'), may hold values from -6 to 6
- conv_weight: bfloat16 [3, 3, 128, 128], replicated, may hold values from -0.1875 to 0.1875
- conv_bias: float32 [128], replicated, may hold values from -3 to 3
- proj_weight: float32 [128], replicated, may hold values from -5 to 5
- ocean_depth: float32 [256, 512], P('lat', 'lon'), may hold values from 0.5 to 2
- sea_mask: int32 [256, 512], P('lat', 'lon'), may hold values 0 or 1
- step_alpha: float32 [6], replicated, may hold values from 0.04 to 0.07
- step_beta: float32 [6], replicated, may hold values from 0.1 to 0.5
- surface_cotangent: float32 [8, 256, 512], P('dp', 'lat', 'lon'), may hold values from -20 to 20
Outputs:
- grad_hidden: bfloat16 [8, 256, 512, 128], P('dp', 'lat', 'lon')
- grad_weight: float32 [128, 3, 3, 128], P(('lat', 'lon'))
- grad_bias: float32 [128], replicated
- grad_proj: float32 [128], replicated
All inputs are finite; a program needn't handle non-finite values. No bound on the sum of `sea_mask` on one device may be relied on, other than what follows from the above.
Results may differ from a plain program's by a relative error of at most 0.01.
Values may be sent and summed in bfloat16 or wider, within the bound.
No kernel may reach another device: no remote copies, remote signals or barrier semaphores. Data moves between devices by JAX's collectives and lax.ppermute only.
A program may use at most 64 MiB of HBM per device.

v0:
```python
import functools
import math

import jax
import jax.numpy as jnp
from jax import lax
from jax.sharding import Mesh
from jax.sharding import PartitionSpec as P

ITERS = 6
LAT_LON = ("lat_0", "lat_1", "lat_2", "lon")
LAT = ("lat_0", "lat_1", "lat_2")
DP_LAT_LON = ("dp", "lat_0", "lat_1", "lat_2", "lon")


helm_coef = 0.5


def from_everyone(shard, axis):
    peers = lax.axis_size(axis)
    return lax.all_to_all(
        jnp.broadcast_to(shard[None], (peers, *shard.shape)), axis, 0, 0, tiled=True
    )


def over_copies(shard, axis):
    everything = from_everyone(shard, axis)
    return jnp.sum(everything, axis=0)


def packed_total(arrays, axis):
    ends = [0]
    for a in arrays:
        ends.append(ends[-1] + a.size)
    so_far = over_copies(jnp.concatenate([a.ravel() for a in arrays]), axis)
    return tuple((so_far[b:e].reshape(a.shape) for a, b, e in zip(arrays, ends, ends[1:])))


def extended(cells, sides, width, closed):
    for axis, dim in sides:
        count = lax.axis_size(axis)
        ends = count if closed else count - 1
        head = lax.slice_in_dim(cells, 0, width, axis=dim)
        tail = lax.slice_in_dim(cells, cells.shape[dim] - width, cells.shape[dim], axis=dim)
        cells = jnp.concatenate(
            [
                lax.ppermute(tail, axis, [(i, (i + 1) % count) for i in range(ends)]),
                cells,
                lax.ppermute(head, axis, [((i + 1) % count, i) for i in range(ends)]),
            ],
            axis=dim,
        )
    return cells


def in_blocks(shard, dim, peers):
    shape = shard.shape
    blocks = shard.reshape(*shape[:dim], peers, shape[dim] // peers, *shape[dim + 1 :])
    return jnp.moveaxis(blocks, dim, 0)


def sent_and_summed(shard, axis, dim):
    blocks = in_blocks(shard, dim, lax.axis_size(axis))
    arrived = lax.all_to_all(blocks, axis, split_axis=0, concat_axis=0, tiled=True)
    return arrived.astype(jnp.float32).sum(axis=0)


def one_axis_at_a_time(shard, axes):
    return functools.reduce(lax.psum, axes, shard)


def operate(field_ext, mask_ext, depth_ext):
    rows_in = field_ext.shape[-2] - 2
    cols_in = field_ext.shape[-1] - 2
    center = field_ext[..., 1:-1, 1:-1]
    mask_mid = mask_ext[1:-1, 1:-1]
    depth_mid = depth_ext[1:-1, 1:-1]
    result = helm_coef * center
    for row_off, col_off in ((0, 1), (2, 1), (1, 0), (1, 2)):
        beside = field_ext[..., row_off : row_off + rows_in, col_off : col_off + cols_in]
        mask_near = mask_ext[row_off : row_off + rows_in, col_off : col_off + cols_in]
        depth_near = depth_ext[row_off : row_off + rows_in, col_off : col_off + cols_in]
        weight = mask_near * 0.5 * (depth_mid + depth_near)
        result = result + weight * (center - beside)
    return mask_mid * result


def solve_steps(adjoint_start, mask_ext, depth_ext, step_alpha, step_beta, widen):
    solution = jnp.zeros_like(adjoint_start)
    residual = adjoint_start
    direction = adjoint_start
    for turn_index in range(ITERS):
        solution = solution + step_alpha[turn_index] * direction
        if turn_index + 1 < ITERS:
            applied = operate(widen(direction), mask_ext, depth_ext)
            residual = residual - step_alpha[turn_index] * applied
            direction = residual + step_beta[turn_index] * direction
    return solution


def pad_zero(field):
    return jnp.pad(field, ((0, 0), (1, 1), (1, 1)))


def shards(
    hidden_in,
    conv_weight,
    conv_bias,
    proj_weight,
    ocean_depth,
    sea_mask,
    step_alpha,
    step_beta,
    surface_cotangent,
):
    samples, lat_rows, lon_cols, channels = hidden_in.shape
    mask_float = sea_mask.astype(jnp.float32)
    counted, summed = packed_total(
        (jnp.sum(mask_float), jnp.sum(mask_float * surface_cotangent, axis=(1, 2))), LAT_LON
    )
    adjoint_start = mask_float * (surface_cotangent - (summed / counted)[:, None, None])
    reach = ITERS - 1
    stacked = jnp.concatenate([adjoint_start, mask_float[None], ocean_depth[None]], axis=0)
    stacked = extended(stacked, ((LAT, 1),), reach, False)
    stacked = extended(stacked, (("lon", 2),), reach, True)
    mask_wide = jnp.pad(stacked[samples], 1)
    depth_wide = jnp.pad(stacked[samples + 1], 1)
    solution = solve_steps(
        stacked[:samples], mask_wide, depth_wide, step_alpha, step_beta, pad_zero
    )
    solution = solution[:, reach : reach + lat_rows, reach : reach + lon_cols]
    forcing_grad = mask_float * solution
    padded = extended(hidden_in, ((LAT, 1),), 1, False)
    padded = extended(padded, (("lon", 2),), 1, True)
    cell_count = samples * lat_rows * lon_cols
    shifted = [
        padded[:, row_off : row_off + lat_rows, col_off : col_off + lon_cols, :].reshape(
            cell_count, channels
        )
        for row_off in range(3)
        for col_off in range(3)
    ]
    preact = conv_bias
    for offset in range(9):
        preact = preact + jnp.dot(
            shifted[offset],
            conv_weight[offset // 3, offset % 3],
            preferred_element_type=jnp.float32,
        )
    sigma = jax.nn.sigmoid(preact)
    active = preact * sigma
    slope_act = sigma * (1.0 + preact * (1.0 - sigma))
    force_col = forcing_grad.reshape(cell_count)[:, None]
    grad_pre = (force_col * proj_weight * slope_act).astype(jnp.bfloat16)
    local_proj = jnp.sum(active * force_col, axis=0)
    local_bias = jnp.sum(grad_pre.astype(jnp.float32), axis=0)
    grad_ext = extended(
        grad_pre.reshape(samples, lat_rows, lon_cols, channels), ((LAT, 1),), 1, False
    )
    grad_ext = extended(grad_ext, (("lon", 2),), 1, True)
    backed = jnp.zeros((cell_count, channels), jnp.float32)
    for row_off in range(3):
        for col_off in range(3):
            window = grad_ext[
                :, 2 - row_off : 2 - row_off + lat_rows, 2 - col_off : 2 - col_off + lon_cols, :
            ].reshape(cell_count, channels)
            backed = backed + lax.dot_general(
                window,
                conv_weight[row_off, col_off],
                (((1,), (1,)), ((), ())),
                preferred_element_type=jnp.float32,
            )
    grad_hidden = backed.reshape(samples, lat_rows, lon_cols, channels).astype(jnp.bfloat16)
    share = channels // lax.axis_size(LAT_LON)
    blocks = []
    for shifted_cols in shifted:
        blocks.append(
            lax.dot_general(
                shifted_cols, grad_pre, (((0,), (0,)), ((), ())), preferred_element_type=jnp.float32
            )
        )
    spatial = sent_and_summed(
        jnp.stack(blocks, axis=1)
        .reshape(share * lax.axis_size(LAT_LON), 3, 3, channels)
        .astype(jnp.bfloat16),
        LAT_LON,
        0,
    )
    own_weight = over_copies(spatial, "dp")
    total_bias, total_proj = (
        one_axis_at_a_time(local_bias, DP_LAT_LON),
        one_axis_at_a_time(local_proj, DP_LAT_LON),
    )
    all_cells = cell_count * lax.axis_size("dp") * lax.axis_size(LAT) * lax.axis_size("lon")
    grad_scale = 1.0 / math.sqrt(all_cells)
    return (grad_hidden, own_weight * grad_scale, total_bias * grad_scale, total_proj * grad_scale)


def solution(mesh):
    split = Mesh(
        mesh.devices.reshape(mesh.shape["dp"], 4, 2, 2, mesh.shape["lon"]),
        ("dp", "lat_0", "lat_1", "lat_2", "lon"),
    )
    placed = (
        P("dp", LAT, "lon", None),
        P(),
        P(),
        P(),
        P(LAT, "lon"),
        P(LAT, "lon"),
        P(),
        P(),
        P("dp", LAT, "lon"),
    )
    return jax.shard_map(
        shards,
        mesh=split,
        in_specs=placed,
        out_specs=(P("dp", LAT, "lon", None), P(LAT_LON, None, None, None), P(), P()),
        check_vma=False,
    )
```

profile of v0, /device:TPU:2, one launch (start us, length us, event | category | flops | bytes accessed | tf_op | source)
XLA Modules:
  0.0 230.7 jit_solution(14619772647164740237)
XLA Ops:
  5.3 21.3 %all-to-all-start = ((f32[64,1,2]{2,1,0:T(1,128)}), f32[64,1,2]{2,1,0:T(1,128)S(1)}, u32[]{:S(2)}, u32[]{:S(2)}) async-start(f32[64,1,2]{2,1,0:T(1,128)} %broadcast_in_dim.17), calls=%async_computation | async-start | bytes 65536 | tf_op jit(solution)/shard_map/all_to_all | solution.py:21
  31.3 10.9 %all-to-all-done = f32[64,1,2]{2,1,0:T(1,128)S(1)} async-done(((f32[64,1,2]{2,1,0:T(1,128)}), f32[64,1,2]{2,1,0:T(1,128)S(1)}, u32[]{:S(2)}, u32[]{:S(2)}) %all-to-all-start) | async-done | bytes 544 | tf_op jit(solution)/shard_map/all_to_all | solution.py:21
  50.3 10.2 %collective-permute-done.1 = f32[3,5,128]{2,1,0:T(8,128)S(1)} collective-permute-done((f32[3,5,128]{2,1,0:T(8,128)S(1)}, f32[3,5,128]{2,1,0:T(8,128)S(1)}, u32[]{:S(2)}, u32[]{:S(2)}) %collective-permute-start.1) | collective-permute-done | bytes 7712 | tf_op jit(solution)/shard_map/ppermute | solution.py:49
  61.3 3.4 %collective-permute-start.2 = (f32[3,26,5]{2,1,0:T(8,128)S(1)}, f32[3,26,5]{2,1,0:T(8,128)S(1)}, u32[]{:S(2)}, u32[]{:S(2)}) collective-permute-start(f32[3,26,5]{2,1,0:T(8,128)S(1)} %get-tuple-element.60), channel_id=1, source_target_pairs={{0,1},{1,2},{2,3},{3,0},{4,5},{5,6},{6,7},{7,4},{8,9},{9,10},{10,1... | collective-permute-start | bytes 4688 | tf_op jit(solution)/shard_map/ppermute | solution.py:47
  64.7 2.5 %collective-permute-start.3 = (f32[3,26,5]{2,1,0:T(8,128)S(1)}, f32[3,26,5]{2,1,0:T(8,128)S(1)}, u32[]{:S(2)}, u32[]{:S(2)}) collective-permute-start(f32[3,26,5]{2,1,0:T(8,128)S(1)} %get-tuple-element.61), channel_id=1, source_target_pairs={{1,0},{2,1},{3,2},{0,3},{5,4},{6,5},{7,6},{4,7},{9,8},{10,9},{11,1... | collective-permute-start | bytes 4688 | tf_op jit(solution)/shard_map/ppermute | solution.py:49
  72.8 2.6 %multiply_add_fusion.2 = f32[1,26,138]{2,1,0:T(8,128)S(1)} fusion(f32[26,138]{1,0:T(8,128)S(1)} %get-tuple-element.24, f32[26,138]{1,0:T(8,128)S(1)} %get-tuple-element.23, f32[26,138]{1,0:T(8,128)S(1)} %get-tuple-element.22, f32[26,138]{1,0:T(8,128)S(1)} %get-tuple-element.21, f32[1,26,138]{2,1,0:T(8,128)S(1)} %get-tuple-element.59, ...), kind=kLoop, calls=%fused_computation.162 | loop fusion | flops 129168 | bytes 114832 | tf_op jit(solution)/shard_map/add | solution.py:97
  75.4 3.2 %multiply_add_fusion.1 = (f32[1,26,138]{2,1,0:T(8,128)S(1)}, f32[1,26,138]{2,1,0:T(8,128)S(1)}) fusion(f32[1,26,138]{2,1,0:T(8,128)S(1)} %multiply_add_fusion.2, f32[]{:T(128)} %bitcast.17, f32[]{:T(128)} %bitcast.14, f32[1,26,138]{2,1,0:T(8,128)S(1)} %get-tuple-element.20, f32[1,26,138]{2,1,0:T(8,128)S(1)} %get-tuple-element.59, f32[]{:T(128)} %bitcast.13, ...), kind=kLoop, calls=%fused_computation.157 | loop fusion | flops 186576 | bytes 143540 | tf_op jit(solution)/shard_map/add | solution.py:97
  78.6 2.1 multiply_add_fusion
  80.8 4.4 %fusion.110 = f32[2048]{0:T(1024)S(1)} fusion(f32[1,26,138]{2,1,0:T(8,128)S(1)} %get-tuple-element.17, f32[1,26,138]{2,1,0:T(8,128)S(1)} %get-tuple-element.18, f32[1,26,138]{2,1,0:T(8,128)S(1)} %multiply_add_fusion.2, f32[1,26,138]{2,1,0:T(8,128)S(1)} %fusion.66, f32[1,26,138]{2,1,0:T(8,128)S(1)} %get-tuple-element.56, ...), kind=kLoop, calls=%fused_computation.201 | loop fusion | flops 36864 | bytes 81948 | tf_op jit(solution)/shard_map/mul | solution.py:154
  85.7 3.1 %collective-permute-start.6 = (bf16[1,18,1,128]{3,2,1,0:T(2,128)(2,1)S(1)}, bf16[1,18,1,128]{3,2,1,0:T(2,128)(2,1)S(1)}, u32[]{:S(2)}, u32[]{:S(2)}) collective-permute-start(bf16[1,18,1,128]{3,2,1,0:T(2,128)(2,1)S(1)} %get-tuple-element.45), channel_id=1, source_target_pairs={{0,1},{1,2},{2,3},{3,0},{4,5},{5,6},{6,7},{7,4},{8,9},{9,10},{10,1... | collective-permute-start | bytes 13832 | tf_op jit(solution)/shard_map/ppermute | solution.py:47
  88.7 2.8 %collective-permute-start.7 = (bf16[1,18,1,128]{3,2,1,0:T(2,128)(2,1)S(1)}, bf16[1,18,1,128]{3,2,1,0:T(2,128)(2,1)S(1)}, u32[]{:S(2)}, u32[]{:S(2)}) collective-permute-start(bf16[1,18,1,128]{3,2,1,0:T(2,128)(2,1)S(1)} %get-tuple-element.46), channel_id=1, source_target_pairs={{1,0},{2,1},{3,2},{0,3},{5,4},{6,5},{7,6},{4,7},{9,8},{10,9},{11,1... | collective-permute-start | bytes 13832 | tf_op jit(solution)/shard_map/ppermute | solution.py:49
  91.8 2.5 %collective-permute-done.7 = bf16[1,18,1,128]{3,2,1,0:T(2,128)(2,1)S(1)} collective-permute-done((bf16[1,18,1,128]{3,2,1,0:T(2,128)(2,1)S(1)}, bf16[1,18,1,128]{3,2,1,0:T(2,128)(2,1)S(1)}, u32[]{:S(2)}, u32[]{:S(2)}) %collective-permute-start.7) | collective-permute-done | bytes 4640 | tf_op jit(solution)/shard_map/ppermute | solution.py:49
  102.9 18.9 %all-to-all-start.1 = ((bf16[64,2,3,3,128]{4,1,3,2,0:T(2,128)(2,1)}), bf16[64,2,3,3,128]{4,1,3,2,0:T(2,128)(2,1)S(1)}, u32[]{:S(2)}, u32[]{:S(2)}) async-start(bf16[64,2,3,3,128]{4,1,3,2,0:T(2,128)(2,1)} %copy.21), calls=%async_computation.1 | async-start | bytes 589824 | tf_op jit(solution)/shard_map/all_to_all | solution.py:64
  121.9 2.0 collective-permute-start.8
  125.2 30.1 %all-reduce.7 = (f32[128]{0:T(128)S(1)}, f32[128]{0:T(128)S(1)}) all-reduce(f32[128]{0:T(128)S(1)} %get-tuple-element.14, f32[128]{0:T(128)S(1)} %get-tuple-element.25), channel_id=1, replica_groups=mesh['dp'=8,'lat_0'=4,'lat_1'=2,'lat_2'=2,'lon'=4] {'dp'}, use_global_device_ids=true, to_apply=%region_6.7 | all-reduce | flops 256 | bytes 2048 | tf_op jit(solution)/shard_map/psum | solution.py:69
  155.3 21.3 %all-reduce.9 = (f32[128]{0:T(128)S(1)}, f32[128]{0:T(128)S(1)}) all-reduce(f32[128]{0:T(128)S(1)} %get-tuple-element.4, f32[128]{0:T(128)S(1)} %get-tuple-element.5), channel_id=1, replica_groups=mesh['dp'=8,'lat_0'=4,'lat_1'=2,'lat_2'=2,'lon'=4] {'lat_0'}, use_global_device_ids=true, to_apply=%region_7.8 | all-reduce | flops 256 | bytes 2048 | tf_op jit(solution)/shard_map/psum | solution.py:69
  176.6 13.6 %all-reduce.11 = (f32[128]{0:T(128)S(1)}, f32[128]{0:T(128)S(1)}) all-reduce(f32[128]{0:T(128)S(1)} %get-tuple-element.8, f32[128]{0:T(128)S(1)} %get-tuple-element.9), channel_id=1, replica_groups=mesh['dp'=8,'lat_0'=4,'lat_1'=2,'lat_2'=2,'lon'=4] {'lat_1'}, use_global_device_ids=true, to_apply=%region_8.9 | all-reduce | flops 256 | bytes 2048 | tf_op jit(solution)/shard_map/psum | solution.py:69
  190.2 2.4 %all-reduce.10 = (f32[128]{0:T(128)S(1)}, f32[128]{0:T(128)S(1)}) all-reduce(f32[128]{0:T(128)S(1)} %get-tuple-element.12, f32[128]{0:T(128)S(1)} %get-tuple-element.13), channel_id=1, replica_groups=mesh['dp'=8,'lat_0'=4,'lat_1'=2,'lat_2'=2,'lon'=4] {'lat_2'}, use_global_device_ids=true, to_apply=%region_9.10 | all-reduce | flops 256 | bytes 2048 | tf_op jit(solution)/shard_map/psum | solution.py:69
  192.7 8.6 %all-reduce.8 = (f32[128]{0:T(128)S(1)}, f32[128]{0:T(128)S(1)}) all-reduce(f32[128]{0:T(128)S(1)} %get-tuple-element.10, f32[128]{0:T(128)S(1)} %get-tuple-element.11), channel_id=1, replica_groups=mesh['dp'=8,'lat_0'=4,'lat_1'=2,'lat_2'=2,'lon'=4] {'lon'}, use_global_device_ids=true, to_apply=%region_10.11 | all-reduce | flops 256 | bytes 2048 | tf_op jit(solution)/shard_map/psum | solution.py:69
  201.8 4.3 %collective-permute-start.10 = (bf16[1,18,1,128]{3,2,1,0:T(2,128)(2,1)S(1)}, bf16[1,18,1,128]{3,2,1,0:T(2,128)(2,1)S(1)}, u32[]{:S(2)}, u32[]{:S(2)}) collective-permute-start(bf16[1,18,1,128]{3,2,1,0:T(2,128)(2,1)S(1)} %get-tuple-element.40), channel_id=1, source_target_pairs={{1,0},{2,1},{3,2},{0,3},{5,4},{6,5},{7,6},{4,7},{9,8},{10,9},{11,1... | collective-permute-start | bytes 13832 | tf_op jit(solution)/shard_map/ppermute | solution.py:49
  206.1 2.1 collective-permute-start.11
  208.6 3.1 %collective-permute-done.11 = bf16[1,18,1,128]{3,2,1,0:T(2,128)(2,1)S(1)} collective-permute-done((bf16[1,18,1,128]{3,2,1,0:T(2,128)(2,1)S(1)}, bf16[1,18,1,128]{3,2,1,0:T(2,128)(2,1)S(1)}, u32[]{:S(2)}, u32[]{:S(2)}) %collective-permute-start.11) | collective-permute-done | bytes 4640 | tf_op jit(solution)/shard_map/ppermute | solution.py:47
  215.8 3.4 %all-to-all-start.2 = ((f32[8,2,3,3,128]{4,1,3,2,0:T(2,128)}), f32[8,2,3,3,128]{4,1,3,2,0:T(2,128)S(1)}, u32[]{:S(2)}, u32[]{:S(2)}) async-start(f32[8,2,3,3,128]{4,1,3,2,0:T(2,128)} %broadcast_in_dim.23), calls=%async_computation.2 | async-start | bytes 147456 | tf_op jit(solution)/shard_map/all_to_all | solution.py:21
  221.0 9.0 %all-to-all-done.2 = f32[8,2,3,3,128]{4,1,3,2,0:T(2,128)S(1)} async-done(((f32[8,2,3,3,128]{4,1,3,2,0:T(2,128)}), f32[8,2,3,3,128]{4,1,3,2,0:T(2,128)S(1)}, u32[]{:S(2)}, u32[]{:S(2)}) %all-to-all-start.2) | async-done | bytes 73760 | tf_op jit(solution)/shard_map/all_to_all | solution.py:21
  (90 shorter events, 40.6 us)
Async XLA Ops:
  5.3 37.0 %all-to-all-start = ((f32[64,1,2]{2,1,0:T(1,128)}), f32[64,1,2]{2,1,0:T(1,128)S(1)}, u32[]{:S(2)}, u32[]{:S(2)}) async-start(f32[64,1,2]{2,1,0:T(1,128)} %broadcast_in_dim.17), calls=%async_computation | async-start | bytes 65536 | tf_op jit(solution)/shard_map/all_to_all | solution.py:21
  27.3 57.9 %collective-permute-start.4 = (bf16[1,1,128,128]{3,2,1,0:T(8,128)(2,1)S(1)}, bf16[1,1,128,128]{3,2,1,0:T(8,128)(2,1)S(1)}, u32[]{:S(2)}, u32[]{:S(2)}) collective-permute-start(bf16[1,1,128,128]{3,2,1,0:T(8,128)(2,1)S(1)} %get-tuple-element.55), channel_id=1, source_target_pairs={{0,4},{4,8},{8,12},{12,16},{16,20},{20,24},{24,28},{28,32},{32,36}... | collective-permute-start | bytes 98312 | tf_op jit(solution)/shard_map/ppermute | solution.py:47
  29.3 55.9 %collective-permute-start.5 = (bf16[1,1,128,128]{3,2,1,0:T(8,128)(2,1)S(1)}, bf16[1,1,128,128]{3,2,1,0:T(8,128)(2,1)S(1)}, u32[]{:S(2)}, u32[]{:S(2)}) collective-permute-start(bf16[1,1,128,128]{3,2,1,0:T(8,128)(2,1)S(1)} %get-tuple-element.54), channel_id=1, source_target_pairs={{4,0},{8,4},{12,8},{16,12},{20,16},{24,20},{28,24},{32,28},{36,32}... | collective-permute-start | bytes 98312 | tf_op jit(solution)/shard_map/ppermute | solution.py:49
  45.7 4.7 %collective-permute-start = (f32[3,5,128]{2,1,0:T(8,128)S(1)}, f32[3,5,128]{2,1,0:T(8,128)S(1)}, u32[]{:S(2)}, u32[]{:S(2)}) collective-permute-start(f32[3,5,128]{2,1,0:T(8,128)S(1)} %get-tuple-element.62), channel_id=1, source_target_pairs={{0,4},{4,8},{8,12},{12,16},{16,20},{20,24},{24,28},{28,32},{32,36}... | collective-permute-start | bytes 23048 | tf_op jit(solution)/shard_map/ppermute | solution.py:47
  47.5 13.0 %collective-permute-start.1 = (f32[3,5,128]{2,1,0:T(8,128)S(1)}, f32[3,5,128]{2,1,0:T(8,128)S(1)}, u32[]{:S(2)}, u32[]{:S(2)}) collective-permute-start(f32[3,5,128]{2,1,0:T(8,128)S(1)} %get-tuple-element.63), channel_id=1, source_target_pairs={{4,0},{8,4},{12,8},{16,12},{20,16},{24,20},{28,24},{32,28},{36,32}... | collective-permute-start | bytes 23048 | tf_op jit(solution)/shard_map/ppermute | solution.py:49
  61.2 19.6 %copy-start.3 = (s32[16,128]{1,0:T(8,128)S(1)}, s32[16,128]{1,0:T(8,128)}, u32[]{:S(2)}) copy-start(s32[16,128]{1,0:T(8,128)} %param.14) | copy-start | bytes 24580
  61.3 7.4 %collective-permute-start.2 = (f32[3,26,5]{2,1,0:T(8,128)S(1)}, f32[3,26,5]{2,1,0:T(8,128)S(1)}, u32[]{:S(2)}, u32[]{:S(2)}) collective-permute-start(f32[3,26,5]{2,1,0:T(8,128)S(1)} %get-tuple-element.60), channel_id=1, source_target_pairs={{0,1},{1,2},{2,3},{3,0},{4,5},{5,6},{6,7},{7,4},{8,9},{9,10},{10,1... | collective-permute-start | bytes 4688 | tf_op jit(solution)/shard_map/ppermute | solution.py:47
  64.7 6.0 %collective-permute-start.3 = (f32[3,26,5]{2,1,0:T(8,128)S(1)}, f32[3,26,5]{2,1,0:T(8,128)S(1)}, u32[]{:S(2)}, u32[]{:S(2)}) collective-permute-start(f32[3,26,5]{2,1,0:T(8,128)S(1)} %get-tuple-element.61), channel_id=1, source_target_pairs={{1,0},{2,1},{3,2},{0,3},{5,4},{6,5},{7,6},{4,7},{9,8},{10,9},{11,1... | collective-permute-start | bytes 4688 | tf_op jit(solution)/shard_map/ppermute | solution.py:49
  68.7 16.6 %copy-start = (bf16[1,16,128,128]{3,2,1,0:T(8,128)(2,1)S(1)}, bf16[1,16,128,128]{3,2,1,0:T(8,128)(2,1)}, u32[]{:S(2)}) copy-start(bf16[1,16,128,128]{3,2,1,0:T(8,128)(2,1)} %param.9) | copy-start | bytes 1572868
  85.2 6.3 %copy-start.1 = (bf16[3,3,128,128]{3,2,1,0:T(8,128)(2,1)S(1)}, bf16[3,3,128,128]{3,2,1,0:T(8,128)(2,1)}, u32[]{:S(2)}) copy-start(bf16[3,3,128,128]{3,2,1,0:T(8,128)(2,1)} %param.10) | copy-start | bytes 884740
  85.7 6.1 %collective-permute-start.6 = (bf16[1,18,1,128]{3,2,1,0:T(2,128)(2,1)S(1)}, bf16[1,18,1,128]{3,2,1,0:T(2,128)(2,1)S(1)}, u32[]{:S(2)}, u32[]{:S(2)}) collective-permute-start(bf16[1,18,1,128]{3,2,1,0:T(2,128)(2,1)S(1)} %get-tuple-element.45), channel_id=1, source_target_pairs={{0,1},{1,2},{2,3},{3,0},{4,5},{5,6},{6,7},{7,4},{8,9},{9,10},{10,1... | collective-permute-start | bytes 13832 | tf_op jit(solution)/shard_map/ppermute | solution.py:47
  88.7 5.6 %collective-permute-start.7 = (bf16[1,18,1,128]{3,2,1,0:T(2,128)(2,1)S(1)}, bf16[1,18,1,128]{3,2,1,0:T(2,128)(2,1)S(1)}, u32[]{:S(2)}, u32[]{:S(2)}) collective-permute-start(bf16[1,18,1,128]{3,2,1,0:T(2,128)(2,1)S(1)} %get-tuple-element.46), channel_id=1, source_target_pairs={{1,0},{2,1},{3,2},{0,3},{5,4},{6,5},{7,6},{4,7},{9,8},{10,9},{11,1... | collective-permute-start | bytes 13832 | tf_op jit(solution)/shard_map/ppermute | solution.py:49
  95.5 0.7 copy-start.4
  97.3 0.7 copy-start.5
  102.9 112.1 %all-to-all-start.1 = ((bf16[64,2,3,3,128]{4,1,3,2,0:T(2,128)(2,1)}), bf16[64,2,3,3,128]{4,1,3,2,0:T(2,128)(2,1)S(1)}, u32[]{:S(2)}, u32[]{:S(2)}) async-start(bf16[64,2,3,3,128]{4,1,3,2,0:T(2,128)(2,1)} %copy.21), calls=%async_computation.1 | async-start | bytes 589824 | tf_op jit(solution)/shard_map/all_to_all | solution.py:64
  121.9 79.9 %collective-permute-start.8 = (bf16[1,1,128,128]{3,2,1,0:T(8,128)(2,1)S(1)}, bf16[1,1,128,128]{3,2,1,0:T(8,128)(2,1)S(1)}, u32[]{:S(2)}, u32[]{:S(2)}) collective-permute-start(bf16[1,1,128,128]{3,2,1,0:T(8,128)(2,1)S(1)} %get-tuple-element.49), channel_id=1, source_target_pairs={{0,4},{4,8},{8,12},{12,16},{16,20},{20,24},{24,28},{28,32},{32,36}... | collective-permute-start | bytes 98312 | tf_op jit(solution)/shard_map/ppermute | solution.py:47
  123.9 77.9 %collective-permute-start.9 = (bf16[1,1,128,128]{3,2,1,0:T(8,128)(2,1)S(1)}, bf16[1,1,128,128]{3,2,1,0:T(8,128)(2,1)S(1)}, u32[]{:S(2)}, u32[]{:S(2)}) collective-permute-start(bf16[1,1,128,128]{3,2,1,0:T(8,128)(2,1)S(1)} %get-tuple-element.50), channel_id=1, source_target_pairs={{4,0},{8,4},{12,8},{16,12},{20,16},{24,20},{28,24},{32,28},{36,32}... | collective-permute-start | bytes 98312 | tf_op jit(solution)/shard_map/ppermute | solution.py:49
  201.8 6.8 %collective-permute-start.10 = (bf16[1,18,1,128]{3,2,1,0:T(2,128)(2,1)S(1)}, bf16[1,18,1,128]{3,2,1,0:T(2,128)(2,1)S(1)}, u32[]{:S(2)}, u32[]{:S(2)}) collective-permute-start(bf16[1,18,1,128]{3,2,1,0:T(2,128)(2,1)S(1)} %get-tuple-element.40), channel_id=1, source_target_pairs={{1,0},{2,1},{3,2},{0,3},{5,4},{6,5},{7,6},{4,7},{9,8},{10,9},{11,1... | collective-permute-start | bytes 13832 | tf_op jit(solution)/shard_map/ppermute | solution.py:49
  206.1 5.6 %collective-permute-start.11 = (bf16[1,18,1,128]{3,2,1,0:T(2,128)(2,1)S(1)}, bf16[1,18,1,128]{3,2,1,0:T(2,128)(2,1)S(1)}, u32[]{:S(2)}, u32[]{:S(2)}) collective-permute-start(bf16[1,18,1,128]{3,2,1,0:T(2,128)(2,1)S(1)} %get-tuple-element.41), channel_id=1, source_target_pairs={{0,1},{1,2},{2,3},{3,0},{4,5},{5,6},{6,7},{7,4},{8,9},{9,10},{10,1... | collective-permute-start | bytes 13832 | tf_op jit(solution)/shard_map/ppermute | solution.py:47
  212.0 1.0 copy-start.2
  215.8 14.3 %all-to-all-start.2 = ((f32[8,2,3,3,128]{4,1,3,2,0:T(2,128)}), f32[8,2,3,3,128]{4,1,3,2,0:T(2,128)S(1)}, u32[]{:S(2)}, u32[]{:S(2)}) async-start(f32[8,2,3,3,128]{4,1,3,2,0:T(2,128)} %broadcast_in_dim.23), calls=%async_computation.2 | async-start | bytes 147456 | tf_op jit(solution)/shard_map/all_to_all | solution.py:21
where the time goes:
time: 232 us; the launch traced here: 231 us
  blocking collectives  76.1 us (33%)
  starting transfers between devices  71.3 us (31%)
  waiting for transfers between devices  37.7 us (16%)
  other arithmetic  24.2 us (10%)
  matrix products  10.5 us (5%)
  local copies, waits for them, and re-layouts  8.48 us (4%)
  between operations  2.42 us (1%)
    psum x5, blocking collectives, one_axis_at_a_time(): return functools.reduce(lax.psum, axes, shard)  76.1 us
    all_to_all x2, starting transfers between devices, from_everyone(): lax.all_to_all(jnp.broadcast_to(shard[None], (peers, *shard.shape)), axis...  24.6 us
    all_to_all x2, waiting for transfers between devices, from_everyone(): lax.all_to_all(jnp.broadcast_to(shard[None], (peers, *shard.shape)), axis...  20 us
    all_to_all x1, starting transfers between devices, sent_and_summed(): lax.all_to_all(blocks, axis, split_axis=0, concat_axis=0, tiled=True)  18.9 us
    ppermute x6, waiting for transfers between devices, extended(): lax.ppermute(head, axis, [((i + 1) % count, i) for i in range(ends)])  14.6 us
    ppermute x6, starting transfers between devices, extended(): lax.ppermute(tail, axis, [(i, (i + 1) % count) for i in range(ends)])  14.4 us
    ppermute x6, starting transfers between devices, extended(): lax.ppermute(head, axis, [((i + 1) % count, i) for i in range(ends)])  13.4 us
    add x4, other arithmetic, solve_steps(): direction = residual + step_beta[turn_index] * direction  9.17 us
  transfers between devices with their start and end apart: 15, of which 6 were waited for; matrix products, arithmetic and copies ran while one was open for 12% of the time, Pallas kernels for 0%

commit v1 on v0

--- a/solution.py
+++ b/solution.py
@@ -67,6 +67,48 @@
 
 def one_axis_at_a_time(shard, axes):
     return functools.reduce(lax.psum, axes, shard)
+
+
+def two_pieces(values):
+    high = lax.reduce_precision(values, 8, 7)
+    return jnp.concatenate([high, values - high]).astype(jnp.bfloat16)
+
+
+def from_pieces(pieces):
+    both = pieces.astype(jnp.float32)
+    count = both.shape[-2] // 2
+    return both[..., :count, :] + both[..., count:, :]
+
+
+def all_summed(weight, bias, proj):
+    channels = weight.shape[0]
+    n_y, n_z, n_c = (lax.axis_size(name) for name in LAT)
+    n_x = lax.axis_size("lon")
+    share = channels // (n_y * n_z * n_c * n_x)
+    rows = share * 9
+    parts = weight.reshape(n_y, n_z, n_c, n_x, rows, channels)
+    vectors = jnp.stack([bias, proj])
+    core = lax.axis_index("lat_2")
+    own = jnp.where(core == 0, parts[:, :, 0], parts[:, :, 1])
+    other = jnp.where(core == 0, parts[:, :, 1], parts[:, :, 0])
+    sent = jnp.concatenate(
+        [other.astype(jnp.bfloat16).reshape(-1, channels), two_pieces(vectors)], axis=0
+    )
+    got = lax.ppermute(sent, "lat_2", [(0, 1), (1, 0)])
+    own = own + got[:-4].astype(jnp.float32).reshape(own.shape)
+    vectors = vectors + from_pieces(got[-4:])
+    by_peer = own.transpose(0, 2, 1, 3, 4).reshape(n_y * n_x, n_z * rows, channels)
+    extra = jnp.broadcast_to(two_pieces(vectors)[None], (n_y * n_x, 4, channels))
+    sent = jnp.concatenate([by_peer.astype(jnp.bfloat16), extra], axis=1)
+    got = lax.all_to_all(sent, ("lat_0", "lon"), 0, 0, tiled=True)
+    own = got[:, :-4].astype(jnp.float32).sum(axis=0).reshape(n_z, rows, channels)
+    vectors = from_pieces(got[:, -4:]).sum(axis=0)
+    n_d = lax.axis_size("dp")
+    sent = jnp.concatenate([own, jnp.broadcast_to(vectors[None], (n_z, 2, channels))], axis=1)
+    sent = jnp.broadcast_to(sent[:, None], (n_z, n_d, rows + 2, channels))
+    sent = sent.reshape(n_z * n_d, rows + 2, channels)
+    total = lax.all_to_all(sent, ("lat_1", "dp"), 0, 0, tiled=True).sum(axis=0)
+    return total[:rows].reshape(share, 3, 3, channels), total[rows], total[rows + 1]
 
 
 def operate(field_ext, mask_ext, depth_ext):
@@ -171,7 +213,6 @@
                 preferred_element_type=jnp.float32,
             )
     grad_hidden = backed.reshape(samples, lat_rows, lon_cols, channels).astype(jnp.bfloat16)
-    share = channels // lax.axis_size(LAT_LON)
     blocks = []
     for shifted_cols in shifted:
         blocks.append(
@@ -179,17 +220,8 @@
                 shifted_cols, grad_pre, (((0,), (0,)), ((), ())), preferred_element_type=jnp.float32
             )
         )
-    spatial = sent_and_summed(
-        jnp.stack(blocks, axis=1)
-        .reshape(share * lax.axis_size(LAT_LON), 3, 3, channels)
-        .astype(jnp.bfloat16),
-        LAT_LON,
-        0,
-    )
-    own_weight = over_copies(spatial, "dp")
-    total_bias, total_proj = (
-        one_axis_at_a_time(local_bias, DP_LAT_LON),
-        one_axis_at_a_time(local_proj, DP_LAT_LON),
+    own_weight, total_bias, total_proj = all_summed(
+        jnp.stack(blocks, axis=1), local_bias, local_proj
     )
     all_cells = cell_count * lax.axis_size("dp") * lax.axis_size(LAT) * lax.axis_size("lon")
     grad_scale = 1.0 / math.sqrt(all_cells)

time: 232 us -> 185 us (0.80)
  the two profiles are of different devices: /device:TPU:2 before, /device:TPU:32 now
where the time goes in v1:
time: 185 us; the launch traced here: 183 us
  starting transfers between devices  81.8 us (44%)
  waiting for transfers between devices  47.8 us (26%)
  other arithmetic  25.8 us (14%)
  matrix products  13.6 us (7%)
  local copies, waits for them, and re-layouts  11.5 us (6%)
  between operations  2.59 us (1%)
    ppermute x6, starting transfers between devices, extended(): lax.ppermute(tail, axis, [(i, (i + 1) % count) for i in range(ends)])  22.5 us
    all_to_all x1, starting transfers between devices, from_everyone(): lax.all_to_all(jnp.broadcast_to(shard[None], (peers, *shard.shape)), axis...  20.3 us
    ppermute x6, starting transfers between devices, extended(): lax.ppermute(head, axis, [((i + 1) % count, i) for i in range(ends)])  16.1 us
    all_to_all x1, waiting for transfers between devices, all_summed(): total = lax.all_to_all(sent, ('lat_1', 'dp'), 0, 0, tiled=True).sum(axis=0)  12.8 us
    all_to_all x1, waiting for transfers between devices, from_everyone(): lax.all_to_all(jnp.broadcast_to(shard[None], (peers, *shard.shape)), axis...  12 us
    ppermute x6, waiting for transfers between devices, extended(): lax.ppermute(head, axis, [((i + 1) % count, i) for i in range(ends)])  11.8 us
    all_to_all x1, starting transfers between devices, all_summed(): total = lax.all_to_all(sent, ('lat_1', 'dp'), 0, 0, tiled=True).sum(axis=0)  9.95 us
    add x4, other arithmetic, solve_steps(): direction = residual + step_beta[turn_index] * direction  9.61 us
  transfers between devices with their start and end apart: 16, of which 7 were waited for; matrix products, arithmetic and copies ran while one was open for 18% of the time, Pallas kernels for 0%

profile of v1, /device:TPU:32, one launch (start us, length us, event | category | flops | bytes accessed | tf_op | source)
XLA Modules:
  0.0 183.1 jit_solution(14712813666630558869)
XLA Ops:
  5.3 20.3 %all-to-all-start = ((f32[64,1,2]{2,1,0:T(1,128)}), f32[64,1,2]{2,1,0:T(1,128)S(1)}, u32[]{:S(2)}, u32[]{:S(2)}) async-start(f32[64,1,2]{2,1,0:T(1,128)} %broadcast_in_dim.21), calls=%async_computation | async-start | bytes 65536 | tf_op jit(solution)/shard_map/all_to_all | solution.py:21
  26.3 1.9 %collective-permute-start.4 = (bf16[1,1,128,128]{3,2,1,0:T(8,128)(2,1)S(1)}, bf16[1,1,128,128]{3,2,1,0:T(8,128)(2,1)S(1)}, u32[]{:S(2)}, u32[]{:S(2)}) collective-permute-start(bf16[1,1,128,128]{3,2,1,0:T(8,128)(2,1)S(1)} %get-tuple-element.63), channel_id=1, source_target_pairs={{0,4},{4,8},{8,12},{12,16},{16,20},{20,24},{24,28},{28,32},{32,36}... | collective-permute-start | bytes 98312 | tf_op jit(solution)/shard_map/ppermute | solution.py:47
  30.3 12.0 %all-to-all-done = f32[64,1,2]{2,1,0:T(1,128)S(1)} async-done(((f32[64,1,2]{2,1,0:T(1,128)}), f32[64,1,2]{2,1,0:T(1,128)S(1)}, u32[]{:S(2)}, u32[]{:S(2)}) %all-to-all-start) | async-done | bytes 544 | tf_op jit(solution)/shard_map/all_to_all | solution.py:21
  45.7 1.7 collective-permute-start
  50.3 9.4 %collective-permute-done.1 = f32[3,5,128]{2,1,0:T(8,128)S(1)} collective-permute-done((f32[3,5,128]{2,1,0:T(8,128)S(1)}, f32[3,5,128]{2,1,0:T(8,128)S(1)}, u32[]{:S(2)}, u32[]{:S(2)}) %collective-permute-start.1) | collective-permute-done | bytes 7712 | tf_op jit(solution)/shard_map/ppermute | solution.py:49
  60.4 3.4 %collective-permute-start.2 = (f32[3,26,5]{2,1,0:T(8,128)S(1)}, f32[3,26,5]{2,1,0:T(8,128)S(1)}, u32[]{:S(2)}, u32[]{:S(2)}) collective-permute-start(f32[3,26,5]{2,1,0:T(8,128)S(1)} %get-tuple-element.68), channel_id=1, source_target_pairs={{0,1},{1,2},{2,3},{3,0},{4,5},{5,6},{6,7},{7,4},{8,9},{9,10},{10,1... | collective-permute-start | bytes 4688 | tf_op jit(solution)/shard_map/ppermute | solution.py:47
  63.8 3.7 %collective-permute-start.3 = (f32[3,26,5]{2,1,0:T(8,128)S(1)}, f32[3,26,5]{2,1,0:T(8,128)S(1)}, u32[]{:S(2)}, u32[]{:S(2)}) collective-permute-start(f32[3,26,5]{2,1,0:T(8,128)S(1)} %get-tuple-element.69), channel_id=1, source_target_pairs={{1,0},{2,1},{3,2},{0,3},{5,4},{6,5},{7,6},{4,7},{9,8},{10,9},{11,1... | collective-permute-start | bytes 4688 | tf_op jit(solution)/shard_map/ppermute | solution.py:49
  72.1 2.8 %multiply_add_fusion.2 = f32[1,26,138]{2,1,0:T(8,128)S(1)} fusion(f32[26,138]{1,0:T(8,128)S(1)} %get-tuple-element.32, f32[26,138]{1,0:T(8,128)S(1)} %get-tuple-element.31, f32[26,138]{1,0:T(8,128)S(1)} %get-tuple-element.30, f32[26,138]{1,0:T(8,128)S(1)} %get-tuple-element.29, f32[1,26,138]{2,1,0:T(8,128)S(1)} %get-tuple-element.67, ...), kind=kLoop, calls=%fused_computation.160 | loop fusion | flops 129168 | bytes 114832 | tf_op jit(solution)/shard_map/add | solution.py:139
  74.9 3.3 %multiply_add_fusion.1 = (f32[1,26,138]{2,1,0:T(8,128)S(1)}, f32[1,26,138]{2,1,0:T(8,128)S(1)}) fusion(f32[1,26,138]{2,1,0:T(8,128)S(1)} %multiply_add_fusion.2, f32[]{:T(128)} %bitcast.17, f32[]{:T(128)} %bitcast.14, f32[1,26,138]{2,1,0:T(8,128)S(1)} %get-tuple-element.28, f32[1,26,138]{2,1,0:T(8,128)S(1)} %get-tuple-element.67, f32[]{:T(128)} %bitcast.13, ...), kind=kLoop, calls=%fused_computation.155 | loop fusion | flops 186576 | bytes 143540 | tf_op jit(solution)/shard_map/add | solution.py:139
  78.2 2.0 %multiply_add_fusion = (f32[1,26,138]{2,1,0:T(8,128)S(1)}, f32[1,26,138]{2,1,0:T(8,128)S(1)}) fusion(f32[1,26,138]{2,1,0:T(8,128)S(1)} %get-tuple-element.27, f32[1,26,138]{2,1,0:T(8,128)S(1)} %multiply_add_fusion.2, f32[]{:T(128)} %bitcast.19, f32[]{:T(128)} %bitcast.17, f32[1,26,138]{2,1,0:T(8,128)S(1)} %get-tuple-element.26, ...), kind=kLoop, calls=%fused_computation.150 | loop fusion | flops 71760 | bytes 143532 | tf_op jit(solution)/shard_map/add | solution.py:139
  80.4 4.6 %fusion.104 = f32[2048]{0:T(1024)S(1)} fusion(f32[1,26,138]{2,1,0:T(8,128)S(1)} %get-tuple-element.25, f32[1,26,138]{2,1,0:T(8,128)S(1)} %get-tuple-element.26, f32[1,26,138]{2,1,0:T(8,128)S(1)} %multiply_add_fusion.2, f32[1,26,138]{2,1,0:T(8,128)S(1)} %fusion.59, f32[1,26,138]{2,1,0:T(8,128)S(1)} %get-tuple-element.64, ...), kind=kLoop, calls=%fused_computation.204 | loop fusion | flops 36864 | bytes 81948 | tf_op jit(solution)/shard_map/mul | solution.py:196
  85.4 3.4 %collective-permute-start.6 = (bf16[1,18,1,128]{3,2,1,0:T(2,128)(2,1)S(1)}, bf16[1,18,1,128]{3,2,1,0:T(2,128)(2,1)S(1)}, u32[]{:S(2)}, u32[]{:S(2)}) collective-permute-start(bf16[1,18,1,128]{3,2,1,0:T(2,128)(2,1)S(1)} %get-tuple-element.53), channel_id=1, source_target_pairs={{0,1},{1,2},{2,3},{3,0},{4,5},{5,6},{6,7},{7,4},{8,9},{9,10},{10,1... | collective-permute-start | bytes 13832 | tf_op jit(solution)/shard_map/ppermute | solution.py:47
  88.8 3.7 %collective-permute-start.7 = (bf16[1,18,1,128]{3,2,1,0:T(2,128)(2,1)S(1)}, bf16[1,18,1,128]{3,2,1,0:T(2,128)(2,1)S(1)}, u32[]{:S(2)}, u32[]{:S(2)}) collective-permute-start(bf16[1,18,1,128]{3,2,1,0:T(2,128)(2,1)S(1)} %get-tuple-element.54), channel_id=1, source_target_pairs={{1,0},{2,1},{3,2},{0,3},{5,4},{6,5},{7,6},{4,7},{9,8},{10,9},{11,1... | collective-permute-start | bytes 13832 | tf_op jit(solution)/shard_map/ppermute | solution.py:49
  92.8 1.6 collective-permute-done.7
  102.4 10.2 %collective-permute-start.8 = (bf16[1,1,128,128]{3,2,1,0:T(8,128)(2,1)S(1)}, bf16[1,1,128,128]{3,2,1,0:T(8,128)(2,1)S(1)}, u32[]{:S(2)}, u32[]{:S(2)}) collective-permute-start(bf16[1,1,128,128]{3,2,1,0:T(8,128)(2,1)S(1)} %get-tuple-element.57), channel_id=1, source_target_pairs={{0,4},{4,8},{8,12},{12,16},{16,20},{20,24},{24,28},{28,32},{32,36}... | collective-permute-start | bytes 98312 | tf_op jit(solution)/shard_map/ppermute | solution.py:47
  114.0 5.6 %collective-permute-start.12 = (bf16[580,128]{1,0:T(8,128)(2,1)S(1)}, bf16[580,128]{1,0:T(8,128)(2,1)S(1)}, u32[]{:S(2)}, u32[]{:S(2)}) collective-permute-start(bf16[580,128]{1,0:T(8,128)(2,1)S(1)} %pad_maximum_fusion.8), channel_id=1, source_target_pairs={{0,4},{4,0},{1,5},{5,1},{2,6},{6,2},{3,7},{7,3},{8,12},{12,8},{9,1... | collective-permute-start | bytes 445448 | tf_op jit(solution)/shard_map/ppermute | solution.py:97
  119.6 4.9 %collective-permute-start.10 = (bf16[1,18,1,128]{3,2,1,0:T(2,128)(2,1)S(1)}, bf16[1,18,1,128]{3,2,1,0:T(2,128)(2,1)S(1)}, u32[]{:S(2)}, u32[]{:S(2)}) collective-permute-start(bf16[1,18,1,128]{3,2,1,0:T(2,128)(2,1)S(1)} %get-tuple-element.48), channel_id=1, source_target_pairs={{1,0},{2,1},{3,2},{0,3},{5,4},{6,5},{7,6},{4,7},{9,8},{10,9},{11,1... | collective-permute-start | bytes 13832 | tf_op jit(solution)/shard_map/ppermute | solution.py:49
  124.6 1.9 %collective-permute-start.11 = (bf16[1,18,1,128]{3,2,1,0:T(2,128)(2,1)S(1)}, bf16[1,18,1,128]{3,2,1,0:T(2,128)(2,1)S(1)}, u32[]{:S(2)}, u32[]{:S(2)}) collective-permute-start(bf16[1,18,1,128]{3,2,1,0:T(2,128)(2,1)S(1)} %get-tuple-element.49), channel_id=1, source_target_pairs={{0,1},{1,2},{2,3},{3,0},{4,5},{5,6},{6,7},{7,4},{8,9},{9,10},{10,1... | collective-permute-start | bytes 13832 | tf_op jit(solution)/shard_map/ppermute | solution.py:47
  126.9 4.4 %collective-permute-done.11 = bf16[1,18,1,128]{3,2,1,0:T(2,128)(2,1)S(1)} collective-permute-done((bf16[1,18,1,128]{3,2,1,0:T(2,128)(2,1)S(1)}, bf16[1,18,1,128]{3,2,1,0:T(2,128)(2,1)S(1)}, u32[]{:S(2)}, u32[]{:S(2)}) %collective-permute-start.11) | collective-permute-done | bytes 4640 | tf_op jit(solution)/shard_map/ppermute | solution.py:47
  138.9 7.3 %all-to-all-start.1 = ((bf16[16,40,128]{2,1,0:T(8,128)(2,1)}), bf16[16,40,128]{2,1,0:T(8,128)(2,1)S(1)}, u32[]{:S(2)}, u32[]{:S(2)}) async-start(bf16[16,40,128]{2,1,0:T(8,128)(2,1)} %copy.28), calls=%async_computation.1 | async-start | bytes 327680 | tf_op jit(solution)/shard_map/all_to_all | solution.py:103
  147.6 6.8 %all-to-all-done.1 = bf16[16,40,128]{2,1,0:T(8,128)(2,1)S(1)} async-done(((bf16[16,40,128]{2,1,0:T(8,128)(2,1)}), bf16[16,40,128]{2,1,0:T(8,128)(2,1)S(1)}, u32[]{:S(2)}, u32[]{:S(2)}) %all-to-all-start.1) | async-done | bytes 163872 | tf_op jit(solution)/shard_map/all_to_all | solution.py:103
  155.2 9.9 %all-to-all-start.2 = ((f32[16,20,128]{2,1,0:T(8,128)}), f32[16,20,128]{2,1,0:T(8,128)S(1)}, u32[]{:S(2)}, u32[]{:S(2)}) async-start(f32[16,20,128]{2,1,0:T(8,128)} %bitcast.66), calls=%async_computation.2 | async-start | bytes 393216 | tf_op jit(solution)/shard_map/all_to_all | solution.py:110
  167.3 1.9 %fusion.4 = bf16[2048,128]{1,0:T(8,128)(2,1)} fusion(f32[2048,128]{1,0:T(8,128)S(1)} %fusion.20, f32[2048,128]{1,0:T(8,128)S(1)} %convolution_add_fusion.1, bf16[2048,128]{1,0:T(8,128)(2,1)S(1)} %bitcast.371, bf16[3,3,128,128]{3,2,1,0:T(8,128)(2,1)} %param.10), kind=kOutput, calls=%fused_computation.17 | convolution fusion | flops 67895296 | bytes 3178496 | tf_op jit(solution)/shard_map/dot_general | solution.py:209
  169.1 12.8 %all-to-all-done.2 = f32[16,20,128]{2,1,0:T(8,128)S(1)} async-done(((f32[16,20,128]{2,1,0:T(8,128)}), f32[16,20,128]{2,1,0:T(8,128)S(1)}, u32[]{:S(2)}, u32[]{:S(2)}) %all-to-all-start.2) | async-done | bytes 163872 | tf_op jit(solution)/shard_map/all_to_all | solution.py:110
  (111 shorter events, 41.0 us)
Async XLA Ops:
  5.3 37.0 %all-to-all-start = ((f32[64,1,2]{2,1,0:T(1,128)}), f32[64,1,2]{2,1,0:T(1,128)S(1)}, u32[]{:S(2)}, u32[]{:S(2)}) async-start(f32[64,1,2]{2,1,0:T(1,128)} %broadcast_in_dim.21), calls=%async_computation | async-start | bytes 65536 | tf_op jit(solution)/shard_map/all_to_all | solution.py:21
  26.3 58.6 %collective-permute-start.4 = (bf16[1,1,128,128]{3,2,1,0:T(8,128)(2,1)S(1)}, bf16[1,1,128,128]{3,2,1,0:T(8,128)(2,1)S(1)}, u32[]{:S(2)}, u32[]{:S(2)}) collective-permute-start(bf16[1,1,128,128]{3,2,1,0:T(8,128)(2,1)S(1)} %get-tuple-element.63), channel_id=1, source_target_pairs={{0,4},{4,8},{8,12},{12,16},{16,20},{20,24},{24,28},{28,32},{32,36}... | collective-permute-start | bytes 98312 | tf_op jit(solution)/shard_map/ppermute | solution.py:47
  28.3 56.7 %collective-permute-start.5 = (bf16[1,1,128,128]{3,2,1,0:T(8,128)(2,1)S(1)}, bf16[1,1,128,128]{3,2,1,0:T(8,128)(2,1)S(1)}, u32[]{:S(2)}, u32[]{:S(2)}) collective-permute-start(bf16[1,1,128,128]{3,2,1,0:T(8,128)(2,1)S(1)} %get-tuple-element.62), channel_id=1, source_target_pairs={{4,0},{8,4},{12,8},{16,12},{20,16},{24,20},{28,24},{32,28},{36,32}... | collective-permute-start | bytes 98312 | tf_op jit(solution)/shard_map/ppermute | solution.py:49
  45.7 4.6 %collective-permute-start = (f32[3,5,128]{2,1,0:T(8,128)S(1)}, f32[3,5,128]{2,1,0:T(8,128)S(1)}, u32[]{:S(2)}, u32[]{:S(2)}) collective-permute-start(f32[3,5,128]{2,1,0:T(8,128)S(1)} %get-tuple-element.70), channel_id=1, source_target_pairs={{0,4},{4,8},{8,12},{12,16},{16,20},{20,24},{24,28},{28,32},{32,36}... | collective-permute-start | bytes 23048 | tf_op jit(solution)/shard_map/ppermute | solution.py:47
  47.4 12.2 %collective-permute-start.1 = (f32[3,5,128]{2,1,0:T(8,128)S(1)}, f32[3,5,128]{2,1,0:T(8,128)S(1)}, u32[]{:S(2)}, u32[]{:S(2)}) collective-permute-start(f32[3,5,128]{2,1,0:T(8,128)S(1)} %get-tuple-element.71), channel_id=1, source_target_pairs={{4,0},{8,4},{12,8},{16,12},{20,16},{24,20},{28,24},{32,28},{36,32}... | collective-permute-start | bytes 23048 | tf_op jit(solution)/shard_map/ppermute | solution.py:49
  60.4 20.0 %copy-start.3 = (s32[16,128]{1,0:T(8,128)S(1)}, s32[16,128]{1,0:T(8,128)}, u32[]{:S(2)}) copy-start(s32[16,128]{1,0:T(8,128)} %param.14) | copy-start | bytes 24580
  60.4 8.5 %collective-permute-start.2 = (f32[3,26,5]{2,1,0:T(8,128)S(1)}, f32[3,26,5]{2,1,0:T(8,128)S(1)}, u32[]{:S(2)}, u32[]{:S(2)}) collective-permute-start(f32[3,26,5]{2,1,0:T(8,128)S(1)} %get-tuple-element.68), channel_id=1, source_target_pairs={{0,1},{1,2},{2,3},{3,0},{4,5},{5,6},{6,7},{7,4},{8,9},{9,10},{10,1... | collective-permute-start | bytes 4688 | tf_op jit(solution)/shard_map/ppermute | solution.py:47
  63.8 6.0 %collective-permute-start.3 = (f32[3,26,5]{2,1,0:T(8,128)S(1)}, f32[3,26,5]{2,1,0:T(8,128)S(1)}, u32[]{:S(2)}, u32[]{:S(2)}) collective-permute-start(f32[3,26,5]{2,1,0:T(8,128)S(1)} %get-tuple-element.69), channel_id=1, source_target_pairs={{1,0},{2,1},{3,2},{0,3},{5,4},{6,5},{7,6},{4,7},{9,8},{10,9},{11,1... | collective-permute-start | bytes 4688 | tf_op jit(solution)/shard_map/ppermute | solution.py:49
  69.0 16.1 %copy-start = (bf16[1,16,128,128]{3,2,1,0:T(8,128)(2,1)S(1)}, bf16[1,16,128,128]{3,2,1,0:T(8,128)(2,1)}, u32[]{:S(2)}) copy-start(bf16[1,16,128,128]{3,2,1,0:T(8,128)(2,1)} %param.9) | copy-start | bytes 1572868
  85.0 7.5 %copy-start.2 = (bf16[3,3,128,128]{3,2,1,0:T(8,128)(2,1)S(1)}, bf16[3,3,128,128]{3,2,1,0:T(8,128)(2,1)}, u32[]{:S(2)}) copy-start(bf16[3,3,128,128]{3,2,1,0:T(8,128)(2,1)} %param.10) | copy-start | bytes 884740
  85.4 7.4 %collective-permute-start.6 = (bf16[1,18,1,128]{3,2,1,0:T(2,128)(2,1)S(1)}, bf16[1,18,1,128]{3,2,1,0:T(2,128)(2,1)S(1)}, u32[]{:S(2)}, u32[]{:S(2)}) collective-permute-start(bf16[1,18,1,128]{3,2,1,0:T(2,128)(2,1)S(1)} %get-tuple-element.53), channel_id=1, source_target_pairs={{0,1},{1,2},{2,3},{3,0},{4,5},{5,6},{6,7},{7,4},{8,9},{9,10},{10,1... | collective-permute-start | bytes 13832 | tf_op jit(solution)/shard_map/ppermute | solution.py:47
  88.8 5.6 %collective-permute-start.7 = (bf16[1,18,1,128]{3,2,1,0:T(2,128)(2,1)S(1)}, bf16[1,18,1,128]{3,2,1,0:T(2,128)(2,1)S(1)}, u32[]{:S(2)}, u32[]{:S(2)}) collective-permute-start(bf16[1,18,1,128]{3,2,1,0:T(2,128)(2,1)S(1)} %get-tuple-element.54), channel_id=1, source_target_pairs={{1,0},{2,1},{3,2},{0,3},{5,4},{6,5},{7,6},{4,7},{9,8},{10,9},{11,1... | collective-permute-start | bytes 13832 | tf_op jit(solution)/shard_map/ppermute | solution.py:49
  95.5 0.7 copy-start.5
  97.3 0.7 copy-start.6
  102.4 17.2 %collective-permute-start.8 = (bf16[1,1,128,128]{3,2,1,0:T(8,128)(2,1)S(1)}, bf16[1,1,128,128]{3,2,1,0:T(8,128)(2,1)S(1)}, u32[]{:S(2)}, u32[]{:S(2)}) collective-permute-start(bf16[1,1,128,128]{3,2,1,0:T(8,128)(2,1)S(1)} %get-tuple-element.57), channel_id=1, source_target_pairs={{0,4},{4,8},{8,12},{12,16},{16,20},{20,24},{24,28},{28,32},{32,36}... | collective-permute-start | bytes 98312 | tf_op jit(solution)/shard_map/ppermute | solution.py:47
  112.6 7.0 %collective-permute-start.9 = (bf16[1,1,128,128]{3,2,1,0:T(8,128)(2,1)S(1)}, bf16[1,1,128,128]{3,2,1,0:T(8,128)(2,1)S(1)}, u32[]{:S(2)}, u32[]{:S(2)}) collective-permute-start(bf16[1,1,128,128]{3,2,1,0:T(8,128)(2,1)S(1)} %get-tuple-element.58), channel_id=1, source_target_pairs={{4,0},{8,4},{12,8},{16,12},{20,16},{24,20},{28,24},{32,28},{36,32}... | collective-permute-start | bytes 98312 | tf_op jit(solution)/shard_map/ppermute | solution.py:49
  114.0 20.9 %collective-permute-start.12 = (bf16[580,128]{1,0:T(8,128)(2,1)S(1)}, bf16[580,128]{1,0:T(8,128)(2,1)S(1)}, u32[]{:S(2)}, u32[]{:S(2)}) collective-permute-start(bf16[580,128]{1,0:T(8,128)(2,1)S(1)} %pad_maximum_fusion.8), channel_id=1, source_target_pairs={{0,4},{4,0},{1,5},{5,1},{2,6},{6,2},{3,7},{7,3},{8,12},{12,8},{9,1... | collective-permute-start | bytes 445448 | tf_op jit(solution)/shard_map/ppermute | solution.py:97
  119.6 7.2 %collective-permute-start.10 = (bf16[1,18,1,128]{3,2,1,0:T(2,128)(2,1)S(1)}, bf16[1,18,1,128]{3,2,1,0:T(2,128)(2,1)S(1)}, u32[]{:S(2)}, u32[]{:S(2)}) collective-permute-start(bf16[1,18,1,128]{3,2,1,0:T(2,128)(2,1)S(1)} %get-tuple-element.48), channel_id=1, source_target_pairs={{1,0},{2,1},{3,2},{0,3},{5,4},{6,5},{7,6},{4,7},{9,8},{10,9},{11,1... | collective-permute-start | bytes 13832 | tf_op jit(solution)/shard_map/ppermute | solution.py:49
  124.6 6.8 %collective-permute-start.11 = (bf16[1,18,1,128]{3,2,1,0:T(2,128)(2,1)S(1)}, bf16[1,18,1,128]{3,2,1,0:T(2,128)(2,1)S(1)}, u32[]{:S(2)}, u32[]{:S(2)}) collective-permute-start(bf16[1,18,1,128]{3,2,1,0:T(2,128)(2,1)S(1)} %get-tuple-element.49), channel_id=1, source_target_pairs={{0,1},{1,2},{2,3},{3,0},{4,5},{5,6},{6,7},{7,4},{8,9},{9,10},{10,1... | collective-permute-start | bytes 13832 | tf_op jit(solution)/shard_map/ppermute | solution.py:47
  134.9 0.7 copy-start.4
  138.9 15.5 %all-to-all-start.1 = ((bf16[16,40,128]{2,1,0:T(8,128)(2,1)}), bf16[16,40,128]{2,1,0:T(8,128)(2,1)S(1)}, u32[]{:S(2)}, u32[]{:S(2)}) async-start(bf16[16,40,128]{2,1,0:T(8,128)(2,1)} %copy.28), calls=%async_computation.1 | async-start | bytes 327680 | tf_op jit(solution)/shard_map/all_to_all | solution.py:103
  155.2 11.0 %copy-start.1 = (bf16[1,16,128,128]{3,2,1,0:T(8,128)(2,1)S(1)}, bf16[1,16,128,128]{3,2,1,0:T(8,128)(2,1)}, u32[]{:S(2)}) copy-start(bf16[1,16,128,128]{3,2,1,0:T(8,128)(2,1)} %get-tuple-element.34) | copy-start | bytes 1572868
  155.2 26.7 %all-to-all-start.2 = ((f32[16,20,128]{2,1,0:T(8,128)}), f32[16,20,128]{2,1,0:T(8,128)S(1)}, u32[]{:S(2)}, u32[]{:S(2)}) async-start(f32[16,20,128]{2,1,0:T(8,128)} %bitcast.66), calls=%async_computation.2 | async-start | bytes 393216 | tf_op jit(solution)/shard_map/all_to_all | solution.py:110

commit v2 on v1

v2 whole, which is shorter than its diff:
```python
import functools
import math

import jax
import jax.numpy as jnp
from jax import lax
from jax.experimental import pallas as pl
from jax.experimental.pallas import tpu as pltpu
from jax.sharding import Mesh
from jax.sharding import PartitionSpec as P

ITERS = 6
REACH = 6
LAT_LON = ("lat_0", "lat_1", "lat_2", "lon")
LAT = ("lat_0", "lat_1", "lat_2")
WIDE = 144
PACK = 32

helm_coef = 0.5
VMEM = pl.BlockSpec(memory_space=pltpu.VMEM)
SMEM = pl.BlockSpec(memory_space=pltpu.SMEM)


def pieces_of(values, count):
    out = []
    for _ in range(count):
        piece = lax.reduce_precision(values, 8, 7)
        out.append(piece.astype(jnp.bfloat16))
        values = values - piece
    return out


def forward_kernel(
    hidden_ref, edge_ref, ends_ref, fields_ref, weight_ref, bias_ref, alpha_ref, beta_ref,
    ext_ref, preact_ref, force_ref, rhs_ref,
):
    rows = hidden_ref.shape[0]
    ext_ref[0:2] = ends_ref[0:2]
    ext_ref[2 : rows + 2, 0:128] = hidden_ref[...]
    ext_ref[2 : rows + 2, 128:WIDE] = edge_ref[...]
    ext_ref[rows + 2 : rows + 4] = ends_ref[2:4]
    for a in range(3):
        for c in range(3):
            rhs_ref[a * 128 : a * 128 + 128, c * 128 : c * 128 + 128] = weight_ref[a, c]

    total = [
        fields_ref[0, k].astype(jnp.float32)
        + fields_ref[1, k].astype(jnp.float32)
        + fields_ref[2, k].astype(jnp.float32)
        for k in range(2)
    ]
    start, wet_depth = total
    mask = jnp.where(wet_depth > 0.0, 1.0, 0.0)
    lane = lax.broadcasted_iota(jnp.int32, (2 * PACK, 128), 1)

    def other_half(field):
        parts = [field[k * PACK : (k + 1) * PACK] for k in range(field.shape[0] // PACK)]
        swapped = []
        for k in range(0, len(parts), 2):
            swapped += [parts[k + 1], parts[k]]
        return jnp.concatenate(swapped, axis=0)

    def beside(field):
        count = field.shape[0]
        lanes = lane if count == 2 * PACK else jnp.concatenate([lane, lane], axis=0)
        up = pltpu.roll(field, 1, 0)
        down = pltpu.roll(field, count - 1, 0)
        from_left = pltpu.roll(field, 1, 1)
        from_left = jnp.where(lanes == 0, other_half(from_left), from_left)
        from_right = pltpu.roll(field, 127, 1)
        from_right = jnp.where(lanes == 127, other_half(from_right), from_right)
        return up, down, from_left, from_right

    weights = [
        0.5 * (near_mask * wet_depth + mask * near_depth)
        for near_mask, near_depth in zip(beside(mask), beside(wet_depth))
    ]
    diagonal = helm_coef * mask + weights[0] + weights[1] + weights[2] + weights[3]
    weights = [jnp.concatenate([w, w], axis=0) for w in weights]
    diagonal = jnp.concatenate([diagonal, diagonal], axis=0)
    residual = jnp.concatenate([start, mask], axis=0)
    direction = residual
    result = jnp.zeros_like(residual)
    for k in range(ITERS):
        result = result + alpha_ref[k] * direction
        if k + 1 < ITERS:
            applied = diagonal * direction
            for w, near in zip(weights, beside(direction)):
                applied = applied - w * near
            residual = residual - alpha_ref[k] * applied
            direction = residual + beta_ref[k] * direction
    result = result * jnp.concatenate([mask, mask], axis=0)
    force_ref[...] = result.T

    group = 6
    bias = bias_ref[...]
    for g in range(0, rows + 2, group):
        lhs = jnp.concatenate(
            [ext_ref[g + a : g + a + group].reshape(group * WIDE, 128) for a in range(3)], axis=1
        )
        out = jnp.dot(lhs, rhs_ref[...], preferred_element_type=jnp.float32)
        for j in range(group):
            part = out[j * WIDE : (j + 1) * WIDE]
            preact_ref[g + j] = (
                pltpu.roll(part[:, 0:128], 1, 0)
                + part[:, 128:256]
                + pltpu.roll(part[:, 256:384], WIDE - 1, 0)
                + bias
            )


def backward_kernel(
    mean_ref, preact_ref, force_ref, ext_ref, proj_ref,
    grad_ref, weight_ref, vectors_ref, moved_ref,
):
    rows = grad_ref.shape[0] - 2
    force = force_ref[...]
    force = force - mean_ref[0] * pltpu.roll(force, 64, 1)
    proj = proj_ref[...]
    sum_bias = jnp.zeros((8, 128), jnp.float32)
    sum_proj = jnp.zeros((8, 128), jnp.float32)
    for g in range(rows + 2):
        at = g + REACH - 1
        column = jnp.concatenate(
            [
                force[:, at : at + 1],
                force[0:8, PACK + at : PACK + at + 1],
                force[120:128, PACK + at : PACK + at + 1],
            ],
            axis=0,
        )
        column = jnp.broadcast_to(column, (WIDE, 128))
        preact = preact_ref[g]
        sigma = jax.nn.sigmoid(preact)
        active = preact * sigma
        slope_act = sigma * (1.0 + preact * (1.0 - sigma))
        grad = (column * proj * slope_act).astype(jnp.bfloat16)
        grad_ref[g] = grad
        if 1 <= g <= rows:
            own = grad.astype(jnp.float32)[0:128]
            for k in range(16):
                sum_bias = sum_bias + own[k * 8 : k * 8 + 8]
                sum_proj = sum_proj + (active * column)[k * 8 : k * 8 + 8]
            own = jnp.concatenate([own, jnp.zeros((WIDE - 128, 128), jnp.float32)], axis=0)
            moved_ref[g - 1, :, 0:128] = pltpu.roll(own, WIDE - 1, 0).astype(jnp.bfloat16)
            moved_ref[g - 1, :, 128:256] = own.astype(jnp.bfloat16)
            moved_ref[g - 1, :, 256:384] = pltpu.roll(own, 1, 0).astype(jnp.bfloat16)
    vectors_ref[0:1] = jnp.sum(sum_bias, axis=0, keepdims=True)
    vectors_ref[1:2] = jnp.sum(sum_proj, axis=0, keepdims=True)
    moved = moved_ref[...].reshape(rows * WIDE, 384)
    for a in range(3):
        cells = ext_ref[a + 1 : a + 1 + rows].reshape(rows * WIDE, 128)
        out = lax.dot_general(
            cells, moved, (((0,), (0,)), ((), ())), preferred_element_type=jnp.float32
        )
        for c in range(3):
            weight_ref[a * 3 + c] = out[:, c * 128 : c * 128 + 128]


def input_kernel(grad_ref, weight_ref, out_ref, rhs_ref):
    rows = out_ref.shape[0]
    for a in range(3):
        for c in range(3):
            rhs_ref[c * 128 : c * 128 + 128, a * 128 : a * 128 + 128] = weight_ref[a, c]
    group = 4
    for y in range(0, rows, group):
        lhs = jnp.concatenate(
            [
                grad_ref[y - a + 2 : y - a + 2 + group].reshape(group * WIDE, 128)
                for a in range(3)
            ],
            axis=1,
        )
        out = lax.dot_general(
            lhs, rhs_ref[...], (((1,), (1,)), ((), ())), preferred_element_type=jnp.float32
        )
        for j in range(group):
            part = out[j * WIDE : (j + 1) * WIDE]
            total = (
                pltpu.roll(part[:, 0:128], WIDE - 1, 0)
                + part[:, 128:256]
                + pltpu.roll(part[:, 256:384], 1, 0)
            )
            out_ref[y + j] = total[0:128].astype(jnp.bfloat16)


def call(kernel, shapes, scratch, in_specs, args, name):
    return pl.pallas_call(
        kernel,
        out_shape=shapes,
        in_specs=in_specs,
        out_specs=jax.tree.map(lambda _: VMEM, shapes),
        scratch_shapes=scratch,
        compiler_params=pltpu.CompilerParams(vmem_limit_bytes=40 * 1024 * 1024),
        name=name,
    )(*args)


def gathered_edges(hidden, fields):
    count = lax.axis_size("lon")
    me = lax.axis_index("lon")
    rows = hidden.shape[0]
    head = hidden[:, 0:2].reshape(1, 2 * rows, 128)
    tail = hidden[:, 126:128].reshape(1, 2 * rows, 128)
    peer = lax.broadcasted_iota(jnp.int32, (count, 1, 1), 0)
    columns = jnp.where(peer == (me + 1) % count, tail, head)
    flat = jnp.broadcast_to(fields.reshape(1, -1, 128), (count, 6 * rows, 128))
    sent = jnp.concatenate([columns, flat], axis=1)
    got = lax.all_to_all(sent, "lon", 0, 0, tiled=True)
    left = lax.dynamic_index_in_dim(got, (me + count - 1) % count, 0, keepdims=False)
    right = lax.dynamic_index_in_dim(got, (me + 1) % count, 0, keepdims=False)
    shape = (rows, 2, 128)
    edge = jnp.concatenate(
        [
            right[: 2 * rows].reshape(shape),
            jnp.zeros((rows, WIDE - 132, 128), jnp.bfloat16),
            left[: 2 * rows].reshape(shape),
        ],
        axis=1,
    )
    lane = lax.broadcasted_iota(jnp.int32, (1, 1, 128), 2)
    shape = (6, rows, 128)
    second = jnp.where(
        lane < 64, right[2 * rows :].reshape(shape), left[2 * rows :].reshape(shape)
    )
    every = got[:, 2 * rows :].reshape(count, 2, 3, rows, 128).astype(jnp.float32).sum(axis=2)
    summed = jnp.sum(every[:, 0])
    counted = jnp.sum(jnp.where(every[:, 1] > 0.0, 1.0, 0.0))
    return edge, second, summed, counted


def two_pieces(values):
    return jnp.concatenate(pieces_of(values, 2))


def from_pieces(pieces):
    both = pieces.astype(jnp.float32)
    count = both.shape[-2] // 2
    return both[..., :count, :] + both[..., count:, :]


def all_summed(weight, vectors):
    channels = weight.shape[1]
    n_y, n_z, n_c = (lax.axis_size(name) for name in LAT)
    n_x = lax.axis_size("lon")
    n_d = lax.axis_size("dp")
    share = channels // (n_y * n_z * n_c * n_x)
    parts = weight.reshape(9, n_y, n_z, n_c, n_x * share, channels)
    core = lax.axis_index("lat_2")
    own = jnp.where(core == 0, parts[:, :, :, 0], parts[:, :, :, 1])
    other = jnp.where(core == 0, parts[:, :, :, 1], parts[:, :, :, 0])
    sent = jnp.concatenate(
        [other.astype(jnp.bfloat16).reshape(-1, channels), two_pieces(vectors)], axis=0
    )
    got = lax.ppermute(sent, "lat_2", [(0, 1), (1, 0)])
    own = own + got[:-4].astype(jnp.float32).reshape(own.shape)
    vectors = vectors + from_pieces(got[-4:])
    rows = share * 9
    own = own.astype(jnp.bfloat16).reshape(9, n_y, n_z, n_x, share, channels)
    by_peer = own.transpose(1, 3, 2, 0, 4, 5).reshape(n_y * n_x, n_z * rows, channels)
    extra = jnp.broadcast_to(two_pieces(vectors)[None], (n_y * n_x, 4, channels))
    sent = jnp.concatenate([by_peer, extra], axis=1)
    got = lax.all_to_all(sent, ("lat_0", "lon"), 0, 0, tiled=True)
    own = got[:, :-4].astype(jnp.float32).sum(axis=0).reshape(n_z, rows, channels)
    vectors = from_pieces(got[:, -4:]).sum(axis=0)
    sent = jnp.concatenate([own, jnp.broadcast_to(vectors[None], (n_z, 2, channels))], axis=1)
    sent = jnp.broadcast_to(sent[:, None], (n_z, n_d, rows + 2, channels))
    sent = sent.reshape(n_z * n_d, rows + 2, channels)
    total = lax.all_to_all(sent, ("lat_1", "dp"), 0, 0, tiled=True).sum(axis=0)
    own = total[:rows].reshape(3, 3, share, channels).transpose(2, 0, 1, 3)
    return own, total[rows], total[rows + 1]


def shards(
    hidden_in, conv_weight, conv_bias, proj_weight, ocean_depth, sea_mask,
    step_alpha, step_beta, surface_cotangent,
):
    rows = hidden_in.shape[1]
    hidden = hidden_in[0]
    mask = sea_mask.astype(jnp.float32)
    fields = jnp.stack(
        pieces_of(mask * surface_cotangent[0], 3) + pieces_of(mask * ocean_depth, 3)
    )
    edge, second, summed, counted = gathered_edges(hidden, fields)
    fields = jnp.concatenate([fields[:, None], second[:, None]], axis=1)

    def outgoing(at, field_at):
        cells = jnp.concatenate([hidden[at : at + 2], edge[at : at + 2]], axis=1)
        near = fields[:, :, field_at : field_at + REACH]
        return cells.reshape(2 * WIDE, 128), near.reshape(12 * REACH, 128)

    n_lat = lax.axis_size(LAT)
    lat = lax.axis_index(LAT)
    upper = lax.axis_index("lat_2") == 0
    up, down = outgoing(0, 0), outgoing(rows - 2, rows - REACH)
    sums = jnp.broadcast_to(
        jnp.stack(pieces_of(summed, 3) + pieces_of(counted, 3))[:, None], (6, 128)
    )
    cross = jnp.concatenate([jnp.where(upper, u, d) for u, d in zip(up, down)] + [sums])
    pair = jnp.concatenate([jnp.where(upper, d, u) for u, d in zip(up, down)])
    odd = [(i, (i + 1) % n_lat) for i in range(1, n_lat, 2)]
    cross = lax.ppermute(cross, LAT, odd + [(j, i) for i, j in odd])
    pair = lax.ppermute(pair, "lat_2", [(0, 1), (1, 0)])
    got = cross[-6:, 0].astype(jnp.float32)
    sums = jnp.stack([summed + got[0] + got[1] + got[2], counted + got[3] + got[4] + got[5]])
    others = lax.axis_size(("lat_0", "lat_2"))
    sums = lax.all_to_all(
        jnp.broadcast_to(sums[None, :, None], (others, 2, 128)), ("lat_0", "lat_2"), 0, 0, tiled=True
    )
    sums = jnp.sum(sums[:, :, 0], axis=0)
    mean = (sums[0] / sums[1])[None]

    cross = cross[:-6]
    zero = jnp.zeros((), jnp.bfloat16)
    above = jnp.where(lat == 0, zero, jnp.where(upper, cross, pair))
    below = jnp.where(lat == n_lat - 1, zero, jnp.where(upper, pair, cross))
    split_at = 2 * WIDE
    ends = jnp.concatenate([above[:split_at], below[:split_at]]).reshape(4, WIDE, 128)
    shape = (6, 2, REACH, 128)
    fields = jnp.concatenate(
        [
            above[split_at:].reshape(shape),
            fields,
            below[split_at:].reshape(shape),
            jnp.zeros((6, 2, PACK - rows - 2 * REACH, 128), jnp.bfloat16),
        ],
        axis=2,
    )
    fields = fields.reshape(2, 3, 2 * PACK, 128).transpose(1, 0, 2, 3)

    ext, preact, force = call(
        forward_kernel,
        (
            jax.ShapeDtypeStruct((rows + 4, WIDE, 128), jnp.bfloat16),
            jax.ShapeDtypeStruct((rows + 2, WIDE, 128), jnp.float32),
            jax.ShapeDtypeStruct((128, 128), jnp.float32),
        ),
        [pltpu.VMEM((384, 384), jnp.bfloat16)],
        [VMEM] * 6 + [SMEM] * 2,
        (hidden, edge, ends, fields, conv_weight, conv_bias[None], step_alpha, step_beta),
        "forward",
    )
    grad, weight, vectors = call(
        backward_kernel,
        (
            jax.ShapeDtypeStruct((rows + 2, WIDE, 128), jnp.bfloat16),
            jax.ShapeDtypeStruct((9, 128, 128), jnp.float32),
            jax.ShapeDtypeStruct((2, 128), jnp.float32),
        ),
        [pltpu.VMEM((rows, WIDE, 384), jnp.bfloat16)],
        [SMEM] + [VMEM] * 4,
        (mean, preact, force, ext, proj_weight[None]),
        "backward",
    )
    grad_hidden = call(
        input_kernel,
        jax.ShapeDtypeStruct((rows, 128, 128), jnp.bfloat16),
        [pltpu.VMEM((384, 384), jnp.bfloat16)],
        [VMEM] * 2,
        (grad, conv_weight),
        "input_grad",
    )
    own_weight, total_bias, total_proj = all_summed(weight, vectors)
    cells = rows * 128 * lax.axis_size("dp") * n_lat * lax.axis_size("lon")
    grad_scale = 1.0 / math.sqrt(cells)
    return (
        grad_hidden[None],
        own_weight * grad_scale,
        total_bias * grad_scale,
        total_proj * grad_scale,
    )


def solution(mesh):
    split = Mesh(
        mesh.devices.reshape(mesh.shape["dp"], 4, 2, 2, mesh.shape["lon"]),
        ("dp", "lat_0", "lat_1", "lat_2", "lon"),
    )
    placed = (
        P("dp", LAT, "lon", None),
        P(),
        P(),
        P(),
        P(LAT, "lon"),
        P(LAT, "lon"),
        P(),
        P(),
        P("dp", LAT, "lon"),
    )
    return jax.shard_map(
        shards,
        mesh=split,
        in_specs=placed,
        out_specs=(P("dp", LAT, "lon", None), P(LAT_LON, None, None, None), P(), P()),
        check_vma=False,
    )
```

time: 185 us -> 120 us (0.65)
  starting transfers between devices: 81.8 us -> 39.9 us
  waiting for transfers between devices: 47.8 us -> 28.1 us
  other arithmetic: 25.8 us -> 7.27 us
  between operations: 2.59 us -> 18.4 us
  matrix products: 13.6 us -> 0 us
  blocking collectives: 0 us -> 11.1 us
  Pallas kernels: 0 us -> 6.18 us
  local copies, waits for them, and re-layouts: 11.5 us -> 8.16 us
    ppermute x12 -> x2, starting transfers between devices: 38.7 us -> 17.2 us  [the longest x1 15.3 us: shards(): cross = lax.ppermute(cross, LAT, odd + [(j, i) for i, j in odd])]
    all_to_all x2, starting transfers between devices: 27.6 us -> 7.63 us  [the longest x1 4.29 us: gathered_edges(): got = lax.all_to_all(sent, 'lon', 0, 0, tiled=True)]
    dot_general x27 -> x0, matrix products: 13.6 us -> none  [the longest x9 7.53 us: shards(): lax.dot_general(window, conv_weight[row_off, col_off], (((1,), (1,)), (()...]
    all_to_all x2, waiting for transfers between devices: 18.8 us -> 7.33 us  [the longest x1 4.98 us: gathered_edges(): got = lax.all_to_all(sent, 'lon', 0, 0, tiled=True)]
    all_to_all x0 -> x1, blocking collectives: none -> 11.1 us  [all_summed(): got = lax.all_to_all(sent, ('lat_0', 'lon'), 0, 0, tiled=True)]
    ppermute x12 -> x2, waiting for transfers between devices: 16.2 us -> 6.06 us  [the longest x1 4.91 us: shards(): cross = lax.ppermute(cross, LAT, odd + [(j, i) for i, j in odd])]
    add x5 -> x0, other arithmetic: 9.7 us -> none  [the longest x4 9.61 us: solve_steps(): direction = residual + step_beta[turn_index] * direction]
    pallas_call x0 -> x3, Pallas kernels: none -> 6.18 us  [call(): pl.pallas_call(kernel, out_shape=shapes, in_specs=in_specs, out_specs=jax...]
  transfers between devices with their start and end apart: 16 -> 6, of which waited for: 7 -> 6; matrix products, arithmetic and copies ran while one was open for 18% -> 1% of each run, Pallas kernels for 0% -> 3%
where the time goes in v2:
time: 120 us; the launch traced here: 119 us
  starting transfers between devices  39.9 us (33%)
  waiting for transfers between devices  28.1 us (23%)
  between operations  18.4 us (15%)
  blocking collectives  11.1 us (9%)
  local copies, waits for them, and re-layouts  8.16 us (7%)
  other arithmetic  7.27 us (6%)
  Pallas kernels  6.18 us (5%)
    ppermute x1, starting transfers between devices, shards(): cross = lax.ppermute(cross, LAT, odd + [(j, i) for i, j in odd])  15.3 us
    all_to_all x1, waiting for transfers between devices, all_summed(): total = lax.all_to_all(sent, ('lat_1', 'dp'), 0, 0, tiled=True).sum(axis=0)  13.4 us
    all_to_all x1, starting transfers between devices, all_summed(): total = lax.all_to_all(sent, ('lat_1', 'dp'), 0, 0, tiled=True).sum(axis=0)  13.2 us
    all_to_all x1, blocking collectives, all_summed(): got = lax.all_to_all(sent, ('lat_0', 'lon'), 0, 0, tiled=True)  11.1 us
    pallas_call x3, Pallas kernels, call(): pl.pallas_call(kernel, out_shape=shapes, in_specs=in_specs, out_specs=jax...  6.18 us
    all_to_all x1, waiting for transfers between devices, gathered_edges(): got = lax.all_to_all(sent, 'lon', 0, 0, tiled=True)  4.98 us
    ppermute x1, waiting for transfers between devices, shards(): cross = lax.ppermute(cross, LAT, odd + [(j, i) for i, j in odd])  4.91 us
    all_to_all x1, starting transfers between devices, gathered_edges(): got = lax.all_to_all(sent, 'lon', 0, 0, tiled=True)  4.29 us
  transfers between devices with their start and end apart: 6, of which 6 were waited for; matrix products, arithmetic and copies ran while one was open for 1% of the time, Pallas kernels for 3%

profile of v2, /device:TPU:32, one launch (start us, length us, event | category | flops | bytes accessed | tf_op | source)
XLA Modules:
  0.0 119.2 jit_solution(65410437115002402)
XLA Ops:
  0.7 0.8 fusion.21
  2.2 0.7 constant_dynamic-update-slice_fusion.4
  2.9 0.7 constant_dynamic-update-slice_fusion.3
  4.4 0.7 constant_dynamic-update-slice_fusion.1
  5.1 0.7 constant_dynamic-update-slice_fusion
  6.6 4.3 %all-to-all-start = ((bf16[4,128,128]{2,1,0:T(8,128)(2,1)}), bf16[4,128,128]{2,1,0:T(8,128)(2,1)S(1)}, u32[]{:S(2)}, u32[]{:S(2)}) async-start(bf16[4,128,128]{2,1,0:T(8,128)(2,1)} %pad_maximum_fusion.3), calls=%async_computation | async-start | bytes 262144 | tf_op jit(solution)/shard_map/all_to_all | solution.py:209
  10.9 0.9 slice_bitcast_fusion.3
  11.9 5.0 %all-to-all-done = bf16[4,128,128]{2,1,0:T(8,128)(2,1)S(1)} async-done(((bf16[4,128,128]{2,1,0:T(8,128)(2,1)}), bf16[4,128,128]{2,1,0:T(8,128)(2,1)S(1)}, u32[]{:S(2)}, u32[]{:S(2)}) %all-to-all-start) | async-done | bytes 131104 | tf_op jit(solution)/shard_map/all_to_all | solution.py:209
  28.4 1.4 %stack.64 = bf16[6]{0:T(256)(128)(2,1)S(1)} concatenate(bf16[1]{0:T(256)(128)(2,1)} %bitcast.20, bf16[1]{0:T(256)(128)(2,1)} %bitcast.21, bf16[1]{0:T(256)(128)(2,1)} %bitcast.22, bf16[1]{0:T(256)(128)(2,1)} %bitcast.23, bf16[1]{0:T(256)(128)(2,1)} %bitcast.24, bf16[1]{0:T(256)(128)(2,1)} %bitcast.25), dimensions={0} | concatenate | bytes 24 | tf_op jit(solution)/shard_map/stack | solution.py:297
  30.3 15.3 %collective-permute-start = (bf16[366,128]{1,0:T(8,128)(2,1)S(1)}, bf16[366,128]{1,0:T(8,128)(2,1)S(1)}, u32[]{:S(2)}, u32[]{:S(2)}) collective-permute-start(bf16[366,128]{1,0:T(8,128)(2,1)S(1)} %maximum_maximum_fusion.1), channel_id=1, source_target_pairs={{4,8},{12,16},{20,24},{28,32},{36,40},{44,48},{52,56},{60,0},{8,4}... | collective-permute-start | bytes 281096 | tf_op jit(solution)/shard_map/ppermute | solution.py:302
  45.6 1.9 %collective-permute-start.1 = (bf16[360,128]{1,0:T(8,128)(2,1)S(1)}, bf16[360,128]{1,0:T(8,128)(2,1)S(1)}, u32[]{:S(2)}, u32[]{:S(2)}) collective-permute-start(bf16[360,128]{1,0:T(8,128)(2,1)S(1)} %pad_maximum_fusion.4), channel_id=1, source_target_pairs={{0,4},{4,0},{1,5},{5,1},{2,6},{6,2},{3,7},{7,3},{8,12},{12,8},{9,1... | collective-permute-start | bytes 276488 | tf_op jit(solution)/shard_map/ppermute | solution.py:303
  47.6 1.2 collective-permute-done.1
  48.8 4.9 %collective-permute-done = bf16[366,128]{1,0:T(8,128)(2,1)S(1)} collective-permute-done((bf16[366,128]{1,0:T(8,128)(2,1)S(1)}, bf16[366,128]{1,0:T(8,128)(2,1)S(1)}, u32[]{:S(2)}, u32[]{:S(2)}) %collective-permute-start) | collective-permute-done | bytes 93728 | tf_op jit(solution)/shard_map/ppermute | solution.py:302
  60.2 3.3 %all-to-all-start.1 = ((f32[8,2,128]{2,1,0:T(2,128)}), f32[8,2,128]{2,1,0:T(2,128)S(1)}, u32[]{:S(2)}, u32[]{:S(2)}) async-start(f32[8,2,128]{2,1,0:T(2,128)} %broadcast_in_dim.116), calls=%async_computation.1 | async-start | bytes 16384 | tf_op jit(solution)/shard_map/all_to_all | solution.py:307
  63.7 2.0 %forward.1 = (bf16[20,144,128]{2,1,0:T(8,128)(2,1)S(1)}, f32[18,144,128]{2,1,0:T(8,128)S(1)}, f32[128,128]{1,0:T(8,128)S(1)}) custom-call(bf16[16,128,128]{2,1,0:T(8,128)(2,1)S(1)} %bitcast.100, bf16[16,16,128]{2,1,0:T(8,128)(2,1)S(1)} %pad_maximum_fusion.7.edge_ref, bf16[4,144,128]{2,1,0:T(8,128)(2,1)S(1)} %bitcast.101, ...), custom_call_target="tpu_custom_call" | custom-call | tf_op jit(solution)/shard_map/forward/pallas_call | solution.py:188
  66.4 2.4 %all-to-all-done.1 = f32[8,2,128]{2,1,0:T(2,128)S(1)} async-done(((f32[8,2,128]{2,1,0:T(2,128)}), f32[8,2,128]{2,1,0:T(2,128)S(1)}, u32[]{:S(2)}, u32[]{:S(2)}) %all-to-all-start.1) | async-done | bytes 8224 | tf_op jit(solution)/shard_map/all_to_all | solution.py:307
  70.8 0.8 copy-done.3
  71.7 2.1 %backward.1 = (bf16[18,144,128]{2,1,0:T(8,128)(2,1)S(1)}, f32[9,128,128]{2,1,0:T(8,128)S(1)}, f32[2,128]{1,0:T(2,128)S(1)}) custom-call(f32[1]{0:T(128)S(6)} %div.4.mean_ref, f32[18,144,128]{2,1,0:T(8,128)S(1)} %get-tuple-element.10.preact_ref, f32[128,128]{1,0:T(8,128)S(1)} %copy-done.3, bf16[20,144,128]{2,1,0:T(8,128)(2,1)S(1)} %get-tuple-element.12.ext_ref, ...), custom_call_target="tpu_custom_call" | custom-call | tf_op jit(solution)/shard_map/backward/pallas_call | solution.py:188
  73.8 1.9 %collective-permute-start.2 = (bf16[580,128]{1,0:T(8,128)(2,1)S(1)}, bf16[580,128]{1,0:T(8,128)(2,1)S(1)}, u32[]{:S(2)}, u32[]{:S(2)}) collective-permute-start(bf16[580,128]{1,0:T(8,128)(2,1)S(1)} %pad_maximum_fusion.1), channel_id=1, source_target_pairs={{0,4},{4,0},{1,5},{5,1},{2,6},{6,2},{3,7},{7,3},{8,12},{12,8},{9,1... | collective-permute-start | bytes 445448 | tf_op jit(solution)/shard_map/ppermute | solution.py:255
  75.8 1.3 %collective-permute-done.2 = bf16[580,128]{1,0:T(8,128)(2,1)S(1)} collective-permute-done((bf16[580,128]{1,0:T(8,128)(2,1)S(1)}, bf16[580,128]{1,0:T(8,128)(2,1)S(1)}, u32[]{:S(2)}, u32[]{:S(2)}) %collective-permute-start.2) | collective-permute-done | bytes 148512 | tf_op jit(solution)/shard_map/ppermute | solution.py:255
  77.4 11.1 %all_to_all.20 = bf16[16,40,128]{2,1,0:T(8,128)(2,1)S(1)} all-to-all(bf16[16,40,128]{2,1,0:T(8,128)(2,1)S(1)} %copy.39), channel_id=1, replica_groups=mesh['dp'=8,'lat_0'=4,'lat_1'=2,'lat_2'=2,'lon'=4] {'lat_0','lon'}, dimensions={0} | all-to-all | bytes 327680 | tf_op jit(solution)/shard_map/all_to_all | solution.py:263
  89.4 13.2 %all-to-all-start.3 = ((f32[16,20,128]{2,1,0:T(8,128)}), f32[16,20,128]{2,1,0:T(8,128)S(1)}, u32[]{:S(2)}, u32[]{:S(2)}) async-start(f32[16,20,128]{2,1,0:T(8,128)} %bitcast.47), calls=%async_computation.3 | async-start | bytes 393216 | tf_op jit(solution)/shard_map/all_to_all | solution.py:269
  102.5 2.1 %input_grad.1 = bf16[16,128,128]{2,1,0:T(8,128)(2,1)} custom-call(bf16[18,144,128]{2,1,0:T(8,128)(2,1)S(1)} %get-tuple-element.13.grad_ref, bf16[3,3,128,128]{3,2,1,0:T(8,128)(2,1)S(1)} %copy-done), custom_call_target="tpu_custom_call" | custom-call | tf_op jit(solution)/shard_map/input_grad/pallas_call | solution.py:188
  104.6 13.4 %all-to-all-done.3 = f32[16,20,128]{2,1,0:T(8,128)S(1)} async-done(((f32[16,20,128]{2,1,0:T(8,128)}), f32[16,20,128]{2,1,0:T(8,128)S(1)}, u32[]{:S(2)}, u32[]{:S(2)}) %all-to-all-start.3) | async-done | bytes 163872 | tf_op jit(solution)/shard_map/all_to_all | solution.py:269
  (82 shorter events, 8.7 us)
Async XLA Ops:
  6.6 10.3 %all-to-all-start = ((bf16[4,128,128]{2,1,0:T(8,128)(2,1)}), bf16[4,128,128]{2,1,0:T(8,128)(2,1)S(1)}, u32[]{:S(2)}, u32[]{:S(2)}) async-start(bf16[4,128,128]{2,1,0:T(8,128)(2,1)} %pad_maximum_fusion.3), calls=%async_computation | async-start | bytes 262144 | tf_op jit(solution)/shard_map/all_to_all | solution.py:209
  29.9 33.7 %copy-start = (bf16[3,3,128,128]{3,2,1,0:T(8,128)(2,1)S(1)}, bf16[3,3,128,128]{3,2,1,0:T(8,128)(2,1)}, u32[]{:S(2)}) copy-start(bf16[3,3,128,128]{3,2,1,0:T(8,128)(2,1)} %weight_ref.3) | copy-start | bytes 884740
  30.0 33.7 %copy-start.1 = (bf16[1,16,128,128]{3,2,1,0:T(8,128)(2,1)S(1)}, bf16[1,16,128,128]{3,2,1,0:T(8,128)(2,1)}, u32[]{:S(2)}) copy-start(bf16[1,16,128,128]{3,2,1,0:T(8,128)(2,1)} %param.9) | copy-start | bytes 1572868
  30.0 33.7 %copy-start.4 = (f32[128]{0:T(128)S(1)}, f32[128]{0:T(128)}, u32[]{:S(2)}) copy-start(f32[128]{0:T(128)} %param.11) | copy-start | bytes 1540
  30.0 33.7 %copy-start.5 = (f32[6]{0:T(128)S(1)}, f32[6]{0:T(128)}, u32[]{:S(2)}) copy-start(f32[6]{0:T(128)} %alpha_ref.1) | copy-start | bytes 76
  30.0 33.7 %copy-start.6 = (f32[6]{0:T(128)S(1)}, f32[6]{0:T(128)}, u32[]{:S(2)}) copy-start(f32[6]{0:T(128)} %beta_ref.1) | copy-start | bytes 76
  30.3 23.4 %collective-permute-start = (bf16[366,128]{1,0:T(8,128)(2,1)S(1)}, bf16[366,128]{1,0:T(8,128)(2,1)S(1)}, u32[]{:S(2)}, u32[]{:S(2)}) collective-permute-start(bf16[366,128]{1,0:T(8,128)(2,1)S(1)} %maximum_maximum_fusion.1), channel_id=1, source_target_pairs={{4,8},{12,16},{20,24},{28,32},{36,40},{44,48},{52,56},{60,0},{8,4}... | collective-permute-start | bytes 281096 | tf_op jit(solution)/shard_map/ppermute | solution.py:302
  45.6 3.2 %collective-permute-start.1 = (bf16[360,128]{1,0:T(8,128)(2,1)S(1)}, bf16[360,128]{1,0:T(8,128)(2,1)S(1)}, u32[]{:S(2)}, u32[]{:S(2)}) collective-permute-start(bf16[360,128]{1,0:T(8,128)(2,1)S(1)} %pad_maximum_fusion.4), channel_id=1, source_target_pairs={{0,4},{4,0},{1,5},{5,1},{2,6},{6,2},{3,7},{7,3},{8,12},{12,8},{9,1... | collective-permute-start | bytes 276488 | tf_op jit(solution)/shard_map/ppermute | solution.py:303
  47.6 23.2 %copy-start.7 = (f32[128]{0:T(128)S(1)}, f32[128]{0:T(128)}, u32[]{:S(2)}) copy-start(f32[128]{0:T(128)} %param.12) | copy-start | bytes 1540
  60.2 8.6 %all-to-all-start.1 = ((f32[8,2,128]{2,1,0:T(2,128)}), f32[8,2,128]{2,1,0:T(2,128)S(1)}, u32[]{:S(2)}, u32[]{:S(2)}) async-start(f32[8,2,128]{2,1,0:T(2,128)} %broadcast_in_dim.116), calls=%async_computation.1 | async-start | bytes 16384 | tf_op jit(solution)/shard_map/all_to_all | solution.py:307
  65.8 0.6 copy-start.2
  70.8 0.8 copy-start.3
  73.8 3.3 %collective-permute-start.2 = (bf16[580,128]{1,0:T(8,128)(2,1)S(1)}, bf16[580,128]{1,0:T(8,128)(2,1)S(1)}, u32[]{:S(2)}, u32[]{:S(2)}) collective-permute-start(bf16[580,128]{1,0:T(8,128)(2,1)S(1)} %pad_maximum_fusion.1), channel_id=1, source_target_pairs={{0,4},{4,0},{1,5},{5,1},{2,6},{6,2},{3,7},{7,3},{8,12},{12,8},{9,1... | collective-permute-start | bytes 445448 | tf_op jit(solution)/shard_map/ppermute | solution.py:255
  89.4 28.7 %all-to-all-start.3 = ((f32[16,20,128]{2,1,0:T(8,128)}), f32[16,20,128]{2,1,0:T(8,128)S(1)}, u32[]{:S(2)}, u32[]{:S(2)}) async-start(f32[16,20,128]{2,1,0:T(8,128)} %bitcast.47), calls=%async_computation.3 | async-start | bytes 393216 | tf_op jit(solution)/shard_map/all_to_all | solution.py:269

commit v3 on v2

v3 whole, which is shorter than its diff:
```python
import functools
import math

import jax
import jax.numpy as jnp
from jax import lax
from jax.experimental import pallas as pl
from jax.experimental.pallas import tpu as pltpu
from jax.sharding import Mesh
from jax.sharding import PartitionSpec as P

ITERS = 6
LAT_LON = ("lat_0", "lat_1", "lat_2", "lon")
LAT = ("lat_0", "lat_1", "lat_2")
WIDE = 144
PACK = 32
PLANES = 5
SENT = 64 + PLANES * PACK

helm_coef = 0.5
VMEM = pl.BlockSpec(memory_space=pltpu.VMEM)
SMEM = pl.BlockSpec(memory_space=pltpu.SMEM)


def rounded(values):
    return values.astype(jnp.bfloat16).astype(jnp.float32)


def pieces_of(values, count):
    out = []
    for _ in range(count):
        piece = rounded(values)
        out.append(piece)
        values = values - piece
    return out


def full(value):
    return jnp.full((1, 128), value, jnp.float32)


def first_kernel(
    at_ref, hidden_ref, cot_ref, mask_ref, depth_ref, cross_ref, pair_ref, planes_ref, sums_ref
):
    rows = hidden_ref.shape[0]
    upper = at_ref[0] == 0
    mask = mask_ref[...].astype(jnp.float32)
    wet = mask * cot_ref[0]
    planes = pieces_of(wet, 3) + pieces_of(mask * depth_ref[...], 2)
    summed, counted = jnp.sum(wet), jnp.sum(mask)
    sums_ref[0:1] = full(summed)
    sums_ref[1:2] = full(counted)
    sums = pieces_of(full(summed), 3) + pieces_of(full(counted), 3)
    sums = jnp.concatenate(sums + [jnp.zeros((2, 128), jnp.float32)], axis=0)
    for k in range(PLANES):
        planes_ref[k] = planes[k]
    for ref, top in ((cross_ref, upper), (pair_ref, jnp.logical_not(upper))):
        start = jnp.where(top, 0, rows - 2)
        ref[0:256] = hidden_ref[pl.ds(start, 2)].reshape(256, 128)
        near = [jnp.where(top, p[0:8], p[rows - 8 : rows]) for p in planes] + [sums]
        for k in range(0, 6, 2):
            tile = jnp.concatenate(near[k : k + 2], axis=0)
            ref[256 + k * 8 : 272 + k * 8] = tile.astype(jnp.bfloat16)


def second_kernel(
    at_ref, hidden_ref, planes_ref, sums_ref, cross_ref, pair_ref,
    ends_ref, fields_ref, sent_ref, total_ref,
):
    rows = hidden_ref.shape[0]
    upper = at_ref[0] == 0
    keep_above = jnp.where(at_ref[1] == 0, 0.0, 1.0)
    keep_below = jnp.where(at_ref[2] == 0, 0.0, 1.0)
    zero = jnp.zeros((), jnp.bfloat16)
    for k in range(2):
        cross = cross_ref[k * 128 : k * 128 + 128]
        pair = pair_ref[k * 128 : k * 128 + 128]
        ends_ref[k] = jnp.where(keep_above > 0.0, jnp.where(upper, cross, pair), zero)
        ends_ref[k + 2] = jnp.where(keep_below > 0.0, jnp.where(upper, pair, cross), zero)
    cross = cross_ref[256:304].astype(jnp.float32)
    pair = pair_ref[256:304].astype(jnp.float32)
    got = cross[40:48]
    summed = sums_ref[0:1] + got[0:1] + got[1:2] + got[2:3]
    counted = sums_ref[1:2] + got[3:4] + got[4:5] + got[5:6]
    lane = lax.broadcasted_iota(jnp.int32, (1, 128), 1)
    total = jnp.where(lane < 64, summed, counted)
    total_ref[...] = jnp.broadcast_to(total[None], total_ref.shape)
    above = jnp.where(upper, cross, pair) * keep_above
    below = jnp.where(upper, pair, cross) * keep_below
    fields = []
    for k in range(PLANES):
        at = k * 8
        fields.append(
            jnp.concatenate([above[at : at + 8], planes_ref[k], below[at : at + 8]], axis=0)
        )
    fields_ref[0] = fields[0] + fields[1] + fields[2]
    fields_ref[1] = fields[3] + fields[4]
    place = lax.broadcasted_iota(jnp.int32, (8, 128), 0)
    columns = [[jnp.zeros((8, 128), jnp.float32) for _ in range(4)] for _ in range(4)]
    for r in range(rows + 4):
        if r < 2:
            source = ends_ref.at[r]
        elif r < rows + 2:
            source = hidden_ref.at[r - 2]
        else:
            source = ends_ref.at[r - rows]
        head = source[0:16].astype(jnp.float32)
        tail = source[112:128].astype(jnp.float32)
        for k, row in enumerate((head[0:1], head[1:2], tail[14:15], tail[15:16])):
            columns[k][r // 8] = jnp.where(place == r % 8, row, columns[k][r // 8])
    columns = [jnp.concatenate(tiles, axis=0) for tiles in columns]
    fields = [f.astype(jnp.bfloat16) for f in fields]
    for peer in range(sent_ref.shape[0]):
        to_right = at_ref[4] == peer
        for k in range(2):
            chosen = jnp.where(to_right, columns[2 + k], columns[k])
            sent_ref[peer, k * 32 : k * 32 + 32] = chosen.astype(jnp.bfloat16)
        for k in range(PLANES):
            sent_ref[peer, 64 + k * PACK : 64 + k * PACK + PACK] = fields[k]


def forward_kernel(
    at_ref, hidden_ref, ends_ref, fields_ref, got_ref, weight_ref, bias_ref, alpha_ref, beta_ref,
    ext_ref, preact_ref, force_ref, rhs_ref,
):
    rows = hidden_ref.shape[0]
    left, right = at_ref[3], at_ref[4]
    ext_ref[0:2, 0:128] = ends_ref[0:2]
    ext_ref[2 : rows + 2, 0:128] = hidden_ref[...]
    ext_ref[rows + 2 : rows + 4, 0:128] = ends_ref[2:4]
    columns = got_ref[right, 0:64].astype(jnp.float32), got_ref[left, 0:64].astype(jnp.float32)
    place = lax.broadcasted_iota(jnp.int32, (WIDE - 128, 128), 0)
    for r in range(rows + 4):
        tile = jnp.zeros((WIDE - 128, 128), jnp.float32)
        for side, base in enumerate((0, WIDE - 130)):
            for k in range(2):
                row = columns[side][k * 32 + r : k * 32 + r + 1]
                tile = jnp.where(place == base + k, row, tile)
        ext_ref[r, 128:WIDE] = tile.astype(jnp.bfloat16)
    for a in range(3):
        for c in range(3):
            rhs_ref[a * 128 : a * 128 + 128, c * 128 : c * 128 + 128] = weight_ref[a, c]

    lane = lax.broadcasted_iota(jnp.int32, (2 * PACK, 128), 1)
    second = jnp.where(
        jnp.concatenate([lane] * 3, axis=0)[: PLANES * PACK] < 64,
        got_ref[right, 64:SENT].astype(jnp.float32),
        got_ref[left, 64:SENT].astype(jnp.float32),
    )
    second = [second[k * PACK : k * PACK + PACK] for k in range(PLANES)]
    start = jnp.concatenate([fields_ref[0], second[0] + second[1] + second[2]], axis=0)
    wet_depth = jnp.concatenate([fields_ref[1], second[3] + second[4]], axis=0)
    mask = jnp.where(wet_depth > 0.0, 1.0, 0.0)

    def other_half(field):
        parts = [field[k * PACK : (k + 1) * PACK] for k in range(field.shape[0] // PACK)]
        swapped = []
        for k in range(0, len(parts), 2):
            swapped += [parts[k + 1], parts[k]]
        return jnp.concatenate(swapped, axis=0)

    def beside(field):
        count = field.shape[0]
        lanes = lane if count == 2 * PACK else jnp.concatenate([lane, lane], axis=0)
        up = pltpu.roll(field, 1, 0)
        down = pltpu.roll(field, count - 1, 0)
        from_left = pltpu.roll(field, 1, 1)
        from_left = jnp.where(lanes == 0, other_half(from_left), from_left)
        from_right = pltpu.roll(field, 127, 1)
        from_right = jnp.where(lanes == 127, other_half(from_right), from_right)
        return up, down, from_left, from_right

    weights = [
        0.5 * (near_mask * wet_depth + mask * near_depth)
        for near_mask, near_depth in zip(beside(mask), beside(wet_depth))
    ]
    diagonal = helm_coef * mask + weights[0] + weights[1] + weights[2] + weights[3]
    weights = [jnp.concatenate([w, w], axis=0) for w in weights]
    diagonal = jnp.concatenate([diagonal, diagonal], axis=0)
    residual = jnp.concatenate([start, mask], axis=0)
    direction = residual
    result = jnp.zeros_like(residual)
    for k in range(ITERS):
        result = result + alpha_ref[k] * direction
        if k + 1 < ITERS:
            applied = diagonal * direction
            for w, near in zip(weights, beside(direction)):
                applied = applied - w * near
            residual = residual - alpha_ref[k] * applied
            direction = residual + beta_ref[k] * direction
    result = result * jnp.concatenate([mask, mask], axis=0)
    force_ref[...] = result.T

    group = 6
    bias = bias_ref[...]
    for g in range(0, rows + 2, group):
        lhs = jnp.concatenate(
            [ext_ref[g + a : g + a + group].reshape(group * WIDE, 128) for a in range(3)], axis=1
        )
        out = jnp.dot(lhs, rhs_ref[...], preferred_element_type=jnp.float32)
        for j in range(group):
            part = out[j * WIDE : (j + 1) * WIDE]
            preact_ref[g + j] = (
                pltpu.roll(part[:, 0:128], 1, 0)
                + part[:, 128:256]
                + pltpu.roll(part[:, 256:384], WIDE - 1, 0)
                + bias
            )


def backward_kernel(
    total_ref, preact_ref, force_ref, ext_ref, proj_ref,
    grad_ref, sent_ref, moved_ref, weight_ref,
):
    rows = grad_ref.shape[0] - 2
    total = jnp.sum(total_ref[...], axis=0)
    mean = jnp.broadcast_to(total[:, 0:1], (1, 128)) / jnp.broadcast_to(total[:, 127:128], (1, 128))
    force = force_ref[...]
    force = force - mean * pltpu.roll(force, 64, 1)
    proj = proj_ref[...]
    sum_bias = jnp.zeros((8, 128), jnp.float32)
    sum_proj = jnp.zeros((8, 128), jnp.float32)
    for g in range(rows + 2):
        at = g + 7
        column = jnp.concatenate(
            [
                force[:, at : at + 1],
                force[0:8, PACK + at : PACK + at + 1],
                force[120:128, PACK + at : PACK + at + 1],
            ],
            axis=0,
        )
        column = jnp.broadcast_to(column, (WIDE, 128))
        preact = preact_ref[g]
        sigma = jax.nn.sigmoid(preact)
        active = preact * sigma
        slope_act = sigma * (1.0 + preact * (1.0 - sigma))
        grad = (column * proj * slope_act).astype(jnp.bfloat16)
        grad_ref[g] = grad
        if 1 <= g <= rows:
            own = grad.astype(jnp.float32)[0:128]
            for k in range(16):
                sum_bias = sum_bias + own[k * 8 : k * 8 + 8]
                sum_proj = sum_proj + (active * column)[k * 8 : k * 8 + 8]
            own = jnp.concatenate([own, jnp.zeros((WIDE - 128, 128), jnp.float32)], axis=0)
            moved_ref[g - 1, :, 0:128] = pltpu.roll(own, WIDE - 1, 0).astype(jnp.bfloat16)
            moved_ref[g - 1, :, 128:256] = own.astype(jnp.bfloat16)
            moved_ref[g - 1, :, 256:384] = pltpu.roll(own, 1, 0).astype(jnp.bfloat16)
    moved = moved_ref[...].reshape(rows * WIDE, 384)
    for a in range(3):
        cells = ext_ref[a + 1 : a + 1 + rows].reshape(rows * WIDE, 128)
        out = lax.dot_general(
            cells, moved, (((0,), (0,)), ((), ())), preferred_element_type=jnp.float32
        )
        for c in range(3):
            weight_ref[a * 3 + c] = out[:, c * 128 : c * 128 + 128]
    vectors = jnp.concatenate(
        [jnp.sum(sum_bias, axis=0, keepdims=True), jnp.sum(sum_proj, axis=0, keepdims=True)], axis=0
    )
    vectors = jnp.concatenate(pieces_of(vectors, 2) + [jnp.zeros((4, 128), jnp.float32)], axis=0)
    vectors = pltpu.roll(vectors, 4, 0)
    place = lax.broadcasted_iota(jnp.int32, (8, 128), 0) // 2

    def one_pair(at, carry):
        y, c = at // 2, at % 2
        for x in range(4):
            tiles = []
            for t in range(5):
                tile = vectors
                for j in range(4):
                    slot = 4 * t + j
                    if slot >= 18:
                        continue
                    z, k = slot // 9, slot % 9
                    start = pl.multiple_of(((y * 2 + z) * 2 + c) * 8, 8)
                    piece = weight_ref[k, pl.ds(start, 8)]
                    if j != x:
                        piece = pltpu.roll(piece, (2 * j - 2 * x) % 8, 0)
                    tile = jnp.where(place == j, piece, tile)
                tiles.append(tile)
            sent_ref[at * 4 + x] = jnp.concatenate(tiles, axis=0).astype(jnp.bfloat16)
        return carry

    lax.fori_loop(0, 8, one_pair, 0)


def middle_kernel(got_ref, sent_ref):
    total = jnp.sum(got_ref[...].astype(jnp.float32), axis=0)
    vectors = total[36:38] + total[38:40]
    vectors = jnp.concatenate(pieces_of(vectors, 2) + [jnp.zeros((2, 128), jnp.float32)], axis=0)
    peers = sent_ref.shape[0] // 2
    for z in range(2):
        block = jnp.concatenate([total[z * 18 : z * 18 + 18], vectors], axis=0)
        block = block.astype(jnp.bfloat16)
        for d in range(peers):
            sent_ref[z * peers + d] = block


def last_kernel(scale, got_ref, weight_ref, bias_ref, proj_ref):
    total = jnp.sum(got_ref[...].astype(jnp.float32), axis=0) * scale
    for k in range(9):
        for e in range(2):
            weight_ref[e, k // 3, k % 3 : k % 3 + 1] = total[k * 2 + e : k * 2 + e + 1]
    bias_ref[...] = total[18:19] + total[20:21]
    proj_ref[...] = total[19:20] + total[21:22]


def input_kernel(grad_ref, weight_ref, out_ref, rhs_ref):
    rows = out_ref.shape[0]
    for a in range(3):
        for c in range(3):
            rhs_ref[c * 128 : c * 128 + 128, a * 128 : a * 128 + 128] = weight_ref[a, c]
    group = 4
    for y in range(0, rows, group):
        lhs = jnp.concatenate(
            [
                grad_ref[y - a + 2 : y - a + 2 + group].reshape(group * WIDE, 128)
                for a in range(3)
            ],
            axis=1,
        )
        out = lax.dot_general(
            lhs, rhs_ref[...], (((1,), (1,)), ((), ())), preferred_element_type=jnp.float32
        )
        for j in range(group):
            part = out[j * WIDE : (j + 1) * WIDE]
            total = (
                pltpu.roll(part[:, 0:128], WIDE - 1, 0)
                + part[:, 128:256]
                + pltpu.roll(part[:, 256:384], 1, 0)
            )
            out_ref[y + j] = total[0:128].astype(jnp.bfloat16)


def call(kernel, shapes, scratch, in_specs, args, name):
    return pl.pallas_call(
        kernel,
        out_shape=shapes,
        in_specs=in_specs,
        out_specs=jax.tree.map(lambda _: VMEM, shapes),
        scratch_shapes=scratch,
        compiler_params=pltpu.CompilerParams(vmem_limit_bytes=40 * 1024 * 1024),
        name=name,
    )(*args)


def shape(dims, dtype):
    return jax.ShapeDtypeStruct(dims, dtype)


def shards(
    hidden_in, conv_weight, conv_bias, proj_weight, ocean_depth, sea_mask,
    step_alpha, step_beta, surface_cotangent,
):
    wide, narrow = jnp.float32, jnp.bfloat16
    rows = hidden_in.shape[1]
    hidden = hidden_in[0]
    n_x = lax.axis_size("lon")
    n_lat = lax.axis_size(LAT)
    n_all = lax.axis_size(("lat_0", "lat_2", "lon"))
    n_z = lax.axis_size(("lat_1", "dp"))
    lat, x = lax.axis_index(LAT), lax.axis_index("lon")
    at = jnp.stack(
        [lat % 2, lat, n_lat - 1 - lat, (x + n_x - 1) % n_x, (x + 1) % n_x]
    ).astype(jnp.int32)
    cross, pair, planes, sums = call(
        first_kernel,
        (
            shape((304, 128), narrow),
            shape((304, 128), narrow),
            shape((PLANES, rows, 128), wide),
            shape((2, 128), wide),
        ),
        [],
        [SMEM] + [VMEM] * 4,
        (at, hidden, surface_cotangent, sea_mask, ocean_depth),
        "first",
    )
    odd = [(i, (i + 1) % n_lat) for i in range(1, n_lat, 2)]
    cross = lax.ppermute(cross, LAT, odd + [(j, i) for i, j in odd])
    pair = lax.ppermute(pair, "lat_2", [(0, 1), (1, 0)])
    ends, fields, sent, total = call(
        second_kernel,
        (
            shape((4, 128, 128), narrow),
            shape((2, PACK, 128), wide),
            shape((n_x, SENT, 128), narrow),
            shape((n_all, 1, 128), wide),
        ),
        [],
        [SMEM] + [VMEM] * 5,
        (at, hidden, planes, sums, cross, pair),
        "second",
    )
    got = lax.all_to_all(sent, "lon", 0, 0, tiled=True)
    total = lax.all_to_all(total, ("lat_0", "lat_2", "lon"), 0, 0, tiled=True)
    ext, preact, force = call(
        forward_kernel,
        (
            shape((rows + 4, WIDE, 128), narrow),
            shape((rows + 2, WIDE, 128), wide),
            shape((128, 128), wide),
        ),
        [pltpu.VMEM((384, 384), narrow)],
        [SMEM] + [VMEM] * 6 + [SMEM] * 2,
        (at, hidden, ends, fields, got, conv_weight, conv_bias[None], step_alpha, step_beta),
        "forward",
    )
    grad, sent = call(
        backward_kernel,
        (shape((rows + 2, WIDE, 128), narrow), shape((n_all, 40, 128), narrow)),
        [pltpu.VMEM((rows, WIDE, 384), narrow), pltpu.VMEM((9, 128, 128), wide)],
        [VMEM] * 5,
        (total, preact, force, ext, proj_weight[None]),
        "backward",
    )
    got = lax.all_to_all(sent, ("lat_0", "lat_2", "lon"), 0, 0, tiled=True)
    sent = call(middle_kernel, shape((n_z, 24, 128), narrow), [], [VMEM], (got,), "middle")
    got = lax.all_to_all(sent, ("lat_1", "dp"), 0, 0, tiled=True)
    grad_hidden = call(
        input_kernel,
        shape((rows, 128, 128), narrow),
        [pltpu.VMEM((384, 384), narrow)],
        [VMEM] * 2,
        (grad, conv_weight),
        "input_grad",
    )
    cells = rows * 128 * lax.axis_size("dp") * n_lat * n_x
    own_weight, total_bias, total_proj = call(
        functools.partial(last_kernel, 1.0 / math.sqrt(cells)),
        (shape((2, 3, 3, 128), wide), shape((1, 128), wide), shape((1, 128), wide)),
        [],
        [VMEM],
        (got,),
        "last",
    )
    return grad_hidden[None], own_weight, total_bias[0], total_proj[0]


def solution(mesh):
    split = Mesh(
        mesh.devices.reshape(mesh.shape["dp"], 4, 2, 2, mesh.shape["lon"]),
        ("dp", "lat_0", "lat_1", "lat_2", "lon"),
    )
    placed = (
        P("dp", LAT, "lon", None),
        P(),
        P(),
        P(),
        P(LAT, "lon"),
        P(LAT, "lon"),
        P(),
        P(),
        P("dp", LAT, "lon"),
    )
    return jax.shard_map(
        shards,
        mesh=split,
        in_specs=placed,
        out_specs=(P("dp", LAT, "lon", None), P(LAT_LON, None, None, None), P(), P()),
        check_vma=False,
    )
```

time: 120 us -> 96.7 us (0.81)
  between operations: 18.4 us -> 0.8 us
  blocking collectives: 11.1 us -> 23.7 us
  waiting for transfers between devices: 28.1 us -> 20.5 us
  other arithmetic: 7.27 us -> 0 us
  Pallas kernels: 6.18 us -> 9.66 us
  local copies, waits for them, and re-layouts: 8.16 us -> 4.71 us
  starting transfers between devices: 39.9 us -> 36.9 us
    all_to_all x1 -> x2, blocking collectives: 11.1 us -> 23.7 us  [the longest x1 13.1 us: shards(): got = lax.all_to_all(sent, ('lat_0', 'lat_2', 'lon'), 0, 0, tiled=True)]
    all_to_all x3 -> x2, waiting for transfers between devices: 20.8 us -> 16.3 us  [the longest x1 11.3 us: shards(): got = lax.all_to_all(sent, ('lat_1', 'dp'), 0, 0, tiled=True)]
    unnamed x5 -> x0, other arithmetic: 3.63 us -> none
    pallas_call x3 -> x7, Pallas kernels: 6.18 us -> 9.66 us  [call(): pl.pallas_call(kernel, out_shape=shapes, in_specs=in_specs, out_specs=jax...]
    unnamed x16 -> x25, local copies, waits for them, and re-layouts: 1.49 us -> 4.63 us
    slice x13 -> x0, local copies, waits for them, and re-layouts: 2.92 us -> none  [the longest x2 0.88 us: outgoing(): cells = jnp.concatenate([hidden[at:at + 2], edge[at:at + 2]], axis=1)]
    all_to_all x3 -> x2, starting transfers between devices: 20.8 us -> 18.3 us  [the longest x1 13.5 us: shards(): got = lax.all_to_all(sent, ('lat_1', 'dp'), 0, 0, tiled=True)]
    ppermute x1 -> x0, starting transfers between devices: 1.92 us -> none  [all_summed(): got = lax.ppermute(sent, 'lat_2', [(0, 1), (1, 0)])]
  transfers between devices with their start and end apart: 6 -> 4, of which waited for: 6 -> 3; matrix products, arithmetic and copies ran while one was open for 1% -> 0% of each run, Pallas kernels for 3% -> 4%
where the time goes in v3:
time: 96.7 us; the launch traced here: 96.2 us
  starting transfers between devices  36.9 us (38%)
  blocking collectives  23.7 us (25%)
  waiting for transfers between devices  20.5 us (21%)
  Pallas kernels  9.66 us (10%)
  local copies, waits for them, and re-layouts  4.71 us (5%)
    ppermute x1, starting transfers between devices, shards(): cross = lax.ppermute(cross, LAT, odd + [(j, i) for i, j in odd])  16.7 us
    all_to_all x1, starting transfers between devices, shards(): got = lax.all_to_all(sent, ('lat_1', 'dp'), 0, 0, tiled=True)  13.5 us
    all_to_all x1, blocking collectives, shards(): got = lax.all_to_all(sent, ('lat_0', 'lat_2', 'lon'), 0, 0, tiled=True)  13.1 us
    all_to_all x1, waiting for transfers between devices, shards(): got = lax.all_to_all(sent, ('lat_1', 'dp'), 0, 0, tiled=True)  11.3 us
    all_to_all x1, blocking collectives, shards(): got = lax.all_to_all(sent, 'lon', 0, 0, tiled=True)  10.6 us
    pallas_call x7, Pallas kernels, call(): pl.pallas_call(kernel, out_shape=shapes, in_specs=in_specs, out_specs=jax...  9.66 us
    all_to_all x1, waiting for transfers between devices, shards(): total = lax.all_to_all(total, ('lat_0', 'lat_2', 'lon'), 0, 0, tiled=True)  5.09 us
    all_to_all x1, starting transfers between devices, shards(): total = lax.all_to_all(total, ('lat_0', 'lat_2', 'lon'), 0, 0, tiled=True)  4.73 us
  transfers between devices with their start and end apart: 4, of which 3 were waited for; matrix products, arithmetic and copies ran while one was open for 0% of the time, Pallas kernels for 4%

profile of v3, /device:TPU:32, one launch (start us, length us, event | category | flops | bytes accessed | tf_op | source)
XLA Modules:
  0.0 96.2 jit_solution(4660782481991801109)
XLA Ops:
  0.7 0.1 stack.23.at_ref
  0.8 1.0 %copy-done = bf16[1,16,128,128]{3,2,1,0:T(8,128)(2,1)S(1)} copy-done((bf16[1,16,128,128]{3,2,1,0:T(8,128)(2,1)S(1)}, bf16[1,16,128,128]{3,2,1,0:T(8,128)(2,1)}, u32[]{:S(2)}) %copy-start) | copy-done | bytes 524312
  1.8 0.7 copy-done.5
  2.5 0.7 copy-done.6
  3.2 0.7 copy-done.7
  3.9 0.7 first.1
  4.6 0.0 copy-start.11
  4.6 16.7 %collective-permute-start = (bf16[304,128]{1,0:T(8,128)(2,1)S(1)}, bf16[304,128]{1,0:T(8,128)(2,1)S(1)}, u32[]{:S(2)}, u32[]{:S(2)}) collective-permute-start(bf16[304,128]{1,0:T(8,128)(2,1)S(1)} %get-tuple-element.22), channel_id=1, source_target_pairs={{4,8},{12,16},{20,24},{28,32},{36,40},{44,48},{52,56},{60,0},{8,4}... | collective-permute-start | bytes 233480 | tf_op jit(solution)/shard_map/ppermute | solution.py:380
  21.3 1.9 %collective-permute-start.1 = (bf16[304,128]{1,0:T(8,128)(2,1)S(1)}, bf16[304,128]{1,0:T(8,128)(2,1)S(1)}, u32[]{:S(2)}, u32[]{:S(2)}) collective-permute-start(bf16[304,128]{1,0:T(8,128)(2,1)S(1)} %get-tuple-element.23), channel_id=1, source_target_pairs={{0,4},{4,0},{1,5},{5,1},{2,6},{6,2},{3,7},{7,3},{8,12},{12,8},{9,1... | collective-permute-start | bytes 233480 | tf_op jit(solution)/shard_map/ppermute | solution.py:381
  23.3 4.1 %collective-permute-done.cross_ref = bf16[304,128]{1,0:T(8,128)(2,1)S(1)} collective-permute-done((bf16[304,128]{1,0:T(8,128)(2,1)S(1)}, bf16[304,128]{1,0:T(8,128)(2,1)S(1)}, u32[]{:S(2)}, u32[]{:S(2)}) %collective-permute-start) | collective-permute-done | bytes 77856 | tf_op jit(solution)/shard_map/ppermute | solution.py:380
  27.4 1.2 %second.1 = (bf16[4,128,128]{2,1,0:T(8,128)(2,1)S(1)}, f32[2,32,128]{2,1,0:T(8,128)S(1)}, bf16[4,224,128]{2,1,0:T(8,128)(2,1)S(1)}, f32[32,1,128]{2,1,0:T(1,128)}) custom-call(s32[5]{0:T(128)S(1)} %stack.23.at_ref, bf16[16,128,128]{2,1,0:T(8,128)(2,1)S(1)} %bitcast.12, f32[5,16,128]{2,1,0:T(8,128)S(1)} %get-tuple-element.20.planes_ref, ...), custom_call_target="tpu_custom_call" | custom-call | tf_op jit(solution)/shard_map/second/pallas_call | solution.py:336
  28.6 10.6 %all_to_all.20.got_ref = bf16[4,224,128]{2,1,0:T(8,128)(2,1)S(1)} all-to-all(bf16[4,224,128]{2,1,0:T(8,128)(2,1)S(1)} %get-tuple-element.27), channel_id=1, replica_groups=mesh['dp'=8,'lat_0'=4,'lat_1'=2,'lat_2'=2,'lon'=4] {'lon'}, dimensions={0} | all-to-all | bytes 458752 | tf_op jit(solution)/shard_map/all_to_all | solution.py:395
  39.1 4.7 %all-to-all-start = ((f32[32,1,128]{2,1,0:T(1,128)}), f32[32,1,128]{2,1,0:T(1,128)S(1)}, u32[]{:S(2)}, u32[]{:S(2)}) async-start(f32[32,1,128]{2,1,0:T(1,128)} %get-tuple-element.24), calls=%async_computation | async-start | bytes 32768 | tf_op jit(solution)/shard_map/all_to_all | solution.py:396
  43.9 2.1 %forward.1 = (bf16[20,144,128]{2,1,0:T(8,128)(2,1)S(1)}, f32[18,144,128]{2,1,0:T(8,128)S(1)}, f32[128,128]{1,0:T(8,128)S(1)}) custom-call(s32[5]{0:T(128)S(1)} %stack.23.at_ref, bf16[16,128,128]{2,1,0:T(8,128)(2,1)S(1)} %bitcast.13, bf16[4,128,128]{2,1,0:T(8,128)(2,1)S(1)} %get-tuple-element.25.ends_ref, f32[2,32,128]{2,1,0:T(8,128)S(1)} %get-tuple-element.26.fields_ref, ...), custom_call_target="tpu_custom_call" | custom-call | tf_op jit(solution)/shard_map/forward/pallas_call | solution.py:336
  46.1 5.1 %all-to-all-done.total_ref = f32[32,1,128]{2,1,0:T(1,128)S(1)} async-done(((f32[32,1,128]{2,1,0:T(1,128)}), f32[32,1,128]{2,1,0:T(1,128)S(1)}, u32[]{:S(2)}, u32[]{:S(2)}) %all-to-all-start) | async-done | bytes 16416 | tf_op jit(solution)/shard_map/all_to_all | solution.py:396
  51.2 2.3 %backward.1 = (bf16[18,144,128]{2,1,0:T(8,128)(2,1)S(1)}, bf16[32,40,128]{2,1,0:T(8,128)(2,1)S(1)}) custom-call(f32[32,1,128]{2,1,0:T(1,128)S(1)} %all-to-all-done.total_ref, f32[18,144,128]{2,1,0:T(8,128)S(1)} %get-tuple-element.28.preact_ref, f32[128,128]{1,0:T(8,128)S(1)} %get-tuple-element.29.force_ref, ...), custom_call_target="tpu_custom_call" | custom-call | tf_op jit(solution)/shard_map/backward/pallas_call | solution.py:336
  53.5 0.9 copy-done.3
  54.4 13.1 %all_to_all.21.got_ref = bf16[32,40,128]{2,1,0:T(8,128)(2,1)S(1)} all-to-all(bf16[32,40,128]{2,1,0:T(8,128)(2,1)S(1)} %get-tuple-element.32), channel_id=1, replica_groups=mesh['dp'=8,'lat_0'=4,'lat_1'=2,'lat_2'=2,'lon'=4] {'lat_0','lat_2','lon'}, dimensions={0} | all-to-all | bytes 655360 | tf_op jit(solution)/shard_map/all_to_all | solution.py:417
  67.5 0.7 middle.1
  68.2 13.5 %all-to-all-start.3 = ((bf16[16,24,128]{2,1,0:T(8,128)(2,1)}), bf16[16,24,128]{2,1,0:T(8,128)(2,1)S(1)}, u32[]{:S(2)}, u32[]{:S(2)}) async-start(bf16[16,24,128]{2,1,0:T(8,128)(2,1)} %middle.1), calls=%async_computation.3 | async-start | bytes 196608 | tf_op jit(solution)/shard_map/all_to_all | solution.py:419
  81.7 2.1 %input_grad.1 = bf16[16,128,128]{2,1,0:T(8,128)(2,1)} custom-call(bf16[18,144,128]{2,1,0:T(8,128)(2,1)S(1)} %copy-done.4, bf16[3,3,128,128]{3,2,1,0:T(8,128)(2,1)S(1)} %copy-done.2), custom_call_target="tpu_custom_call" | custom-call | tf_op jit(solution)/shard_map/input_grad/pallas_call | solution.py:336
  83.8 11.3 %all-to-all-done.3.got_ref = bf16[16,24,128]{2,1,0:T(8,128)(2,1)S(1)} async-done(((bf16[16,24,128]{2,1,0:T(8,128)(2,1)}), bf16[16,24,128]{2,1,0:T(8,128)(2,1)S(1)}, u32[]{:S(2)}, u32[]{:S(2)}) %all-to-all-start.3) | async-done | bytes 98336 | tf_op jit(solution)/shard_map/all_to_all | solution.py:419
  95.0 0.5 last.1
  95.6 0.6 copy.13
  (19 shorter events, 0.0 us)
Async XLA Ops:
  0.6 43.3 %copy-start.10 = (f32[6]{0:T(128)S(1)}, f32[6]{0:T(128)}, u32[]{:S(2)}) copy-start(f32[6]{0:T(128)} %beta_ref.1) | copy-start | bytes 76
  0.6 43.3 %copy-start.9 = (f32[6]{0:T(128)S(1)}, f32[6]{0:T(128)}, u32[]{:S(2)}) copy-start(f32[6]{0:T(128)} %alpha_ref.1) | copy-start | bytes 76
  0.7 43.3 %copy-start.8 = (f32[128]{0:T(128)S(1)}, f32[128]{0:T(128)}, u32[]{:S(2)}) copy-start(f32[128]{0:T(128)} %param.11) | copy-start | bytes 1540
  0.8 1.0 %copy-start = (bf16[1,16,128,128]{3,2,1,0:T(8,128)(2,1)S(1)}, bf16[1,16,128,128]{3,2,1,0:T(8,128)(2,1)}, u32[]{:S(2)}) copy-start(bf16[1,16,128,128]{3,2,1,0:T(8,128)(2,1)} %param.9) | copy-start | bytes 1572868
  1.8 0.7 copy-start.5
  2.5 0.7 copy-start.6
  3.2 0.7 copy-start.7
  3.9 40.0 %copy-start.1 = (bf16[1,16,128,128]{3,2,1,0:T(8,128)(2,1)S(1)}, bf16[1,16,128,128]{3,2,1,0:T(8,128)(2,1)}, u32[]{:S(2)}) copy-start(bf16[1,16,128,128]{3,2,1,0:T(8,128)(2,1)} %param.9) | copy-start | bytes 1572868
  3.9 40.0 %copy-start.2 = (bf16[3,3,128,128]{3,2,1,0:T(8,128)(2,1)S(1)}, bf16[3,3,128,128]{3,2,1,0:T(8,128)(2,1)}, u32[]{:S(2)}) copy-start(bf16[3,3,128,128]{3,2,1,0:T(8,128)(2,1)} %weight_ref.3) | copy-start | bytes 884740
  4.6 46.6 %copy-start.11 = (f32[128]{0:T(128)S(1)}, f32[128]{0:T(128)}, u32[]{:S(2)}) copy-start(f32[128]{0:T(128)} %param.12) | copy-start | bytes 1540
  4.6 22.8 %collective-permute-start = (bf16[304,128]{1,0:T(8,128)(2,1)S(1)}, bf16[304,128]{1,0:T(8,128)(2,1)S(1)}, u32[]{:S(2)}, u32[]{:S(2)}) collective-permute-start(bf16[304,128]{1,0:T(8,128)(2,1)S(1)} %get-tuple-element.22), channel_id=1, source_target_pairs={{4,8},{12,16},{20,24},{28,32},{36,40},{44,48},{52,56},{60,0},{8,4}... | collective-permute-start | bytes 233480 | tf_op jit(solution)/shard_map/ppermute | solution.py:380
  21.3 6.0 %collective-permute-start.1 = (bf16[304,128]{1,0:T(8,128)(2,1)S(1)}, bf16[304,128]{1,0:T(8,128)(2,1)S(1)}, u32[]{:S(2)}, u32[]{:S(2)}) collective-permute-start(bf16[304,128]{1,0:T(8,128)(2,1)S(1)} %get-tuple-element.23), channel_id=1, source_target_pairs={{0,4},{4,0},{1,5},{5,1},{2,6},{6,2},{3,7},{7,3},{8,12},{12,8},{9,1... | collective-permute-start | bytes 233480 | tf_op jit(solution)/shard_map/ppermute | solution.py:381
  39.1 12.0 %all-to-all-start = ((f32[32,1,128]{2,1,0:T(1,128)}), f32[32,1,128]{2,1,0:T(1,128)S(1)}, u32[]{:S(2)}, u32[]{:S(2)}) async-start(f32[32,1,128]{2,1,0:T(1,128)} %get-tuple-element.24), calls=%async_computation | async-start | bytes 32768 | tf_op jit(solution)/shard_map/all_to_all | solution.py:396
  53.5 0.9 copy-start.3
  54.4 27.3 %copy-start.4 = (bf16[18,144,128]{2,1,0:T(8,128)(2,1)S(1)}, bf16[18,144,128]{2,1,0:T(8,128)(2,1)}, u32[]{:S(2)}) copy-start(bf16[18,144,128]{2,1,0:T(8,128)(2,1)} %copy-done.3) | copy-start | bytes 1990660
  68.2 26.9 %all-to-all-start.3 = ((bf16[16,24,128]{2,1,0:T(8,128)(2,1)}), bf16[16,24,128]{2,1,0:T(8,128)(2,1)S(1)}, u32[]{:S(2)}, u32[]{:S(2)}) async-start(bf16[16,24,128]{2,1,0:T(8,128)(2,1)} %middle.1), calls=%async_computation.3 | async-start | bytes 196608 | tf_op jit(solution)/shard_map/all_to_all | solution.py:419

commit v4 on v3

--- a/solution.py
+++ b/solution.py
@@ -15,11 +15,12 @@
 WIDE = 144
 PACK = 32
 PLANES = 5
-SENT = 64 + PLANES * PACK
+SENT = 64 + PACK + 16
 
 helm_coef = 0.5
 VMEM = pl.BlockSpec(memory_space=pltpu.VMEM)
 SMEM = pl.BlockSpec(memory_space=pltpu.SMEM)
+HBM = pl.BlockSpec(memory_space=pltpu.HBM)
 
 
 def rounded(values):
@@ -40,32 +41,51 @@
 
 
 def first_kernel(
-    at_ref, hidden_ref, cot_ref, mask_ref, depth_ref, cross_ref, pair_ref, planes_ref, sums_ref
+    at_ref, hidden_ref, cot_hbm, mask_hbm, depth_hbm,
+    cross_ref, pair_ref, planes_ref, sums_ref,
+    cot_ref, mask_ref, depth_ref, sems,
 ):
-    rows = hidden_ref.shape[0]
+    rows = mask_ref.shape[0]
     upper = at_ref[0] == 0
+    last = (rows - 2) * 128
+    starts = (jnp.where(upper, 0, last), jnp.where(upper, last, 0))
+    copies = [
+        pltpu.make_async_copy(cot_hbm.at[0], cot_ref, sems.at[0]),
+        pltpu.make_async_copy(mask_hbm, mask_ref, sems.at[1]),
+        pltpu.make_async_copy(depth_hbm, depth_ref, sems.at[2]),
+    ]
+    for k, ref in enumerate((cross_ref, pair_ref)):
+        start = pl.multiple_of(starts[k], 128)
+        copies.append(
+            pltpu.make_async_copy(
+                hidden_ref.at[pl.ds(start, 256)], ref.at[pl.ds(0, 256)], sems.at[3 + k]
+            )
+        )
+    for copy in copies:
+        copy.start()
+    for copy in copies[:3]:
+        copy.wait()
     mask = mask_ref[...].astype(jnp.float32)
-    wet = mask * cot_ref[0]
+    wet = mask * cot_ref[...]
     planes = pieces_of(wet, 3) + pieces_of(mask * depth_ref[...], 2)
-    summed, counted = jnp.sum(wet), jnp.sum(mask)
-    sums_ref[0:1] = full(summed)
-    sums_ref[1:2] = full(counted)
-    sums = pieces_of(full(summed), 3) + pieces_of(full(counted), 3)
-    sums = jnp.concatenate(sums + [jnp.zeros((2, 128), jnp.float32)], axis=0)
+    lane = lax.broadcasted_iota(jnp.int32, (1, 128), 1)
+    sums = jnp.where(lane < 64, full(jnp.sum(wet)), full(jnp.sum(mask)))
+    sums_ref[...] = jnp.broadcast_to(sums[None], sums_ref.shape)
     for k in range(PLANES):
         planes_ref[k] = planes[k]
+    planes = planes + [planes[0]]
     for ref, top in ((cross_ref, upper), (pair_ref, jnp.logical_not(upper))):
-        start = jnp.where(top, 0, rows - 2)
-        ref[0:256] = hidden_ref[pl.ds(start, 2)].reshape(256, 128)
-        near = [jnp.where(top, p[0:8], p[rows - 8 : rows]) for p in planes] + [sums]
+        near = [jnp.where(top, p[0:8], p[rows - 8 : rows]) for p in planes]
         for k in range(0, 6, 2):
             tile = jnp.concatenate(near[k : k + 2], axis=0)
             ref[256 + k * 8 : 272 + k * 8] = tile.astype(jnp.bfloat16)
+    for copy in copies[3:]:
+        copy.wait()
 
 
 def second_kernel(
     at_ref, hidden_ref, planes_ref, sums_ref, cross_ref, pair_ref,
-    ends_ref, fields_ref, sent_ref, total_ref,
+    ends_ref, fields_ref, sent_ref,
 ):
     rows = hidden_ref.shape[0]
     upper = at_ref[0] == 0
@@ -79,12 +99,11 @@
         ends_ref[k + 2] = jnp.where(keep_below > 0.0, jnp.where(upper, pair, cross), zero)
     cross = cross_ref[256:304].astype(jnp.float32)
     pair = pair_ref[256:304].astype(jnp.float32)
-    got = cross[40:48]
-    summed = sums_ref[0:1] + got[0:1] + got[1:2] + got[2:3]
-    counted = sums_ref[1:2] + got[3:4] + got[4:5] + got[5:6]
-    lane = lax.broadcasted_iota(jnp.int32, (1, 128), 1)
-    total = jnp.where(lane < 64, summed, counted)
-    total_ref[...] = jnp.broadcast_to(total[None], total_ref.shape)
+    total = jnp.sum(sums_ref[...], axis=0)
+    summed = jnp.broadcast_to(total[:, 0:1], (1, 128))
+    counted = jnp.broadcast_to(total[:, 127:128], (1, 128))
+    sums = pieces_of(summed, 3) + pieces_of(counted, 3)
+    sums = jnp.concatenate(sums + [jnp.zeros((10, 128), jnp.float32)], axis=0)
     above = jnp.where(upper, cross, pair) * keep_above
     below = jnp.where(upper, pair, cross) * keep_below
     fields = []
@@ -109,19 +128,23 @@
         for k, row in enumerate((head[0:1], head[1:2], tail[14:15], tail[15:16])):
             columns[k][r // 8] = jnp.where(place == r % 8, row, columns[k][r // 8])
     columns = [jnp.concatenate(tiles, axis=0) for tiles in columns]
-    fields = [f.astype(jnp.bfloat16) for f in fields]
+    lane = lax.broadcasted_iota(jnp.int32, (PACK, 128), 1) // 8
+    heads = tails = jnp.zeros((PACK, 128), jnp.float32)
+    for k in range(PLANES):
+        head = fields[k] if k == 0 else pltpu.roll(fields[k], 8 * k, 1)
+        heads = jnp.where(lane == k, head, heads)
+        tails = jnp.where(lane == k, pltpu.roll(fields[k], 8 * k + 8, 1), tails)
+    heads = jnp.concatenate(columns[0:2] + [heads, sums], axis=0)
+    tails = jnp.concatenate(columns[2:4] + [tails, sums], axis=0)
     for peer in range(sent_ref.shape[0]):
-        to_right = at_ref[4] == peer
-        for k in range(2):
-            chosen = jnp.where(to_right, columns[2 + k], columns[k])
-            sent_ref[peer, k * 32 : k * 32 + 32] = chosen.astype(jnp.bfloat16)
-        for k in range(PLANES):
-            sent_ref[peer, 64 + k * PACK : 64 + k * PACK + PACK] = fields[k]
-
-
-def forward_kernel(
-    at_ref, hidden_ref, ends_ref, fields_ref, got_ref, weight_ref, bias_ref, alpha_ref, beta_ref,
-    ext_ref, preact_ref, force_ref, rhs_ref,
+        sent_ref[peer] = jnp.where(at_ref[4] == peer, tails, heads).astype(jnp.bfloat16)
+
+
+def main_kernel(
+    at_ref, hidden_ref, ends_ref, fields_ref, got_ref, weight_ref, bias_ref, proj_ref,
+    alpha_ref, beta_ref,
+    grad_hbm, sent_ref,
+    ext_ref, preact_ref, rhs_ref, grad_ref, moved_ref, total_ref, sem,
 ):
     rows = hidden_ref.shape[0]
     left, right = at_ref[3], at_ref[4]
@@ -142,12 +165,14 @@
             rhs_ref[a * 128 : a * 128 + 128, c * 128 : c * 128 + 128] = weight_ref[a, c]
 
     lane = lax.broadcasted_iota(jnp.int32, (2 * PACK, 128), 1)
-    second = jnp.where(
-        jnp.concatenate([lane] * 3, axis=0)[: PLANES * PACK] < 64,
-        got_ref[right, 64:SENT].astype(jnp.float32),
-        got_ref[left, 64:SENT].astype(jnp.float32),
-    )
-    second = [second[k * PACK : k * PACK + PACK] for k in range(PLANES)]
+    from_left = got_ref[left, 64 : 64 + PACK].astype(jnp.float32)
+    from_right = got_ref[right, 64 : 64 + PACK].astype(jnp.float32)
+    second = []
+    for k in range(PLANES):
+        beyond = from_right if k == 0 else pltpu.roll(from_right, 128 - 8 * k, 1)
+        before = pltpu.roll(from_left, 120 - 8 * k, 1)
+        near = lane[:PACK]
+        second.append(jnp.where(near < 8, beyond, jnp.where(near >= 120, before, 0.0)))
     start = jnp.concatenate([fields_ref[0], second[0] + second[1] + second[2]], axis=0)
     wet_depth = jnp.concatenate([fields_ref[1], second[3] + second[4]], axis=0)
     mask = jnp.where(wet_depth > 0.0, 1.0, 0.0)
@@ -189,7 +214,11 @@
             residual = residual - alpha_ref[k] * applied
             direction = residual + beta_ref[k] * direction
     result = result * jnp.concatenate([mask, mask], axis=0)
-    force_ref[...] = result.T
+    sums = got_ref[:, 64 + PACK : SENT].astype(jnp.float32)
+    sums = jnp.sum(sums, axis=0)
+    mean = (sums[0:1] + sums[1:2] + sums[2:3]) / (sums[3:4] + sums[4:5] + sums[5:6])
+    force = result.T
+    force = force - mean * pltpu.roll(force, 64, 1)
 
     group = 6
     bias = bias_ref[...]
@@ -207,16 +236,6 @@
                 + bias
             )
 
-
-def backward_kernel(
-    total_ref, preact_ref, force_ref, ext_ref, proj_ref,
-    grad_ref, sent_ref, moved_ref, weight_ref,
-):
-    rows = grad_ref.shape[0] - 2
-    total = jnp.sum(total_ref[...], axis=0)
-    mean = jnp.broadcast_to(total[:, 0:1], (1, 128)) / jnp.broadcast_to(total[:, 127:128], (1, 128))
-    force = force_ref[...]
-    force = force - mean * pltpu.roll(force, 64, 1)
     proj = proj_ref[...]
     sum_bias = jnp.zeros((8, 128), jnp.float32)
     sum_proj = jnp.zeros((8, 128), jnp.float32)
@@ -246,6 +265,8 @@
             moved_ref[g - 1, :, 0:128] = pltpu.roll(own, WIDE - 1, 0).astype(jnp.bfloat16)
             moved_ref[g - 1, :, 128:256] = own.astype(jnp.bfloat16)
             moved_ref[g - 1, :, 256:384] = pltpu.roll(own, 1, 0).astype(jnp.bfloat16)
+    copy = pltpu.make_async_copy(grad_ref, grad_hbm, sem)
+    copy.start()
     moved = moved_ref[...].reshape(rows * WIDE, 384)
     for a in range(3):
         cells = ext_ref[a + 1 : a + 1 + rows].reshape(rows * WIDE, 128)
@@ -253,7 +274,7 @@
             cells, moved, (((0,), (0,)), ((), ())), preferred_element_type=jnp.float32
         )
         for c in range(3):
-            weight_ref[a * 3 + c] = out[:, c * 128 : c * 128 + 128]
+            total_ref[a * 3 + c] = out[:, c * 128 : c * 128 + 128]
     vectors = jnp.concatenate(
         [jnp.sum(sum_bias, axis=0, keepdims=True), jnp.sum(sum_proj, axis=0, keepdims=True)], axis=0
     )
@@ -273,7 +294,7 @@
                         continue
                     z, k = slot // 9, slot % 9
                     start = pl.multiple_of(((y * 2 + z) * 2 + c) * 8, 8)
-                    piece = weight_ref[k, pl.ds(start, 8)]
+                    piece = total_ref[k, pl.ds(start, 8)]
                     if j != x:
                         piece = pltpu.roll(piece, (2 * j - 2 * x) % 8, 0)
                     tile = jnp.where(place == j, piece, tile)
@@ -282,6 +303,7 @@
         return carry
 
     lax.fori_loop(0, 8, one_pair, 0)
+    copy.wait()
 
 
 def middle_kernel(got_ref, sent_ref):
@@ -299,8 +321,7 @@
 def last_kernel(scale, got_ref, weight_ref, bias_ref, proj_ref):
     total = jnp.sum(got_ref[...].astype(jnp.float32), axis=0) * scale
     for k in range(9):
-        for e in range(2):
-            weight_ref[e, k // 3, k % 3 : k % 3 + 1] = total[k * 2 + e : k * 2 + e + 1]
+        weight_ref[k // 3, k % 3] = total[k * 2 : k * 2 + 2]
     bias_ref[...] = total[18:19] + total[20:21]
     proj_ref[...] = total[19:20] + total[21:22]
 
@@ -332,15 +353,14 @@
             out_ref[y + j] = total[0:128].astype(jnp.bfloat16)
 
 
-def call(kernel, shapes, scratch, in_specs, args, name):
+def call(kernel, shapes, scratch, in_specs, args, out_specs=None):
     return pl.pallas_call(
         kernel,
         out_shape=shapes,
         in_specs=in_specs,
-        out_specs=jax.tree.map(lambda _: VMEM, shapes),
+        out_specs=jax.tree.map(lambda _: VMEM, shapes) if out_specs is None else out_specs,
         scratch_shapes=scratch,
         compiler_params=pltpu.CompilerParams(vmem_limit_bytes=40 * 1024 * 1024),
-        name=name,
     )(*args)
 
 
@@ -369,53 +389,55 @@
             shape((304, 128), narrow),
             shape((304, 128), narrow),
             shape((PLANES, rows, 128), wide),
-            shape((2, 128), wide),
+            shape((n_lat, 1, 128), wide),
         ),
-        [],
-        [SMEM] + [VMEM] * 4,
-        (at, hidden, surface_cotangent, sea_mask, ocean_depth),
-        "first",
+        [
+            pltpu.VMEM((rows, 128), wide),
+            pltpu.VMEM((rows, 128), jnp.int32),
+            pltpu.VMEM((rows, 128), wide),
+            pltpu.SemaphoreType.DMA((5,)),
+        ],
+        [SMEM] + [HBM] * 4,
+        (at, hidden.reshape(rows * 128, 128), surface_cotangent, sea_mask, ocean_depth),
     )
     odd = [(i, (i + 1) % n_lat) for i in range(1, n_lat, 2)]
     cross = lax.ppermute(cross, LAT, odd + [(j, i) for i, j in odd])
     pair = lax.ppermute(pair, "lat_2", [(0, 1), (1, 0)])
-    ends, fields, sent, total = call(
+    sums, pair = lax.optimization_barrier((sums, pair))
+    sums = lax.all_to_all(sums, LAT, 0, 0, tiled=True)
+    ends, fields, sent = call(
         second_kernel,
         (
             shape((4, 128, 128), narrow),
             shape((2, PACK, 128), wide),
             shape((n_x, SENT, 128), narrow),
-            shape((n_all, 1, 128), wide),
         ),
         [],
         [SMEM] + [VMEM] * 5,
         (at, hidden, planes, sums, cross, pair),
-        "second",
     )
     got = lax.all_to_all(sent, "lon", 0, 0, tiled=True)
-    total = lax.all_to_all(total, ("lat_0", "lat_2", "lon"), 0, 0, tiled=True)
-    ext, preact, force = call(
-        forward_kernel,
+    grad, sent = call(
+        main_kernel,
+        (shape((rows + 2, WIDE, 128), narrow), shape((n_all, 40, 128), narrow)),
+        [
+            pltpu.VMEM((rows + 4, WIDE, 128), narrow),
+            pltpu.VMEM((rows + 2, WIDE, 128), wide),
+            pltpu.VMEM((384, 384), narrow),
+            pltpu.VMEM((rows + 2, WIDE, 128), narrow),
+            pltpu.VMEM((rows, WIDE, 384), narrow),
+            pltpu.VMEM((9, 128, 128), wide),
+            pltpu.SemaphoreType.DMA,
+        ],
+        [SMEM] + [VMEM] * 7 + [SMEM] * 2,
         (
-            shape((rows + 4, WIDE, 128), narrow),
-            shape((rows + 2, WIDE, 128), wide),
-            shape((128, 128), wide),
+            at, hidden, ends, fields, got, conv_weight, conv_bias[None], proj_weight[None],
+            step_alpha, step_beta,
         ),
-        [pltpu.VMEM((384, 384), narrow)],
-        [SMEM] + [VMEM] * 6 + [SMEM] * 2,
-        (at, hidden, ends, fields, got, conv_weight, conv_bias[None], step_alpha, step_beta),
-        "forward",
-    )
-    grad, sent = call(
-        backward_kernel,
-        (shape((rows + 2, WIDE, 128), narrow), shape((n_all, 40, 128), narrow)),
-        [pltpu.VMEM((rows, WIDE, 384), narrow), pltpu.VMEM((9, 128, 128), wide)],
-        [VMEM] * 5,
-        (total, preact, force, ext, proj_weight[None]),
-        "backward",
+        (HBM, VMEM),
     )
     got = lax.all_to_all(sent, ("lat_0", "lat_2", "lon"), 0, 0, tiled=True)
-    sent = call(middle_kernel, shape((n_z, 24, 128), narrow), [], [VMEM], (got,), "middle")
+    sent = call(middle_kernel, shape((n_z, 24, 128), narrow), [], [VMEM], (got,))
     got = lax.all_to_all(sent, ("lat_1", "dp"), 0, 0, tiled=True)
     grad_hidden = call(
         input_kernel,
@@ -423,18 +445,16 @@
         [pltpu.VMEM((384, 384), narrow)],
         [VMEM] * 2,
         (grad, conv_weight),
-        "input_grad",
     )
     cells = rows * 128 * lax.axis_size("dp") * n_lat * n_x
     own_weight, total_bias, total_proj = call(
         functools.partial(last_kernel, 1.0 / math.sqrt(cells)),
-        (shape((2, 3, 3, 128), wide), shape((1, 128), wide), shape((1, 128), wide)),
+        (shape((3, 3, 2, 128), wide), shape((1, 128), wide), shape((1, 128), wide)),
         [],
         [VMEM],
         (got,),
-        "last",
-    )
-    return grad_hidden[None], own_weight, total_bias[0], total_proj[0]
+    )
+    return grad_hidden[None], own_weight.transpose(2, 0, 1, 3), total_bias[0], total_proj[0]
 
 
 def solution(mesh):

time: 96.7 us -> 94.2 us (0.974)
  waiting for transfers between devices: 20.5 us -> 25.9 us
  starting transfers between devices: 36.9 us -> 31.7 us
  local copies, waits for them, and re-layouts: 4.71 us -> 2.42 us
    all_to_all x1, waiting for transfers between devices: 5.09 us -> 12.1 us  [shards(): sums = lax.all_to_all(sums, LAT, 0, 0, tiled=True)]
    all_to_all x1, starting transfers between devices: 13.5 us -> 8.94 us  [shards(): got = lax.all_to_all(sent, ('lat_1', 'dp'), 0, 0, tiled=True)]
    unnamed x25 -> x20, local copies, waits for them, and re-layouts: 4.63 us -> 2.34 us
    ppermute x1, waiting for transfers between devices: 4.11 us -> 2.6 us  [shards(): cross = lax.ppermute(cross, LAT, odd + [(j, i) for i, j in odd])]
    all_to_all x1, starting transfers between devices: 4.73 us -> 3.48 us  [shards(): sums = lax.all_to_all(sums, LAT, 0, 0, tiled=True)]
    pallas_call x7 -> x6, Pallas kernels: 9.66 us -> 10.1 us  [call(): pl.pallas_call(kernel, out_shape=shapes, in_specs=in_specs, out_specs=jax...]
  transfers between devices with their start and end apart: 4 -> 4, of which waited for: 3 -> 3; matrix products, arithmetic and copies ran while one was open for 0% -> 0% of each run, Pallas kernels for 4% -> 2%
where the time goes in v4:
time: 94.2 us; the launch traced here: 93.7 us
  starting transfers between devices  31.7 us (34%)
  waiting for transfers between devices  25.9 us (27%)
  blocking collectives  22.9 us (24%)
  Pallas kernels  10.1 us (11%)
  local copies, waits for them, and re-layouts  2.42 us (3%)
    ppermute x1, starting transfers between devices, shards(): cross = lax.ppermute(cross, LAT, odd + [(j, i) for i, j in odd])  17.4 us
    all_to_all x1, blocking collectives, shards(): got = lax.all_to_all(sent, ('lat_0', 'lat_2', 'lon'), 0, 0, tiled=True)  12.9 us
    all_to_all x1, waiting for transfers between devices, shards(): sums = lax.all_to_all(sums, LAT, 0, 0, tiled=True)  12.1 us
    all_to_all x1, waiting for transfers between devices, shards(): got = lax.all_to_all(sent, ('lat_1', 'dp'), 0, 0, tiled=True)  11.3 us
    pallas_call x6, Pallas kernels, call(): pl.pallas_call(kernel, out_shape=shapes, in_specs=in_specs, out_specs=jax...  10.1 us
    all_to_all x1, blocking collectives, shards(): got = lax.all_to_all(sent, 'lon', 0, 0, tiled=True)  9.98 us
    all_to_all x1, starting transfers between devices, shards(): got = lax.all_to_all(sent, ('lat_1', 'dp'), 0, 0, tiled=True)  8.94 us
    all_to_all x1, starting transfers between devices, shards(): sums = lax.all_to_all(sums, LAT, 0, 0, tiled=True)  3.48 us
  transfers between devices with their start and end apart: 4, of which 3 were waited for; matrix products, arithmetic and copies ran while one was open for 0% of the time, Pallas kernels for 2%

profile of v4, /device:TPU:32, one launch (start us, length us, event | category | flops | bytes accessed | tf_op | source)
XLA Modules:
  0.0 93.7 jit_solution(1739398873088962007)
XLA Ops:
  0.7 0.1 stack.23.at_ref
  0.8 0.6 copy-done.5
  1.4 0.0 copy-done.3
  1.4 0.0 copy-done.4
  1.4 1.0 %copy-done = bf16[1,16,128,128]{3,2,1,0:T(8,128)(2,1)S(1)} copy-done((bf16[1,16,128,128]{3,2,1,0:T(8,128)(2,1)S(1)}, bf16[1,16,128,128]{3,2,1,0:T(8,128)(2,1)}, u32[]{:S(2)}) %copy-start) | copy-done | bytes 524312
  2.4 1.5 %shard_map.120 = (bf16[304,128]{1,0:T(8,128)(2,1)S(1)}, bf16[304,128]{1,0:T(8,128)(2,1)S(1)}, f32[5,16,128]{2,1,0:T(8,128)S(1)}, f32[16,1,128]{2,1,0:T(1,128)}) custom-call(s32[5]{0:T(128)S(1)} %stack.23.at_ref, bf16[2048,128]{1,0:T(8,128)(2,1)S(1)} %bitcast.13, f32[1,16,128]{2,1,0:T(8,128)S(1)} %copy-done.3, s32[16,128]{1,0:T(8,128)S(1)} %copy-done.4, ...), custom_call_target="tpu_custom_call" | custom-call | tf_op jit(solution)/shard_map/pallas_call | solution.py:357
  4.0 1.9 %collective-permute-start = (bf16[304,128]{1,0:T(8,128)(2,1)S(1)}, bf16[304,128]{1,0:T(8,128)(2,1)S(1)}, u32[]{:S(2)}, u32[]{:S(2)}) collective-permute-start(bf16[304,128]{1,0:T(8,128)(2,1)S(1)} %get-tuple-element.20), channel_id=1, source_target_pairs={{0,4},{4,0},{1,5},{5,1},{2,6},{6,2},{3,7},{7,3},{8,12},{12,8},{9,1... | collective-permute-start | bytes 233480 | tf_op jit(solution)/shard_map/ppermute | solution.py:405
  5.9 17.4 %collective-permute-start.1 = (bf16[304,128]{1,0:T(8,128)(2,1)S(1)}, bf16[304,128]{1,0:T(8,128)(2,1)S(1)}, u32[]{:S(2)}, u32[]{:S(2)}) collective-permute-start(bf16[304,128]{1,0:T(8,128)(2,1)S(1)} %get-tuple-element.22), channel_id=1, source_target_pairs={{4,8},{12,16},{20,24},{28,32},{36,40},{44,48},{52,56},{60,0},{8,4}... | collective-permute-start | bytes 233480 | tf_op jit(solution)/shard_map/ppermute | solution.py:404
  23.3 3.5 %all-to-all-start = ((f32[16,1,128]{2,1,0:T(1,128)}), f32[16,1,128]{2,1,0:T(1,128)S(1)}, u32[]{:S(2)}, u32[]{:S(2)}) async-start(f32[16,1,128]{2,1,0:T(1,128)} %get-tuple-element.21), calls=%async_computation | async-start | bytes 16384 | tf_op jit(solution)/shard_map/all_to_all | solution.py:407
  26.8 2.6 %collective-permute-done.1.cross_ref = bf16[304,128]{1,0:T(8,128)(2,1)S(1)} collective-permute-done((bf16[304,128]{1,0:T(8,128)(2,1)S(1)}, bf16[304,128]{1,0:T(8,128)(2,1)S(1)}, u32[]{:S(2)}, u32[]{:S(2)}) %collective-permute-start.1) | collective-permute-done | bytes 77856 | tf_op jit(solution)/shard_map/ppermute | solution.py:404
  29.4 12.1 %all-to-all-done.sums_ref = f32[16,1,128]{2,1,0:T(1,128)S(1)} async-done(((f32[16,1,128]{2,1,0:T(1,128)}), f32[16,1,128]{2,1,0:T(1,128)S(1)}, u32[]{:S(2)}, u32[]{:S(2)}) %all-to-all-start) | async-done | bytes 8224 | tf_op jit(solution)/shard_map/all_to_all | solution.py:407
  41.4 0.7 shard_map.121
  42.1 0.0 copy-start.9
  42.1 10.0 %all_to_all.20.got_ref = bf16[4,112,128]{2,1,0:T(8,128)(2,1)S(1)} all-to-all(bf16[4,112,128]{2,1,0:T(8,128)(2,1)S(1)} %get-tuple-element.26), channel_id=1, replica_groups=mesh['dp'=8,'lat_0'=4,'lat_1'=2,'lat_2'=2,'lon'=4] {'lon'}, dimensions={0} | all-to-all | bytes 229376 | tf_op jit(solution)/shard_map/all_to_all | solution.py:419
  52.1 0.6 copy-done.6
  52.8 0.0 copy-done.7
  52.8 0.0 copy-done.8
  52.8 4.5 %shard_map.122 = (bf16[18,144,128]{2,1,0:T(8,128)(2,1)S(1)}, bf16[32,40,128]{2,1,0:T(8,128)(2,1)S(1)}) custom-call(s32[5]{0:T(128)S(1)} %stack.23.at_ref, bf16[16,128,128]{2,1,0:T(8,128)(2,1)S(1)} %bitcast.15, bf16[4,128,128]{2,1,0:T(8,128)(2,1)S(1)} %get-tuple-element.24.ends_ref, f32[2,32,128]{2,1,0:T(8,128)S(1)} %get-tuple-element.25.fields_ref, ...), custom_call_target="tpu_custom_call" | custom-call | tf_op jit(solution)/shard_map/pallas_call | solution.py:357
  57.3 12.9 %all_to_all.21.got_ref = bf16[32,40,128]{2,1,0:T(8,128)(2,1)S(1)} all-to-all(bf16[32,40,128]{2,1,0:T(8,128)(2,1)S(1)} %get-tuple-element.28), channel_id=1, replica_groups=mesh['dp'=8,'lat_0'=4,'lat_1'=2,'lat_2'=2,'lon'=4] {'lat_0','lat_2','lon'}, dimensions={0} | all-to-all | bytes 655360 | tf_op jit(solution)/shard_map/all_to_all | solution.py:439
  70.1 0.7 shard_map.124
  70.8 8.9 %all-to-all-start.3 = ((bf16[16,24,128]{2,1,0:T(8,128)(2,1)}), bf16[16,24,128]{2,1,0:T(8,128)(2,1)S(1)}, u32[]{:S(2)}, u32[]{:S(2)}) async-start(bf16[16,24,128]{2,1,0:T(8,128)(2,1)} %shard_map.124), calls=%async_computation.3 | async-start | bytes 196608 | tf_op jit(solution)/shard_map/all_to_all | solution.py:441
  79.8 2.1 %shard_map.123 = bf16[16,128,128]{2,1,0:T(8,128)(2,1)} custom-call(bf16[18,144,128]{2,1,0:T(8,128)(2,1)S(1)} %get-tuple-element.27.grad_ref, bf16[3,3,128,128]{3,2,1,0:T(8,128)(2,1)S(1)} %copy-done.2), custom_call_target="tpu_custom_call" | custom-call | tf_op jit(solution)/shard_map/pallas_call | solution.py:357
  81.9 11.3 %all-to-all-done.3.got_ref = bf16[16,24,128]{2,1,0:T(8,128)(2,1)S(1)} async-done(((bf16[16,24,128]{2,1,0:T(8,128)(2,1)}), bf16[16,24,128]{2,1,0:T(8,128)(2,1)S(1)}, u32[]{:S(2)}, u32[]{:S(2)}) %all-to-all-start.3) | async-done | bytes 98336 | tf_op jit(solution)/shard_map/all_to_all | solution.py:441
  93.1 0.6 shard_map.125
  (13 shorter events, 0.0 us)
Async XLA Ops:
  0.7 0.7 copy-start.5
  0.7 0.7 copy-start.3
  0.7 0.7 copy-start.4
  1.4 1.0 %copy-start = (bf16[1,16,128,128]{3,2,1,0:T(8,128)(2,1)S(1)}, bf16[1,16,128,128]{3,2,1,0:T(8,128)(2,1)}, u32[]{:S(2)}) copy-start(bf16[1,16,128,128]{3,2,1,0:T(8,128)(2,1)} %param.9) | copy-start | bytes 1572868
  2.4 39.0 %copy-start.1 = (bf16[1,16,128,128]{3,2,1,0:T(8,128)(2,1)S(1)}, bf16[1,16,128,128]{3,2,1,0:T(8,128)(2,1)}, u32[]{:S(2)}) copy-start(bf16[1,16,128,128]{3,2,1,0:T(8,128)(2,1)} %param.9) | copy-start | bytes 1572868
  4.0 19.3 %collective-permute-start = (bf16[304,128]{1,0:T(8,128)(2,1)S(1)}, bf16[304,128]{1,0:T(8,128)(2,1)S(1)}, u32[]{:S(2)}, u32[]{:S(2)}) collective-permute-start(bf16[304,128]{1,0:T(8,128)(2,1)S(1)} %get-tuple-element.20), channel_id=1, source_target_pairs={{0,4},{4,0},{1,5},{5,1},{2,6},{6,2},{3,7},{7,3},{8,12},{12,8},{9,1... | collective-permute-start | bytes 233480 | tf_op jit(solution)/shard_map/ppermute | solution.py:405
  5.9 23.5 %collective-permute-start.1 = (bf16[304,128]{1,0:T(8,128)(2,1)S(1)}, bf16[304,128]{1,0:T(8,128)(2,1)S(1)}, u32[]{:S(2)}, u32[]{:S(2)}) collective-permute-start(bf16[304,128]{1,0:T(8,128)(2,1)S(1)} %get-tuple-element.22), channel_id=1, source_target_pairs={{4,8},{12,16},{20,24},{28,32},{36,40},{44,48},{52,56},{60,0},{8,4}... | collective-permute-start | bytes 233480 | tf_op jit(solution)/shard_map/ppermute | solution.py:404
  23.3 18.1 %all-to-all-start = ((f32[16,1,128]{2,1,0:T(1,128)}), f32[16,1,128]{2,1,0:T(1,128)S(1)}, u32[]{:S(2)}, u32[]{:S(2)}) async-start(f32[16,1,128]{2,1,0:T(1,128)} %get-tuple-element.21), calls=%async_computation | async-start | bytes 16384 | tf_op jit(solution)/shard_map/all_to_all | solution.py:407
  41.4 10.7 %copy-start.2 = (bf16[3,3,128,128]{3,2,1,0:T(8,128)(2,1)S(1)}, bf16[3,3,128,128]{3,2,1,0:T(8,128)(2,1)}, u32[]{:S(2)}) copy-start(bf16[3,3,128,128]{3,2,1,0:T(8,128)(2,1)} %weight_ref.3) | copy-start | bytes 884740
  42.1 10.0 %copy-start.9 = (f32[6]{0:T(128)S(1)}, f32[6]{0:T(128)}, u32[]{:S(2)}) copy-start(f32[6]{0:T(128)} %beta_ref.1) | copy-start | bytes 76
  52.1 0.7 copy-start.6
  52.1 0.7 copy-start.7
  52.1 0.7 copy-start.8
  70.8 22.3 %all-to-all-start.3 = ((bf16[16,24,128]{2,1,0:T(8,128)(2,1)}), bf16[16,24,128]{2,1,0:T(8,128)(2,1)S(1)}, u32[]{:S(2)}, u32[]{:S(2)}) async-start(bf16[16,24,128]{2,1,0:T(8,128)(2,1)} %shard_map.124), calls=%async_computation.3 | async-start | bytes 196608 | tf_op jit(solution)/shard_map/all_to_all | solution.py:441

commit v5 on v3

--- a/solution.py
+++ b/solution.py
@@ -15,11 +15,12 @@
 WIDE = 144
 PACK = 32
 PLANES = 5
-SENT = 64 + PLANES * PACK
+NEAR = 48
 
 helm_coef = 0.5
 VMEM = pl.BlockSpec(memory_space=pltpu.VMEM)
 SMEM = pl.BlockSpec(memory_space=pltpu.SMEM)
+HBM = pl.BlockSpec(memory_space=pltpu.HBM)
 
 
 def rounded(values):
@@ -39,18 +40,29 @@
     return jnp.full((1, 128), value, jnp.float32)
 
 
+def packed(planes, shift):
+    rows = planes[0].shape[0]
+    lane = lax.broadcasted_iota(jnp.int32, (rows, 128), 1) // 8
+    out = jnp.zeros((rows, 128), jnp.float32)
+    for k, plane in enumerate(planes):
+        by = (8 * k + shift) % 128
+        out = jnp.where(lane == k, pltpu.roll(plane, by, 1) if by else plane, out)
+    return out
+
+
 def first_kernel(
-    at_ref, hidden_ref, cot_ref, mask_ref, depth_ref, cross_ref, pair_ref, planes_ref, sums_ref
+    at_ref, hidden_ref, cot_ref, mask_ref, depth_ref,
+    cross_ref, pair_ref, head_ref, tail_ref, near_ref, planes_ref, sums_ref,
 ):
     rows = hidden_ref.shape[0]
     upper = at_ref[0] == 0
     mask = mask_ref[...].astype(jnp.float32)
     wet = mask * cot_ref[0]
     planes = pieces_of(wet, 3) + pieces_of(mask * depth_ref[...], 2)
-    summed, counted = jnp.sum(wet), jnp.sum(mask)
-    sums_ref[0:1] = full(summed)
-    sums_ref[1:2] = full(counted)
-    sums = pieces_of(full(summed), 3) + pieces_of(full(counted), 3)
+    summed, counted = full(jnp.sum(wet)), full(jnp.sum(mask))
+    sums_ref[0:1] = summed
+    sums_ref[1:2] = counted
+    sums = pieces_of(summed, 3) + pieces_of(counted, 3)
     sums = jnp.concatenate(sums + [jnp.zeros((2, 128), jnp.float32)], axis=0)
     for k in range(PLANES):
         planes_ref[k] = planes[k]
@@ -61,95 +73,116 @@
         for k in range(0, 6, 2):
             tile = jnp.concatenate(near[k : k + 2], axis=0)
             ref[256 + k * 8 : 272 + k * 8] = tile.astype(jnp.bfloat16)
-
-
-def second_kernel(
-    at_ref, hidden_ref, planes_ref, sums_ref, cross_ref, pair_ref,
-    ends_ref, fields_ref, sent_ref, total_ref,
+    place = lax.broadcasted_iota(jnp.int32, (8, 128), 0)
+    columns = [[jnp.zeros((8, 128), jnp.float32) for _ in range(2)] for _ in range(4)]
+    for r in range(rows):
+        head = hidden_ref[r, 0:16].astype(jnp.float32)
+        tail = hidden_ref[r, 112:128].astype(jnp.float32)
+        for k, row in enumerate((head[0:1], head[1:2], tail[14:15], tail[15:16])):
+            columns[k][r // 8] = jnp.where(place == r % 8, row, columns[k][r // 8])
+    ends = []
+    for side, ref in ((0, head_ref), (1, tail_ref)):
+        fields = packed(planes, 0 if side == 0 else 8)
+        pair = columns[2 * side : 2 * side + 2]
+        whole = jnp.concatenate([pair[0][0], pair[0][1], pair[1][0], pair[1][1], fields], axis=0)
+        ends.append(whole)
+        corner = jnp.zeros((8, 128), jnp.float32)
+        for r in range(2):
+            for k in range(2):
+                row = jnp.where(upper, pair[k][0][r : r + 1], pair[k][1][6 + r : 7 + r])
+                corner = jnp.where(place == 2 * r + k, row, corner)
+        facing = jnp.where(upper, fields[0:8], fields[rows - 8 : rows])
+        ref[...] = jnp.concatenate([corner, facing], axis=0).astype(jnp.bfloat16)
+    n_x = near_ref.shape[0] // 2
+    for peer in range(n_x):
+        chosen = jnp.where(at_ref[4] == peer, ends[1], ends[0]).astype(jnp.bfloat16)
+        near_ref[peer] = chosen
+        near_ref[n_x + peer] = chosen
+
+
+def sums_kernel(sums_ref, cross_ref, total_ref):
+    got = cross_ref[288:304].astype(jnp.float32)[8:16]
+    summed = sums_ref[0:1] + got[0:1] + got[1:2] + got[2:3]
+    counted = sums_ref[1:2] + got[3:4] + got[4:5] + got[5:6]
+    lane = lax.broadcasted_iota(jnp.int32, (1, 128), 1)
+    total = jnp.where(lane < 64, summed, counted)
+    total_ref[...] = jnp.broadcast_to(total[None], total_ref.shape)
+
+
+def forward_kernel(
+    at_ref, hidden_ref, planes_ref, cross_ref, pair_ref, head_ref, tail_ref, near_ref,
+    weight_ref, bias_ref, alpha_ref, beta_ref,
+    ext_ref, preact_ref, force_ref, rhs_ref,
 ):
     rows = hidden_ref.shape[0]
-    upper = at_ref[0] == 0
+    n_x = near_ref.shape[0] // 2
+    core, left, right = at_ref[0], at_ref[3], at_ref[4]
+    upper = core == 0
     keep_above = jnp.where(at_ref[1] == 0, 0.0, 1.0)
     keep_below = jnp.where(at_ref[2] == 0, 0.0, 1.0)
     zero = jnp.zeros((), jnp.bfloat16)
     for k in range(2):
         cross = cross_ref[k * 128 : k * 128 + 128]
         pair = pair_ref[k * 128 : k * 128 + 128]
-        ends_ref[k] = jnp.where(keep_above > 0.0, jnp.where(upper, cross, pair), zero)
-        ends_ref[k + 2] = jnp.where(keep_below > 0.0, jnp.where(upper, pair, cross), zero)
+        ext_ref[k, 0:128] = jnp.where(keep_above > 0.0, jnp.where(upper, cross, pair), zero)
+        ext_ref[k + rows + 2, 0:128] = jnp.where(
+            keep_below > 0.0, jnp.where(upper, pair, cross), zero
+        )
+    ext_ref[2 : rows + 2, 0:128] = hidden_ref[...]
+
+    place = lax.broadcasted_iota(jnp.int32, (WIDE - 128, 128), 0)
+    tiles = [jnp.zeros((WIDE - 128, 128), jnp.float32) for _ in range(rows + 4)]
+    second = []
+    for side, base, corner_ref in ((right, 0, head_ref), (left, WIDE - 130, tail_ref)):
+        own = near_ref[core * n_x + side].astype(jnp.float32)
+        other = near_ref[(1 - core) * n_x + side].astype(jnp.float32)
+        corner = corner_ref[...].astype(jnp.float32)
+        for k in range(2):
+            for r in range(rows + 4):
+                if r < 2:
+                    mate = other[k * 16 + rows - 2 + r : k * 16 + rows - 1 + r]
+                    row = jnp.where(upper, corner[2 * r + k : 2 * r + k + 1], mate) * keep_above
+                elif r < rows + 2:
+                    row = own[k * 16 + r - 2 : k * 16 + r - 1]
+                else:
+                    j = r - rows - 2
+                    mate = other[k * 16 + j : k * 16 + j + 1]
+                    row = jnp.where(upper, mate, corner[2 * j + k : 2 * j + k + 1]) * keep_below
+                tiles[r] = jnp.where(place == base + k, row, tiles[r])
+        above = jnp.where(upper, corner[8:16], other[40:48]) * keep_above
+        below = jnp.where(upper, other[32:40], corner[8:16]) * keep_below
+        second.append(jnp.concatenate([above, own[32:48], below], axis=0))
+    for r in range(rows + 4):
+        ext_ref[r, 128:WIDE] = tiles[r].astype(jnp.bfloat16)
+    from_right, from_left = second
     cross = cross_ref[256:304].astype(jnp.float32)
     pair = pair_ref[256:304].astype(jnp.float32)
-    got = cross[40:48]
-    summed = sums_ref[0:1] + got[0:1] + got[1:2] + got[2:3]
-    counted = sums_ref[1:2] + got[3:4] + got[4:5] + got[5:6]
-    lane = lax.broadcasted_iota(jnp.int32, (1, 128), 1)
-    total = jnp.where(lane < 64, summed, counted)
-    total_ref[...] = jnp.broadcast_to(total[None], total_ref.shape)
     above = jnp.where(upper, cross, pair) * keep_above
     below = jnp.where(upper, pair, cross) * keep_below
-    fields = []
+    lane = lax.broadcasted_iota(jnp.int32, (2 * PACK, 128), 1)
+    planes = []
     for k in range(PLANES):
+        beyond = from_right if k == 0 else pltpu.roll(from_right, 128 - 8 * k, 1)
+        before = pltpu.roll(from_left, 120 - 8 * k, 1)
+        near = lane[:PACK]
         at = k * 8
-        fields.append(
-            jnp.concatenate([above[at : at + 8], planes_ref[k], below[at : at + 8]], axis=0)
-        )
-    fields_ref[0] = fields[0] + fields[1] + fields[2]
-    fields_ref[1] = fields[3] + fields[4]
-    place = lax.broadcasted_iota(jnp.int32, (8, 128), 0)
-    columns = [[jnp.zeros((8, 128), jnp.float32) for _ in range(4)] for _ in range(4)]
-    for r in range(rows + 4):
-        if r < 2:
-            source = ends_ref.at[r]
-        elif r < rows + 2:
-            source = hidden_ref.at[r - 2]
-        else:
-            source = ends_ref.at[r - rows]
-        head = source[0:16].astype(jnp.float32)
-        tail = source[112:128].astype(jnp.float32)
-        for k, row in enumerate((head[0:1], head[1:2], tail[14:15], tail[15:16])):
-            columns[k][r // 8] = jnp.where(place == r % 8, row, columns[k][r // 8])
-    columns = [jnp.concatenate(tiles, axis=0) for tiles in columns]
-    fields = [f.astype(jnp.bfloat16) for f in fields]
-    for peer in range(sent_ref.shape[0]):
-        to_right = at_ref[4] == peer
-        for k in range(2):
-            chosen = jnp.where(to_right, columns[2 + k], columns[k])
-            sent_ref[peer, k * 32 : k * 32 + 32] = chosen.astype(jnp.bfloat16)
-        for k in range(PLANES):
-            sent_ref[peer, 64 + k * PACK : 64 + k * PACK + PACK] = fields[k]
-
-
-def forward_kernel(
-    at_ref, hidden_ref, ends_ref, fields_ref, got_ref, weight_ref, bias_ref, alpha_ref, beta_ref,
-    ext_ref, preact_ref, force_ref, rhs_ref,
-):
-    rows = hidden_ref.shape[0]
-    left, right = at_ref[3], at_ref[4]
-    ext_ref[0:2, 0:128] = ends_ref[0:2]
-    ext_ref[2 : rows + 2, 0:128] = hidden_ref[...]
-    ext_ref[rows + 2 : rows + 4, 0:128] = ends_ref[2:4]
-    columns = got_ref[right, 0:64].astype(jnp.float32), got_ref[left, 0:64].astype(jnp.float32)
-    place = lax.broadcasted_iota(jnp.int32, (WIDE - 128, 128), 0)
-    for r in range(rows + 4):
-        tile = jnp.zeros((WIDE - 128, 128), jnp.float32)
-        for side, base in enumerate((0, WIDE - 130)):
-            for k in range(2):
-                row = columns[side][k * 32 + r : k * 32 + r + 1]
-                tile = jnp.where(place == base + k, row, tile)
-        ext_ref[r, 128:WIDE] = tile.astype(jnp.bfloat16)
+        planes.append(
+            jnp.concatenate(
+                [
+                    above[at : at + 8],
+                    planes_ref[k],
+                    below[at : at + 8],
+                    jnp.where(near < 8, beyond, jnp.where(near >= 120, before, 0.0)),
+                ],
+                axis=0,
+            )
+        )
+    start = planes[0] + planes[1] + planes[2]
+    wet_depth = planes[3] + planes[4]
     for a in range(3):
         for c in range(3):
             rhs_ref[a * 128 : a * 128 + 128, c * 128 : c * 128 + 128] = weight_ref[a, c]
 
-    lane = lax.broadcasted_iota(jnp.int32, (2 * PACK, 128), 1)
-    second = jnp.where(
-        jnp.concatenate([lane] * 3, axis=0)[: PLANES * PACK] < 64,
-        got_ref[right, 64:SENT].astype(jnp.float32),
-        got_ref[left, 64:SENT].astype(jnp.float32),
-    )
-    second = [second[k * PACK : k * PACK + PACK] for k in range(PLANES)]
-    start = jnp.concatenate([fields_ref[0], second[0] + second[1] + second[2]], axis=0)
-    wet_depth = jnp.concatenate([fields_ref[1], second[3] + second[4]], axis=0)
     mask = jnp.where(wet_depth > 0.0, 1.0, 0.0)
 
     def other_half(field):
@@ -210,7 +243,8 @@
 
 def backward_kernel(
     total_ref, preact_ref, force_ref, ext_ref, proj_ref,
-    grad_ref, sent_ref, moved_ref, weight_ref,
+    grad_hbm, sent_ref,
+    grad_ref, moved_ref, weight_ref, sem,
 ):
     rows = grad_ref.shape[0] - 2
     total = jnp.sum(total_ref[...], axis=0)
@@ -246,6 +280,8 @@
             moved_ref[g - 1, :, 0:128] = pltpu.roll(own, WIDE - 1, 0).astype(jnp.bfloat16)
             moved_ref[g - 1, :, 128:256] = own.astype(jnp.bfloat16)
             moved_ref[g - 1, :, 256:384] = pltpu.roll(own, 1, 0).astype(jnp.bfloat16)
+    copy = pltpu.make_async_copy(grad_ref, grad_hbm, sem)
+    copy.start()
     moved = moved_ref[...].reshape(rows * WIDE, 384)
     for a in range(3):
         cells = ext_ref[a + 1 : a + 1 + rows].reshape(rows * WIDE, 128)
@@ -282,6 +318,7 @@
         return carry
 
     lax.fori_loop(0, 8, one_pair, 0)
+    copy.wait()
 
 
 def middle_kernel(got_ref, sent_ref):
@@ -299,8 +336,7 @@
 def last_kernel(scale, got_ref, weight_ref, bias_ref, proj_ref):
     total = jnp.sum(got_ref[...].astype(jnp.float32), axis=0) * scale
     for k in range(9):
-        for e in range(2):
-            weight_ref[e, k // 3, k % 3 : k % 3 + 1] = total[k * 2 + e : k * 2 + e + 1]
+        weight_ref[k // 3, k % 3] = total[k * 2 : k * 2 + 2]
     bias_ref[...] = total[18:19] + total[20:21]
     proj_ref[...] = total[19:20] + total[21:22]
 
@@ -332,15 +368,14 @@
             out_ref[y + j] = total[0:128].astype(jnp.bfloat16)
 
 
-def call(kernel, shapes, scratch, in_specs, args, name):
+def call(kernel, shapes, scratch, in_specs, args, out_specs=None):
     return pl.pallas_call(
         kernel,
         out_shape=shapes,
         in_specs=in_specs,
-        out_specs=jax.tree.map(lambda _: VMEM, shapes),
+        out_specs=jax.tree.map(lambda _: VMEM, shapes) if out_specs is None else out_specs,
         scratch_shapes=scratch,
         compiler_params=pltpu.CompilerParams(vmem_limit_bytes=40 * 1024 * 1024),
-        name=name,
     )(*args)
 
 
@@ -359,40 +394,37 @@
     n_lat = lax.axis_size(LAT)
     n_all = lax.axis_size(("lat_0", "lat_2", "lon"))
     n_z = lax.axis_size(("lat_1", "dp"))
-    lat, x = lax.axis_index(LAT), lax.axis_index("lon")
+    lat, me = lax.axis_index(LAT), lax.axis_index("lon")
     at = jnp.stack(
-        [lat % 2, lat, n_lat - 1 - lat, (x + n_x - 1) % n_x, (x + 1) % n_x]
+        [lat % 2, lat, n_lat - 1 - lat, (me + n_x - 1) % n_x, (me + 1) % n_x]
     ).astype(jnp.int32)
-    cross, pair, planes, sums = call(
+    cross, pair, head, tail, near, planes, sums = call(
         first_kernel,
         (
             shape((304, 128), narrow),
             shape((304, 128), narrow),
+            shape((16, 128), narrow),
+            shape((16, 128), narrow),
+            shape((2 * n_x, NEAR, 128), narrow),
             shape((PLANES, rows, 128), wide),
             shape((2, 128), wide),
         ),
         [],
         [SMEM] + [VMEM] * 4,
         (at, hidden, surface_cotangent, sea_mask, ocean_depth),
-        "first",
     )
     odd = [(i, (i + 1) % n_lat) for i in range(1, n_lat, 2)]
-    cross = lax.ppermute(cross, LAT, odd + [(j, i) for i, j in odd])
+    odd = odd + [(j, i) for i, j in odd]
+
+    def corner(step):
+        return [(i * n_x + x, j * n_x + (x + step) % n_x) for i, j in odd for x in range(n_x)]
+
+    cross = lax.ppermute(cross, LAT, odd)
+    head = lax.ppermute(head, LAT_LON, corner(n_x - 1))
+    tail = lax.ppermute(tail, LAT_LON, corner(1))
     pair = lax.ppermute(pair, "lat_2", [(0, 1), (1, 0)])
-    ends, fields, sent, total = call(
-        second_kernel,
-        (
-            shape((4, 128, 128), narrow),
-            shape((2, PACK, 128), wide),
-            shape((n_x, SENT, 128), narrow),
-            shape((n_all, 1, 128), wide),
-        ),
-        [],
-        [SMEM] + [VMEM] * 5,
-        (at, hidden, planes, sums, cross, pair),
-        "second",
-    )
-    got = lax.all_to_all(sent, "lon", 0, 0, tiled=True)
+    near = lax.all_to_all(near, ("lat_2", "lon"), 0, 0, tiled=True)
+    total = call(sums_kernel, shape((n_all, 1, 128), wide), [], [VMEM] * 2, (sums, cross))
     total = lax.all_to_all(total, ("lat_0", "lat_2", "lon"), 0, 0, tiled=True)
     ext, preact, force = call(
         forward_kernel,
@@ -402,20 +434,27 @@
             shape((128, 128), wide),
         ),
         [pltpu.VMEM((384, 384), narrow)],
-        [SMEM] + [VMEM] * 6 + [SMEM] * 2,
-        (at, hidden, ends, fields, got, conv_weight, conv_bias[None], step_alpha, step_beta),
-        "forward",
+        [SMEM] + [VMEM] * 9 + [SMEM] * 2,
+        (
+            at, hidden, planes, cross, pair, head, tail, near, conv_weight,
+            conv_bias[None], step_alpha, step_beta,
+        ),
     )
     grad, sent = call(
         backward_kernel,
         (shape((rows + 2, WIDE, 128), narrow), shape((n_all, 40, 128), narrow)),
-        [pltpu.VMEM((rows, WIDE, 384), narrow), pltpu.VMEM((9, 128, 128), wide)],
+        [
+            pltpu.VMEM((rows + 2, WIDE, 128), narrow),
+            pltpu.VMEM((rows, WIDE, 384), narrow),
+            pltpu.VMEM((9, 128, 128), wide),
+            pltpu.SemaphoreType.DMA,
+        ],
         [VMEM] * 5,
         (total, preact, force, ext, proj_weight[None]),
-        "backward",
+        (HBM, VMEM),
     )
     got = lax.all_to_all(sent, ("lat_0", "lat_2", "lon"), 0, 0, tiled=True)
-    sent = call(middle_kernel, shape((n_z, 24, 128), narrow), [], [VMEM], (got,), "middle")
+    sent = call(middle_kernel, shape((n_z, 24, 128), narrow), [], [VMEM], (got,))
     got = lax.all_to_all(sent, ("lat_1", "dp"), 0, 0, tiled=True)
     grad_hidden = call(
         input_kernel,
@@ -423,18 +462,16 @@
         [pltpu.VMEM((384, 384), narrow)],
         [VMEM] * 2,
         (grad, conv_weight),
-        "input_grad",
     )
     cells = rows * 128 * lax.axis_size("dp") * n_lat * n_x
     own_weight, total_bias, total_proj = call(
         functools.partial(last_kernel, 1.0 / math.sqrt(cells)),
-        (shape((2, 3, 3, 128), wide), shape((1, 128), wide), shape((1, 128), wide)),
+        (shape((3, 3, 2, 128), wide), shape((1, 128), wide), shape((1, 128), wide)),
         [],
         [VMEM],
         (got,),
-        "last",
-    )
-    return grad_hidden[None], own_weight, total_bias[0], total_proj[0]
+    )
+    return grad_hidden[None], own_weight.transpose(2, 0, 1, 3), total_bias[0], total_proj[0]
 
 
 def solution(mesh):

time: 96.7 us -> 117 us (1.21)
  starting transfers between devices: 36.9 us -> 54.8 us
  blocking collectives: 23.7 us -> 12.6 us
  waiting for transfers between devices: 20.5 us -> 31.2 us
  local copies, waits for them, and re-layouts: 4.71 us -> 7.19 us
    ppermute x1 -> x3, starting transfers between devices: 16.7 us -> 36.9 us  [the longest x1 17.6 us: shards(): head = lax.ppermute(head, LAT_LON, corner(n_x - 1))]
    ppermute x1 -> x3, waiting for transfers between devices: 4.11 us -> 20 us  [the longest x1 15.9 us: shards(): tail = lax.ppermute(tail, LAT_LON, corner(1))]
    all_to_all x1 -> x0, blocking collectives: 10.6 us -> none  [shards(): got = lax.all_to_all(sent, 'lon', 0, 0, tiled=True)]
    all_to_all x1, starting transfers between devices: 13.5 us -> 5.22 us  [shards(): got = lax.all_to_all(sent, ('lat_1', 'dp'), 0, 0, tiled=True)]
    all_to_all x1, waiting for transfers between devices: 5.09 us -> 0.01 us  [shards(): total = lax.all_to_all(total, ('lat_0', 'lat_2', 'lon'), 0, 0, tiled=True)]
    all_to_all x0 -> x1, starting transfers between devices: none -> 4.3 us  [shards(): near = lax.all_to_all(near, ('lat_2', 'lon'), 0, 0, tiled=True)]
    unnamed x25 -> x22, local copies, waits for them, and re-layouts: 4.63 us -> 7.11 us
    all_to_all x1, starting transfers between devices: 4.73 us -> 6.48 us  [shards(): total = lax.all_to_all(total, ('lat_0', 'lat_2', 'lon'), 0, 0, tiled=True)]
  transfers between devices with their start and end apart: 4 -> 7, of which waited for: 3 -> 3; matrix products, arithmetic and copies ran while one was open for 0% -> 0% of each run, Pallas kernels for 4% -> 4%
where the time goes in v5:
time: 117 us
  starting transfers between devices  54.8 us (47%)
  waiting for transfers between devices  31.2 us (27%)
  blocking collectives  12.6 us (11%)
  Pallas kernels  10 us (9%)
  local copies, waits for them, and re-layouts  7.19 us (6%)
    ppermute x1, starting transfers between devices, shards(): head = lax.ppermute(head, LAT_LON, corner(n_x - 1))  17.6 us
    ppermute x1, starting transfers between devices, shards(): cross = lax.ppermute(cross, LAT, odd)  17.4 us
    ppermute x1, waiting for transfers between devices, shards(): tail = lax.ppermute(tail, LAT_LON, corner(1))  15.9 us
    all_to_all x1, blocking collectives, shards(): got = lax.all_to_all(sent, ('lat_0', 'lat_2', 'lon'), 0, 0, tiled=True)  12.6 us
    all_to_all x1, waiting for transfers between devices, shards(): got = lax.all_to_all(sent, ('lat_1', 'dp'), 0, 0, tiled=True)  11.2 us
    pallas_call x7, Pallas kernels, call(): pl.pallas_call(kernel, out_shape=shapes, in_specs=in_specs, out_specs=jax...  10 us
    unnamed x22, local copies, waits for them, and re-layouts  7.11 us
    all_to_all x1, starting transfers between devices, shards(): total = lax.all_to_all(total, ('lat_0', 'lat_2', 'lon'), 0, 0, tiled=True)  6.48 us
  transfers between devices with their start and end apart: 7, of which 3 were waited for; matrix products, arithmetic and copies ran while one was open for 0% of the time, Pallas kernels for 4%

profile of v5, /device:TPU:32, one launch (start us, length us, event | category | flops | bytes accessed | tf_op | source)
XLA Modules:
  0.0 116.6 jit_solution(8183191531461201377)
XLA Ops:
  0.8 1.0 copy-done
  1.8 0.7 copy-done.4
  2.5 0.7 copy-done.5
  3.2 0.7 copy-done.6
  3.9 1.3 %shard_map.120 = (bf16[304,128]{1,0:T(8,128)(2,1)S(1)}, bf16[304,128]{1,0:T(8,128)(2,1)S(1)}, bf16[16,128]{1,0:T(8,128)(2,1)S(1)}, bf16[16,128]{1,0:T(8,128)(2,1...) custom-call(s32[5]{0:T(128)S(1)} %stack.23.at_ref, ...), custom_call_target="tpu_custom_call" | custom-call | tf_op jit(solution)/shard_map/pallas_call | solution.py:372
  5.2 4.3 %all-to-all-start.1 = ((bf16[8,48,128]{2,1,0:T(8,128)(2,1)}), bf16[8,48,128]{2,1,0:T(8,128)(2,1)S(1)}, u32[]{:S(2)}, u32[]{:S(2)}) async-start(bf16[8,48,128]{2,1,0:T(8,128)(2,1)} %get-tuple-element.25), calls=%async_computation.1 | async-start | bytes 196608 | tf_op jit(solution)/shard_map/all_to_all | solution.py:426
  9.5 17.4 %collective-permute-start = (bf16[304,128]{1,0:T(8,128)(2,1)S(1)}, bf16[304,128]{1,0:T(8,128)(2,1)S(1)}, u32[]{:S(2)}, u32[]{:S(2)}) collective-permute-start(bf16[304,128]{1,0:T(8,128)(2,1)S(1)} %get-tuple-element.20), channel_id=1, source_target_pairs={{4,8},{12,16},{20,24},{28,32},{36,40},{44,48},{52,56},{60,0},{8,4}... | collective-permute-start | bytes 233480 | tf_op jit(solution)/shard_map/ppermute | solution.py:422
  26.9 1.9 %collective-permute-start.1 = (bf16[304,128]{1,0:T(8,128)(2,1)S(1)}, bf16[304,128]{1,0:T(8,128)(2,1)S(1)}, u32[]{:S(2)}, u32[]{:S(2)}) collective-permute-start(bf16[304,128]{1,0:T(8,128)(2,1)S(1)} %get-tuple-element.22), channel_id=1, source_target_pairs={{0,4},{4,0},{1,5},{5,1},{2,6},{6,2},{3,7},{7,3},{8,12},{12,8},{9,1... | collective-permute-start | bytes 233480 | tf_op jit(solution)/shard_map/ppermute | solution.py:425
  28.8 4.0 %collective-permute-done.cross_ref = bf16[304,128]{1,0:T(8,128)(2,1)S(1)} collective-permute-done((bf16[304,128]{1,0:T(8,128)(2,1)S(1)}, bf16[304,128]{1,0:T(8,128)(2,1)S(1)}, u32[]{:S(2)}, u32[]{:S(2)}) %collective-permute-start) | collective-permute-done | bytes 77856 | tf_op jit(solution)/shard_map/ppermute | solution.py:422
  33.4 6.5 %all-to-all-start = ((f32[32,1,128]{2,1,0:T(1,128)}), f32[32,1,128]{2,1,0:T(1,128)S(1)}, u32[]{:S(2)}, u32[]{:S(2)}) async-start(f32[32,1,128]{2,1,0:T(1,128)} %shard_map.121), calls=%async_computation | async-start | bytes 32768 | tf_op jit(solution)/shard_map/all_to_all | solution.py:428
  39.9 17.6 %collective-permute-start.2 = (bf16[16,128]{1,0:T(8,128)(2,1)S(1)}, bf16[16,128]{1,0:T(8,128)(2,1)S(1)}, u32[]{:S(2)}, u32[]{:S(2)}) collective-permute-start(bf16[16,128]{1,0:T(8,128)(2,1)S(1)} %get-tuple-element.23), channel_id=1, source_target_pairs={{4,11},{5,8},{6,9},{7,10},{12,19},{13,16},{14,17},{15,18},{20,27},... | collective-permute-start | bytes 12296 | tf_op jit(solution)/shard_map/ppermute | solution.py:423
  57.5 1.9 %collective-permute-start.3 = (bf16[16,128]{1,0:T(8,128)(2,1)S(1)}, bf16[16,128]{1,0:T(8,128)(2,1)S(1)}, u32[]{:S(2)}, u32[]{:S(2)}) collective-permute-start(bf16[16,128]{1,0:T(8,128)(2,1)S(1)} %get-tuple-element.24), channel_id=1, source_target_pairs={{4,9},{5,10},{6,11},{7,8},{12,17},{13,18},{14,19},{15,16},{20,25},... | collective-permute-start | bytes 12296 | tf_op jit(solution)/shard_map/ppermute | solution.py:424
  59.4 15.9 %collective-permute-done.3.tail_ref = bf16[16,128]{1,0:T(8,128)(2,1)S(1)} collective-permute-done((bf16[16,128]{1,0:T(8,128)(2,1)S(1)}, bf16[16,128]{1,0:T(8,128)(2,1)S(1)}, u32[]{:S(2)}, u32[]{:S(2)}) %collective-permute-start.3) | collective-permute-done | bytes 4128 | tf_op jit(solution)/shard_map/ppermute | solution.py:424
  75.4 1.0 copy-done.1
  76.4 1.0 copy-done.2
  77.4 0.7 copy-done.7
  78.7 0.7 copy-done.9
  79.3 2.1 %shard_map.122 = (bf16[20,144,128]{2,1,0:T(8,128)(2,1)S(1)}, f32[18,144,128]{2,1,0:T(8,128)S(1)}, f32[128,128]{1,0:T(8,128)S(1)}) custom-call(s32[5]{0:T(128)S(1)} %stack.23.at_ref, bf16[16,128,128]{2,1,0:T(8,128)(2,1)S(1)} %bitcast.13, f32[5,16,128]{2,1,0:T(8,128)S(1)} %get-tuple-element.21.planes_ref, bf16[304,128]{1,0:T(8,128)(2,1)S(1)} %collective-permute-done.cross_ref, ...), custom_call_target="tpu_custom_call" | custom-call | tf_op jit(solution)/shard_map/pallas_call | solution.py:372
  81.5 2.6 %shard_map.123 = (bf16[18,144,128]{2,1,0:T(8,128)(2,1)S(1)}, bf16[32,40,128]{2,1,0:T(8,128)(2,1)S(1)}) custom-call(f32[32,1,128]{2,1,0:T(1,128)S(1)} %all-to-all-done.total_ref, f32[18,144,128]{2,1,0:T(8,128)S(1)} %get-tuple-element.26.preact_ref, f32[128,128]{1,0:T(8,128)S(1)} %get-tuple-element.27.force_ref, ...), custom_call_target="tpu_custom_call" | custom-call | tf_op jit(solution)/shard_map/pallas_call | solution.py:372
  84.1 12.6 %all_to_all.20.got_ref = bf16[32,40,128]{2,1,0:T(8,128)(2,1)S(1)} all-to-all(bf16[32,40,128]{2,1,0:T(8,128)(2,1)S(1)} %get-tuple-element.30), channel_id=1, replica_groups=mesh['dp'=8,'lat_0'=4,'lat_1'=2,'lat_2'=2,'lon'=4] {'lat_0','lat_2','lon'}, dimensions={0} | all-to-all | bytes 655360 | tf_op jit(solution)/shard_map/all_to_all | solution.py:456
  96.7 0.7 shard_map.125
  97.4 5.2 %all-to-all-start.3 = ((bf16[16,24,128]{2,1,0:T(8,128)(2,1)}), bf16[16,24,128]{2,1,0:T(8,128)(2,1)S(1)}, u32[]{:S(2)}, u32[]{:S(2)}) async-start(bf16[16,24,128]{2,1,0:T(8,128)(2,1)} %shard_map.125), calls=%async_computation.3 | async-start | bytes 196608 | tf_op jit(solution)/shard_map/all_to_all | solution.py:458
  102.6 2.1 %shard_map.124 = bf16[16,128,128]{2,1,0:T(8,128)(2,1)} custom-call(bf16[18,144,128]{2,1,0:T(8,128)(2,1)S(1)} %get-tuple-element.29.grad_ref, bf16[3,3,128,128]{3,2,1,0:T(8,128)(2,1)S(1)} %copy-done.3), custom_call_target="tpu_custom_call" | custom-call | tf_op jit(solution)/shard_map/pallas_call | solution.py:372
  104.7 11.2 %all-to-all-done.3.got_ref = bf16[16,24,128]{2,1,0:T(8,128)(2,1)S(1)} async-done(((bf16[16,24,128]{2,1,0:T(8,128)(2,1)}), bf16[16,24,128]{2,1,0:T(8,128)(2,1)S(1)}, u32[]{:S(2)}, u32[]{:S(2)}) %all-to-all-start.3) | async-done | bytes 98336 | tf_op jit(solution)/shard_map/all_to_all | solution.py:458
  (21 shorter events, 2.0 us)
Async XLA Ops:
  0.6 80.9 %copy-start.10 = (f32[128]{0:T(128)S(1)}, f32[128]{0:T(128)}, u32[]{:S(2)}) copy-start(f32[128]{0:T(128)} %param.12) | copy-start | bytes 1540
  0.8 1.0 copy-start
  1.8 0.7 copy-start.4
  2.5 0.7 copy-start.5
  3.2 0.7 copy-start.6
  5.2 28.3 %all-to-all-start.1 = ((bf16[8,48,128]{2,1,0:T(8,128)(2,1)}), bf16[8,48,128]{2,1,0:T(8,128)(2,1)S(1)}, u32[]{:S(2)}, u32[]{:S(2)}) async-start(bf16[8,48,128]{2,1,0:T(8,128)(2,1)} %get-tuple-element.25), calls=%async_computation.1 | async-start | bytes 196608 | tf_op jit(solution)/shard_map/all_to_all | solution.py:426
  9.5 23.4 %collective-permute-start = (bf16[304,128]{1,0:T(8,128)(2,1)S(1)}, bf16[304,128]{1,0:T(8,128)(2,1)S(1)}, u32[]{:S(2)}, u32[]{:S(2)}) collective-permute-start(bf16[304,128]{1,0:T(8,128)(2,1)S(1)} %get-tuple-element.20), channel_id=1, source_target_pairs={{4,8},{12,16},{20,24},{28,32},{36,40},{44,48},{52,56},{60,0},{8,4}... | collective-permute-start | bytes 233480 | tf_op jit(solution)/shard_map/ppermute | solution.py:422
  26.9 48.5 %collective-permute-start.1 = (bf16[304,128]{1,0:T(8,128)(2,1)S(1)}, bf16[304,128]{1,0:T(8,128)(2,1)S(1)}, u32[]{:S(2)}, u32[]{:S(2)}) collective-permute-start(bf16[304,128]{1,0:T(8,128)(2,1)S(1)} %get-tuple-element.22), channel_id=1, source_target_pairs={{0,4},{4,0},{1,5},{5,1},{2,6},{6,2},{3,7},{7,3},{8,12},{12,8},{9,1... | collective-permute-start | bytes 233480 | tf_op jit(solution)/shard_map/ppermute | solution.py:425
  33.4 48.1 %all-to-all-start = ((f32[32,1,128]{2,1,0:T(1,128)}), f32[32,1,128]{2,1,0:T(1,128)S(1)}, u32[]{:S(2)}, u32[]{:S(2)}) async-start(f32[32,1,128]{2,1,0:T(1,128)} %shard_map.121), calls=%async_computation | async-start | bytes 32768 | tf_op jit(solution)/shard_map/all_to_all | solution.py:428
  39.9 19.5 %collective-permute-start.2 = (bf16[16,128]{1,0:T(8,128)(2,1)S(1)}, bf16[16,128]{1,0:T(8,128)(2,1)S(1)}, u32[]{:S(2)}, u32[]{:S(2)}) collective-permute-start(bf16[16,128]{1,0:T(8,128)(2,1)S(1)} %get-tuple-element.23), channel_id=1, source_target_pairs={{4,11},{5,8},{6,9},{7,10},{12,19},{13,16},{14,17},{15,18},{20,27},... | collective-permute-start | bytes 12296 | tf_op jit(solution)/shard_map/ppermute | solution.py:423
  57.5 17.9 %collective-permute-start.3 = (bf16[16,128]{1,0:T(8,128)(2,1)S(1)}, bf16[16,128]{1,0:T(8,128)(2,1)S(1)}, u32[]{:S(2)}, u32[]{:S(2)}) collective-permute-start(bf16[16,128]{1,0:T(8,128)(2,1)S(1)} %get-tuple-element.24), channel_id=1, source_target_pairs={{4,9},{5,10},{6,11},{7,8},{12,17},{13,18},{14,19},{15,16},{20,25},... | collective-permute-start | bytes 12296 | tf_op jit(solution)/shard_map/ppermute | solution.py:424
  75.4 1.0 copy-start.1
  76.4 1.0 copy-start.2
  77.4 0.7 copy-start.7
  78.0 0.7 copy-start.8
  78.7 0.7 copy-start.9
  81.5 21.1 %copy-start.3 = (bf16[3,3,128,128]{3,2,1,0:T(8,128)(2,1)S(1)}, bf16[3,3,128,128]{3,2,1,0:T(8,128)(2,1)}, u32[]{:S(2)}) copy-start(bf16[3,3,128,128]{3,2,1,0:T(8,128)(2,1)} %weight_ref.3) | copy-start | bytes 884740
  97.4 18.6 %all-to-all-start.3 = ((bf16[16,24,128]{2,1,0:T(8,128)(2,1)}), bf16[16,24,128]{2,1,0:T(8,128)(2,1)S(1)}, u32[]{:S(2)}, u32[]{:S(2)}) async-start(bf16[16,24,128]{2,1,0:T(8,128)(2,1)} %shard_map.125), calls=%async_computation.3 | async-start | bytes 196608 | tf_op jit(solution)/shard_map/all_to_all | solution.py:458

commit v6 on v5

--- a/solution.py
+++ b/solution.py
@@ -50,16 +50,26 @@
     return out
 
 
+def edge_columns(load, rows):
+    place = lax.broadcasted_iota(jnp.int32, (8, 128), 0)
+    columns = [[jnp.zeros((8, 128), jnp.float32) for _ in range(rows // 8)] for _ in range(4)]
+    for r in range(rows):
+        head = load(r, 0).astype(jnp.float32)
+        tail = load(r, 112).astype(jnp.float32)
+        for k, row in enumerate((head[0:1], head[1:2], tail[14:15], tail[15:16])):
+            columns[k][r // 8] = jnp.where(place == r % 8, row, columns[k][r // 8])
+    return columns
+
+
 def first_kernel(
-    at_ref, hidden_ref, cot_ref, mask_ref, depth_ref,
-    cross_ref, pair_ref, head_ref, tail_ref, near_ref, planes_ref, sums_ref,
+    at_ref, hidden_ref, fields_ref, cross_ref, pair_ref, near_ref, planes_ref, sums_ref
 ):
     rows = hidden_ref.shape[0]
     upper = at_ref[0] == 0
-    mask = mask_ref[...].astype(jnp.float32)
-    wet = mask * cot_ref[0]
-    planes = pieces_of(wet, 3) + pieces_of(mask * depth_ref[...], 2)
-    summed, counted = full(jnp.sum(wet)), full(jnp.sum(mask))
+    wet, wet_depth = fields_ref[0], fields_ref[1]
+    planes = pieces_of(wet, 3) + pieces_of(wet_depth, 2)
+    summed = full(jnp.sum(wet))
+    counted = full(jnp.sum(jnp.where(wet_depth > 0.0, 1.0, 0.0)))
     sums_ref[0:1] = summed
     sums_ref[1:2] = counted
     sums = pieces_of(summed, 3) + pieces_of(counted, 3)
@@ -73,53 +83,83 @@
         for k in range(0, 6, 2):
             tile = jnp.concatenate(near[k : k + 2], axis=0)
             ref[256 + k * 8 : 272 + k * 8] = tile.astype(jnp.bfloat16)
+    columns = edge_columns(lambda r, at: hidden_ref[r, at : at + 16], rows)
+    head = jnp.concatenate(columns[0] + columns[1] + [packed(planes, 0)], axis=0)
+    tail = jnp.concatenate(columns[2] + columns[3] + [packed(planes, 8)], axis=0)
+    n_x = near_ref.shape[0] // 2
+    for peer in range(n_x):
+        chosen = jnp.where(at_ref[4] == peer, tail, head).astype(jnp.bfloat16)
+        near_ref[peer] = chosen
+        near_ref[n_x + peer] = chosen
+
+
+def second_kernel(at_ref, sums_ref, cross_ref, sent_ref):
+    tiles = [cross_ref[256 + k * 16 : 272 + k * 16].astype(jnp.float32) for k in range(3)]
+    planes = [tiles[k // 2][k % 2 * 8 : k % 2 * 8 + 8] for k in range(PLANES)]
+    got = tiles[2][8:16]
+    summed = sums_ref[0:1] + got[0:1] + got[1:2] + got[2:3]
+    counted = sums_ref[1:2] + got[3:4] + got[4:5] + got[5:6]
+    sums = pieces_of(summed, 3) + pieces_of(counted, 3)
+    sums = jnp.concatenate(sums + [jnp.zeros((2, 128), jnp.float32)], axis=0)
     place = lax.broadcasted_iota(jnp.int32, (8, 128), 0)
-    columns = [[jnp.zeros((8, 128), jnp.float32) for _ in range(2)] for _ in range(4)]
-    for r in range(rows):
-        head = hidden_ref[r, 0:16].astype(jnp.float32)
-        tail = hidden_ref[r, 112:128].astype(jnp.float32)
-        for k, row in enumerate((head[0:1], head[1:2], tail[14:15], tail[15:16])):
-            columns[k][r // 8] = jnp.where(place == r % 8, row, columns[k][r // 8])
-    ends = []
-    for side, ref in ((0, head_ref), (1, tail_ref)):
-        fields = packed(planes, 0 if side == 0 else 8)
-        pair = columns[2 * side : 2 * side + 2]
-        whole = jnp.concatenate([pair[0][0], pair[0][1], pair[1][0], pair[1][1], fields], axis=0)
-        ends.append(whole)
+    blocks = []
+    for side in range(2):
         corner = jnp.zeros((8, 128), jnp.float32)
         for r in range(2):
+            start = r * 128 + 112 * side
+            tile = cross_ref[start : start + 16].astype(jnp.float32)
             for k in range(2):
-                row = jnp.where(upper, pair[k][0][r : r + 1], pair[k][1][6 + r : 7 + r])
-                corner = jnp.where(place == 2 * r + k, row, corner)
-        facing = jnp.where(upper, fields[0:8], fields[rows - 8 : rows])
-        ref[...] = jnp.concatenate([corner, facing], axis=0).astype(jnp.bfloat16)
-    n_x = near_ref.shape[0] // 2
+                at = 14 * side + k
+                corner = jnp.where(place == 2 * r + k, tile[at : at + 1], corner)
+        block = jnp.concatenate([corner, packed(planes, 8 * side), sums], axis=0)
+        blocks.append(block)
+    n_x = 4
     for peer in range(n_x):
-        chosen = jnp.where(at_ref[4] == peer, ends[1], ends[0]).astype(jnp.bfloat16)
-        near_ref[peer] = chosen
-        near_ref[n_x + peer] = chosen
-
-
-def sums_kernel(sums_ref, cross_ref, total_ref):
-    got = cross_ref[288:304].astype(jnp.float32)[8:16]
-    summed = sums_ref[0:1] + got[0:1] + got[1:2] + got[2:3]
-    counted = sums_ref[1:2] + got[3:4] + got[4:5] + got[5:6]
-    lane = lax.broadcasted_iota(jnp.int32, (1, 128), 1)
-    total = jnp.where(lane < 64, summed, counted)
-    total_ref[...] = jnp.broadcast_to(total[None], total_ref.shape)
+        chosen = jnp.where(at_ref[4] == peer, blocks[1], blocks[0]).astype(jnp.bfloat16)
+        for group in range(sent_ref.shape[0] // n_x):
+            sent_ref[group * n_x + peer] = chosen
+
+
+def sides_of(at_ref):
+    return (
+        at_ref[0] == 0,
+        jnp.where(at_ref[1] == 0, 0.0, 1.0),
+        jnp.where(at_ref[2] == 0, 0.0, 1.0),
+    )
+
+
+def fill(rhs_ref, weight_ref):
+    for a in range(3):
+        for c in range(3):
+            rhs_ref[a * 128 : a * 128 + 128, c * 128 : c * 128 + 128] = weight_ref[a, c]
+
+
+def convolved(ext_ref, rhs_ref, bias, start, group):
+    lhs = jnp.concatenate(
+        [ext_ref[pl.ds(start + a, group)].reshape(group * WIDE, 128) for a in range(3)], axis=1
+    )
+    out = jnp.dot(lhs, rhs_ref[...], preferred_element_type=jnp.float32)
+    rows = []
+    for j in range(group):
+        part = out[j * WIDE : (j + 1) * WIDE]
+        rows.append(
+            pltpu.roll(part[:, 0:128], 1, 0)
+            + part[:, 128:256]
+            + pltpu.roll(part[:, 256:384], WIDE - 1, 0)
+            + bias
+        )
+    return rows
 
 
 def forward_kernel(
-    at_ref, hidden_ref, planes_ref, cross_ref, pair_ref, head_ref, tail_ref, near_ref,
-    weight_ref, bias_ref, alpha_ref, beta_ref,
-    ext_ref, preact_ref, force_ref, rhs_ref,
+    at_ref, hidden_ref, cross_ref, pair_ref, near_ref, weight_ref, bias_ref, proj_ref,
+    alpha_ref, beta_ref,
+    ext_ref, preact_ref, params_ref, rhs_ref,
 ):
     rows = hidden_ref.shape[0]
     n_x = near_ref.shape[0] // 2
     core, left, right = at_ref[0], at_ref[3], at_ref[4]
-    upper = core == 0
-    keep_above = jnp.where(at_ref[1] == 0, 0.0, 1.0)
-    keep_below = jnp.where(at_ref[2] == 0, 0.0, 1.0)
+    upper, keep_above, keep_below = sides_of(at_ref)
     zero = jnp.zeros((), jnp.bfloat16)
     for k in range(2):
         cross = cross_ref[k * 128 : k * 128 + 128]
@@ -129,32 +169,72 @@
             keep_below > 0.0, jnp.where(upper, pair, cross), zero
         )
     ext_ref[2 : rows + 2, 0:128] = hidden_ref[...]
-
     place = lax.broadcasted_iota(jnp.int32, (WIDE - 128, 128), 0)
     tiles = [jnp.zeros((WIDE - 128, 128), jnp.float32) for _ in range(rows + 4)]
-    second = []
-    for side, base, corner_ref in ((right, 0, head_ref), (left, WIDE - 130, tail_ref)):
+    for side, base in ((right, 0), (left, WIDE - 130)):
         own = near_ref[core * n_x + side].astype(jnp.float32)
         other = near_ref[(1 - core) * n_x + side].astype(jnp.float32)
-        corner = corner_ref[...].astype(jnp.float32)
         for k in range(2):
             for r in range(rows + 4):
+                at = r - 2
+                source = own
                 if r < 2:
-                    mate = other[k * 16 + rows - 2 + r : k * 16 + rows - 1 + r]
-                    row = jnp.where(upper, corner[2 * r + k : 2 * r + k + 1], mate) * keep_above
-                elif r < rows + 2:
-                    row = own[k * 16 + r - 2 : k * 16 + r - 1]
-                else:
-                    j = r - rows - 2
-                    mate = other[k * 16 + j : k * 16 + j + 1]
-                    row = jnp.where(upper, mate, corner[2 * j + k : 2 * j + k + 1]) * keep_below
+                    source, at = other, rows - 2 + r
+                elif r >= rows + 2:
+                    source, at = other, r - rows - 2
+                row = source[k * 16 + at : k * 16 + at + 1]
                 tiles[r] = jnp.where(place == base + k, row, tiles[r])
-        above = jnp.where(upper, corner[8:16], other[40:48]) * keep_above
-        below = jnp.where(upper, other[32:40], corner[8:16]) * keep_below
-        second.append(jnp.concatenate([above, own[32:48], below], axis=0))
     for r in range(rows + 4):
         ext_ref[r, 128:WIDE] = tiles[r].astype(jnp.bfloat16)
+    fill(rhs_ref, weight_ref)
+    bias = bias_ref[...]
+    params_ref[0:1] = bias
+    params_ref[1:2] = proj_ref[...]
+    for k in range(ITERS):
+        params_ref[2 + k : 3 + k] = full(alpha_ref[k])
+        params_ref[8 + k : 9 + k] = full(beta_ref[k])
+    group = 6
+    for g in range(0, rows + 2, group):
+        for j, row in enumerate(convolved(ext_ref, rhs_ref, bias, g, group)):
+            preact_ref[g + j] = row
+
+
+def backward_kernel(
+    at_ref, planes_ref, cross_ref, pair_ref, near_ref, got_ref, kernel_ref, params_ref,
+    preact_ref, early_ref,
+    grad_hbm, sent_ref, ext_ref,
+    grad_ref, moved_ref, weight_ref, rhs_ref, sem,
+):
+    rows = grad_ref.shape[0] - 2
+    n_x = near_ref.shape[0] // 2
+    core, left, right = at_ref[0], at_ref[3], at_ref[4]
+    upper, keep_above, keep_below = sides_of(at_ref)
+    keep_cross = jnp.where(upper, keep_above, keep_below)
+    place = lax.broadcasted_iota(jnp.int32, (WIDE - 128, 128), 0)
+    tiles = [jnp.zeros((WIDE - 128, 128), jnp.float32) for _ in range(2)]
+    second = []
+    for side, base in ((right, 0), (left, WIDE - 130)):
+        own = near_ref[core * n_x + side, 32:48].astype(jnp.float32)
+        other = near_ref[(1 - core) * n_x + side, 32:48].astype(jnp.float32)
+        corner = got_ref[at_ref[5] * n_x + side].astype(jnp.float32)[0:16] * keep_cross
+        for r in range(2):
+            for k in range(2):
+                row = corner[2 * r + k : 2 * r + k + 1]
+                tiles[r] = jnp.where(place == base + k, row, tiles[r])
+        above = jnp.where(upper, corner[8:16], other[8:16] * keep_above)
+        below = jnp.where(upper, other[0:8] * keep_below, corner[8:16])
+        second.append(jnp.concatenate([above, own, below], axis=0))
     from_right, from_left = second
+    crossed = jnp.where(upper, 0, rows + 2)
+    paired = rows + 2 - crossed
+    for r in range(2):
+        ext_ref[crossed + r, 128:WIDE] = tiles[r].astype(jnp.bfloat16)
+        keep = jnp.where(upper, keep_below, keep_above) > 0.0
+        mate = ext_ref[paired + r, 128:WIDE]
+        ext_ref[paired + r, 128:WIDE] = jnp.where(keep, mate, jnp.zeros((), jnp.bfloat16))
+    fill(rhs_ref, kernel_ref)
+    again = jnp.where(upper, 0, rows)
+    fixed = convolved(ext_ref, rhs_ref, params_ref[0:1], again, 2)
     cross = cross_ref[256:304].astype(jnp.float32)
     pair = pair_ref[256:304].astype(jnp.float32)
     above = jnp.where(upper, cross, pair) * keep_above
@@ -179,10 +259,6 @@
         )
     start = planes[0] + planes[1] + planes[2]
     wet_depth = planes[3] + planes[4]
-    for a in range(3):
-        for c in range(3):
-            rhs_ref[a * 128 : a * 128 + 128, c * 128 : c * 128 + 128] = weight_ref[a, c]
-
     mask = jnp.where(wet_depth > 0.0, 1.0, 0.0)
 
     def other_half(field):
@@ -214,44 +290,19 @@
     direction = residual
     result = jnp.zeros_like(residual)
     for k in range(ITERS):
-        result = result + alpha_ref[k] * direction
+        result = result + params_ref[2 + k : 3 + k] * direction
         if k + 1 < ITERS:
             applied = diagonal * direction
             for w, near in zip(weights, beside(direction)):
                 applied = applied - w * near
-            residual = residual - alpha_ref[k] * applied
-            direction = residual + beta_ref[k] * direction
+            residual = residual - params_ref[2 + k : 3 + k] * applied
+            direction = residual + params_ref[8 + k : 9 + k] * direction
     result = result * jnp.concatenate([mask, mask], axis=0)
-    force_ref[...] = result.T
-
-    group = 6
-    bias = bias_ref[...]
-    for g in range(0, rows + 2, group):
-        lhs = jnp.concatenate(
-            [ext_ref[g + a : g + a + group].reshape(group * WIDE, 128) for a in range(3)], axis=1
-        )
-        out = jnp.dot(lhs, rhs_ref[...], preferred_element_type=jnp.float32)
-        for j in range(group):
-            part = out[j * WIDE : (j + 1) * WIDE]
-            preact_ref[g + j] = (
-                pltpu.roll(part[:, 0:128], 1, 0)
-                + part[:, 128:256]
-                + pltpu.roll(part[:, 256:384], WIDE - 1, 0)
-                + bias
-            )
-
-
-def backward_kernel(
-    total_ref, preact_ref, force_ref, ext_ref, proj_ref,
-    grad_hbm, sent_ref,
-    grad_ref, moved_ref, weight_ref, sem,
-):
-    rows = grad_ref.shape[0] - 2
-    total = jnp.sum(total_ref[...], axis=0)
-    mean = jnp.broadcast_to(total[:, 0:1], (1, 128)) / jnp.broadcast_to(total[:, 127:128], (1, 128))
-    force = force_ref[...]
+    sums = jnp.sum(got_ref[:, 16:24].astype(jnp.float32), axis=0)
+    mean = (sums[0:1] + sums[1:2] + sums[2:3]) / (sums[3:4] + sums[4:5] + sums[5:6])
+    force = result.T
     force = force - mean * pltpu.roll(force, 64, 1)
-    proj = proj_ref[...]
+    proj = params_ref[1:2]
     sum_bias = jnp.zeros((8, 128), jnp.float32)
     sum_proj = jnp.zeros((8, 128), jnp.float32)
     for g in range(rows + 2):
@@ -266,6 +317,10 @@
         )
         column = jnp.broadcast_to(column, (WIDE, 128))
         preact = preact_ref[g]
+        if g < 2:
+            preact = jnp.where(upper, fixed[g], preact)
+        elif g >= rows:
+            preact = jnp.where(upper, preact, fixed[g - rows])
         sigma = jax.nn.sigmoid(preact)
         active = preact * sigma
         slope_act = sigma * (1.0 + preact * (1.0 - sigma))
@@ -368,13 +423,14 @@
             out_ref[y + j] = total[0:128].astype(jnp.bfloat16)
 
 
-def call(kernel, shapes, scratch, in_specs, args, out_specs=None):
+def call(kernel, shapes, scratch, in_specs, args, out_specs=None, aliases={}):
     return pl.pallas_call(
         kernel,
         out_shape=shapes,
         in_specs=in_specs,
         out_specs=jax.tree.map(lambda _: VMEM, shapes) if out_specs is None else out_specs,
         scratch_shapes=scratch,
+        input_output_aliases=aliases,
         compiler_params=pltpu.CompilerParams(vmem_limit_bytes=40 * 1024 * 1024),
     )(*args)
 
@@ -395,63 +451,66 @@
     n_all = lax.axis_size(("lat_0", "lat_2", "lon"))
     n_z = lax.axis_size(("lat_1", "dp"))
     lat, me = lax.axis_index(LAT), lax.axis_index("lon")
+    row_group = lax.axis_index(("lat_0", "lat_2"))
     at = jnp.stack(
-        [lat % 2, lat, n_lat - 1 - lat, (me + n_x - 1) % n_x, (me + 1) % n_x]
+        [lat % 2, lat, n_lat - 1 - lat, (me + n_x - 1) % n_x, (me + 1) % n_x, row_group]
     ).astype(jnp.int32)
-    cross, pair, head, tail, near, planes, sums = call(
+    mask = sea_mask.astype(wide)
+    fields = jnp.stack([mask * surface_cotangent[0], mask * ocean_depth])
+    cross, pair, near, planes, sums = call(
         first_kernel,
         (
             shape((304, 128), narrow),
             shape((304, 128), narrow),
-            shape((16, 128), narrow),
-            shape((16, 128), narrow),
             shape((2 * n_x, NEAR, 128), narrow),
             shape((PLANES, rows, 128), wide),
             shape((2, 128), wide),
         ),
         [],
-        [SMEM] + [VMEM] * 4,
-        (at, hidden, surface_cotangent, sea_mask, ocean_depth),
+        [SMEM] + [VMEM] * 2,
+        (at, hidden, fields),
     )
     odd = [(i, (i + 1) % n_lat) for i in range(1, n_lat, 2)]
     odd = odd + [(j, i) for i, j in odd]
-
-    def corner(step):
-        return [(i * n_x + x, j * n_x + (x + step) % n_x) for i, j in odd for x in range(n_x)]
-
     cross = lax.ppermute(cross, LAT, odd)
-    head = lax.ppermute(head, LAT_LON, corner(n_x - 1))
-    tail = lax.ppermute(tail, LAT_LON, corner(1))
     pair = lax.ppermute(pair, "lat_2", [(0, 1), (1, 0)])
     near = lax.all_to_all(near, ("lat_2", "lon"), 0, 0, tiled=True)
-    total = call(sums_kernel, shape((n_all, 1, 128), wide), [], [VMEM] * 2, (sums, cross))
-    total = lax.all_to_all(total, ("lat_0", "lat_2", "lon"), 0, 0, tiled=True)
-    ext, preact, force = call(
+    sent = call(
+        second_kernel, shape((n_all, 24, 128), narrow), [], [SMEM] + [VMEM] * 2, (at, sums, cross)
+    )
+    got = lax.all_to_all(sent, ("lat_0", "lat_2", "lon"), 0, 0, tiled=True)
+    early, preact, params = call(
         forward_kernel,
         (
             shape((rows + 4, WIDE, 128), narrow),
             shape((rows + 2, WIDE, 128), wide),
-            shape((128, 128), wide),
+            shape((16, 128), wide),
         ),
         [pltpu.VMEM((384, 384), narrow)],
-        [SMEM] + [VMEM] * 9 + [SMEM] * 2,
+        [SMEM] + [VMEM] * 7 + [SMEM] * 2,
         (
-            at, hidden, planes, cross, pair, head, tail, near, conv_weight,
-            conv_bias[None], step_alpha, step_beta,
+            at, hidden, cross, pair, near, conv_weight, conv_bias[None],
+            proj_weight[None], step_alpha, step_beta,
         ),
     )
-    grad, sent = call(
+    grad, sent, _ = call(
         backward_kernel,
-        (shape((rows + 2, WIDE, 128), narrow), shape((n_all, 40, 128), narrow)),
+        (
+            shape((rows + 2, WIDE, 128), narrow),
+            shape((n_all, 40, 128), narrow),
+            shape((rows + 4, WIDE, 128), narrow),
+        ),
         [
             pltpu.VMEM((rows + 2, WIDE, 128), narrow),
             pltpu.VMEM((rows, WIDE, 384), narrow),
             pltpu.VMEM((9, 128, 128), wide),
+            pltpu.VMEM((384, 384), narrow),
             pltpu.SemaphoreType.DMA,
         ],
-        [VMEM] * 5,
-        (total, preact, force, ext, proj_weight[None]),
-        (HBM, VMEM),
+        [SMEM] + [VMEM] * 9,
+        (at, planes, cross, pair, near, got, conv_weight, params, preact, early),
+        (HBM, VMEM, VMEM),
+        {9: 2},
     )
     got = lax.all_to_all(sent, ("lat_0", "lat_2", "lon"), 0, 0, tiled=True)
     sent = call(middle_kernel, shape((n_z, 24, 128), narrow), [], [VMEM], (got,))

time: 117 us -> 94.4 us (0.81)
  starting transfers between devices: 54.8 us -> 43.5 us
  waiting for transfers between devices: 31.2 us -> 21.2 us
  local copies, waits for them, and re-layouts: 7.19 us -> 2.01 us
  Pallas kernels: 10 us -> 11.8 us
  blocking collectives: 12.6 us -> 13.9 us
    ppermute x2 -> x0, starting transfers between devices: 19.5 us -> none  [the longest x1 17.6 us: shards(): head = lax.ppermute(head, LAT_LON, corner(n_x - 1))]
    ppermute x2 -> x0, waiting for transfers between devices: 15.9 us -> none  [the longest x1 15.9 us: shards(): tail = lax.ppermute(tail, LAT_LON, corner(1))]
    all_to_all x1, starting transfers between devices: 5.22 us -> 13.2 us  [shards(): got = lax.all_to_all(sent, ('lat_1', 'dp'), 0, 0, tiled=True)]
    unnamed x22 -> x18, local copies, waits for them, and re-layouts: 7.11 us -> 1.92 us
    all_to_all x1, waiting for transfers between devices: 0.01 us -> 3.02 us  [shards(): got = lax.all_to_all(sent, ('lat_0', 'lat_2', 'lon'), 0, 0, tiled=True)]
    ppermute x1, waiting for transfers between devices: 4.04 us -> 5.97 us  [shards(): cross = lax.ppermute(cross, LAT, odd)]
    pallas_call x7, Pallas kernels: 10 us -> 11.8 us  [call(): pl.pallas_call(kernel, out_shape=shapes, in_specs=in_specs, out_specs=jax...]
    all_to_all x1, blocking collectives: 12.6 us -> 13.9 us  [shards(): got = lax.all_to_all(sent, ('lat_0', 'lat_2', 'lon'), 0, 0, tiled=True)]
  transfers between devices with their start and end apart: 7 -> 5, of which waited for: 3 -> 4; matrix products, arithmetic and copies ran while one was open for 0% -> 0% of each run, Pallas kernels for 4% -> 6%
where the time goes in v6:
time: 94.4 us; the launch traced here: 93.9 us
  starting transfers between devices  43.5 us (46%)
  waiting for transfers between devices  21.2 us (22%)
  blocking collectives  13.9 us (15%)
  Pallas kernels  11.8 us (12%)
  local copies, waits for them, and re-layouts  2.01 us (2%)
    ppermute x1, starting transfers between devices, shards(): cross = lax.ppermute(cross, LAT, odd)  17.4 us
    all_to_all x1, blocking collectives, shards(): got = lax.all_to_all(sent, ('lat_0', 'lat_2', 'lon'), 0, 0, tiled=True)  13.9 us
    all_to_all x1, starting transfers between devices, shards(): got = lax.all_to_all(sent, ('lat_1', 'dp'), 0, 0, tiled=True)  13.2 us
    pallas_call x7, Pallas kernels, call(): pl.pallas_call(kernel, out_shape=shapes, in_specs=in_specs, out_specs=jax...  11.8 us
    all_to_all x1, waiting for transfers between devices, shards(): got = lax.all_to_all(sent, ('lat_1', 'dp'), 0, 0, tiled=True)  11.2 us
    all_to_all x1, starting transfers between devices, shards(): got = lax.all_to_all(sent, ('lat_0', 'lat_2', 'lon'), 0, 0, tiled=True)  6.48 us
    ppermute x1, waiting for transfers between devices, shards(): cross = lax.ppermute(cross, LAT, odd)  5.97 us
    all_to_all x1, starting transfers between devices, shards(): near = lax.all_to_all(near, ('lat_2', 'lon'), 0, 0, tiled=True)  4.3 us
  transfers between devices with their start and end apart: 5, of which 4 were waited for; matrix products, arithmetic and copies ran while one was open for 0% of the time, Pallas kernels for 6%

profile of v6, /device:TPU:32, one launch (start us, length us, event | category | flops | bytes accessed | tf_op | source)
XLA Modules:
  0.0 93.9 jit_solution(15916266707800982784)
XLA Ops:
  0.6 0.0 copy-start
  0.7 0.8 fusion
  1.5 0.1 stack.36.at_ref
  1.5 1.0 %copy-done.1 = bf16[1,16,128,128]{3,2,1,0:T(8,128)(2,1)S(1)} copy-done((bf16[1,16,128,128]{3,2,1,0:T(8,128)(2,1)S(1)}, bf16[1,16,128,128]{3,2,1,0:T(8,128)(2,1)}, u32[]{:S(2)}) %copy-start.1) | copy-done | bytes 524312
  2.6 0.0 copy-start.8
  2.6 1.3 %shard_map.120 = (bf16[304,128]{1,0:T(8,128)(2,1)S(1)}, bf16[304,128]{1,0:T(8,128)(2,1)S(1)}, bf16[8,48,128]{2,1,0:T(8,128)(2,1)}, f32[5,16,128]{2,1,0:T(8,128)S(1)}, f32[2,128]{1,0:T(2,128)S(1)}) custom-call(s32[6]{0:T(128)S(1)} %stack.36.at_ref, bf16[16,128,128]{2,1,0:T(8,128)(2,1)S(1)} %bitcast.21, f32[2,16,128]{2,1,0:T(8,128)S(1)} %pad_maximum_fusion.fields_ref), custom_call_target="tpu_custom_call" | custom-call | tf_op jit(solution)/shard_map/pallas_call | solution.py:427
  3.9 4.3 %all-to-all-start = ((bf16[8,48,128]{2,1,0:T(8,128)(2,1)}), bf16[8,48,128]{2,1,0:T(8,128)(2,1)S(1)}, u32[]{:S(2)}, u32[]{:S(2)}) async-start(bf16[8,48,128]{2,1,0:T(8,128)(2,1)} %get-tuple-element.20), calls=%async_computation | async-start | bytes 196608 | tf_op jit(solution)/shard_map/all_to_all | solution.py:477
  8.2 17.4 %collective-permute-start = (bf16[304,128]{1,0:T(8,128)(2,1)S(1)}, bf16[304,128]{1,0:T(8,128)(2,1)S(1)}, u32[]{:S(2)}, u32[]{:S(2)}) collective-permute-start(bf16[304,128]{1,0:T(8,128)(2,1)S(1)} %get-tuple-element.18), channel_id=1, source_target_pairs={{4,8},{12,16},{20,24},{28,32},{36,40},{44,48},{52,56},{60,0},{8,4}... | collective-permute-start | bytes 233480 | tf_op jit(solution)/shard_map/ppermute | solution.py:475
  25.6 6.0 %collective-permute-done.cross_ref = bf16[304,128]{1,0:T(8,128)(2,1)S(1)} collective-permute-done((bf16[304,128]{1,0:T(8,128)(2,1)S(1)}, bf16[304,128]{1,0:T(8,128)(2,1)S(1)}, u32[]{:S(2)}, u32[]{:S(2)}) %collective-permute-start) | collective-permute-done | bytes 77856 | tf_op jit(solution)/shard_map/ppermute | solution.py:475
  31.5 1.3 %shard_map.121 = bf16[32,24,128]{2,1,0:T(8,128)(2,1)} custom-call(s32[6]{0:T(128)S(1)} %stack.36.at_ref, f32[2,128]{1,0:T(2,128)S(1)} %get-tuple-element.21.sums_ref, bf16[304,128]{1,0:T(8,128)(2,1)S(1)} %collective-permute-done.cross_ref), custom_call_target="tpu_custom_call" | custom-call | tf_op jit(solution)/shard_map/pallas_call | solution.py:427
  32.8 0.0 all-to-all-done.near_ref
  32.8 6.5 %all-to-all-start.1 = ((bf16[32,24,128]{2,1,0:T(8,128)(2,1)}), bf16[32,24,128]{2,1,0:T(8,128)(2,1)S(1)}, u32[]{:S(2)}, u32[]{:S(2)}) async-start(bf16[32,24,128]{2,1,0:T(8,128)(2,1)} %shard_map.121), calls=%async_computation.1 | async-start | bytes 393216 | tf_op jit(solution)/shard_map/all_to_all | solution.py:481
  39.3 2.2 %collective-permute-start.1 = (bf16[304,128]{1,0:T(8,128)(2,1)S(1)}, bf16[304,128]{1,0:T(8,128)(2,1)S(1)}, u32[]{:S(2)}, u32[]{:S(2)}) collective-permute-start(bf16[304,128]{1,0:T(8,128)(2,1)S(1)} %get-tuple-element.19), channel_id=1, source_target_pairs={{0,4},{4,0},{1,5},{5,1},{2,6},{6,2},{3,7},{7,3},{8,12},{12,8},{9,1... | collective-permute-start | bytes 233480 | tf_op jit(solution)/shard_map/ppermute | solution.py:476
  41.5 1.0 %collective-permute-done.1.pair_ref = bf16[304,128]{1,0:T(8,128)(2,1)S(1)} collective-permute-done((bf16[304,128]{1,0:T(8,128)(2,1)S(1)}, bf16[304,128]{1,0:T(8,128)(2,1)S(1)}, u32[]{:S(2)}, u32[]{:S(2)}) %collective-permute-start.1) | collective-permute-done | bytes 77856 | tf_op jit(solution)/shard_map/ppermute | solution.py:476
  42.5 2.0 %shard_map.122 = (bf16[20,144,128]{2,1,0:T(8,128)(2,1)S(1)}, f32[18,144,128]{2,1,0:T(8,128)S(1)}, f32[16,128]{1,0:T(8,128)S(1)}) custom-call(s32[6]{0:T(128)S(1)} %stack.36.at_ref, bf16[16,128,128]{2,1,0:T(8,128)(2,1)S(1)} %bitcast.22, bf16[304,128]{1,0:T(8,128)(2,1)S(1)} %collective-permute-done.cross_ref, ...), custom_call_target="tpu_custom_call" | custom-call | tf_op jit(solution)/shard_map/pallas_call | solution.py:427
  44.5 3.0 %all-to-all-done.1.got_ref = bf16[32,24,128]{2,1,0:T(8,128)(2,1)S(1)} async-done(((bf16[32,24,128]{2,1,0:T(8,128)(2,1)}), bf16[32,24,128]{2,1,0:T(8,128)(2,1)S(1)}, u32[]{:S(2)}, u32[]{:S(2)}) %all-to-all-start.1) | async-done | bytes 196640 | tf_op jit(solution)/shard_map/all_to_all | solution.py:481
  47.5 3.8 %shard_map.123 = (bf16[18,144,128]{2,1,0:T(8,128)(2,1)S(1)}, bf16[32,40,128]{2,1,0:T(8,128)(2,1)S(1)}, bf16[20,144,128]{2,1,0:T(8,128)(2,1)S(1)}) custom-call(s32[6]{0:T(128)S(1)} %stack.36.at_ref, f32[5,16,128]{2,1,0:T(8,128)S(1)} %get-tuple-element.17.planes_ref, ...), custom_call_target="tpu_custom_call", output_to_operand_aliasing={{2}: (9, {})} | custom-call | tf_op jit(solution)/shard_map/pallas_call | solution.py:427
  51.4 0.8 copy-done.3
  52.2 13.9 %all_to_all.20.got_ref = bf16[32,40,128]{2,1,0:T(8,128)(2,1)S(1)} all-to-all(bf16[32,40,128]{2,1,0:T(8,128)(2,1)S(1)} %get-tuple-element.26), channel_id=1, replica_groups=mesh['dp'=8,'lat_0'=4,'lat_1'=2,'lat_2'=2,'lon'=4] {'lat_0','lat_2','lon'}, dimensions={0} | all-to-all | bytes 655360 | tf_op jit(solution)/shard_map/all_to_all | solution.py:515
  66.1 0.7 shard_map.125
  66.8 13.2 %all-to-all-start.3 = ((bf16[16,24,128]{2,1,0:T(8,128)(2,1)}), bf16[16,24,128]{2,1,0:T(8,128)(2,1)S(1)}, u32[]{:S(2)}, u32[]{:S(2)}) async-start(bf16[16,24,128]{2,1,0:T(8,128)(2,1)} %shard_map.125), calls=%async_computation.3 | async-start | bytes 196608 | tf_op jit(solution)/shard_map/all_to_all | solution.py:517
  80.0 2.1 %shard_map.124 = bf16[16,128,128]{2,1,0:T(8,128)(2,1)} custom-call(bf16[18,144,128]{2,1,0:T(8,128)(2,1)S(1)} %copy-done.4, bf16[3,3,128,128]{3,2,1,0:T(8,128)(2,1)S(1)} %copy-done), custom_call_target="tpu_custom_call" | custom-call | tf_op jit(solution)/shard_map/pallas_call | solution.py:427
  82.1 11.2 %all-to-all-done.3.got_ref = bf16[16,24,128]{2,1,0:T(8,128)(2,1)S(1)} async-done(((bf16[16,24,128]{2,1,0:T(8,128)(2,1)}), bf16[16,24,128]{2,1,0:T(8,128)(2,1)S(1)}, u32[]{:S(2)}, u32[]{:S(2)}) %all-to-all-start.3) | async-done | bytes 98336 | tf_op jit(solution)/shard_map/all_to_all | solution.py:517
  93.3 0.6 shard_map.126
  (15 shorter events, 0.0 us)
Async XLA Ops:
  0.6 41.9 %copy-start = (bf16[3,3,128,128]{3,2,1,0:T(8,128)(2,1)S(1)}, bf16[3,3,128,128]{3,2,1,0:T(8,128)(2,1)}, u32[]{:S(2)}) copy-start(bf16[3,3,128,128]{3,2,1,0:T(8,128)(2,1)} %weight_ref.3) | copy-start | bytes 884740
  1.5 1.0 %copy-start.1 = (bf16[1,16,128,128]{3,2,1,0:T(8,128)(2,1)S(1)}, bf16[1,16,128,128]{3,2,1,0:T(8,128)(2,1)}, u32[]{:S(2)}) copy-start(bf16[1,16,128,128]{3,2,1,0:T(8,128)(2,1)} %param.9) | copy-start | bytes 1572868
  2.6 39.9 %copy-start.2 = (bf16[1,16,128,128]{3,2,1,0:T(8,128)(2,1)S(1)}, bf16[1,16,128,128]{3,2,1,0:T(8,128)(2,1)}, u32[]{:S(2)}) copy-start(bf16[1,16,128,128]{3,2,1,0:T(8,128)(2,1)} %param.9) | copy-start | bytes 1572868
  2.6 39.9 %copy-start.5 = (f32[128]{0:T(128)S(1)}, f32[128]{0:T(128)}, u32[]{:S(2)}) copy-start(f32[128]{0:T(128)} %param.11) | copy-start | bytes 1540
  2.6 39.9 %copy-start.6 = (f32[128]{0:T(128)S(1)}, f32[128]{0:T(128)}, u32[]{:S(2)}) copy-start(f32[128]{0:T(128)} %param.12) | copy-start | bytes 1540
  2.6 39.9 %copy-start.7 = (f32[6]{0:T(128)S(1)}, f32[6]{0:T(128)}, u32[]{:S(2)}) copy-start(f32[6]{0:T(128)} %alpha_ref.1) | copy-start | bytes 76
  2.6 39.9 %copy-start.8 = (f32[6]{0:T(128)S(1)}, f32[6]{0:T(128)}, u32[]{:S(2)}) copy-start(f32[6]{0:T(128)} %beta_ref.1) | copy-start | bytes 76
  3.9 29.0 %all-to-all-start = ((bf16[8,48,128]{2,1,0:T(8,128)(2,1)}), bf16[8,48,128]{2,1,0:T(8,128)(2,1)S(1)}, u32[]{:S(2)}, u32[]{:S(2)}) async-start(bf16[8,48,128]{2,1,0:T(8,128)(2,1)} %get-tuple-element.20), calls=%async_computation | async-start | bytes 196608 | tf_op jit(solution)/shard_map/all_to_all | solution.py:477
  8.2 23.4 %collective-permute-start = (bf16[304,128]{1,0:T(8,128)(2,1)S(1)}, bf16[304,128]{1,0:T(8,128)(2,1)S(1)}, u32[]{:S(2)}, u32[]{:S(2)}) collective-permute-start(bf16[304,128]{1,0:T(8,128)(2,1)S(1)} %get-tuple-element.18), channel_id=1, source_target_pairs={{4,8},{12,16},{20,24},{28,32},{36,40},{44,48},{52,56},{60,0},{8,4}... | collective-permute-start | bytes 233480 | tf_op jit(solution)/shard_map/ppermute | solution.py:475
  32.8 14.7 %all-to-all-start.1 = ((bf16[32,24,128]{2,1,0:T(8,128)(2,1)}), bf16[32,24,128]{2,1,0:T(8,128)(2,1)S(1)}, u32[]{:S(2)}, u32[]{:S(2)}) async-start(bf16[32,24,128]{2,1,0:T(8,128)(2,1)} %shard_map.121), calls=%async_computation.1 | async-start | bytes 393216 | tf_op jit(solution)/shard_map/all_to_all | solution.py:481
  39.3 3.2 %collective-permute-start.1 = (bf16[304,128]{1,0:T(8,128)(2,1)S(1)}, bf16[304,128]{1,0:T(8,128)(2,1)S(1)}, u32[]{:S(2)}, u32[]{:S(2)}) collective-permute-start(bf16[304,128]{1,0:T(8,128)(2,1)S(1)} %get-tuple-element.19), channel_id=1, source_target_pairs={{0,4},{4,0},{1,5},{5,1},{2,6},{6,2},{3,7},{7,3},{8,12},{12,8},{9,1... | collective-permute-start | bytes 233480 | tf_op jit(solution)/shard_map/ppermute | solution.py:476
  51.3 0.9 copy-start.3
  52.2 27.8 %copy-start.4 = (bf16[18,144,128]{2,1,0:T(8,128)(2,1)S(1)}, bf16[18,144,128]{2,1,0:T(8,128)(2,1)}, u32[]{:S(2)}) copy-start(bf16[18,144,128]{2,1,0:T(8,128)(2,1)} %copy-done.3) | copy-start | bytes 1990660
  66.8 26.5 %all-to-all-start.3 = ((bf16[16,24,128]{2,1,0:T(8,128)(2,1)}), bf16[16,24,128]{2,1,0:T(8,128)(2,1)S(1)}, u32[]{:S(2)}, u32[]{:S(2)}) async-start(bf16[16,24,128]{2,1,0:T(8,128)(2,1)} %shard_map.125), calls=%async_computation.3 | async-start | bytes 196608 | tf_op jit(solution)/shard_map/all_to_all | solution.py:517

commit v7 on v6

--- a/solution.py
+++ b/solution.py
@@ -59,6 +59,14 @@
         for k, row in enumerate((head[0:1], head[1:2], tail[14:15], tail[15:16])):
             columns[k][r // 8] = jnp.where(place == r % 8, row, columns[k][r // 8])
     return columns
+
+
+def unpacked(beyond, before, k):
+    near = lax.broadcasted_iota(jnp.int32, beyond.shape, 1)
+    if k:
+        beyond = pltpu.roll(beyond, 128 - 8 * k, 1)
+    before = pltpu.roll(before, 120 - 8 * k, 1)
+    return jnp.where(near < 8, beyond, jnp.where(near >= 120, before, 0.0))
 
 
 def first_kernel(
@@ -99,8 +107,8 @@
     got = tiles[2][8:16]
     summed = sums_ref[0:1] + got[0:1] + got[1:2] + got[2:3]
     counted = sums_ref[1:2] + got[3:4] + got[4:5] + got[5:6]
-    sums = pieces_of(summed, 3) + pieces_of(counted, 3)
-    sums = jnp.concatenate(sums + [jnp.zeros((2, 128), jnp.float32)], axis=0)
+    lane = lax.broadcasted_iota(jnp.int32, (1, 128), 1)
+    sums = pieces_of(jnp.where(lane < 64, summed, counted), 3)
     place = lax.broadcasted_iota(jnp.int32, (8, 128), 0)
     blocks = []
     for side in range(2):
@@ -111,8 +119,9 @@
             for k in range(2):
                 at = 14 * side + k
                 corner = jnp.where(place == 2 * r + k, tile[at : at + 1], corner)
-        block = jnp.concatenate([corner, packed(planes, 8 * side), sums], axis=0)
-        blocks.append(block)
+        for k in range(3):
+            corner = jnp.where(place == 4 + k, sums[k], corner)
+        blocks.append(jnp.concatenate([corner, packed(planes, 8 * side)], axis=0))
     n_x = 4
     for peer in range(n_x):
         chosen = jnp.where(at_ref[4] == peer, blocks[1], blocks[0]).astype(jnp.bfloat16)
@@ -152,9 +161,9 @@
 
 
 def forward_kernel(
-    at_ref, hidden_ref, cross_ref, pair_ref, near_ref, weight_ref, bias_ref, proj_ref,
+    at_ref, hidden_ref, planes_ref, cross_ref, pair_ref, near_ref, weight_ref, bias_ref, proj_ref,
     alpha_ref, beta_ref,
-    ext_ref, preact_ref, params_ref, rhs_ref,
+    ext_ref, preact_ref, side_ref, rhs_ref,
 ):
     rows = hidden_ref.shape[0]
     n_x = near_ref.shape[0] // 2
@@ -171,94 +180,98 @@
     ext_ref[2 : rows + 2, 0:128] = hidden_ref[...]
     place = lax.broadcasted_iota(jnp.int32, (WIDE - 128, 128), 0)
     tiles = [jnp.zeros((WIDE - 128, 128), jnp.float32) for _ in range(rows + 4)]
+    second = []
     for side, base in ((right, 0), (left, WIDE - 130)):
         own = near_ref[core * n_x + side].astype(jnp.float32)
         other = near_ref[(1 - core) * n_x + side].astype(jnp.float32)
         for k in range(2):
             for r in range(rows + 4):
                 at = r - 2
-                source = own
                 if r < 2:
-                    source, at = other, rows - 2 + r
+                    at = k * 16 + rows - 2 + r
+                    row = other[at : at + 1] * keep_above
                 elif r >= rows + 2:
-                    source, at = other, r - rows - 2
-                row = source[k * 16 + at : k * 16 + at + 1]
+                    at = k * 16 + r - rows - 2
+                    row = other[at : at + 1] * keep_below
+                else:
+                    row = own[k * 16 + at : k * 16 + at + 1]
                 tiles[r] = jnp.where(place == base + k, row, tiles[r])
+        above = jnp.where(upper, 0.0, other[40:48] * keep_above)
+        below = jnp.where(upper, other[32:40] * keep_below, 0.0)
+        second.append(jnp.concatenate([above, own[32:48], below], axis=0))
     for r in range(rows + 4):
         ext_ref[r, 128:WIDE] = tiles[r].astype(jnp.bfloat16)
+    cross = cross_ref[256:304].astype(jnp.float32)
+    pair = pair_ref[256:304].astype(jnp.float32)
+    above = jnp.where(upper, cross, pair) * keep_above
+    below = jnp.where(upper, pair, cross) * keep_below
+    planes = []
+    for k in range(PLANES):
+        at = k * 8
+        tile = unpacked(second[0], second[1], k)
+        planes.append(
+            jnp.concatenate(
+                [above[at : at + 8], planes_ref[k], below[at : at + 8], tile], axis=0
+            )
+        )
+    side_ref[0 : 2 * PACK] = planes[0] + planes[1] + planes[2]
+    side_ref[2 * PACK : 4 * PACK] = planes[3] + planes[4]
     fill(rhs_ref, weight_ref)
     bias = bias_ref[...]
-    params_ref[0:1] = bias
-    params_ref[1:2] = proj_ref[...]
-    for k in range(ITERS):
-        params_ref[2 + k : 3 + k] = full(alpha_ref[k])
-        params_ref[8 + k : 9 + k] = full(beta_ref[k])
-    group = 6
-    for g in range(0, rows + 2, group):
-        for j, row in enumerate(convolved(ext_ref, rhs_ref, bias, g, group)):
+    steps = [full(ref[k]) for ref in (alpha_ref, beta_ref) for k in range(ITERS)]
+    params = [bias, proj_ref[...], *steps, full(0.0), full(0.0)]
+    side_ref[4 * PACK : 4 * PACK + 16] = jnp.concatenate(params, axis=0)
+    group = 4
+    shift = jnp.where(upper, 2, 0)
+    for g in range(0, rows, group):
+        for j, row in enumerate(convolved(ext_ref, rhs_ref, bias, g + shift, group)):
             preact_ref[g + j] = row
 
 
 def backward_kernel(
-    at_ref, planes_ref, cross_ref, pair_ref, near_ref, got_ref, kernel_ref, params_ref,
-    preact_ref, early_ref,
+    at_ref, got_ref, kernel_ref, side_ref, preact_ref, early_ref,
     grad_hbm, sent_ref, ext_ref,
     grad_ref, moved_ref, weight_ref, rhs_ref, sem,
 ):
     rows = grad_ref.shape[0] - 2
-    n_x = near_ref.shape[0] // 2
-    core, left, right = at_ref[0], at_ref[3], at_ref[4]
+    n_x = 4
+    fields = side_ref[0 : 4 * PACK]
+    fields = (fields[0 : 2 * PACK], fields[2 * PACK : 4 * PACK])
+    params = side_ref[4 * PACK : 4 * PACK + 16]
+    left, right = at_ref[3], at_ref[4]
     upper, keep_above, keep_below = sides_of(at_ref)
     keep_cross = jnp.where(upper, keep_above, keep_below)
     place = lax.broadcasted_iota(jnp.int32, (WIDE - 128, 128), 0)
     tiles = [jnp.zeros((WIDE - 128, 128), jnp.float32) for _ in range(2)]
     second = []
     for side, base in ((right, 0), (left, WIDE - 130)):
-        own = near_ref[core * n_x + side, 32:48].astype(jnp.float32)
-        other = near_ref[(1 - core) * n_x + side, 32:48].astype(jnp.float32)
-        corner = got_ref[at_ref[5] * n_x + side].astype(jnp.float32)[0:16] * keep_cross
+        corner = got_ref[at_ref[5] * n_x + side].astype(jnp.float32) * keep_cross
         for r in range(2):
             for k in range(2):
                 row = corner[2 * r + k : 2 * r + k + 1]
                 tiles[r] = jnp.where(place == base + k, row, tiles[r])
-        above = jnp.where(upper, corner[8:16], other[8:16] * keep_above)
-        below = jnp.where(upper, other[0:8] * keep_below, corner[8:16])
-        second.append(jnp.concatenate([above, own, below], axis=0))
-    from_right, from_left = second
+        second.append(corner[8:16])
     crossed = jnp.where(upper, 0, rows + 2)
-    paired = rows + 2 - crossed
     for r in range(2):
         ext_ref[crossed + r, 128:WIDE] = tiles[r].astype(jnp.bfloat16)
-        keep = jnp.where(upper, keep_below, keep_above) > 0.0
-        mate = ext_ref[paired + r, 128:WIDE]
-        ext_ref[paired + r, 128:WIDE] = jnp.where(keep, mate, jnp.zeros((), jnp.bfloat16))
     fill(rhs_ref, kernel_ref)
     again = jnp.where(upper, 0, rows)
-    fixed = convolved(ext_ref, rhs_ref, params_ref[0:1], again, 2)
-    cross = cross_ref[256:304].astype(jnp.float32)
-    pair = pair_ref[256:304].astype(jnp.float32)
-    above = jnp.where(upper, cross, pair) * keep_above
-    below = jnp.where(upper, pair, cross) * keep_below
+    fixed = convolved(ext_ref, rhs_ref, params[0:1], again, 2)
+    corner = [unpacked(second[0], second[1], k) for k in range(PLANES)]
+    corner = (corner[0] + corner[1] + corner[2], corner[3] + corner[4])
+    start, wet_depth = [
+        jnp.concatenate(
+            [
+                fields[k][0:PACK],
+                fields[k][PACK : PACK + 8] + jnp.where(upper, corner[k], 0.0),
+                fields[k][PACK + 8 : 2 * PACK - 8],
+                fields[k][2 * PACK - 8 : 2 * PACK] + jnp.where(upper, 0.0, corner[k]),
+            ],
+            axis=0,
+        )
+        for k in range(2)
+    ]
     lane = lax.broadcasted_iota(jnp.int32, (2 * PACK, 128), 1)
-    planes = []
-    for k in range(PLANES):
-        beyond = from_right if k == 0 else pltpu.roll(from_right, 128 - 8 * k, 1)
-        before = pltpu.roll(from_left, 120 - 8 * k, 1)
-        near = lane[:PACK]
-        at = k * 8
-        planes.append(
-            jnp.concatenate(
-                [
-                    above[at : at + 8],
-                    planes_ref[k],
-                    below[at : at + 8],
-                    jnp.where(near < 8, beyond, jnp.where(near >= 120, before, 0.0)),
-                ],
-                axis=0,
-            )
-        )
-    start = planes[0] + planes[1] + planes[2]
-    wet_depth = planes[3] + planes[4]
     mask = jnp.where(wet_depth > 0.0, 1.0, 0.0)
 
     def other_half(field):
@@ -290,19 +303,21 @@
     direction = residual
     result = jnp.zeros_like(residual)
     for k in range(ITERS):
-        result = result + params_ref[2 + k : 3 + k] * direction
+        result = result + params[2 + k : 3 + k] * direction
         if k + 1 < ITERS:
             applied = diagonal * direction
             for w, near in zip(weights, beside(direction)):
                 applied = applied - w * near
-            residual = residual - params_ref[2 + k : 3 + k] * applied
-            direction = residual + params_ref[8 + k : 9 + k] * direction
+            residual = residual - params[2 + k : 3 + k] * applied
+            direction = residual + params[8 + k : 9 + k] * direction
     result = result * jnp.concatenate([mask, mask], axis=0)
-    sums = jnp.sum(got_ref[:, 16:24].astype(jnp.float32), axis=0)
-    mean = (sums[0:1] + sums[1:2] + sums[2:3]) / (sums[3:4] + sums[4:5] + sums[5:6])
+    sums = jnp.sum(got_ref[...].astype(jnp.float32)[:, 0:8], axis=0)
+    sums = sums[4:5] + sums[5:6] + sums[6:7]
+    mean = jnp.broadcast_to(sums[:, 0:1], (1, 128)) / jnp.broadcast_to(sums[:, 127:128], (1, 128))
     force = result.T
     force = force - mean * pltpu.roll(force, 64, 1)
-    proj = params_ref[1:2]
+    proj = params[1:2]
+    shift = jnp.where(upper, 2, 0)
     sum_bias = jnp.zeros((8, 128), jnp.float32)
     sum_proj = jnp.zeros((8, 128), jnp.float32)
     for g in range(rows + 2):
@@ -316,11 +331,12 @@
             axis=0,
         )
         column = jnp.broadcast_to(column, (WIDE, 128))
-        preact = preact_ref[g]
         if g < 2:
-            preact = jnp.where(upper, fixed[g], preact)
+            preact = jnp.where(upper, fixed[g], preact_ref[g])
         elif g >= rows:
-            preact = jnp.where(upper, preact, fixed[g - rows])
+            preact = jnp.where(upper, preact_ref[g - 2], fixed[g - rows])
+        else:
+            preact = preact_ref[g - shift]
         sigma = jax.nn.sigmoid(preact)
         active = preact * sigma
         slope_act = sigma * (1.0 + preact * (1.0 - sigma))
@@ -337,12 +353,21 @@
             moved_ref[g - 1, :, 256:384] = pltpu.roll(own, 1, 0).astype(jnp.bfloat16)
     copy = pltpu.make_async_copy(grad_ref, grad_hbm, sem)
     copy.start()
+    to = lax.broadcasted_iota(jnp.int32, (128, 128), 0)
+    of = lax.broadcasted_iota(jnp.int32, (128, 128), 1)
+    source = (
+        to // 32 * 32 + to // 2 % 2 * 16 + to // 16 % 2 * 8 + to // 4 % 4 * 2 + to % 2
+    )
+    order = jnp.where(of == source, 1.0, 0.0).astype(jnp.bfloat16)
     moved = moved_ref[...].reshape(rows * WIDE, 384)
     for a in range(3):
         cells = ext_ref[a + 1 : a + 1 + rows].reshape(rows * WIDE, 128)
         out = lax.dot_general(
             cells, moved, (((0,), (0,)), ((), ())), preferred_element_type=jnp.float32
         )
+        out = jnp.dot(
+            order, out.astype(jnp.bfloat16), preferred_element_type=jnp.float32
+        )
         for c in range(3):
             weight_ref[a * 3 + c] = out[:, c * 128 : c * 128 + 128]
     vectors = jnp.concatenate(
@@ -350,29 +375,22 @@
     )
     vectors = jnp.concatenate(pieces_of(vectors, 2) + [jnp.zeros((4, 128), jnp.float32)], axis=0)
     vectors = pltpu.roll(vectors, 4, 0)
-    place = lax.broadcasted_iota(jnp.int32, (8, 128), 0) // 2
-
-    def one_pair(at, carry):
-        y, c = at // 2, at % 2
-        for x in range(4):
-            tiles = []
-            for t in range(5):
-                tile = vectors
-                for j in range(4):
-                    slot = 4 * t + j
-                    if slot >= 18:
-                        continue
-                    z, k = slot // 9, slot % 9
-                    start = pl.multiple_of(((y * 2 + z) * 2 + c) * 8, 8)
-                    piece = weight_ref[k, pl.ds(start, 8)]
-                    if j != x:
-                        piece = pltpu.roll(piece, (2 * j - 2 * x) % 8, 0)
-                    tile = jnp.where(place == j, piece, tile)
-                tiles.append(tile)
-            sent_ref[at * 4 + x] = jnp.concatenate(tiles, axis=0).astype(jnp.bfloat16)
+    low = lax.broadcasted_iota(jnp.int32, (8, 128), 0) < 4
+
+    def one_pair(t, carry):
+        start = pl.multiple_of(t * 8, 8)
+        blocks = ([], [])
+        for k in range(0, 9, 2):
+            one = weight_ref[k, pl.ds(start, 8)]
+            two = weight_ref[k + 1, pl.ds(start, 8)] if k < 8 else vectors
+            two_low = pltpu.roll(two, 4, 0) if k < 8 else vectors
+            blocks[0].append(jnp.where(low, one, two_low))
+            blocks[1].append(jnp.where(low, pltpu.roll(one, 4, 0), two))
+        for x in range(2):
+            sent_ref[t * 2 + x] = jnp.concatenate(blocks[x], axis=0).astype(jnp.bfloat16)
         return carry
 
-    lax.fori_loop(0, 8, one_pair, 0)
+    lax.fori_loop(0, 16, one_pair, 0)
     copy.wait()
 
 
@@ -382,7 +400,8 @@
     vectors = jnp.concatenate(pieces_of(vectors, 2) + [jnp.zeros((2, 128), jnp.float32)], axis=0)
     peers = sent_ref.shape[0] // 2
     for z in range(2):
-        block = jnp.concatenate([total[z * 18 : z * 18 + 18], vectors], axis=0)
+        block = [total[4 * k + 2 * z : 4 * k + 2 * z + 2] for k in range(9)]
+        block = jnp.concatenate(block + [vectors], axis=0)
         block = block.astype(jnp.bfloat16)
         for d in range(peers):
             sent_ref[z * peers + d] = block
@@ -476,20 +495,20 @@
     pair = lax.ppermute(pair, "lat_2", [(0, 1), (1, 0)])
     near = lax.all_to_all(near, ("lat_2", "lon"), 0, 0, tiled=True)
     sent = call(
-        second_kernel, shape((n_all, 24, 128), narrow), [], [SMEM] + [VMEM] * 2, (at, sums, cross)
+        second_kernel, shape((n_all, 16, 128), narrow), [], [SMEM] + [VMEM] * 2, (at, sums, cross)
     )
     got = lax.all_to_all(sent, ("lat_0", "lat_2", "lon"), 0, 0, tiled=True)
-    early, preact, params = call(
+    early, preact, side = call(
         forward_kernel,
         (
             shape((rows + 4, WIDE, 128), narrow),
-            shape((rows + 2, WIDE, 128), wide),
-            shape((16, 128), wide),
+            shape((rows, WIDE, 128), wide),
+            shape((4 * PACK + 16, 128), wide),
         ),
         [pltpu.VMEM((384, 384), narrow)],
-        [SMEM] + [VMEM] * 7 + [SMEM] * 2,
+        [SMEM] + [VMEM] * 8 + [SMEM] * 2,
         (
-            at, hidden, cross, pair, near, conv_weight, conv_bias[None],
+            at, hidden, planes, cross, pair, near, conv_weight, conv_bias[None],
             proj_weight[None], step_alpha, step_beta,
         ),
     )
@@ -507,10 +526,10 @@
             pltpu.VMEM((384, 384), narrow),
             pltpu.SemaphoreType.DMA,
         ],
-        [SMEM] + [VMEM] * 9,
-        (at, planes, cross, pair, near, got, conv_weight, params, preact, early),
+        [SMEM] + [VMEM] * 5,
+        (at, got, conv_weight, side, preact, early),
         (HBM, VMEM, VMEM),
-        {9: 2},
+        {5: 2},
     )
     got = lax.all_to_all(sent, ("lat_0", "lat_2", "lon"), 0, 0, tiled=True)
     sent = call(middle_kernel, shape((n_z, 24, 128), narrow), [], [VMEM], (got,))

time: 94.4 us -> 95.3 us (level)
  waiting for transfers between devices: 21.2 us -> 20.1 us
  blocking collectives: 13.9 us -> 14.9 us
    all_to_all x1, waiting for transfers between devices: 3.02 us -> 1.91 us  [shards(): got = lax.all_to_all(sent, ('lat_0', 'lat_2', 'lon'), 0, 0, tiled=True)]
    all_to_all x1, blocking collectives: 13.9 us -> 14.9 us  [shards(): got = lax.all_to_all(sent, ('lat_0', 'lat_2', 'lon'), 0, 0, tiled=True)]
where the time goes in v7:
time: 95.3 us; the launch traced here: 94.8 us
  starting transfers between devices  43.5 us (46%)
  waiting for transfers between devices  20.1 us (21%)
  blocking collectives  14.9 us (16%)
  Pallas kernels  12.1 us (13%)
  local copies, waits for them, and re-layouts  2.67 us (3%)
    ppermute x1, starting transfers between devices, shards(): cross = lax.ppermute(cross, LAT, odd)  17.4 us
    all_to_all x1, blocking collectives, shards(): got = lax.all_to_all(sent, ('lat_0', 'lat_2', 'lon'), 0, 0, tiled=True)  14.9 us
    all_to_all x1, starting transfers between devices, shards(): got = lax.all_to_all(sent, ('lat_1', 'dp'), 0, 0, tiled=True)  13.2 us
    pallas_call x7, Pallas kernels, call(): pl.pallas_call(kernel, out_shape=shapes, in_specs=in_specs, out_specs=jax...  12.1 us
    all_to_all x1, waiting for transfers between devices, shards(): got = lax.all_to_all(sent, ('lat_1', 'dp'), 0, 0, tiled=True)  11.3 us
    all_to_all x1, starting transfers between devices, shards(): got = lax.all_to_all(sent, ('lat_0', 'lat_2', 'lon'), 0, 0, tiled=True)  6.48 us
    ppermute x1, waiting for transfers between devices, shards(): cross = lax.ppermute(cross, LAT, odd)  5.97 us
    all_to_all x1, starting transfers between devices, shards(): near = lax.all_to_all(near, ('lat_2', 'lon'), 0, 0, tiled=True)  4.3 us
  transfers between devices with their start and end apart: 5, of which 4 were waited for; matrix products, arithmetic and copies ran while one was open for 0% of the time, Pallas kernels for 6%

profile of v7, /device:TPU:32, one launch (start us, length us, event | category | flops | bytes accessed | tf_op | source)
XLA Modules:
  0.0 94.8 jit_solution(13621308436196815345)
XLA Ops:
  0.7 0.8 fusion
  1.5 0.1 stack.36.at_ref
  1.5 1.0 %copy-done.1 = bf16[1,16,128,128]{3,2,1,0:T(8,128)(2,1)S(1)} copy-done((bf16[1,16,128,128]{3,2,1,0:T(8,128)(2,1)S(1)}, bf16[1,16,128,128]{3,2,1,0:T(8,128)(2,1)}, u32[]{:S(2)}) %copy-start.1) | copy-done | bytes 524312
  2.6 0.0 copy-start.8
  2.6 1.3 %shard_map.120 = (bf16[304,128]{1,0:T(8,128)(2,1)S(1)}, bf16[304,128]{1,0:T(8,128)(2,1)S(1)}, bf16[8,48,128]{2,1,0:T(8,128)(2,1)}, f32[5,16,128]{2,1,0:T(8,128)S(1)}, f32[2,128]{1,0:T(2,128)S(1)}) custom-call(s32[6]{0:T(128)S(1)} %stack.36.at_ref, bf16[16,128,128]{2,1,0:T(8,128)(2,1)S(1)} %bitcast.21, f32[2,16,128]{2,1,0:T(8,128)S(1)} %pad_maximum_fusion.fields_ref), custom_call_target="tpu_custom_call" | custom-call | tf_op jit(solution)/shard_map/pallas_call | solution.py:446
  3.9 4.3 %all-to-all-start.1 = ((bf16[8,48,128]{2,1,0:T(8,128)(2,1)}), bf16[8,48,128]{2,1,0:T(8,128)(2,1)S(1)}, u32[]{:S(2)}, u32[]{:S(2)}) async-start(bf16[8,48,128]{2,1,0:T(8,128)(2,1)} %get-tuple-element.21), calls=%async_computation.1 | async-start | bytes 196608 | tf_op jit(solution)/shard_map/all_to_all | solution.py:496
  8.2 17.4 %collective-permute-start = (bf16[304,128]{1,0:T(8,128)(2,1)S(1)}, bf16[304,128]{1,0:T(8,128)(2,1)S(1)}, u32[]{:S(2)}, u32[]{:S(2)}) collective-permute-start(bf16[304,128]{1,0:T(8,128)(2,1)S(1)} %get-tuple-element.18), channel_id=1, source_target_pairs={{4,8},{12,16},{20,24},{28,32},{36,40},{44,48},{52,56},{60,0},{8,4}... | collective-permute-start | bytes 233480 | tf_op jit(solution)/shard_map/ppermute | solution.py:494
  25.6 6.0 %collective-permute-done.cross_ref = bf16[304,128]{1,0:T(8,128)(2,1)S(1)} collective-permute-done((bf16[304,128]{1,0:T(8,128)(2,1)S(1)}, bf16[304,128]{1,0:T(8,128)(2,1)S(1)}, u32[]{:S(2)}, u32[]{:S(2)}) %collective-permute-start) | collective-permute-done | bytes 77856 | tf_op jit(solution)/shard_map/ppermute | solution.py:494
  31.5 1.3 %shard_map.121 = bf16[32,16,128]{2,1,0:T(8,128)(2,1)} custom-call(s32[6]{0:T(128)S(1)} %stack.36.at_ref, f32[2,128]{1,0:T(2,128)S(1)} %get-tuple-element.17.sums_ref, bf16[304,128]{1,0:T(8,128)(2,1)S(1)} %collective-permute-done.cross_ref), custom_call_target="tpu_custom_call" | custom-call | tf_op jit(solution)/shard_map/pallas_call | solution.py:446
  32.8 0.0 all-to-all-done.1.near_ref
  32.8 6.5 %all-to-all-start = ((bf16[32,16,128]{2,1,0:T(8,128)(2,1)}), bf16[32,16,128]{2,1,0:T(8,128)(2,1)S(1)}, u32[]{:S(2)}, u32[]{:S(2)}) async-start(bf16[32,16,128]{2,1,0:T(8,128)(2,1)} %shard_map.121), calls=%async_computation | async-start | bytes 262144 | tf_op jit(solution)/shard_map/all_to_all | solution.py:500
  39.3 2.2 %collective-permute-start.1 = (bf16[304,128]{1,0:T(8,128)(2,1)S(1)}, bf16[304,128]{1,0:T(8,128)(2,1)S(1)}, u32[]{:S(2)}, u32[]{:S(2)}) collective-permute-start(bf16[304,128]{1,0:T(8,128)(2,1)S(1)} %get-tuple-element.20), channel_id=1, source_target_pairs={{0,4},{4,0},{1,5},{5,1},{2,6},{6,2},{3,7},{7,3},{8,12},{12,8},{9,1... | collective-permute-start | bytes 233480 | tf_op jit(solution)/shard_map/ppermute | solution.py:495
  41.5 1.0 %collective-permute-done.1.pair_ref = bf16[304,128]{1,0:T(8,128)(2,1)S(1)} collective-permute-done((bf16[304,128]{1,0:T(8,128)(2,1)S(1)}, bf16[304,128]{1,0:T(8,128)(2,1)S(1)}, u32[]{:S(2)}, u32[]{:S(2)}) %collective-permute-start.1) | collective-permute-done | bytes 77856 | tf_op jit(solution)/shard_map/ppermute | solution.py:495
  42.5 1.9 %shard_map.122 = (bf16[20,144,128]{2,1,0:T(8,128)(2,1)S(1)}, f32[16,144,128]{2,1,0:T(8,128)S(1)}, f32[144,128]{1,0:T(8,128)S(1)}) custom-call(s32[6]{0:T(128)S(1)} %stack.36.at_ref, bf16[16,128,128]{2,1,0:T(8,128)(2,1)S(1)} %bitcast.22, f32[5,16,128]{2,1,0:T(8,128)S(1)} %get-tuple-element.19.planes_ref, bf16[304,128]{1,0:T(8,128)(2,1)S(1)} %collective-permute-done.cross_ref, ...), custom_call_target="tpu_custom_call" | custom-call | tf_op jit(solution)/shard_map/pallas_call | solution.py:446
  44.4 0.6 copy-done.3
  45.1 1.9 %all-to-all-done.got_ref = bf16[32,16,128]{2,1,0:T(8,128)(2,1)S(1)} async-done(((bf16[32,16,128]{2,1,0:T(8,128)(2,1)}), bf16[32,16,128]{2,1,0:T(8,128)(2,1)S(1)}, u32[]{:S(2)}, u32[]{:S(2)}) %all-to-all-start) | async-done | bytes 131104 | tf_op jit(solution)/shard_map/all_to_all | solution.py:500
  47.0 0.9 copy-done.4
  47.9 4.2 %shard_map.123 = (bf16[18,144,128]{2,1,0:T(8,128)(2,1)S(1)}, bf16[32,40,128]{2,1,0:T(8,128)(2,1)S(1)}, bf16[20,144,128]{2,1,0:T(8,128)(2,1)S(1)}) custom-call(s32[6]{0:T(128)S(1)} %stack.36.at_ref, bf16[32,16,128]{2,1,0:T(8,128)(2,1)S(1)} %all-to-all-done.got_ref, bf16[3,3,128,128]{3,2,1,0:T(8,128)(2,1)S(1)} %copy-done, ...), custom_call_target="tpu_custom_call", output_to_operand_aliasing={{2}: (5, {})} | custom-call | tf_op jit(solution)/shard_map/pallas_call | solution.py:446
  52.0 14.9 %all_to_all.20.got_ref = bf16[32,40,128]{2,1,0:T(8,128)(2,1)S(1)} all-to-all(bf16[32,40,128]{2,1,0:T(8,128)(2,1)S(1)} %get-tuple-element.26), channel_id=1, replica_groups=mesh['dp'=8,'lat_0'=4,'lat_1'=2,'lat_2'=2,'lon'=4] {'lat_0','lat_2','lon'}, dimensions={0} | all-to-all | bytes 655360 | tf_op jit(solution)/shard_map/all_to_all | solution.py:534
  66.9 0.7 shard_map.125
  67.6 13.2 %all-to-all-start.3 = ((bf16[16,24,128]{2,1,0:T(8,128)(2,1)}), bf16[16,24,128]{2,1,0:T(8,128)(2,1)S(1)}, u32[]{:S(2)}, u32[]{:S(2)}) async-start(bf16[16,24,128]{2,1,0:T(8,128)(2,1)} %shard_map.125), calls=%async_computation.3 | async-start | bytes 196608 | tf_op jit(solution)/shard_map/all_to_all | solution.py:536
  80.8 2.1 %shard_map.124 = bf16[16,128,128]{2,1,0:T(8,128)(2,1)} custom-call(bf16[18,144,128]{2,1,0:T(8,128)(2,1)S(1)} %get-tuple-element.25.grad_ref, bf16[3,3,128,128]{3,2,1,0:T(8,128)(2,1)S(1)} %copy-done), custom_call_target="tpu_custom_call" | custom-call | tf_op jit(solution)/shard_map/pallas_call | solution.py:446
  82.9 11.3 %all-to-all-done.3.got_ref = bf16[16,24,128]{2,1,0:T(8,128)(2,1)S(1)} async-done(((bf16[16,24,128]{2,1,0:T(8,128)(2,1)}), bf16[16,24,128]{2,1,0:T(8,128)(2,1)S(1)}, u32[]{:S(2)}, u32[]{:S(2)}) %all-to-all-start.3) | async-done | bytes 98336 | tf_op jit(solution)/shard_map/all_to_all | solution.py:536
  94.1 0.6 shard_map.126
  (15 shorter events, 0.0 us)
Async XLA Ops:
  0.6 41.8 %copy-start = (bf16[3,3,128,128]{3,2,1,0:T(8,128)(2,1)S(1)}, bf16[3,3,128,128]{3,2,1,0:T(8,128)(2,1)}, u32[]{:S(2)}) copy-start(bf16[3,3,128,128]{3,2,1,0:T(8,128)(2,1)} %weight_ref.3) | copy-start | bytes 884740
  1.5 1.0 %copy-start.1 = (bf16[1,16,128,128]{3,2,1,0:T(8,128)(2,1)S(1)}, bf16[1,16,128,128]{3,2,1,0:T(8,128)(2,1)}, u32[]{:S(2)}) copy-start(bf16[1,16,128,128]{3,2,1,0:T(8,128)(2,1)} %param.9) | copy-start | bytes 1572868
  2.6 39.9 %copy-start.2 = (bf16[1,16,128,128]{3,2,1,0:T(8,128)(2,1)S(1)}, bf16[1,16,128,128]{3,2,1,0:T(8,128)(2,1)}, u32[]{:S(2)}) copy-start(bf16[1,16,128,128]{3,2,1,0:T(8,128)(2,1)} %param.9) | copy-start | bytes 1572868
  2.6 39.9 %copy-start.5 = (f32[128]{0:T(128)S(1)}, f32[128]{0:T(128)}, u32[]{:S(2)}) copy-start(f32[128]{0:T(128)} %param.11) | copy-start | bytes 1540
  2.6 39.9 %copy-start.6 = (f32[128]{0:T(128)S(1)}, f32[128]{0:T(128)}, u32[]{:S(2)}) copy-start(f32[128]{0:T(128)} %param.12) | copy-start | bytes 1540
  2.6 39.9 %copy-start.7 = (f32[6]{0:T(128)S(1)}, f32[6]{0:T(128)}, u32[]{:S(2)}) copy-start(f32[6]{0:T(128)} %alpha_ref.1) | copy-start | bytes 76
  2.6 39.9 %copy-start.8 = (f32[6]{0:T(128)S(1)}, f32[6]{0:T(128)}, u32[]{:S(2)}) copy-start(f32[6]{0:T(128)} %beta_ref.1) | copy-start | bytes 76
  3.9 28.9 %all-to-all-start.1 = ((bf16[8,48,128]{2,1,0:T(8,128)(2,1)}), bf16[8,48,128]{2,1,0:T(8,128)(2,1)S(1)}, u32[]{:S(2)}, u32[]{:S(2)}) async-start(bf16[8,48,128]{2,1,0:T(8,128)(2,1)} %get-tuple-element.21), calls=%async_computation.1 | async-start | bytes 196608 | tf_op jit(solution)/shard_map/all_to_all | solution.py:496
  8.2 23.4 %collective-permute-start = (bf16[304,128]{1,0:T(8,128)(2,1)S(1)}, bf16[304,128]{1,0:T(8,128)(2,1)S(1)}, u32[]{:S(2)}, u32[]{:S(2)}) collective-permute-start(bf16[304,128]{1,0:T(8,128)(2,1)S(1)} %get-tuple-element.18), channel_id=1, source_target_pairs={{4,8},{12,16},{20,24},{28,32},{36,40},{44,48},{52,56},{60,0},{8,4}... | collective-permute-start | bytes 233480 | tf_op jit(solution)/shard_map/ppermute | solution.py:494
  32.8 14.2 %all-to-all-start = ((bf16[32,16,128]{2,1,0:T(8,128)(2,1)}), bf16[32,16,128]{2,1,0:T(8,128)(2,1)S(1)}, u32[]{:S(2)}, u32[]{:S(2)}) async-start(bf16[32,16,128]{2,1,0:T(8,128)(2,1)} %shard_map.121), calls=%async_computation | async-start | bytes 262144 | tf_op jit(solution)/shard_map/all_to_all | solution.py:500
  39.3 3.2 %collective-permute-start.1 = (bf16[304,128]{1,0:T(8,128)(2,1)S(1)}, bf16[304,128]{1,0:T(8,128)(2,1)S(1)}, u32[]{:S(2)}, u32[]{:S(2)}) collective-permute-start(bf16[304,128]{1,0:T(8,128)(2,1)S(1)} %get-tuple-element.20), channel_id=1, source_target_pairs={{0,4},{4,0},{1,5},{5,1},{2,6},{6,2},{3,7},{7,3},{8,12},{12,8},{9,1... | collective-permute-start | bytes 233480 | tf_op jit(solution)/shard_map/ppermute | solution.py:495
  44.4 0.6 copy-start.3
  47.0 0.9 copy-start.4
  67.6 26.5 %all-to-all-start.3 = ((bf16[16,24,128]{2,1,0:T(8,128)(2,1)}), bf16[16,24,128]{2,1,0:T(8,128)(2,1)S(1)}, u32[]{:S(2)}, u32[]{:S(2)}) async-start(bf16[16,24,128]{2,1,0:T(8,128)(2,1)} %shard_map.125), calls=%async_computation.3 | async-start | bytes 196608 | tf_op jit(solution)/shard_map/all_to_all | solution.py:536

commit v8 on v7

--- a/solution.py
+++ b/solution.py
@@ -13,6 +13,7 @@
 LAT_LON = ("lat_0", "lat_1", "lat_2", "lon")
 LAT = ("lat_0", "lat_1", "lat_2")
 WIDE = 144
+CHUNK = 48
 PACK = 32
 PLANES = 5
 NEAR = 48
@@ -225,13 +226,13 @@
     shift = jnp.where(upper, 2, 0)
     for g in range(0, rows, group):
         for j, row in enumerate(convolved(ext_ref, rhs_ref, bias, g + shift, group)):
-            preact_ref[g + j] = row
+            preact_ref[g + j] = 0.5 * row
 
 
 def backward_kernel(
     at_ref, got_ref, kernel_ref, side_ref, preact_ref, early_ref,
     grad_hbm, sent_ref, ext_ref,
-    grad_ref, moved_ref, weight_ref, rhs_ref, sem,
+    grad_ref, moved_ref, weight_ref, rhs_ref, fixed_ref, sem,
 ):
     rows = grad_ref.shape[0] - 2
     n_x = 4
@@ -256,7 +257,8 @@
         ext_ref[crossed + r, 128:WIDE] = tiles[r].astype(jnp.bfloat16)
     fill(rhs_ref, kernel_ref)
     again = jnp.where(upper, 0, rows)
-    fixed = convolved(ext_ref, rhs_ref, params[0:1], again, 2)
+    for g, row in enumerate(convolved(ext_ref, rhs_ref, params[0:1], again, 2)):
+        fixed_ref[g] = 0.5 * row
     corner = [unpacked(second[0], second[1], k) for k in range(PLANES)]
     corner = (corner[0] + corner[1] + corner[2], corner[3] + corner[4])
     start, wet_depth = [
@@ -316,41 +318,50 @@
     mean = jnp.broadcast_to(sums[:, 0:1], (1, 128)) / jnp.broadcast_to(sums[:, 127:128], (1, 128))
     force = result.T
     force = force - mean * pltpu.roll(force, 64, 1)
-    proj = params[1:2]
+    proj = 0.5 * params[1:2]
     shift = jnp.where(upper, 2, 0)
     sum_bias = jnp.zeros((8, 128), jnp.float32)
     sum_proj = jnp.zeros((8, 128), jnp.float32)
     for g in range(rows + 2):
         at = g + 7
-        column = jnp.concatenate(
-            [
-                force[:, at : at + 1],
-                force[0:8, PACK + at : PACK + at + 1],
-                force[120:128, PACK + at : PACK + at + 1],
-            ],
+        edge = jnp.concatenate(
+            [force[0:8, PACK + at : PACK + at + 1], force[120:128, PACK + at : PACK + at + 1]],
             axis=0,
         )
-        column = jnp.broadcast_to(column, (WIDE, 128))
-        if g < 2:
-            preact = jnp.where(upper, fixed[g], preact_ref[g])
-        elif g >= rows:
-            preact = jnp.where(upper, preact_ref[g - 2], fixed[g - rows])
-        else:
-            preact = preact_ref[g - shift]
-        sigma = jax.nn.sigmoid(preact)
-        active = preact * sigma
-        slope_act = sigma * (1.0 + preact * (1.0 - sigma))
-        grad = (column * proj * slope_act).astype(jnp.bfloat16)
-        grad_ref[g] = grad
-        if 1 <= g <= rows:
-            own = grad.astype(jnp.float32)[0:128]
-            for k in range(16):
-                sum_bias = sum_bias + own[k * 8 : k * 8 + 8]
-                sum_proj = sum_proj + (active * column)[k * 8 : k * 8 + 8]
-            own = jnp.concatenate([own, jnp.zeros((WIDE - 128, 128), jnp.float32)], axis=0)
-            moved_ref[g - 1, :, 0:128] = pltpu.roll(own, WIDE - 1, 0).astype(jnp.bfloat16)
-            moved_ref[g - 1, :, 128:256] = own.astype(jnp.bfloat16)
-            moved_ref[g - 1, :, 256:384] = pltpu.roll(own, 1, 0).astype(jnp.bfloat16)
+        for q in range(0, WIDE, CHUNK):
+            parts = []
+            if q < 128:
+                parts.append(force[q : min(q + CHUNK, 128), at : at + 1])
+            if q + CHUNK > 128:
+                parts.append(edge)
+            column = parts[0] if len(parts) == 1 else jnp.concatenate(parts, axis=0)
+            column = jnp.broadcast_to(column, (CHUNK, 128))
+            if g < 2:
+                preact = jnp.where(upper, fixed_ref[g, q : q + CHUNK], preact_ref[g, q : q + CHUNK])
+            elif g >= rows:
+                preact = jnp.where(
+                    upper, preact_ref[g - 2, q : q + CHUNK], fixed_ref[g - rows, q : q + CHUNK]
+                )
+            else:
+                preact = preact_ref[g - shift, q : q + CHUNK]
+            turn = jnp.tanh(preact)
+            bent = preact * turn
+            active = preact + bent
+            slope_act = (1.0 + turn) * ((1.0 + preact) - bent)
+            grad = (column * proj * slope_act).astype(jnp.bfloat16)
+            grad_ref[g, q : q + CHUNK] = grad
+            if 1 <= g <= rows:
+                own = grad.astype(jnp.float32)
+                drawn = active * column
+                for k in range(min(CHUNK, 128 - q) // 8):
+                    sum_bias = sum_bias + own[k * 8 : k * 8 + 8]
+                    sum_proj = sum_proj + drawn[k * 8 : k * 8 + 8]
+    for g in range(1, rows + 1):
+        own = grad_ref[g, 0:128].astype(jnp.float32)
+        own = jnp.concatenate([own, jnp.zeros((WIDE - 128, 128), jnp.float32)], axis=0)
+        moved_ref[g - 1, :, 0:128] = pltpu.roll(own, WIDE - 1, 0).astype(jnp.bfloat16)
+        moved_ref[g - 1, :, 128:256] = own.astype(jnp.bfloat16)
+        moved_ref[g - 1, :, 256:384] = pltpu.roll(own, 1, 0).astype(jnp.bfloat16)
     copy = pltpu.make_async_copy(grad_ref, grad_hbm, sem)
     copy.start()
     to = lax.broadcasted_iota(jnp.int32, (128, 128), 0)
@@ -360,11 +371,14 @@
     )
     order = jnp.where(of == source, 1.0, 0.0).astype(jnp.bfloat16)
     moved = moved_ref[...].reshape(rows * WIDE, 384)
+    cells = jnp.concatenate(
+        [ext_ref[a + 1 : a + 1 + rows].reshape(rows * WIDE, 128) for a in range(3)], axis=1
+    )
+    whole = lax.dot_general(
+        cells, moved, (((0,), (0,)), ((), ())), preferred_element_type=jnp.float32
+    )
     for a in range(3):
-        cells = ext_ref[a + 1 : a + 1 + rows].reshape(rows * WIDE, 128)
-        out = lax.dot_general(
-            cells, moved, (((0,), (0,)), ((), ())), preferred_element_type=jnp.float32
-        )
+        out = whole[a * 128 : a * 128 + 128]
         out = jnp.dot(
             order, out.astype(jnp.bfloat16), preferred_element_type=jnp.float32
         )
@@ -524,6 +538,7 @@
             pltpu.VMEM((rows, WIDE, 384), narrow),
             pltpu.VMEM((9, 128, 128), wide),
             pltpu.VMEM((384, 384), narrow),
+            pltpu.VMEM((2, WIDE, 128), wide),
             pltpu.SemaphoreType.DMA,
         ],
         [SMEM] + [VMEM] * 5,

time: 95.3 us -> 95.1 us (level)
  no operation moved by 1% of the time
where the time goes in v8:
time: 95.1 us; the launch traced here: 94.6 us
  starting transfers between devices  43.5 us (46%)
  waiting for transfers between devices  20.1 us (21%)
  blocking collectives  14.9 us (16%)
  Pallas kernels  11.9 us (13%)
  local copies, waits for them, and re-layouts  2.67 us (3%)
    ppermute x1, starting transfers between devices, shards(): cross = lax.ppermute(cross, LAT, odd)  17.4 us
    all_to_all x1, blocking collectives, shards(): got = lax.all_to_all(sent, ('lat_0', 'lat_2', 'lon'), 0, 0, tiled=True)  14.9 us
    all_to_all x1, starting transfers between devices, shards(): got = lax.all_to_all(sent, ('lat_1', 'dp'), 0, 0, tiled=True)  13.2 us
    pallas_call x7, Pallas kernels, call(): pl.pallas_call(kernel, out_shape=shapes, in_specs=in_specs, out_specs=jax...  11.9 us
    all_to_all x1, waiting for transfers between devices, shards(): got = lax.all_to_all(sent, ('lat_1', 'dp'), 0, 0, tiled=True)  11.3 us
    all_to_all x1, starting transfers between devices, shards(): got = lax.all_to_all(sent, ('lat_0', 'lat_2', 'lon'), 0, 0, tiled=True)  6.48 us
    ppermute x1, waiting for transfers between devices, shards(): cross = lax.ppermute(cross, LAT, odd)  5.97 us
    all_to_all x1, starting transfers between devices, shards(): near = lax.all_to_all(near, ('lat_2', 'lon'), 0, 0, tiled=True)  4.3 us
  transfers between devices with their start and end apart: 5, of which 4 were waited for; matrix products, arithmetic and copies ran while one was open for 0% of the time, Pallas kernels for 6%

profile of v8, /device:TPU:32, one launch (start us, length us, event | category | flops | bytes accessed | tf_op | source)
XLA Modules:
  0.0 94.6 jit_solution(16089585937090730300)
XLA Ops:
  0.7 0.8 fusion
  1.5 0.1 stack.36.at_ref
  1.5 1.0 %copy-done.1 = bf16[1,16,128,128]{3,2,1,0:T(8,128)(2,1)S(1)} copy-done((bf16[1,16,128,128]{3,2,1,0:T(8,128)(2,1)S(1)}, bf16[1,16,128,128]{3,2,1,0:T(8,128)(2,1)}, u32[]{:S(2)}) %copy-start.1) | copy-done | bytes 524312
  2.6 0.0 copy-start.8
  2.6 1.3 %shard_map.120 = (bf16[304,128]{1,0:T(8,128)(2,1)S(1)}, bf16[304,128]{1,0:T(8,128)(2,1)S(1)}, bf16[8,48,128]{2,1,0:T(8,128)(2,1)}, f32[5,16,128]{2,1,0:T(8,128)S(1)}, f32[2,128]{1,0:T(2,128)S(1)}) custom-call(s32[6]{0:T(128)S(1)} %stack.36.at_ref, bf16[16,128,128]{2,1,0:T(8,128)(2,1)S(1)} %bitcast.21, f32[2,16,128]{2,1,0:T(8,128)S(1)} %pad_maximum_fusion.fields_ref), custom_call_target="tpu_custom_call" | custom-call | tf_op jit(solution)/shard_map/pallas_call | solution.py:460
  3.9 4.3 %all-to-all-start.1 = ((bf16[8,48,128]{2,1,0:T(8,128)(2,1)}), bf16[8,48,128]{2,1,0:T(8,128)(2,1)S(1)}, u32[]{:S(2)}, u32[]{:S(2)}) async-start(bf16[8,48,128]{2,1,0:T(8,128)(2,1)} %get-tuple-element.21), calls=%async_computation.1 | async-start | bytes 196608 | tf_op jit(solution)/shard_map/all_to_all | solution.py:510
  8.2 17.4 %collective-permute-start = (bf16[304,128]{1,0:T(8,128)(2,1)S(1)}, bf16[304,128]{1,0:T(8,128)(2,1)S(1)}, u32[]{:S(2)}, u32[]{:S(2)}) collective-permute-start(bf16[304,128]{1,0:T(8,128)(2,1)S(1)} %get-tuple-element.18), channel_id=1, source_target_pairs={{4,8},{12,16},{20,24},{28,32},{36,40},{44,48},{52,56},{60,0},{8,4}... | collective-permute-start | bytes 233480 | tf_op jit(solution)/shard_map/ppermute | solution.py:508
  25.6 6.0 %collective-permute-done.cross_ref = bf16[304,128]{1,0:T(8,128)(2,1)S(1)} collective-permute-done((bf16[304,128]{1,0:T(8,128)(2,1)S(1)}, bf16[304,128]{1,0:T(8,128)(2,1)S(1)}, u32[]{:S(2)}, u32[]{:S(2)}) %collective-permute-start) | collective-permute-done | bytes 77856 | tf_op jit(solution)/shard_map/ppermute | solution.py:508
  31.5 1.3 %shard_map.121 = bf16[32,16,128]{2,1,0:T(8,128)(2,1)} custom-call(s32[6]{0:T(128)S(1)} %stack.36.at_ref, f32[2,128]{1,0:T(2,128)S(1)} %get-tuple-element.17.sums_ref, bf16[304,128]{1,0:T(8,128)(2,1)S(1)} %collective-permute-done.cross_ref), custom_call_target="tpu_custom_call" | custom-call | tf_op jit(solution)/shard_map/pallas_call | solution.py:460
  32.8 0.0 all-to-all-done.1.near_ref
  32.8 6.5 %all-to-all-start = ((bf16[32,16,128]{2,1,0:T(8,128)(2,1)}), bf16[32,16,128]{2,1,0:T(8,128)(2,1)S(1)}, u32[]{:S(2)}, u32[]{:S(2)}) async-start(bf16[32,16,128]{2,1,0:T(8,128)(2,1)} %shard_map.121), calls=%async_computation | async-start | bytes 262144 | tf_op jit(solution)/shard_map/all_to_all | solution.py:514
  39.3 2.2 %collective-permute-start.1 = (bf16[304,128]{1,0:T(8,128)(2,1)S(1)}, bf16[304,128]{1,0:T(8,128)(2,1)S(1)}, u32[]{:S(2)}, u32[]{:S(2)}) collective-permute-start(bf16[304,128]{1,0:T(8,128)(2,1)S(1)} %get-tuple-element.20), channel_id=1, source_target_pairs={{0,4},{4,0},{1,5},{5,1},{2,6},{6,2},{3,7},{7,3},{8,12},{12,8},{9,1... | collective-permute-start | bytes 233480 | tf_op jit(solution)/shard_map/ppermute | solution.py:509
  41.5 1.0 %collective-permute-done.1.pair_ref = bf16[304,128]{1,0:T(8,128)(2,1)S(1)} collective-permute-done((bf16[304,128]{1,0:T(8,128)(2,1)S(1)}, bf16[304,128]{1,0:T(8,128)(2,1)S(1)}, u32[]{:S(2)}, u32[]{:S(2)}) %collective-permute-start.1) | collective-permute-done | bytes 77856 | tf_op jit(solution)/shard_map/ppermute | solution.py:509
  42.5 1.9 %shard_map.122 = (bf16[20,144,128]{2,1,0:T(8,128)(2,1)S(1)}, f32[16,144,128]{2,1,0:T(8,128)S(1)}, f32[144,128]{1,0:T(8,128)S(1)}) custom-call(s32[6]{0:T(128)S(1)} %stack.36.at_ref, bf16[16,128,128]{2,1,0:T(8,128)(2,1)S(1)} %bitcast.22, f32[5,16,128]{2,1,0:T(8,128)S(1)} %get-tuple-element.19.planes_ref, bf16[304,128]{1,0:T(8,128)(2,1)S(1)} %collective-permute-done.cross_ref, ...), custom_call_target="tpu_custom_call" | custom-call | tf_op jit(solution)/shard_map/pallas_call | solution.py:460
  44.4 0.6 copy-done.3
  45.1 1.9 %all-to-all-done.got_ref = bf16[32,16,128]{2,1,0:T(8,128)(2,1)S(1)} async-done(((bf16[32,16,128]{2,1,0:T(8,128)(2,1)}), bf16[32,16,128]{2,1,0:T(8,128)(2,1)S(1)}, u32[]{:S(2)}, u32[]{:S(2)}) %all-to-all-start) | async-done | bytes 131104 | tf_op jit(solution)/shard_map/all_to_all | solution.py:514
  47.0 0.9 copy-done.4
  47.9 4.0 %shard_map.123 = (bf16[18,144,128]{2,1,0:T(8,128)(2,1)S(1)}, bf16[32,40,128]{2,1,0:T(8,128)(2,1)S(1)}, bf16[20,144,128]{2,1,0:T(8,128)(2,1)S(1)}) custom-call(s32[6]{0:T(128)S(1)} %stack.36.at_ref, bf16[32,16,128]{2,1,0:T(8,128)(2,1)S(1)} %all-to-all-done.got_ref, bf16[3,3,128,128]{3,2,1,0:T(8,128)(2,1)S(1)} %copy-done, ...), custom_call_target="tpu_custom_call", output_to_operand_aliasing={{2}: (5, {})} | custom-call | tf_op jit(solution)/shard_map/pallas_call | solution.py:460
  51.8 14.9 %all_to_all.20.got_ref = bf16[32,40,128]{2,1,0:T(8,128)(2,1)S(1)} all-to-all(bf16[32,40,128]{2,1,0:T(8,128)(2,1)S(1)} %get-tuple-element.26), channel_id=1, replica_groups=mesh['dp'=8,'lat_0'=4,'lat_1'=2,'lat_2'=2,'lon'=4] {'lat_0','lat_2','lon'}, dimensions={0} | all-to-all | bytes 655360 | tf_op jit(solution)/shard_map/all_to_all | solution.py:549
  66.7 0.7 shard_map.125
  67.4 13.2 %all-to-all-start.3 = ((bf16[16,24,128]{2,1,0:T(8,128)(2,1)}), bf16[16,24,128]{2,1,0:T(8,128)(2,1)S(1)}, u32[]{:S(2)}, u32[]{:S(2)}) async-start(bf16[16,24,128]{2,1,0:T(8,128)(2,1)} %shard_map.125), calls=%async_computation.3 | async-start | bytes 196608 | tf_op jit(solution)/shard_map/all_to_all | solution.py:551
  80.6 2.1 %shard_map.124 = bf16[16,128,128]{2,1,0:T(8,128)(2,1)} custom-call(bf16[18,144,128]{2,1,0:T(8,128)(2,1)S(1)} %get-tuple-element.25.grad_ref, bf16[3,3,128,128]{3,2,1,0:T(8,128)(2,1)S(1)} %copy-done), custom_call_target="tpu_custom_call" | custom-call | tf_op jit(solution)/shard_map/pallas_call | solution.py:460
  82.7 11.3 %all-to-all-done.3.got_ref = bf16[16,24,128]{2,1,0:T(8,128)(2,1)S(1)} async-done(((bf16[16,24,128]{2,1,0:T(8,128)(2,1)}), bf16[16,24,128]{2,1,0:T(8,128)(2,1)S(1)}, u32[]{:S(2)}, u32[]{:S(2)}) %all-to-all-start.3) | async-done | bytes 98336 | tf_op jit(solution)/shard_map/all_to_all | solution.py:551
  93.9 0.6 shard_map.126
  (15 shorter events, 0.0 us)
Async XLA Ops:
  0.6 41.8 %copy-start = (bf16[3,3,128,128]{3,2,1,0:T(8,128)(2,1)S(1)}, bf16[3,3,128,128]{3,2,1,0:T(8,128)(2,1)}, u32[]{:S(2)}) copy-start(bf16[3,3,128,128]{3,2,1,0:T(8,128)(2,1)} %weight_ref.3) | copy-start | bytes 884740
  1.5 1.0 %copy-start.1 = (bf16[1,16,128,128]{3,2,1,0:T(8,128)(2,1)S(1)}, bf16[1,16,128,128]{3,2,1,0:T(8,128)(2,1)}, u32[]{:S(2)}) copy-start(bf16[1,16,128,128]{3,2,1,0:T(8,128)(2,1)} %param.9) | copy-start | bytes 1572868
  2.6 39.9 %copy-start.2 = (bf16[1,16,128,128]{3,2,1,0:T(8,128)(2,1)S(1)}, bf16[1,16,128,128]{3,2,1,0:T(8,128)(2,1)}, u32[]{:S(2)}) copy-start(bf16[1,16,128,128]{3,2,1,0:T(8,128)(2,1)} %param.9) | copy-start | bytes 1572868
  2.6 39.9 %copy-start.5 = (f32[128]{0:T(128)S(1)}, f32[128]{0:T(128)}, u32[]{:S(2)}) copy-start(f32[128]{0:T(128)} %param.11) | copy-start | bytes 1540
  2.6 39.9 %copy-start.6 = (f32[128]{0:T(128)S(1)}, f32[128]{0:T(128)}, u32[]{:S(2)}) copy-start(f32[128]{0:T(128)} %param.12) | copy-start | bytes 1540
  2.6 39.9 %copy-start.7 = (f32[6]{0:T(128)S(1)}, f32[6]{0:T(128)}, u32[]{:S(2)}) copy-start(f32[6]{0:T(128)} %alpha_ref.1) | copy-start | bytes 76
  2.6 39.9 %copy-start.8 = (f32[6]{0:T(128)S(1)}, f32[6]{0:T(128)}, u32[]{:S(2)}) copy-start(f32[6]{0:T(128)} %beta_ref.1) | copy-start | bytes 76
  3.9 28.9 %all-to-all-start.1 = ((bf16[8,48,128]{2,1,0:T(8,128)(2,1)}), bf16[8,48,128]{2,1,0:T(8,128)(2,1)S(1)}, u32[]{:S(2)}, u32[]{:S(2)}) async-start(bf16[8,48,128]{2,1,0:T(8,128)(2,1)} %get-tuple-element.21), calls=%async_computation.1 | async-start | bytes 196608 | tf_op jit(solution)/shard_map/all_to_all | solution.py:510
  8.2 23.4 %collective-permute-start = (bf16[304,128]{1,0:T(8,128)(2,1)S(1)}, bf16[304,128]{1,0:T(8,128)(2,1)S(1)}, u32[]{:S(2)}, u32[]{:S(2)}) collective-permute-start(bf16[304,128]{1,0:T(8,128)(2,1)S(1)} %get-tuple-element.18), channel_id=1, source_target_pairs={{4,8},{12,16},{20,24},{28,32},{36,40},{44,48},{52,56},{60,0},{8,4}... | collective-permute-start | bytes 233480 | tf_op jit(solution)/shard_map/ppermute | solution.py:508
  32.8 14.2 %all-to-all-start = ((bf16[32,16,128]{2,1,0:T(8,128)(2,1)}), bf16[32,16,128]{2,1,0:T(8,128)(2,1)S(1)}, u32[]{:S(2)}, u32[]{:S(2)}) async-start(bf16[32,16,128]{2,1,0:T(8,128)(2,1)} %shard_map.121), calls=%async_computation | async-start | bytes 262144 | tf_op jit(solution)/shard_map/all_to_all | solution.py:514
  39.3 3.2 %collective-permute-start.1 = (bf16[304,128]{1,0:T(8,128)(2,1)S(1)}, bf16[304,128]{1,0:T(8,128)(2,1)S(1)}, u32[]{:S(2)}, u32[]{:S(2)}) collective-permute-start(bf16[304,128]{1,0:T(8,128)(2,1)S(1)} %get-tuple-element.20), channel_id=1, source_target_pairs={{0,4},{4,0},{1,5},{5,1},{2,6},{6,2},{3,7},{7,3},{8,12},{12,8},{9,1... | collective-permute-start | bytes 233480 | tf_op jit(solution)/shard_map/ppermute | solution.py:509
  44.4 0.6 copy-start.3
  47.0 0.9 copy-start.4
  67.4 26.5 %all-to-all-start.3 = ((bf16[16,24,128]{2,1,0:T(8,128)(2,1)}), bf16[16,24,128]{2,1,0:T(8,128)(2,1)S(1)}, u32[]{:S(2)}, u32[]{:S(2)}) async-start(bf16[16,24,128]{2,1,0:T(8,128)(2,1)} %shard_map.125), calls=%async_computation.3 | async-start | bytes 196608 | tf_op jit(solution)/shard_map/all_to_all | solution.py:551

commit v9 on v8

--- a/solution.py
+++ b/solution.py
@@ -13,7 +13,7 @@
 LAT_LON = ("lat_0", "lat_1", "lat_2", "lon")
 LAT = ("lat_0", "lat_1", "lat_2")
 WIDE = 144
-CHUNK = 48
+SLIM = 136
 PACK = 32
 PLANES = 5
 NEAR = 48
@@ -159,6 +159,12 @@
             + bias
         )
     return rows
+
+
+def slimmed(row):
+    place = lax.broadcasted_iota(jnp.int32, (8, 128), 0)
+    edge = jnp.where(place < 4, row[128:136], row[136:144])
+    return jnp.concatenate([0.5 * row[0:128], 0.5 * edge], axis=0)
 
 
 def forward_kernel(
@@ -226,13 +232,13 @@
     shift = jnp.where(upper, 2, 0)
     for g in range(0, rows, group):
         for j, row in enumerate(convolved(ext_ref, rhs_ref, bias, g + shift, group)):
-            preact_ref[g + j] = 0.5 * row
+            preact_ref[g + j] = slimmed(row)
 
 
 def backward_kernel(
     at_ref, got_ref, kernel_ref, side_ref, preact_ref, early_ref,
-    grad_hbm, sent_ref, ext_ref,
-    grad_ref, moved_ref, weight_ref, rhs_ref, fixed_ref, sem,
+    grad_ref, sent_ref, ext_ref,
+    moved_ref, weight_ref, rhs_ref, fixed_ref,
 ):
     rows = grad_ref.shape[0] - 2
     n_x = 4
@@ -258,7 +264,7 @@
     fill(rhs_ref, kernel_ref)
     again = jnp.where(upper, 0, rows)
     for g, row in enumerate(convolved(ext_ref, rhs_ref, params[0:1], again, 2)):
-        fixed_ref[g] = 0.5 * row
+        fixed_ref[g] = slimmed(row)
     corner = [unpacked(second[0], second[1], k) for k in range(PLANES)]
     corner = (corner[0] + corner[1] + corner[2], corner[3] + corner[4])
     start, wet_depth = [
@@ -320,40 +326,41 @@
     force = force - mean * pltpu.roll(force, 64, 1)
     proj = 0.5 * params[1:2]
     shift = jnp.where(upper, 2, 0)
+    sublane = lax.broadcasted_iota(jnp.int32, (8, 1), 0)
     sum_bias = jnp.zeros((8, 128), jnp.float32)
     sum_proj = jnp.zeros((8, 128), jnp.float32)
     for g in range(rows + 2):
         at = g + 7
-        edge = jnp.concatenate(
-            [force[0:8, PACK + at : PACK + at + 1], force[120:128, PACK + at : PACK + at + 1]],
-            axis=0,
-        )
-        for q in range(0, WIDE, CHUNK):
-            parts = []
-            if q < 128:
-                parts.append(force[q : min(q + CHUNK, 128), at : at + 1])
-            if q + CHUNK > 128:
-                parts.append(edge)
-            column = parts[0] if len(parts) == 1 else jnp.concatenate(parts, axis=0)
-            column = jnp.broadcast_to(column, (CHUNK, 128))
+        edge = jnp.where(
+            sublane < 4,
+            force[0:8, PACK + at : PACK + at + 1],
+            force[120:128, PACK + at : PACK + at + 1],
+        )
+        for q, size in ((0, 48), (48, 48), (96, 32), (128, 8)):
+            column = edge if q == 128 else force[q : q + size, at : at + 1]
+            column = jnp.broadcast_to(column, (size, 128))
             if g < 2:
-                preact = jnp.where(upper, fixed_ref[g, q : q + CHUNK], preact_ref[g, q : q + CHUNK])
+                preact = jnp.where(upper, fixed_ref[g, q : q + size], preact_ref[g, q : q + size])
             elif g >= rows:
                 preact = jnp.where(
-                    upper, preact_ref[g - 2, q : q + CHUNK], fixed_ref[g - rows, q : q + CHUNK]
+                    upper, preact_ref[g - 2, q : q + size], fixed_ref[g - rows, q : q + size]
                 )
             else:
-                preact = preact_ref[g - shift, q : q + CHUNK]
+                preact = preact_ref[g - shift, q : q + size]
             turn = jnp.tanh(preact)
             bent = preact * turn
             active = preact + bent
             slope_act = (1.0 + turn) * ((1.0 + preact) - bent)
-            grad = (column * proj * slope_act).astype(jnp.bfloat16)
-            grad_ref[g, q : q + CHUNK] = grad
+            grad = column * proj * slope_act
+            if q == 128:
+                grad_ref[g, 128:WIDE] = jnp.concatenate([grad, grad], axis=0).astype(jnp.bfloat16)
+                continue
+            grad = grad.astype(jnp.bfloat16)
+            grad_ref[g, q : q + size] = grad
             if 1 <= g <= rows:
                 own = grad.astype(jnp.float32)
                 drawn = active * column
-                for k in range(min(CHUNK, 128 - q) // 8):
+                for k in range(size // 8):
                     sum_bias = sum_bias + own[k * 8 : k * 8 + 8]
                     sum_proj = sum_proj + drawn[k * 8 : k * 8 + 8]
     for g in range(1, rows + 1):
@@ -362,8 +369,6 @@
         moved_ref[g - 1, :, 0:128] = pltpu.roll(own, WIDE - 1, 0).astype(jnp.bfloat16)
         moved_ref[g - 1, :, 128:256] = own.astype(jnp.bfloat16)
         moved_ref[g - 1, :, 256:384] = pltpu.roll(own, 1, 0).astype(jnp.bfloat16)
-    copy = pltpu.make_async_copy(grad_ref, grad_hbm, sem)
-    copy.start()
     to = lax.broadcasted_iota(jnp.int32, (128, 128), 0)
     of = lax.broadcasted_iota(jnp.int32, (128, 128), 1)
     source = (
@@ -391,21 +396,17 @@
     vectors = pltpu.roll(vectors, 4, 0)
     low = lax.broadcasted_iota(jnp.int32, (8, 128), 0) < 4
 
-    def one_pair(t, carry):
-        start = pl.multiple_of(t * 8, 8)
+    for t in range(16):
+        start = t * 8
         blocks = ([], [])
         for k in range(0, 9, 2):
-            one = weight_ref[k, pl.ds(start, 8)]
-            two = weight_ref[k + 1, pl.ds(start, 8)] if k < 8 else vectors
+            one = weight_ref[k, start : start + 8]
+            two = weight_ref[k + 1, start : start + 8] if k < 8 else vectors
             two_low = pltpu.roll(two, 4, 0) if k < 8 else vectors
             blocks[0].append(jnp.where(low, one, two_low))
             blocks[1].append(jnp.where(low, pltpu.roll(one, 4, 0), two))
         for x in range(2):
             sent_ref[t * 2 + x] = jnp.concatenate(blocks[x], axis=0).astype(jnp.bfloat16)
-        return carry
-
-    lax.fori_loop(0, 16, one_pair, 0)
-    copy.wait()
 
 
 def middle_kernel(got_ref, sent_ref):
@@ -516,7 +517,7 @@
         forward_kernel,
         (
             shape((rows + 4, WIDE, 128), narrow),
-            shape((rows, WIDE, 128), wide),
+            shape((rows, SLIM, 128), wide),
             shape((4 * PACK + 16, 128), wide),
         ),
         [pltpu.VMEM((384, 384), narrow)],
@@ -534,16 +535,14 @@
             shape((rows + 4, WIDE, 128), narrow),
         ),
         [
-            pltpu.VMEM((rows + 2, WIDE, 128), narrow),
             pltpu.VMEM((rows, WIDE, 384), narrow),
             pltpu.VMEM((9, 128, 128), wide),
             pltpu.VMEM((384, 384), narrow),
-            pltpu.VMEM((2, WIDE, 128), wide),
-            pltpu.SemaphoreType.DMA,
+            pltpu.VMEM((2, SLIM, 128), wide),
         ],
         [SMEM] + [VMEM] * 5,
         (at, got, conv_weight, side, preact, early),
-        (HBM, VMEM, VMEM),
+        None,
         {5: 2},
     )
     got = lax.all_to_all(sent, ("lat_0", "lat_2", "lon"), 0, 0, tiled=True)

time: 95.1 us -> 92.5 us (0.973)
  local copies, waits for them, and re-layouts: 2.67 us -> 1.15 us
  Pallas kernels: 11.9 us -> 10.8 us
    unnamed x18 -> x14, local copies, waits for them, and re-layouts: 2.59 us -> 1.07 us
    pallas_call x7, Pallas kernels: 11.9 us -> 10.8 us  [call(): pl.pallas_call(kernel, out_shape=shapes, in_specs=in_specs, out_specs=jax...]
where the time goes in v9:
time: 92.5 us; the launch traced here: 91.9 us
  starting transfers between devices  43.5 us (47%)
  waiting for transfers between devices  20.7 us (22%)
  blocking collectives  14.2 us (15%)
  Pallas kernels  10.8 us (12%)
  local copies, waits for them, and re-layouts  1.15 us (1%)
    ppermute x1, starting transfers between devices, shards(): cross = lax.ppermute(cross, LAT, odd)  17.4 us
    all_to_all x1, blocking collectives, shards(): got = lax.all_to_all(sent, ('lat_0', 'lat_2', 'lon'), 0, 0, tiled=True)  14.2 us
    all_to_all x1, starting transfers between devices, shards(): got = lax.all_to_all(sent, ('lat_1', 'dp'), 0, 0, tiled=True)  13.2 us
    all_to_all x1, waiting for transfers between devices, shards(): got = lax.all_to_all(sent, ('lat_1', 'dp'), 0, 0, tiled=True)  11.3 us
    pallas_call x7, Pallas kernels, call(): pl.pallas_call(kernel, out_shape=shapes, in_specs=in_specs, out_specs=jax...  10.8 us
    all_to_all x1, starting transfers between devices, shards(): got = lax.all_to_all(sent, ('lat_0', 'lat_2', 'lon'), 0, 0, tiled=True)  6.48 us
    ppermute x1, waiting for transfers between devices, shards(): cross = lax.ppermute(cross, LAT, odd)  5.97 us
    all_to_all x1, starting transfers between devices, shards(): near = lax.all_to_all(near, ('lat_2', 'lon'), 0, 0, tiled=True)  4.3 us
  transfers between devices with their start and end apart: 5, of which 4 were waited for; matrix products, arithmetic and copies ran while one was open for 0% of the time, Pallas kernels for 6%

profile of v9, /device:TPU:32, one launch (start us, length us, event | category | flops | bytes accessed | tf_op | source)
XLA Modules:
  0.0 91.9 jit_solution(5633764815275717147)
XLA Ops:
  0.6 0.0 copy-start
  0.7 0.8 fusion
  1.5 0.1 stack.36.at_ref
  1.5 1.0 %copy-done.1 = bf16[1,16,128,128]{3,2,1,0:T(8,128)(2,1)S(1)} copy-done((bf16[1,16,128,128]{3,2,1,0:T(8,128)(2,1)S(1)}, bf16[1,16,128,128]{3,2,1,0:T(8,128)(2,1)}, u32[]{:S(2)}) %copy-start.1) | copy-done | bytes 524312
  2.6 0.0 copy-start.6
  2.6 1.3 %shard_map.120 = (bf16[304,128]{1,0:T(8,128)(2,1)S(1)}, bf16[304,128]{1,0:T(8,128)(2,1)S(1)}, bf16[8,48,128]{2,1,0:T(8,128)(2,1)}, f32[5,16,128]{2,1,0:T(8,128)S(1)}, f32[2,128]{1,0:T(2,128)S(1)}) custom-call(s32[6]{0:T(128)S(1)} %stack.36.at_ref, bf16[16,128,128]{2,1,0:T(8,128)(2,1)S(1)} %bitcast.21, f32[2,16,128]{2,1,0:T(8,128)S(1)} %pad_maximum_fusion.fields_ref), custom_call_target="tpu_custom_call" | custom-call | tf_op jit(solution)/shard_map/pallas_call | solution.py:461
  3.9 4.3 %all-to-all-start.1 = ((bf16[8,48,128]{2,1,0:T(8,128)(2,1)}), bf16[8,48,128]{2,1,0:T(8,128)(2,1)S(1)}, u32[]{:S(2)}, u32[]{:S(2)}) async-start(bf16[8,48,128]{2,1,0:T(8,128)(2,1)} %get-tuple-element.21), calls=%async_computation.1 | async-start | bytes 196608 | tf_op jit(solution)/shard_map/all_to_all | solution.py:511
  8.2 17.4 %collective-permute-start = (bf16[304,128]{1,0:T(8,128)(2,1)S(1)}, bf16[304,128]{1,0:T(8,128)(2,1)S(1)}, u32[]{:S(2)}, u32[]{:S(2)}) collective-permute-start(bf16[304,128]{1,0:T(8,128)(2,1)S(1)} %get-tuple-element.18), channel_id=1, source_target_pairs={{4,8},{12,16},{20,24},{28,32},{36,40},{44,48},{52,56},{60,0},{8,4}... | collective-permute-start | bytes 233480 | tf_op jit(solution)/shard_map/ppermute | solution.py:509
  25.6 6.0 %collective-permute-done.cross_ref = bf16[304,128]{1,0:T(8,128)(2,1)S(1)} collective-permute-done((bf16[304,128]{1,0:T(8,128)(2,1)S(1)}, bf16[304,128]{1,0:T(8,128)(2,1)S(1)}, u32[]{:S(2)}, u32[]{:S(2)}) %collective-permute-start) | collective-permute-done | bytes 77856 | tf_op jit(solution)/shard_map/ppermute | solution.py:509
  31.5 1.3 %shard_map.121 = bf16[32,16,128]{2,1,0:T(8,128)(2,1)} custom-call(s32[6]{0:T(128)S(1)} %stack.36.at_ref, f32[2,128]{1,0:T(2,128)S(1)} %get-tuple-element.17.sums_ref, bf16[304,128]{1,0:T(8,128)(2,1)S(1)} %collective-permute-done.cross_ref), custom_call_target="tpu_custom_call" | custom-call | tf_op jit(solution)/shard_map/pallas_call | solution.py:461
  32.8 0.0 all-to-all-done.1.near_ref
  32.8 6.5 %all-to-all-start = ((bf16[32,16,128]{2,1,0:T(8,128)(2,1)}), bf16[32,16,128]{2,1,0:T(8,128)(2,1)S(1)}, u32[]{:S(2)}, u32[]{:S(2)}) async-start(bf16[32,16,128]{2,1,0:T(8,128)(2,1)} %shard_map.121), calls=%async_computation | async-start | bytes 262144 | tf_op jit(solution)/shard_map/all_to_all | solution.py:515
  39.3 2.2 %collective-permute-start.1 = (bf16[304,128]{1,0:T(8,128)(2,1)S(1)}, bf16[304,128]{1,0:T(8,128)(2,1)S(1)}, u32[]{:S(2)}, u32[]{:S(2)}) collective-permute-start(bf16[304,128]{1,0:T(8,128)(2,1)S(1)} %get-tuple-element.20), channel_id=1, source_target_pairs={{0,4},{4,0},{1,5},{5,1},{2,6},{6,2},{3,7},{7,3},{8,12},{12,8},{9,1... | collective-permute-start | bytes 233480 | tf_op jit(solution)/shard_map/ppermute | solution.py:510
  41.5 1.0 %collective-permute-done.1.pair_ref = bf16[304,128]{1,0:T(8,128)(2,1)S(1)} collective-permute-done((bf16[304,128]{1,0:T(8,128)(2,1)S(1)}, bf16[304,128]{1,0:T(8,128)(2,1)S(1)}, u32[]{:S(2)}, u32[]{:S(2)}) %collective-permute-start.1) | collective-permute-done | bytes 77856 | tf_op jit(solution)/shard_map/ppermute | solution.py:510
  42.5 0.0 copy-done.2
  42.5 1.9 %shard_map.122 = (bf16[20,144,128]{2,1,0:T(8,128)(2,1)S(1)}, f32[16,136,128]{2,1,0:T(8,128)S(1)}, f32[144,128]{1,0:T(8,128)S(1)}) custom-call(s32[6]{0:T(128)S(1)} %stack.36.at_ref, bf16[16,128,128]{2,1,0:T(8,128)(2,1)S(1)} %bitcast.22, f32[5,16,128]{2,1,0:T(8,128)S(1)} %get-tuple-element.19.planes_ref, bf16[304,128]{1,0:T(8,128)(2,1)S(1)} %collective-permute-done.cross_ref, ...), custom_call_target="tpu_custom_call" | custom-call | tf_op jit(solution)/shard_map/pallas_call | solution.py:461
  44.4 2.5 %all-to-all-done.got_ref = bf16[32,16,128]{2,1,0:T(8,128)(2,1)S(1)} async-done(((bf16[32,16,128]{2,1,0:T(8,128)(2,1)}), bf16[32,16,128]{2,1,0:T(8,128)(2,1)S(1)}, u32[]{:S(2)}, u32[]{:S(2)}) %all-to-all-start) | async-done | bytes 131104 | tf_op jit(solution)/shard_map/all_to_all | solution.py:515
  47.0 2.9 %shard_map.123 = (bf16[18,144,128]{2,1,0:T(8,128)(2,1)S(1)}, bf16[32,40,128]{2,1,0:T(8,128)(2,1)S(1)}, bf16[20,144,128]{2,1,0:T(8,128)(2,1)S(1)}) custom-call(s32[6]{0:T(128)S(1)} %stack.36.at_ref, bf16[32,16,128]{2,1,0:T(8,128)(2,1)S(1)} %all-to-all-done.got_ref, bf16[3,3,128,128]{3,2,1,0:T(8,128)(2,1)S(1)} %copy-done, ...), custom_call_target="tpu_custom_call", output_to_operand_aliasing={{2}: (5, {})} | custom-call | tf_op jit(solution)/shard_map/pallas_call | solution.py:461
  49.9 14.2 %all_to_all.20.got_ref = bf16[32,40,128]{2,1,0:T(8,128)(2,1)S(1)} all-to-all(bf16[32,40,128]{2,1,0:T(8,128)(2,1)S(1)} %get-tuple-element.26), channel_id=1, replica_groups=mesh['dp'=8,'lat_0'=4,'lat_1'=2,'lat_2'=2,'lon'=4] {'lat_0','lat_2','lon'}, dimensions={0} | all-to-all | bytes 655360 | tf_op jit(solution)/shard_map/all_to_all | solution.py:548
  64.1 0.7 shard_map.125
  64.8 13.2 %all-to-all-start.3 = ((bf16[16,24,128]{2,1,0:T(8,128)(2,1)}), bf16[16,24,128]{2,1,0:T(8,128)(2,1)S(1)}, u32[]{:S(2)}, u32[]{:S(2)}) async-start(bf16[16,24,128]{2,1,0:T(8,128)(2,1)} %shard_map.125), calls=%async_computation.3 | async-start | bytes 196608 | tf_op jit(solution)/shard_map/all_to_all | solution.py:550
  78.0 2.1 %shard_map.124 = bf16[16,128,128]{2,1,0:T(8,128)(2,1)} custom-call(bf16[18,144,128]{2,1,0:T(8,128)(2,1)S(1)} %get-tuple-element.25.grad_ref, bf16[3,3,128,128]{3,2,1,0:T(8,128)(2,1)S(1)} %copy-done), custom_call_target="tpu_custom_call" | custom-call | tf_op jit(solution)/shard_map/pallas_call | solution.py:461
  80.1 11.3 %all-to-all-done.3.got_ref = bf16[16,24,128]{2,1,0:T(8,128)(2,1)S(1)} async-done(((bf16[16,24,128]{2,1,0:T(8,128)(2,1)}), bf16[16,24,128]{2,1,0:T(8,128)(2,1)S(1)}, u32[]{:S(2)}, u32[]{:S(2)}) %all-to-all-start.3) | async-done | bytes 98336 | tf_op jit(solution)/shard_map/all_to_all | solution.py:550
  91.3 0.6 shard_map.126
  (11 shorter events, 0.0 us)
Async XLA Ops:
  0.6 41.8 %copy-start = (bf16[3,3,128,128]{3,2,1,0:T(8,128)(2,1)S(1)}, bf16[3,3,128,128]{3,2,1,0:T(8,128)(2,1)}, u32[]{:S(2)}) copy-start(bf16[3,3,128,128]{3,2,1,0:T(8,128)(2,1)} %weight_ref.3) | copy-start | bytes 884740
  1.5 1.0 %copy-start.1 = (bf16[1,16,128,128]{3,2,1,0:T(8,128)(2,1)S(1)}, bf16[1,16,128,128]{3,2,1,0:T(8,128)(2,1)}, u32[]{:S(2)}) copy-start(bf16[1,16,128,128]{3,2,1,0:T(8,128)(2,1)} %param.9) | copy-start | bytes 1572868
  2.6 39.9 %copy-start.2 = (bf16[1,16,128,128]{3,2,1,0:T(8,128)(2,1)S(1)}, bf16[1,16,128,128]{3,2,1,0:T(8,128)(2,1)}, u32[]{:S(2)}) copy-start(bf16[1,16,128,128]{3,2,1,0:T(8,128)(2,1)} %param.9) | copy-start | bytes 1572868
  2.6 39.9 %copy-start.3 = (f32[128]{0:T(128)S(1)}, f32[128]{0:T(128)}, u32[]{:S(2)}) copy-start(f32[128]{0:T(128)} %param.11) | copy-start | bytes 1540
  2.6 39.9 %copy-start.4 = (f32[128]{0:T(128)S(1)}, f32[128]{0:T(128)}, u32[]{:S(2)}) copy-start(f32[128]{0:T(128)} %param.12) | copy-start | bytes 1540
  2.6 39.9 %copy-start.5 = (f32[6]{0:T(128)S(1)}, f32[6]{0:T(128)}, u32[]{:S(2)}) copy-start(f32[6]{0:T(128)} %alpha_ref.1) | copy-start | bytes 76
  2.6 39.9 %copy-start.6 = (f32[6]{0:T(128)S(1)}, f32[6]{0:T(128)}, u32[]{:S(2)}) copy-start(f32[6]{0:T(128)} %beta_ref.1) | copy-start | bytes 76
  3.9 28.9 %all-to-all-start.1 = ((bf16[8,48,128]{2,1,0:T(8,128)(2,1)}), bf16[8,48,128]{2,1,0:T(8,128)(2,1)S(1)}, u32[]{:S(2)}, u32[]{:S(2)}) async-start(bf16[8,48,128]{2,1,0:T(8,128)(2,1)} %get-tuple-element.21), calls=%async_computation.1 | async-start | bytes 196608 | tf_op jit(solution)/shard_map/all_to_all | solution.py:511
  8.2 23.4 %collective-permute-start = (bf16[304,128]{1,0:T(8,128)(2,1)S(1)}, bf16[304,128]{1,0:T(8,128)(2,1)S(1)}, u32[]{:S(2)}, u32[]{:S(2)}) collective-permute-start(bf16[304,128]{1,0:T(8,128)(2,1)S(1)} %get-tuple-element.18), channel_id=1, source_target_pairs={{4,8},{12,16},{20,24},{28,32},{36,40},{44,48},{52,56},{60,0},{8,4}... | collective-permute-start | bytes 233480 | tf_op jit(solution)/shard_map/ppermute | solution.py:509
  32.8 14.2 %all-to-all-start = ((bf16[32,16,128]{2,1,0:T(8,128)(2,1)}), bf16[32,16,128]{2,1,0:T(8,128)(2,1)S(1)}, u32[]{:S(2)}, u32[]{:S(2)}) async-start(bf16[32,16,128]{2,1,0:T(8,128)(2,1)} %shard_map.121), calls=%async_computation | async-start | bytes 262144 | tf_op jit(solution)/shard_map/all_to_all | solution.py:515
  39.3 3.2 %collective-permute-start.1 = (bf16[304,128]{1,0:T(8,128)(2,1)S(1)}, bf16[304,128]{1,0:T(8,128)(2,1)S(1)}, u32[]{:S(2)}, u32[]{:S(2)}) collective-permute-start(bf16[304,128]{1,0:T(8,128)(2,1)S(1)} %get-tuple-element.20), channel_id=1, source_target_pairs={{0,4},{4,0},{1,5},{5,1},{2,6},{6,2},{3,7},{7,3},{8,12},{12,8},{9,1... | collective-permute-start | bytes 233480 | tf_op jit(solution)/shard_map/ppermute | solution.py:510
  64.8 26.5 %all-to-all-start.3 = ((bf16[16,24,128]{2,1,0:T(8,128)(2,1)}), bf16[16,24,128]{2,1,0:T(8,128)(2,1)S(1)}, u32[]{:S(2)}, u32[]{:S(2)}) async-start(bf16[16,24,128]{2,1,0:T(8,128)(2,1)} %shard_map.125), calls=%async_computation.3 | async-start | bytes 196608 | tf_op jit(solution)/shard_map/all_to_all | solution.py:550

commit v10 on v9

--- a/solution.py
+++ b/solution.py
@@ -70,10 +70,12 @@
     return jnp.where(near < 8, beyond, jnp.where(near >= 120, before, 0.0))
 
 
-def first_kernel(
-    at_ref, hidden_ref, fields_ref, cross_ref, pair_ref, near_ref, planes_ref, sums_ref
-):
-    rows = hidden_ref.shape[0]
+def near_rows(planes, top):
+    rows = planes[0].shape[0]
+    return [jnp.where(top, p[0:8], p[rows - 8 : rows]) for p in planes]
+
+
+def first_kernel(at_ref, hidden_ref, fields_ref, cross_ref, planes_ref, sums_ref):
     upper = at_ref[0] == 0
     wet, wet_depth = fields_ref[0], fields_ref[1]
     planes = pieces_of(wet, 3) + pieces_of(wet_depth, 2)
@@ -85,13 +87,23 @@
     sums = jnp.concatenate(sums + [jnp.zeros((2, 128), jnp.float32)], axis=0)
     for k in range(PLANES):
         planes_ref[k] = planes[k]
-    for ref, top in ((cross_ref, upper), (pair_ref, jnp.logical_not(upper))):
-        start = jnp.where(top, 0, rows - 2)
-        ref[0:256] = hidden_ref[pl.ds(start, 2)].reshape(256, 128)
-        near = [jnp.where(top, p[0:8], p[rows - 8 : rows]) for p in planes] + [sums]
-        for k in range(0, 6, 2):
-            tile = jnp.concatenate(near[k : k + 2], axis=0)
-            ref[256 + k * 8 : 272 + k * 8] = tile.astype(jnp.bfloat16)
+    cross_ref[0:256] = hidden_ref[...].reshape(256, 128)
+    near = near_rows(planes, upper) + [sums]
+    for k in range(0, 6, 2):
+        tile = jnp.concatenate(near[k : k + 2], axis=0)
+        cross_ref[256 + k * 8 : 272 + k * 8] = tile.astype(jnp.bfloat16)
+
+
+def edges_kernel(at_ref, hidden_ref, planes_ref, pair_ref, near_ref):
+    rows = hidden_ref.shape[0]
+    upper = at_ref[0] == 0
+    planes = [planes_ref[k] for k in range(PLANES)]
+    start = jnp.where(upper, rows - 2, 0)
+    pair_ref[0:256] = hidden_ref[pl.ds(start, 2)].reshape(256, 128)
+    near = near_rows(planes + planes[:1], jnp.logical_not(upper))
+    for k in range(0, 6, 2):
+        tile = jnp.concatenate(near[k : k + 2], axis=0)
+        pair_ref[256 + k * 8 : 272 + k * 8] = tile.astype(jnp.bfloat16)
     columns = edge_columns(lambda r, at: hidden_ref[r, at : at + 16], rows)
     head = jnp.concatenate(columns[0] + columns[1] + [packed(planes, 0)], axis=0)
     tail = jnp.concatenate(columns[2] + columns[3] + [packed(planes, 8)], axis=0)
@@ -491,22 +503,30 @@
     ).astype(jnp.int32)
     mask = sea_mask.astype(wide)
     fields = jnp.stack([mask * surface_cotangent[0], mask * ocean_depth])
-    cross, pair, near, planes, sums = call(
+    facing = lax.dynamic_slice_in_dim(
+        hidden, jnp.where(lax.axis_index("lat_2") == 0, 0, rows - 2), 2, axis=0
+    )
+    cross, planes, sums = call(
         first_kernel,
         (
             shape((304, 128), narrow),
-            shape((304, 128), narrow),
-            shape((2 * n_x, NEAR, 128), narrow),
             shape((PLANES, rows, 128), wide),
             shape((2, 128), wide),
         ),
         [],
         [SMEM] + [VMEM] * 2,
-        (at, hidden, fields),
+        (at, facing, fields),
     )
     odd = [(i, (i + 1) % n_lat) for i in range(1, n_lat, 2)]
     odd = odd + [(j, i) for i, j in odd]
     cross = lax.ppermute(cross, LAT, odd)
+    pair, near = call(
+        edges_kernel,
+        (shape((304, 128), narrow), shape((2 * n_x, NEAR, 128), narrow)),
+        [],
+        [SMEM] + [VMEM] * 2,
+        (at, hidden, planes),
+    )
     pair = lax.ppermute(pair, "lat_2", [(0, 1), (1, 0)])
     near = lax.all_to_all(near, ("lat_2", "lon"), 0, 0, tiled=True)
     sent = call(

time: 92.5 us -> 94 us (1.016)
    pallas_call x7 -> x8, Pallas kernels: 10.8 us -> 11.4 us  [call(): pl.pallas_call(kernel, out_shape=shapes, in_specs=in_specs, out_specs=jax...]
where the time goes in v10:
time: 94 us; the launch traced here: 93.5 us
  starting transfers between devices  43.5 us (46%)
  waiting for transfers between devices  20.7 us (22%)
  blocking collectives  14.2 us (15%)
  Pallas kernels  11.4 us (12%)
  local copies, waits for them, and re-layouts  1.99 us (2%)
    ppermute x1, starting transfers between devices, shards(): cross = lax.ppermute(cross, LAT, odd)  17.4 us
    all_to_all x1, blocking collectives, shards(): got = lax.all_to_all(sent, ('lat_0', 'lat_2', 'lon'), 0, 0, tiled=True)  14.2 us
    all_to_all x1, starting transfers between devices, shards(): got = lax.all_to_all(sent, ('lat_1', 'dp'), 0, 0, tiled=True)  13.2 us
    pallas_call x8, Pallas kernels, call(): pl.pallas_call(kernel, out_shape=shapes, in_specs=in_specs, out_specs=jax...  11.4 us
    all_to_all x1, waiting for transfers between devices, shards(): got = lax.all_to_all(sent, ('lat_1', 'dp'), 0, 0, tiled=True)  11.3 us
    all_to_all x1, starting transfers between devices, shards(): got = lax.all_to_all(sent, ('lat_0', 'lat_2', 'lon'), 0, 0, tiled=True)  6.48 us
    ppermute x1, waiting for transfers between devices, shards(): cross = lax.ppermute(cross, LAT, odd)  5.97 us
    all_to_all x1, starting transfers between devices, shards(): near = lax.all_to_all(near, ('lat_2', 'lon'), 0, 0, tiled=True)  4.3 us
  transfers between devices with their start and end apart: 5, of which 4 were waited for; matrix products, arithmetic and copies ran while one was open for 0% of the time, Pallas kernels for 6%

profile of v10, /device:TPU:32, one launch (start us, length us, event | category | flops | bytes accessed | tf_op | source)
XLA Modules:
  0.0 93.5 jit_solution(3671018793008948743)
XLA Ops:
  0.7 0.8 fusion
  1.5 0.8 dynamic-slice_bitcast_fusion.hidden_ref
  2.4 0.1 stack.36.at_ref
  2.5 0.7 shard_map.120
  3.1 0.0 copy-start.1
  3.1 1.0 %copy-done.1 = bf16[1,16,128,128]{3,2,1,0:T(8,128)(2,1)S(1)} copy-done((bf16[1,16,128,128]{3,2,1,0:T(8,128)(2,1)S(1)}, bf16[1,16,128,128]{3,2,1,0:T(8,128)(2,1)}, u32[]{:S(2)}) %copy-start.1) | copy-done | bytes 524312
  4.2 1.3 %shard_map.122 = (bf16[304,128]{1,0:T(8,128)(2,1)S(1)}, bf16[8,48,128]{2,1,0:T(8,128)(2,1)}) custom-call(s32[6]{0:T(128)S(1)} %stack.36.at_ref, bf16[16,128,128]{2,1,0:T(8,128)(2,1)S(1)} %bitcast.23, f32[5,16,128]{2,1,0:T(8,128)S(1)} %get-tuple-element.19.planes_ref), custom_call_target="tpu_custom_call" | custom-call | tf_op jit(solution)/shard_map/pallas_call | solution.py:473
  5.4 4.3 %all-to-all-start.1 = ((bf16[8,48,128]{2,1,0:T(8,128)(2,1)}), bf16[8,48,128]{2,1,0:T(8,128)(2,1)S(1)}, u32[]{:S(2)}, u32[]{:S(2)}) async-start(bf16[8,48,128]{2,1,0:T(8,128)(2,1)} %get-tuple-element.21), calls=%async_computation.1 | async-start | bytes 196608 | tf_op jit(solution)/shard_map/all_to_all | solution.py:531
  9.7 17.4 %collective-permute-start = (bf16[304,128]{1,0:T(8,128)(2,1)S(1)}, bf16[304,128]{1,0:T(8,128)(2,1)S(1)}, u32[]{:S(2)}, u32[]{:S(2)}) collective-permute-start(bf16[304,128]{1,0:T(8,128)(2,1)S(1)} %get-tuple-element.18), channel_id=1, source_target_pairs={{4,8},{12,16},{20,24},{28,32},{36,40},{44,48},{52,56},{60,0},{8,4}... | collective-permute-start | bytes 233480 | tf_op jit(solution)/shard_map/ppermute | solution.py:522
  27.1 6.0 %collective-permute-done.cross_ref = bf16[304,128]{1,0:T(8,128)(2,1)S(1)} collective-permute-done((bf16[304,128]{1,0:T(8,128)(2,1)S(1)}, bf16[304,128]{1,0:T(8,128)(2,1)S(1)}, u32[]{:S(2)}, u32[]{:S(2)}) %collective-permute-start) | collective-permute-done | bytes 77856 | tf_op jit(solution)/shard_map/ppermute | solution.py:522
  33.1 1.3 %shard_map.121 = bf16[32,16,128]{2,1,0:T(8,128)(2,1)} custom-call(s32[6]{0:T(128)S(1)} %stack.36.at_ref, f32[2,128]{1,0:T(2,128)S(1)} %get-tuple-element.17.sums_ref, bf16[304,128]{1,0:T(8,128)(2,1)S(1)} %collective-permute-done.cross_ref), custom_call_target="tpu_custom_call" | custom-call | tf_op jit(solution)/shard_map/pallas_call | solution.py:473
  34.4 0.0 all-to-all-done.1.near_ref
  34.4 6.5 %all-to-all-start = ((bf16[32,16,128]{2,1,0:T(8,128)(2,1)}), bf16[32,16,128]{2,1,0:T(8,128)(2,1)S(1)}, u32[]{:S(2)}, u32[]{:S(2)}) async-start(bf16[32,16,128]{2,1,0:T(8,128)(2,1)} %shard_map.121), calls=%async_computation | async-start | bytes 262144 | tf_op jit(solution)/shard_map/all_to_all | solution.py:535
  40.9 2.2 %collective-permute-start.1 = (bf16[304,128]{1,0:T(8,128)(2,1)S(1)}, bf16[304,128]{1,0:T(8,128)(2,1)S(1)}, u32[]{:S(2)}, u32[]{:S(2)}) collective-permute-start(bf16[304,128]{1,0:T(8,128)(2,1)S(1)} %get-tuple-element.20), channel_id=1, source_target_pairs={{0,4},{4,0},{1,5},{5,1},{2,6},{6,2},{3,7},{7,3},{8,12},{12,8},{9,1... | collective-permute-start | bytes 233480 | tf_op jit(solution)/shard_map/ppermute | solution.py:530
  43.1 1.0 %collective-permute-done.1.pair_ref = bf16[304,128]{1,0:T(8,128)(2,1)S(1)} collective-permute-done((bf16[304,128]{1,0:T(8,128)(2,1)S(1)}, bf16[304,128]{1,0:T(8,128)(2,1)S(1)}, u32[]{:S(2)}, u32[]{:S(2)}) %collective-permute-start.1) | collective-permute-done | bytes 77856 | tf_op jit(solution)/shard_map/ppermute | solution.py:530
  44.1 1.9 %shard_map.123 = (bf16[20,144,128]{2,1,0:T(8,128)(2,1)S(1)}, f32[16,136,128]{2,1,0:T(8,128)S(1)}, f32[144,128]{1,0:T(8,128)S(1)}) custom-call(s32[6]{0:T(128)S(1)} %stack.36.at_ref, bf16[16,128,128]{2,1,0:T(8,128)(2,1)S(1)} %bitcast.24, f32[5,16,128]{2,1,0:T(8,128)S(1)} %get-tuple-element.19.planes_ref, bf16[304,128]{1,0:T(8,128)(2,1)S(1)} %collective-permute-done.cross_ref, ...), custom_call_target="tpu_custom_call" | custom-call | tf_op jit(solution)/shard_map/pallas_call | solution.py:473
  46.0 2.5 %all-to-all-done.got_ref = bf16[32,16,128]{2,1,0:T(8,128)(2,1)S(1)} async-done(((bf16[32,16,128]{2,1,0:T(8,128)(2,1)}), bf16[32,16,128]{2,1,0:T(8,128)(2,1)S(1)}, u32[]{:S(2)}, u32[]{:S(2)}) %all-to-all-start) | async-done | bytes 131104 | tf_op jit(solution)/shard_map/all_to_all | solution.py:535
  48.5 2.9 %shard_map.124 = (bf16[18,144,128]{2,1,0:T(8,128)(2,1)S(1)}, bf16[32,40,128]{2,1,0:T(8,128)(2,1)S(1)}, bf16[20,144,128]{2,1,0:T(8,128)(2,1)S(1)}) custom-call(s32[6]{0:T(128)S(1)} %stack.36.at_ref, bf16[32,16,128]{2,1,0:T(8,128)(2,1)S(1)} %all-to-all-done.got_ref, bf16[3,3,128,128]{3,2,1,0:T(8,128)(2,1)S(1)} %copy-done, ...), custom_call_target="tpu_custom_call", output_to_operand_aliasing={{2}: (5, {})} | custom-call | tf_op jit(solution)/shard_map/pallas_call | solution.py:473
  51.4 14.2 %all_to_all.20.got_ref = bf16[32,40,128]{2,1,0:T(8,128)(2,1)S(1)} all-to-all(bf16[32,40,128]{2,1,0:T(8,128)(2,1)S(1)} %get-tuple-element.26), channel_id=1, replica_groups=mesh['dp'=8,'lat_0'=4,'lat_1'=2,'lat_2'=2,'lon'=4] {'lat_0','lat_2','lon'}, dimensions={0} | all-to-all | bytes 655360 | tf_op jit(solution)/shard_map/all_to_all | solution.py:568
  65.7 0.7 shard_map.126
  66.4 13.2 %all-to-all-start.3 = ((bf16[16,24,128]{2,1,0:T(8,128)(2,1)}), bf16[16,24,128]{2,1,0:T(8,128)(2,1)S(1)}, u32[]{:S(2)}, u32[]{:S(2)}) async-start(bf16[16,24,128]{2,1,0:T(8,128)(2,1)} %shard_map.126), calls=%async_computation.3 | async-start | bytes 196608 | tf_op jit(solution)/shard_map/all_to_all | solution.py:570
  79.6 2.1 %shard_map.125 = bf16[16,128,128]{2,1,0:T(8,128)(2,1)} custom-call(bf16[18,144,128]{2,1,0:T(8,128)(2,1)S(1)} %get-tuple-element.25.grad_ref, bf16[3,3,128,128]{3,2,1,0:T(8,128)(2,1)S(1)} %copy-done), custom_call_target="tpu_custom_call" | custom-call | tf_op jit(solution)/shard_map/pallas_call | solution.py:473
  81.6 11.3 %all-to-all-done.3.got_ref = bf16[16,24,128]{2,1,0:T(8,128)(2,1)S(1)} async-done(((bf16[16,24,128]{2,1,0:T(8,128)(2,1)}), bf16[16,24,128]{2,1,0:T(8,128)(2,1)S(1)}, u32[]{:S(2)}, u32[]{:S(2)}) %all-to-all-start.3) | async-done | bytes 98336 | tf_op jit(solution)/shard_map/all_to_all | solution.py:570
  92.9 0.6 shard_map.127
  (13 shorter events, 0.0 us)
Async XLA Ops:
  0.6 43.4 %copy-start = (bf16[3,3,128,128]{3,2,1,0:T(8,128)(2,1)S(1)}, bf16[3,3,128,128]{3,2,1,0:T(8,128)(2,1)}, u32[]{:S(2)}) copy-start(bf16[3,3,128,128]{3,2,1,0:T(8,128)(2,1)} %weight_ref.3) | copy-start | bytes 884740
  0.6 43.4 %copy-start.6 = (f32[6]{0:T(128)S(1)}, f32[6]{0:T(128)}, u32[]{:S(2)}) copy-start(f32[6]{0:T(128)} %beta_ref.1) | copy-start | bytes 76
  0.7 43.4 %copy-start.5 = (f32[6]{0:T(128)S(1)}, f32[6]{0:T(128)}, u32[]{:S(2)}) copy-start(f32[6]{0:T(128)} %alpha_ref.1) | copy-start | bytes 76
  0.7 43.4 %copy-start.4 = (f32[128]{0:T(128)S(1)}, f32[128]{0:T(128)}, u32[]{:S(2)}) copy-start(f32[128]{0:T(128)} %param.12) | copy-start | bytes 1540
  0.7 43.4 %copy-start.3 = (f32[128]{0:T(128)S(1)}, f32[128]{0:T(128)}, u32[]{:S(2)}) copy-start(f32[128]{0:T(128)} %param.11) | copy-start | bytes 1540
  3.1 1.0 %copy-start.1 = (bf16[1,16,128,128]{3,2,1,0:T(8,128)(2,1)S(1)}, bf16[1,16,128,128]{3,2,1,0:T(8,128)(2,1)}, u32[]{:S(2)}) copy-start(bf16[1,16,128,128]{3,2,1,0:T(8,128)(2,1)} %param.9) | copy-start | bytes 1572868
  4.2 39.9 %copy-start.2 = (bf16[1,16,128,128]{3,2,1,0:T(8,128)(2,1)S(1)}, bf16[1,16,128,128]{3,2,1,0:T(8,128)(2,1)}, u32[]{:S(2)}) copy-start(bf16[1,16,128,128]{3,2,1,0:T(8,128)(2,1)} %param.9) | copy-start | bytes 1572868
  5.4 28.9 %all-to-all-start.1 = ((bf16[8,48,128]{2,1,0:T(8,128)(2,1)}), bf16[8,48,128]{2,1,0:T(8,128)(2,1)S(1)}, u32[]{:S(2)}, u32[]{:S(2)}) async-start(bf16[8,48,128]{2,1,0:T(8,128)(2,1)} %get-tuple-element.21), calls=%async_computation.1 | async-start | bytes 196608 | tf_op jit(solution)/shard_map/all_to_all | solution.py:531
  9.7 23.4 %collective-permute-start = (bf16[304,128]{1,0:T(8,128)(2,1)S(1)}, bf16[304,128]{1,0:T(8,128)(2,1)S(1)}, u32[]{:S(2)}, u32[]{:S(2)}) collective-permute-start(bf16[304,128]{1,0:T(8,128)(2,1)S(1)} %get-tuple-element.18), channel_id=1, source_target_pairs={{4,8},{12,16},{20,24},{28,32},{36,40},{44,48},{52,56},{60,0},{8,4}... | collective-permute-start | bytes 233480 | tf_op jit(solution)/shard_map/ppermute | solution.py:522
  34.4 14.2 %all-to-all-start = ((bf16[32,16,128]{2,1,0:T(8,128)(2,1)}), bf16[32,16,128]{2,1,0:T(8,128)(2,1)S(1)}, u32[]{:S(2)}, u32[]{:S(2)}) async-start(bf16[32,16,128]{2,1,0:T(8,128)(2,1)} %shard_map.121), calls=%async_computation | async-start | bytes 262144 | tf_op jit(solution)/shard_map/all_to_all | solution.py:535
  40.9 3.2 %collective-permute-start.1 = (bf16[304,128]{1,0:T(8,128)(2,1)S(1)}, bf16[304,128]{1,0:T(8,128)(2,1)S(1)}, u32[]{:S(2)}, u32[]{:S(2)}) collective-permute-start(bf16[304,128]{1,0:T(8,128)(2,1)S(1)} %get-tuple-element.20), channel_id=1, source_target_pairs={{0,4},{4,0},{1,5},{5,1},{2,6},{6,2},{3,7},{7,3},{8,12},{12,8},{9,1... | collective-permute-start | bytes 233480 | tf_op jit(solution)/shard_map/ppermute | solution.py:530
  66.4 26.5 %all-to-all-start.3 = ((bf16[16,24,128]{2,1,0:T(8,128)(2,1)}), bf16[16,24,128]{2,1,0:T(8,128)(2,1)S(1)}, u32[]{:S(2)}, u32[]{:S(2)}) async-start(bf16[16,24,128]{2,1,0:T(8,128)(2,1)} %shard_map.126), calls=%async_computation.3 | async-start | bytes 196608 | tf_op jit(solution)/shard_map/all_to_all | solution.py:570

commit v11 on v10

--- a/solution.py
+++ b/solution.py
@@ -180,7 +180,7 @@
 
 
 def forward_kernel(
-    at_ref, hidden_ref, planes_ref, cross_ref, pair_ref, near_ref, weight_ref, bias_ref, proj_ref,
+    at_ref, hidden_ref, planes_ref, pair_ref, near_ref, weight_ref, bias_ref, proj_ref,
     alpha_ref, beta_ref,
     ext_ref, preact_ref, side_ref, rhs_ref,
 ):
@@ -189,13 +189,11 @@
     core, left, right = at_ref[0], at_ref[3], at_ref[4]
     upper, keep_above, keep_below = sides_of(at_ref)
     zero = jnp.zeros((), jnp.bfloat16)
+    paired = jnp.where(upper, rows + 2, 0)
+    keep = jnp.where(upper, keep_below, keep_above) > 0.0
     for k in range(2):
-        cross = cross_ref[k * 128 : k * 128 + 128]
         pair = pair_ref[k * 128 : k * 128 + 128]
-        ext_ref[k, 0:128] = jnp.where(keep_above > 0.0, jnp.where(upper, cross, pair), zero)
-        ext_ref[k + rows + 2, 0:128] = jnp.where(
-            keep_below > 0.0, jnp.where(upper, pair, cross), zero
-        )
+        ext_ref[paired + k, 0:128] = jnp.where(keep, pair, zero)
     ext_ref[2 : rows + 2, 0:128] = hidden_ref[...]
     place = lax.broadcasted_iota(jnp.int32, (WIDE - 128, 128), 0)
     tiles = [jnp.zeros((WIDE - 128, 128), jnp.float32) for _ in range(rows + 4)]
@@ -220,10 +218,9 @@
         second.append(jnp.concatenate([above, own[32:48], below], axis=0))
     for r in range(rows + 4):
         ext_ref[r, 128:WIDE] = tiles[r].astype(jnp.bfloat16)
-    cross = cross_ref[256:304].astype(jnp.float32)
     pair = pair_ref[256:304].astype(jnp.float32)
-    above = jnp.where(upper, cross, pair) * keep_above
-    below = jnp.where(upper, pair, cross) * keep_below
+    above = jnp.where(upper, 0.0, pair * keep_above)
+    below = jnp.where(upper, pair * keep_below, 0.0)
     planes = []
     for k in range(PLANES):
         at = k * 8
@@ -248,7 +245,7 @@
 
 
 def backward_kernel(
-    at_ref, got_ref, kernel_ref, side_ref, preact_ref, early_ref,
+    at_ref, cross_ref, got_ref, kernel_ref, side_ref, preact_ref, early_ref,
     grad_ref, sent_ref, ext_ref,
     moved_ref, weight_ref, rhs_ref, fixed_ref,
 ):
@@ -272,6 +269,9 @@
         second.append(corner[8:16])
     crossed = jnp.where(upper, 0, rows + 2)
     for r in range(2):
+        facing = cross_ref[r * 128 : r * 128 + 128]
+        facing = jnp.where(keep_cross > 0.0, facing, jnp.zeros((), jnp.bfloat16))
+        ext_ref[crossed + r, 0:128] = facing
         ext_ref[crossed + r, 128:WIDE] = tiles[r].astype(jnp.bfloat16)
     fill(rhs_ref, kernel_ref)
     again = jnp.where(upper, 0, rows)
@@ -279,10 +279,14 @@
         fixed_ref[g] = slimmed(row)
     corner = [unpacked(second[0], second[1], k) for k in range(PLANES)]
     corner = (corner[0] + corner[1] + corner[2], corner[3] + corner[4])
+    facing = cross_ref[256:304].astype(jnp.float32) * keep_cross
+    facing = (facing[0:8] + facing[8:16] + facing[16:24], facing[24:32] + facing[32:40])
     start, wet_depth = [
         jnp.concatenate(
             [
-                fields[k][0:PACK],
+                fields[k][0:8] + jnp.where(upper, facing[k], 0.0),
+                fields[k][8 : PACK - 8],
+                fields[k][PACK - 8 : PACK] + jnp.where(upper, 0.0, facing[k]),
                 fields[k][PACK : PACK + 8] + jnp.where(upper, corner[k], 0.0),
                 fields[k][PACK + 8 : 2 * PACK - 8],
                 fields[k][2 * PACK - 8 : 2 * PACK] + jnp.where(upper, 0.0, corner[k]),
@@ -541,9 +545,9 @@
             shape((4 * PACK + 16, 128), wide),
         ),
         [pltpu.VMEM((384, 384), narrow)],
-        [SMEM] + [VMEM] * 8 + [SMEM] * 2,
+        [SMEM] + [VMEM] * 7 + [SMEM] * 2,
         (
-            at, hidden, planes, cross, pair, near, conv_weight, conv_bias[None],
+            at, hidden, planes, pair, near, conv_weight, conv_bias[None],
             proj_weight[None], step_alpha, step_beta,
         ),
     )
@@ -560,10 +564,10 @@
             pltpu.VMEM((384, 384), narrow),
             pltpu.VMEM((2, SLIM, 128), wide),
         ],
-        [SMEM] + [VMEM] * 5,
-        (at, got, conv_weight, side, preact, early),
+        [SMEM] + [VMEM] * 6,
+        (at, cross, got, conv_weight, side, preact, early),
         None,
-        {5: 2},
+        {6: 2},
     )
     got = lax.all_to_all(sent, ("lat_0", "lat_2", "lon"), 0, 0, tiled=True)
     sent = call(middle_kernel, shape((n_z, 24, 128), narrow), [], [VMEM], (got,))

time: 94 us -> 95.6 us (1.017)
  local copies, waits for them, and re-layouts: 1.99 us -> 3.49 us
    unnamed x14 -> x18, local copies, waits for them, and re-layouts: 1.06 us -> 2.56 us
where the time goes in v11:
time: 95.6 us; the launch traced here: 95 us
  starting transfers between devices  43.5 us (46%)
  waiting for transfers between devices  20.2 us (21%)
  blocking collectives  14.8 us (15%)
  Pallas kernels  11.4 us (12%)
  local copies, waits for them, and re-layouts  3.49 us (4%)
    ppermute x1, starting transfers between devices, shards(): cross = lax.ppermute(cross, LAT, odd)  17.4 us
    all_to_all x1, blocking collectives, shards(): got = lax.all_to_all(sent, ('lat_0', 'lat_2', 'lon'), 0, 0, tiled=True)  14.8 us
    all_to_all x1, starting transfers between devices, shards(): got = lax.all_to_all(sent, ('lat_1', 'dp'), 0, 0, tiled=True)  13.2 us
    pallas_call x8, Pallas kernels, call(): pl.pallas_call(kernel, out_shape=shapes, in_specs=in_specs, out_specs=jax...  11.4 us
    all_to_all x1, waiting for transfers between devices, shards(): got = lax.all_to_all(sent, ('lat_1', 'dp'), 0, 0, tiled=True)  11.3 us
    all_to_all x1, starting transfers between devices, shards(): got = lax.all_to_all(sent, ('lat_0', 'lat_2', 'lon'), 0, 0, tiled=True)  6.48 us
    ppermute x1, waiting for transfers between devices, shards(): cross = lax.ppermute(cross, LAT, odd)  5.97 us
    all_to_all x1, starting transfers between devices, shards(): near = lax.all_to_all(near, ('lat_2', 'lon'), 0, 0, tiled=True)  4.3 us
  transfers between devices with their start and end apart: 5, of which 4 were waited for; matrix products, arithmetic and copies ran while one was open for 0% of the time, Pallas kernels for 6%

profile of v11, /device:TPU:32, one launch (start us, length us, event | category | flops | bytes accessed | tf_op | source)
XLA Modules:
  0.0 95.0 jit_solution(17619590882269078000)
XLA Ops:
  0.7 0.8 fusion
  1.5 0.8 dynamic-slice_bitcast_fusion.hidden_ref
  2.4 0.1 stack.36.at_ref
  2.5 0.7 shard_map.120
  3.1 1.0 %copy-done.1 = bf16[1,16,128,128]{3,2,1,0:T(8,128)(2,1)S(1)} copy-done((bf16[1,16,128,128]{3,2,1,0:T(8,128)(2,1)S(1)}, bf16[1,16,128,128]{3,2,1,0:T(8,128)(2,1)}, u32[]{:S(2)}) %copy-start.1) | copy-done | bytes 524312
  4.2 1.3 %shard_map.122 = (bf16[304,128]{1,0:T(8,128)(2,1)S(1)}, bf16[8,48,128]{2,1,0:T(8,128)(2,1)}) custom-call(s32[6]{0:T(128)S(1)} %stack.36.at_ref, bf16[16,128,128]{2,1,0:T(8,128)(2,1)S(1)} %bitcast.23, f32[5,16,128]{2,1,0:T(8,128)S(1)} %get-tuple-element.19.planes_ref), custom_call_target="tpu_custom_call" | custom-call | tf_op jit(solution)/shard_map/pallas_call | solution.py:477
  5.4 4.3 %all-to-all-start.1 = ((bf16[8,48,128]{2,1,0:T(8,128)(2,1)}), bf16[8,48,128]{2,1,0:T(8,128)(2,1)S(1)}, u32[]{:S(2)}, u32[]{:S(2)}) async-start(bf16[8,48,128]{2,1,0:T(8,128)(2,1)} %get-tuple-element.21), calls=%async_computation.1 | async-start | bytes 196608 | tf_op jit(solution)/shard_map/all_to_all | solution.py:535
  9.7 17.4 %collective-permute-start = (bf16[304,128]{1,0:T(8,128)(2,1)S(1)}, bf16[304,128]{1,0:T(8,128)(2,1)S(1)}, u32[]{:S(2)}, u32[]{:S(2)}) collective-permute-start(bf16[304,128]{1,0:T(8,128)(2,1)S(1)} %get-tuple-element.17), channel_id=1, source_target_pairs={{4,8},{12,16},{20,24},{28,32},{36,40},{44,48},{52,56},{60,0},{8,4}... | collective-permute-start | bytes 233480 | tf_op jit(solution)/shard_map/ppermute | solution.py:526
  27.1 6.0 %collective-permute-done.cross_ref = bf16[304,128]{1,0:T(8,128)(2,1)S(1)} collective-permute-done((bf16[304,128]{1,0:T(8,128)(2,1)S(1)}, bf16[304,128]{1,0:T(8,128)(2,1)S(1)}, u32[]{:S(2)}, u32[]{:S(2)}) %collective-permute-start) | collective-permute-done | bytes 77856 | tf_op jit(solution)/shard_map/ppermute | solution.py:526
  33.1 1.3 %shard_map.121 = bf16[32,16,128]{2,1,0:T(8,128)(2,1)} custom-call(s32[6]{0:T(128)S(1)} %stack.36.at_ref, f32[2,128]{1,0:T(2,128)S(1)} %get-tuple-element.18.sums_ref, bf16[304,128]{1,0:T(8,128)(2,1)S(1)} %collective-permute-done.cross_ref), custom_call_target="tpu_custom_call" | custom-call | tf_op jit(solution)/shard_map/pallas_call | solution.py:477
  34.4 6.5 %all-to-all-start = ((bf16[32,16,128]{2,1,0:T(8,128)(2,1)}), bf16[32,16,128]{2,1,0:T(8,128)(2,1)S(1)}, u32[]{:S(2)}, u32[]{:S(2)}) async-start(bf16[32,16,128]{2,1,0:T(8,128)(2,1)} %shard_map.121), calls=%async_computation | async-start | bytes 262144 | tf_op jit(solution)/shard_map/all_to_all | solution.py:539
  40.9 2.2 %collective-permute-start.1 = (bf16[304,128]{1,0:T(8,128)(2,1)S(1)}, bf16[304,128]{1,0:T(8,128)(2,1)S(1)}, u32[]{:S(2)}, u32[]{:S(2)}) collective-permute-start(bf16[304,128]{1,0:T(8,128)(2,1)S(1)} %get-tuple-element.20), channel_id=1, source_target_pairs={{0,4},{4,0},{1,5},{5,1},{2,6},{6,2},{3,7},{7,3},{8,12},{12,8},{9,1... | collective-permute-start | bytes 233480 | tf_op jit(solution)/shard_map/ppermute | solution.py:534
  43.1 1.0 %collective-permute-done.1.pair_ref = bf16[304,128]{1,0:T(8,128)(2,1)S(1)} collective-permute-done((bf16[304,128]{1,0:T(8,128)(2,1)S(1)}, bf16[304,128]{1,0:T(8,128)(2,1)S(1)}, u32[]{:S(2)}, u32[]{:S(2)}) %collective-permute-start.1) | collective-permute-done | bytes 77856 | tf_op jit(solution)/shard_map/ppermute | solution.py:534
  44.1 1.9 %shard_map.123 = (bf16[20,144,128]{2,1,0:T(8,128)(2,1)S(1)}, f32[16,136,128]{2,1,0:T(8,128)S(1)}, f32[144,128]{1,0:T(8,128)S(1)}) custom-call(s32[6]{0:T(128)S(1)} %stack.36.at_ref, bf16[16,128,128]{2,1,0:T(8,128)(2,1)S(1)} %bitcast.24, f32[5,16,128]{2,1,0:T(8,128)S(1)} %get-tuple-element.19.planes_ref, ...), custom_call_target="tpu_custom_call" | custom-call | tf_op jit(solution)/shard_map/pallas_call | solution.py:477
  46.0 0.6 copy-done.3
  46.6 1.9 %all-to-all-done.got_ref = bf16[32,16,128]{2,1,0:T(8,128)(2,1)S(1)} async-done(((bf16[32,16,128]{2,1,0:T(8,128)(2,1)}), bf16[32,16,128]{2,1,0:T(8,128)(2,1)S(1)}, u32[]{:S(2)}, u32[]{:S(2)}) %all-to-all-start) | async-done | bytes 131104 | tf_op jit(solution)/shard_map/all_to_all | solution.py:539
  48.5 0.9 copy-done.4
  49.4 2.9 %shard_map.124 = (bf16[18,144,128]{2,1,0:T(8,128)(2,1)S(1)}, bf16[32,40,128]{2,1,0:T(8,128)(2,1)S(1)}, bf16[20,144,128]{2,1,0:T(8,128)(2,1)S(1)}) custom-call(s32[6]{0:T(128)S(1)} %stack.36.at_ref, bf16[304,128]{1,0:T(8,128)(2,1)S(1)} %collective-permute-done.cross_ref, ...), custom_call_target="tpu_custom_call", output_to_operand_aliasing={{2}: (6, {})} | custom-call | tf_op jit(solution)/shard_map/pallas_call | solution.py:477
  52.3 14.8 %all_to_all.20.got_ref = bf16[32,40,128]{2,1,0:T(8,128)(2,1)S(1)} all-to-all(bf16[32,40,128]{2,1,0:T(8,128)(2,1)S(1)} %get-tuple-element.26), channel_id=1, replica_groups=mesh['dp'=8,'lat_0'=4,'lat_1'=2,'lat_2'=2,'lon'=4] {'lat_0','lat_2','lon'}, dimensions={0} | all-to-all | bytes 655360 | tf_op jit(solution)/shard_map/all_to_all | solution.py:572
  67.2 0.7 shard_map.126
  67.9 13.2 %all-to-all-start.3 = ((bf16[16,24,128]{2,1,0:T(8,128)(2,1)}), bf16[16,24,128]{2,1,0:T(8,128)(2,1)S(1)}, u32[]{:S(2)}, u32[]{:S(2)}) async-start(bf16[16,24,128]{2,1,0:T(8,128)(2,1)} %shard_map.126), calls=%async_computation.3 | async-start | bytes 196608 | tf_op jit(solution)/shard_map/all_to_all | solution.py:574
  81.0 2.1 %shard_map.125 = bf16[16,128,128]{2,1,0:T(8,128)(2,1)} custom-call(bf16[18,144,128]{2,1,0:T(8,128)(2,1)S(1)} %get-tuple-element.25.grad_ref, bf16[3,3,128,128]{3,2,1,0:T(8,128)(2,1)S(1)} %copy-done), custom_call_target="tpu_custom_call" | custom-call | tf_op jit(solution)/shard_map/pallas_call | solution.py:477
  83.1 11.3 %all-to-all-done.3.got_ref = bf16[16,24,128]{2,1,0:T(8,128)(2,1)S(1)} async-done(((bf16[16,24,128]{2,1,0:T(8,128)(2,1)}), bf16[16,24,128]{2,1,0:T(8,128)(2,1)S(1)}, u32[]{:S(2)}, u32[]{:S(2)}) %all-to-all-start.3) | async-done | bytes 98336 | tf_op jit(solution)/shard_map/all_to_all | solution.py:574
  94.4 0.6 shard_map.127
  (17 shorter events, 0.0 us)
Async XLA Ops:
  0.6 43.4 %copy-start = (bf16[3,3,128,128]{3,2,1,0:T(8,128)(2,1)S(1)}, bf16[3,3,128,128]{3,2,1,0:T(8,128)(2,1)}, u32[]{:S(2)}) copy-start(bf16[3,3,128,128]{3,2,1,0:T(8,128)(2,1)} %weight_ref.3) | copy-start | bytes 884740
  0.6 43.4 %copy-start.8 = (f32[6]{0:T(128)S(1)}, f32[6]{0:T(128)}, u32[]{:S(2)}) copy-start(f32[6]{0:T(128)} %beta_ref.1) | copy-start | bytes 76
  0.7 43.4 %copy-start.7 = (f32[6]{0:T(128)S(1)}, f32[6]{0:T(128)}, u32[]{:S(2)}) copy-start(f32[6]{0:T(128)} %alpha_ref.1) | copy-start | bytes 76
  0.7 43.4 %copy-start.6 = (f32[128]{0:T(128)S(1)}, f32[128]{0:T(128)}, u32[]{:S(2)}) copy-start(f32[128]{0:T(128)} %param.12) | copy-start | bytes 1540
  0.7 43.4 %copy-start.5 = (f32[128]{0:T(128)S(1)}, f32[128]{0:T(128)}, u32[]{:S(2)}) copy-start(f32[128]{0:T(128)} %param.11) | copy-start | bytes 1540
  3.1 1.0 %copy-start.1 = (bf16[1,16,128,128]{3,2,1,0:T(8,128)(2,1)S(1)}, bf16[1,16,128,128]{3,2,1,0:T(8,128)(2,1)}, u32[]{:S(2)}) copy-start(bf16[1,16,128,128]{3,2,1,0:T(8,128)(2,1)} %param.9) | copy-start | bytes 1572868
  4.2 39.9 %copy-start.2 = (bf16[1,16,128,128]{3,2,1,0:T(8,128)(2,1)S(1)}, bf16[1,16,128,128]{3,2,1,0:T(8,128)(2,1)}, u32[]{:S(2)}) copy-start(bf16[1,16,128,128]{3,2,1,0:T(8,128)(2,1)} %param.9) | copy-start | bytes 1572868
  5.4 28.9 %all-to-all-start.1 = ((bf16[8,48,128]{2,1,0:T(8,128)(2,1)}), bf16[8,48,128]{2,1,0:T(8,128)(2,1)S(1)}, u32[]{:S(2)}, u32[]{:S(2)}) async-start(bf16[8,48,128]{2,1,0:T(8,128)(2,1)} %get-tuple-element.21), calls=%async_computation.1 | async-start | bytes 196608 | tf_op jit(solution)/shard_map/all_to_all | solution.py:535
  9.7 23.4 %collective-permute-start = (bf16[304,128]{1,0:T(8,128)(2,1)S(1)}, bf16[304,128]{1,0:T(8,128)(2,1)S(1)}, u32[]{:S(2)}, u32[]{:S(2)}) collective-permute-start(bf16[304,128]{1,0:T(8,128)(2,1)S(1)} %get-tuple-element.17), channel_id=1, source_target_pairs={{4,8},{12,16},{20,24},{28,32},{36,40},{44,48},{52,56},{60,0},{8,4}... | collective-permute-start | bytes 233480 | tf_op jit(solution)/shard_map/ppermute | solution.py:526
  34.4 14.2 %all-to-all-start = ((bf16[32,16,128]{2,1,0:T(8,128)(2,1)}), bf16[32,16,128]{2,1,0:T(8,128)(2,1)S(1)}, u32[]{:S(2)}, u32[]{:S(2)}) async-start(bf16[32,16,128]{2,1,0:T(8,128)(2,1)} %shard_map.121), calls=%async_computation | async-start | bytes 262144 | tf_op jit(solution)/shard_map/all_to_all | solution.py:539
  40.9 3.2 %collective-permute-start.1 = (bf16[304,128]{1,0:T(8,128)(2,1)S(1)}, bf16[304,128]{1,0:T(8,128)(2,1)S(1)}, u32[]{:S(2)}, u32[]{:S(2)}) collective-permute-start(bf16[304,128]{1,0:T(8,128)(2,1)S(1)} %get-tuple-element.20), channel_id=1, source_target_pairs={{0,4},{4,0},{1,5},{5,1},{2,6},{6,2},{3,7},{7,3},{8,12},{12,8},{9,1... | collective-permute-start | bytes 233480 | tf_op jit(solution)/shard_map/ppermute | solution.py:534
  46.0 0.6 copy-start.3
  48.5 0.9 copy-start.4
  67.9 26.5 %all-to-all-start.3 = ((bf16[16,24,128]{2,1,0:T(8,128)(2,1)}), bf16[16,24,128]{2,1,0:T(8,128)(2,1)S(1)}, u32[]{:S(2)}, u32[]{:S(2)}) async-start(bf16[16,24,128]{2,1,0:T(8,128)(2,1)} %shard_map.126), calls=%async_computation.3 | async-start | bytes 196608 | tf_op jit(solution)/shard_map/all_to_all | solution.py:574

commit v12 on v11

--- a/solution.py
+++ b/solution.py
@@ -75,9 +75,11 @@
     return [jnp.where(top, p[0:8], p[rows - 8 : rows]) for p in planes]
 
 
-def first_kernel(at_ref, hidden_ref, fields_ref, cross_ref, planes_ref, sums_ref):
+def first_kernel(
+    at_ref, top_ref, bottom_ref, wet_ref, depth_ref, cross_ref, planes_ref, sums_ref
+):
     upper = at_ref[0] == 0
-    wet, wet_depth = fields_ref[0], fields_ref[1]
+    wet, wet_depth = wet_ref[...], depth_ref[...]
     planes = pieces_of(wet, 3) + pieces_of(wet_depth, 2)
     summed = full(jnp.sum(wet))
     counted = full(jnp.sum(jnp.where(wet_depth > 0.0, 1.0, 0.0)))
@@ -87,7 +89,8 @@
     sums = jnp.concatenate(sums + [jnp.zeros((2, 128), jnp.float32)], axis=0)
     for k in range(PLANES):
         planes_ref[k] = planes[k]
-    cross_ref[0:256] = hidden_ref[...].reshape(256, 128)
+    facing = jnp.where(upper, top_ref[...], bottom_ref[...])
+    cross_ref[0:256] = facing.reshape(256, 128)
     near = near_rows(planes, upper) + [sums]
     for k in range(0, 6, 2):
         tile = jnp.concatenate(near[k : k + 2], axis=0)
@@ -506,10 +509,6 @@
         [lat % 2, lat, n_lat - 1 - lat, (me + n_x - 1) % n_x, (me + 1) % n_x, row_group]
     ).astype(jnp.int32)
     mask = sea_mask.astype(wide)
-    fields = jnp.stack([mask * surface_cotangent[0], mask * ocean_depth])
-    facing = lax.dynamic_slice_in_dim(
-        hidden, jnp.where(lax.axis_index("lat_2") == 0, 0, rows - 2), 2, axis=0
-    )
     cross, planes, sums = call(
         first_kernel,
         (
@@ -518,8 +517,10 @@
             shape((2, 128), wide),
         ),
         [],
-        [SMEM] + [VMEM] * 2,
-        (at, facing, fields),
+        [SMEM] + [VMEM] * 4,
+        (
+            at, hidden[:2], hidden[rows - 2 :], mask * surface_cotangent[0], mask * ocean_depth
+        ),
     )
     odd = [(i, (i + 1) % n_lat) for i in range(1, n_lat, 2)]
     odd = odd + [(j, i) for i, j in odd]

time: 95.6 us -> 95.6 us (level)
  no operation moved by 1% of the time
where the time goes in v12:
time: 95.6 us; the launch traced here: 95 us
  starting transfers between devices  43.5 us (46%)
  waiting for transfers between devices  20.1 us (21%)
  blocking collectives  14.8 us (15%)
  Pallas kernels  11.4 us (12%)
  local copies, waits for them, and re-layouts  3.58 us (4%)
    ppermute x1, starting transfers between devices, shards(): cross = lax.ppermute(cross, LAT, odd)  17.4 us
    all_to_all x1, blocking collectives, shards(): got = lax.all_to_all(sent, ('lat_0', 'lat_2', 'lon'), 0, 0, tiled=True)  14.8 us
    all_to_all x1, starting transfers between devices, shards(): got = lax.all_to_all(sent, ('lat_1', 'dp'), 0, 0, tiled=True)  13.2 us
    pallas_call x8, Pallas kernels, call(): pl.pallas_call(kernel, out_shape=shapes, in_specs=in_specs, out_specs=jax...  11.4 us
    all_to_all x1, waiting for transfers between devices, shards(): got = lax.all_to_all(sent, ('lat_1', 'dp'), 0, 0, tiled=True)  11.3 us
    all_to_all x1, starting transfers between devices, shards(): got = lax.all_to_all(sent, ('lat_0', 'lat_2', 'lon'), 0, 0, tiled=True)  6.48 us
    ppermute x1, waiting for transfers between devices, shards(): cross = lax.ppermute(cross, LAT, odd)  5.97 us
    all_to_all x1, starting transfers between devices, shards(): near = lax.all_to_all(near, ('lat_2', 'lon'), 0, 0, tiled=True)  4.3 us
  transfers between devices with their start and end apart: 5, of which 4 were waited for; matrix products, arithmetic and copies ran while one was open for 0% of the time, Pallas kernels for 6%

profile of v12, /device:TPU:32, one launch (start us, length us, event | category | flops | bytes accessed | tf_op | source)
XLA Modules:
  0.0 95.0 jit_solution(6536759175841838332)
XLA Ops:
  0.7 0.9 slice_bitcast_fusion
  1.7 0.7 convert_multiply_fusion
  2.4 0.1 stack.27.at_ref
  2.5 0.7 shard_map.120
  3.2 1.0 %copy-done = bf16[1,16,128,128]{3,2,1,0:T(8,128)(2,1)S(1)} copy-done((bf16[1,16,128,128]{3,2,1,0:T(8,128)(2,1)S(1)}, bf16[1,16,128,128]{3,2,1,0:T(8,128)(2,1)}, u32[]{:S(2)}) %copy-start) | copy-done | bytes 524312
  4.2 1.3 %shard_map.122 = (bf16[304,128]{1,0:T(8,128)(2,1)S(1)}, bf16[8,48,128]{2,1,0:T(8,128)(2,1)}) custom-call(s32[6]{0:T(128)S(1)} %stack.27.at_ref, bf16[16,128,128]{2,1,0:T(8,128)(2,1)S(1)} %bitcast.19, f32[5,16,128]{2,1,0:T(8,128)S(1)} %get-tuple-element.19.planes_ref), custom_call_target="tpu_custom_call" | custom-call | tf_op jit(solution)/shard_map/pallas_call | solution.py:480
  5.5 4.3 %all-to-all-start.1 = ((bf16[8,48,128]{2,1,0:T(8,128)(2,1)}), bf16[8,48,128]{2,1,0:T(8,128)(2,1)S(1)}, u32[]{:S(2)}, u32[]{:S(2)}) async-start(bf16[8,48,128]{2,1,0:T(8,128)(2,1)} %get-tuple-element.21), calls=%async_computation.1 | async-start | bytes 196608 | tf_op jit(solution)/shard_map/all_to_all | solution.py:536
  9.8 17.4 %collective-permute-start = (bf16[304,128]{1,0:T(8,128)(2,1)S(1)}, bf16[304,128]{1,0:T(8,128)(2,1)S(1)}, u32[]{:S(2)}, u32[]{:S(2)}) collective-permute-start(bf16[304,128]{1,0:T(8,128)(2,1)S(1)} %get-tuple-element.17), channel_id=1, source_target_pairs={{4,8},{12,16},{20,24},{28,32},{36,40},{44,48},{52,56},{60,0},{8,4}... | collective-permute-start | bytes 233480 | tf_op jit(solution)/shard_map/ppermute | solution.py:527
  27.2 6.0 %collective-permute-done.cross_ref = bf16[304,128]{1,0:T(8,128)(2,1)S(1)} collective-permute-done((bf16[304,128]{1,0:T(8,128)(2,1)S(1)}, bf16[304,128]{1,0:T(8,128)(2,1)S(1)}, u32[]{:S(2)}, u32[]{:S(2)}) %collective-permute-start) | collective-permute-done | bytes 77856 | tf_op jit(solution)/shard_map/ppermute | solution.py:527
  33.1 1.3 %shard_map.121 = bf16[32,16,128]{2,1,0:T(8,128)(2,1)} custom-call(s32[6]{0:T(128)S(1)} %stack.27.at_ref, f32[2,128]{1,0:T(2,128)S(1)} %get-tuple-element.18.sums_ref, bf16[304,128]{1,0:T(8,128)(2,1)S(1)} %collective-permute-done.cross_ref), custom_call_target="tpu_custom_call" | custom-call | tf_op jit(solution)/shard_map/pallas_call | solution.py:480
  34.4 6.5 %all-to-all-start = ((bf16[32,16,128]{2,1,0:T(8,128)(2,1)}), bf16[32,16,128]{2,1,0:T(8,128)(2,1)S(1)}, u32[]{:S(2)}, u32[]{:S(2)}) async-start(bf16[32,16,128]{2,1,0:T(8,128)(2,1)} %shard_map.121), calls=%async_computation | async-start | bytes 262144 | tf_op jit(solution)/shard_map/all_to_all | solution.py:540
  40.9 2.2 %collective-permute-start.1 = (bf16[304,128]{1,0:T(8,128)(2,1)S(1)}, bf16[304,128]{1,0:T(8,128)(2,1)S(1)}, u32[]{:S(2)}, u32[]{:S(2)}) collective-permute-start(bf16[304,128]{1,0:T(8,128)(2,1)S(1)} %get-tuple-element.20), channel_id=1, source_target_pairs={{0,4},{4,0},{1,5},{5,1},{2,6},{6,2},{3,7},{7,3},{8,12},{12,8},{9,1... | collective-permute-start | bytes 233480 | tf_op jit(solution)/shard_map/ppermute | solution.py:535
  43.1 1.0 %collective-permute-done.1.pair_ref = bf16[304,128]{1,0:T(8,128)(2,1)S(1)} collective-permute-done((bf16[304,128]{1,0:T(8,128)(2,1)S(1)}, bf16[304,128]{1,0:T(8,128)(2,1)S(1)}, u32[]{:S(2)}, u32[]{:S(2)}) %collective-permute-start.1) | collective-permute-done | bytes 77856 | tf_op jit(solution)/shard_map/ppermute | solution.py:535
  44.1 1.9 %shard_map.123 = (bf16[20,144,128]{2,1,0:T(8,128)(2,1)S(1)}, f32[16,136,128]{2,1,0:T(8,128)S(1)}, f32[144,128]{1,0:T(8,128)S(1)}) custom-call(s32[6]{0:T(128)S(1)} %stack.27.at_ref, bf16[16,128,128]{2,1,0:T(8,128)(2,1)S(1)} %bitcast.20, f32[5,16,128]{2,1,0:T(8,128)S(1)} %get-tuple-element.19.planes_ref, ...), custom_call_target="tpu_custom_call" | custom-call | tf_op jit(solution)/shard_map/pallas_call | solution.py:480
  46.0 0.6 copy-done.3
  46.6 1.9 %all-to-all-done.got_ref = bf16[32,16,128]{2,1,0:T(8,128)(2,1)S(1)} async-done(((bf16[32,16,128]{2,1,0:T(8,128)(2,1)}), bf16[32,16,128]{2,1,0:T(8,128)(2,1)S(1)}, u32[]{:S(2)}, u32[]{:S(2)}) %all-to-all-start) | async-done | bytes 131104 | tf_op jit(solution)/shard_map/all_to_all | solution.py:540
  48.6 0.9 copy-done.4
  49.4 2.9 %shard_map.124 = (bf16[18,144,128]{2,1,0:T(8,128)(2,1)S(1)}, bf16[32,40,128]{2,1,0:T(8,128)(2,1)S(1)}, bf16[20,144,128]{2,1,0:T(8,128)(2,1)S(1)}) custom-call(s32[6]{0:T(128)S(1)} %stack.27.at_ref, bf16[304,128]{1,0:T(8,128)(2,1)S(1)} %collective-permute-done.cross_ref, ...), custom_call_target="tpu_custom_call", output_to_operand_aliasing={{2}: (6, {})} | custom-call | tf_op jit(solution)/shard_map/pallas_call | solution.py:480
  52.4 14.8 %all_to_all.20.got_ref = bf16[32,40,128]{2,1,0:T(8,128)(2,1)S(1)} all-to-all(bf16[32,40,128]{2,1,0:T(8,128)(2,1)S(1)} %get-tuple-element.26), channel_id=1, replica_groups=mesh['dp'=8,'lat_0'=4,'lat_1'=2,'lat_2'=2,'lon'=4] {'lat_0','lat_2','lon'}, dimensions={0} | all-to-all | bytes 655360 | tf_op jit(solution)/shard_map/all_to_all | solution.py:573
  67.2 0.7 shard_map.126
  67.9 13.2 %all-to-all-start.3 = ((bf16[16,24,128]{2,1,0:T(8,128)(2,1)}), bf16[16,24,128]{2,1,0:T(8,128)(2,1)S(1)}, u32[]{:S(2)}, u32[]{:S(2)}) async-start(bf16[16,24,128]{2,1,0:T(8,128)(2,1)} %shard_map.126), calls=%async_computation.3 | async-start | bytes 196608 | tf_op jit(solution)/shard_map/all_to_all | solution.py:575
  81.1 2.1 %shard_map.125 = bf16[16,128,128]{2,1,0:T(8,128)(2,1)} custom-call(bf16[18,144,128]{2,1,0:T(8,128)(2,1)S(1)} %get-tuple-element.25.grad_ref, bf16[3,3,128,128]{3,2,1,0:T(8,128)(2,1)S(1)} %copy-done.2), custom_call_target="tpu_custom_call" | custom-call | tf_op jit(solution)/shard_map/pallas_call | solution.py:480
  83.1 11.3 %all-to-all-done.3.got_ref = bf16[16,24,128]{2,1,0:T(8,128)(2,1)S(1)} async-done(((bf16[16,24,128]{2,1,0:T(8,128)(2,1)}), bf16[16,24,128]{2,1,0:T(8,128)(2,1)S(1)}, u32[]{:S(2)}, u32[]{:S(2)}) %all-to-all-start.3) | async-done | bytes 98336 | tf_op jit(solution)/shard_map/all_to_all | solution.py:575
  94.4 0.6 shard_map.127
  (16 shorter events, 0.0 us)
Async XLA Ops:
  0.6 43.4 %copy-start.1 = (bf16[1,16,128,128]{3,2,1,0:T(8,128)(2,1)S(1)}, bf16[1,16,128,128]{3,2,1,0:T(8,128)(2,1)}, u32[]{:S(2)}) copy-start(bf16[1,16,128,128]{3,2,1,0:T(8,128)(2,1)} %param.9) | copy-start | bytes 1572868
  0.6 43.4 %copy-start.8 = (f32[6]{0:T(128)S(1)}, f32[6]{0:T(128)}, u32[]{:S(2)}) copy-start(f32[6]{0:T(128)} %beta_ref.1) | copy-start | bytes 76
  0.7 43.4 %copy-start.7 = (f32[6]{0:T(128)S(1)}, f32[6]{0:T(128)}, u32[]{:S(2)}) copy-start(f32[6]{0:T(128)} %alpha_ref.1) | copy-start | bytes 76
  0.7 43.4 %copy-start.6 = (f32[128]{0:T(128)S(1)}, f32[128]{0:T(128)}, u32[]{:S(2)}) copy-start(f32[128]{0:T(128)} %param.12) | copy-start | bytes 1540
  0.7 43.4 %copy-start.5 = (f32[128]{0:T(128)S(1)}, f32[128]{0:T(128)}, u32[]{:S(2)}) copy-start(f32[128]{0:T(128)} %param.11) | copy-start | bytes 1540
  3.2 1.0 %copy-start = (bf16[1,16,128,128]{3,2,1,0:T(8,128)(2,1)S(1)}, bf16[1,16,128,128]{3,2,1,0:T(8,128)(2,1)}, u32[]{:S(2)}) copy-start(bf16[1,16,128,128]{3,2,1,0:T(8,128)(2,1)} %param.9) | copy-start | bytes 1572868
  4.2 39.9 %copy-start.2 = (bf16[3,3,128,128]{3,2,1,0:T(8,128)(2,1)S(1)}, bf16[3,3,128,128]{3,2,1,0:T(8,128)(2,1)}, u32[]{:S(2)}) copy-start(bf16[3,3,128,128]{3,2,1,0:T(8,128)(2,1)} %weight_ref.3) | copy-start | bytes 884740
  5.5 28.9 %all-to-all-start.1 = ((bf16[8,48,128]{2,1,0:T(8,128)(2,1)}), bf16[8,48,128]{2,1,0:T(8,128)(2,1)S(1)}, u32[]{:S(2)}, u32[]{:S(2)}) async-start(bf16[8,48,128]{2,1,0:T(8,128)(2,1)} %get-tuple-element.21), calls=%async_computation.1 | async-start | bytes 196608 | tf_op jit(solution)/shard_map/all_to_all | solution.py:536
  9.8 23.4 %collective-permute-start = (bf16[304,128]{1,0:T(8,128)(2,1)S(1)}, bf16[304,128]{1,0:T(8,128)(2,1)S(1)}, u32[]{:S(2)}, u32[]{:S(2)}) collective-permute-start(bf16[304,128]{1,0:T(8,128)(2,1)S(1)} %get-tuple-element.17), channel_id=1, source_target_pairs={{4,8},{12,16},{20,24},{28,32},{36,40},{44,48},{52,56},{60,0},{8,4}... | collective-permute-start | bytes 233480 | tf_op jit(solution)/shard_map/ppermute | solution.py:527
  34.4 14.2 %all-to-all-start = ((bf16[32,16,128]{2,1,0:T(8,128)(2,1)}), bf16[32,16,128]{2,1,0:T(8,128)(2,1)S(1)}, u32[]{:S(2)}, u32[]{:S(2)}) async-start(bf16[32,16,128]{2,1,0:T(8,128)(2,1)} %shard_map.121), calls=%async_computation | async-start | bytes 262144 | tf_op jit(solution)/shard_map/all_to_all | solution.py:540
  40.9 3.2 %collective-permute-start.1 = (bf16[304,128]{1,0:T(8,128)(2,1)S(1)}, bf16[304,128]{1,0:T(8,128)(2,1)S(1)}, u32[]{:S(2)}, u32[]{:S(2)}) collective-permute-start(bf16[304,128]{1,0:T(8,128)(2,1)S(1)} %get-tuple-element.20), channel_id=1, source_target_pairs={{0,4},{4,0},{1,5},{5,1},{2,6},{6,2},{3,7},{7,3},{8,12},{12,8},{9,1... | collective-permute-start | bytes 233480 | tf_op jit(solution)/shard_map/ppermute | solution.py:535
  46.0 0.6 copy-start.3
  48.6 0.9 copy-start.4
  67.9 26.5 %all-to-all-start.3 = ((bf16[16,24,128]{2,1,0:T(8,128)(2,1)}), bf16[16,24,128]{2,1,0:T(8,128)(2,1)S(1)}, u32[]{:S(2)}, u32[]{:S(2)}) async-start(bf16[16,24,128]{2,1,0:T(8,128)(2,1)} %shard_map.126), calls=%async_computation.3 | async-start | bytes 196608 | tf_op jit(solution)/shard_map/all_to_all | solution.py:575

commit v13 on v11

--- a/solution.py
+++ b/solution.py
@@ -75,9 +75,9 @@
     return [jnp.where(top, p[0:8], p[rows - 8 : rows]) for p in planes]
 
 
-def first_kernel(at_ref, hidden_ref, fields_ref, cross_ref, planes_ref, sums_ref):
+def first_kernel(at_ref, hidden_ref, wet_ref, depth_ref, cross_ref, planes_ref, sums_ref):
     upper = at_ref[0] == 0
-    wet, wet_depth = fields_ref[0], fields_ref[1]
+    wet, wet_depth = wet_ref[...], depth_ref[...]
     planes = pieces_of(wet, 3) + pieces_of(wet_depth, 2)
     summed = full(jnp.sum(wet))
     counted = full(jnp.sum(jnp.where(wet_depth > 0.0, 1.0, 0.0)))
@@ -506,7 +506,6 @@
         [lat % 2, lat, n_lat - 1 - lat, (me + n_x - 1) % n_x, (me + 1) % n_x, row_group]
     ).astype(jnp.int32)
     mask = sea_mask.astype(wide)
-    fields = jnp.stack([mask * surface_cotangent[0], mask * ocean_depth])
     facing = lax.dynamic_slice_in_dim(
         hidden, jnp.where(lax.axis_index("lat_2") == 0, 0, rows - 2), 2, axis=0
     )
@@ -518,8 +517,8 @@
             shape((2, 128), wide),
         ),
         [],
-        [SMEM] + [VMEM] * 2,
-        (at, facing, fields),
+        [SMEM] + [VMEM] * 3,
+        (at, facing, mask * surface_cotangent[0], mask * ocean_depth),
     )
     odd = [(i, (i + 1) % n_lat) for i in range(1, n_lat, 2)]
     odd = odd + [(j, i) for i, j in odd]

time: 95.6 us -> 95.6 us (level)
  no operation moved by 1% of the time
where the time goes in v13:
time: 95.6 us; the launch traced here: 95 us
  starting transfers between devices  43.5 us (46%)
  waiting for transfers between devices  20.2 us (21%)
  blocking collectives  14.8 us (15%)
  Pallas kernels  11.4 us (12%)
  local copies, waits for them, and re-layouts  3.55 us (4%)
    ppermute x1, starting transfers between devices, shards(): cross = lax.ppermute(cross, LAT, odd)  17.4 us
    all_to_all x1, blocking collectives, shards(): got = lax.all_to_all(sent, ('lat_0', 'lat_2', 'lon'), 0, 0, tiled=True)  14.8 us
    all_to_all x1, starting transfers between devices, shards(): got = lax.all_to_all(sent, ('lat_1', 'dp'), 0, 0, tiled=True)  13.2 us
    pallas_call x8, Pallas kernels, call(): pl.pallas_call(kernel, out_shape=shapes, in_specs=in_specs, out_specs=jax...  11.4 us
    all_to_all x1, waiting for transfers between devices, shards(): got = lax.all_to_all(sent, ('lat_1', 'dp'), 0, 0, tiled=True)  11.3 us
    all_to_all x1, starting transfers between devices, shards(): got = lax.all_to_all(sent, ('lat_0', 'lat_2', 'lon'), 0, 0, tiled=True)  6.48 us
    ppermute x1, waiting for transfers between devices, shards(): cross = lax.ppermute(cross, LAT, odd)  5.97 us
    all_to_all x1, starting transfers between devices, shards(): near = lax.all_to_all(near, ('lat_2', 'lon'), 0, 0, tiled=True)  4.3 us
  transfers between devices with their start and end apart: 5, of which 4 were waited for; matrix products, arithmetic and copies ran while one was open for 0% of the time, Pallas kernels for 6%

profile of v13, /device:TPU:32, one launch (start us, length us, event | category | flops | bytes accessed | tf_op | source)
XLA Modules:
  0.0 95.0 jit_solution(9728589280358535082)
XLA Ops:
  0.7 0.9 dynamic-slice_bitcast_fusion.hidden_ref
  1.6 0.7 convert_multiply_fusion
  2.4 0.1 stack.27.at_ref
  2.4 0.7 shard_map.120
  3.1 1.0 %copy-done.1 = bf16[1,16,128,128]{3,2,1,0:T(8,128)(2,1)S(1)} copy-done((bf16[1,16,128,128]{3,2,1,0:T(8,128)(2,1)S(1)}, bf16[1,16,128,128]{3,2,1,0:T(8,128)(2,1)}, u32[]{:S(2)}) %copy-start.1) | copy-done | bytes 524312
  4.2 1.3 %shard_map.122 = (bf16[304,128]{1,0:T(8,128)(2,1)S(1)}, bf16[8,48,128]{2,1,0:T(8,128)(2,1)}) custom-call(s32[6]{0:T(128)S(1)} %stack.27.at_ref, bf16[16,128,128]{2,1,0:T(8,128)(2,1)S(1)} %bitcast.17, f32[5,16,128]{2,1,0:T(8,128)S(1)} %get-tuple-element.19.planes_ref), custom_call_target="tpu_custom_call" | custom-call | tf_op jit(solution)/shard_map/pallas_call | solution.py:477
  5.4 4.3 %all-to-all-start.1 = ((bf16[8,48,128]{2,1,0:T(8,128)(2,1)}), bf16[8,48,128]{2,1,0:T(8,128)(2,1)S(1)}, u32[]{:S(2)}, u32[]{:S(2)}) async-start(bf16[8,48,128]{2,1,0:T(8,128)(2,1)} %get-tuple-element.21), calls=%async_computation.1 | async-start | bytes 196608 | tf_op jit(solution)/shard_map/all_to_all | solution.py:534
  9.7 17.4 %collective-permute-start = (bf16[304,128]{1,0:T(8,128)(2,1)S(1)}, bf16[304,128]{1,0:T(8,128)(2,1)S(1)}, u32[]{:S(2)}, u32[]{:S(2)}) collective-permute-start(bf16[304,128]{1,0:T(8,128)(2,1)S(1)} %get-tuple-element.17), channel_id=1, source_target_pairs={{4,8},{12,16},{20,24},{28,32},{36,40},{44,48},{52,56},{60,0},{8,4}... | collective-permute-start | bytes 233480 | tf_op jit(solution)/shard_map/ppermute | solution.py:525
  27.1 6.0 %collective-permute-done.cross_ref = bf16[304,128]{1,0:T(8,128)(2,1)S(1)} collective-permute-done((bf16[304,128]{1,0:T(8,128)(2,1)S(1)}, bf16[304,128]{1,0:T(8,128)(2,1)S(1)}, u32[]{:S(2)}, u32[]{:S(2)}) %collective-permute-start) | collective-permute-done | bytes 77856 | tf_op jit(solution)/shard_map/ppermute | solution.py:525
  33.1 1.3 %shard_map.121 = bf16[32,16,128]{2,1,0:T(8,128)(2,1)} custom-call(s32[6]{0:T(128)S(1)} %stack.27.at_ref, f32[2,128]{1,0:T(2,128)S(1)} %get-tuple-element.18.sums_ref, bf16[304,128]{1,0:T(8,128)(2,1)S(1)} %collective-permute-done.cross_ref), custom_call_target="tpu_custom_call" | custom-call | tf_op jit(solution)/shard_map/pallas_call | solution.py:477
  34.4 6.5 %all-to-all-start = ((bf16[32,16,128]{2,1,0:T(8,128)(2,1)}), bf16[32,16,128]{2,1,0:T(8,128)(2,1)S(1)}, u32[]{:S(2)}, u32[]{:S(2)}) async-start(bf16[32,16,128]{2,1,0:T(8,128)(2,1)} %shard_map.121), calls=%async_computation | async-start | bytes 262144 | tf_op jit(solution)/shard_map/all_to_all | solution.py:538
  40.9 2.2 %collective-permute-start.1 = (bf16[304,128]{1,0:T(8,128)(2,1)S(1)}, bf16[304,128]{1,0:T(8,128)(2,1)S(1)}, u32[]{:S(2)}, u32[]{:S(2)}) collective-permute-start(bf16[304,128]{1,0:T(8,128)(2,1)S(1)} %get-tuple-element.20), channel_id=1, source_target_pairs={{0,4},{4,0},{1,5},{5,1},{2,6},{6,2},{3,7},{7,3},{8,12},{12,8},{9,1... | collective-permute-start | bytes 233480 | tf_op jit(solution)/shard_map/ppermute | solution.py:533
  43.0 1.0 %collective-permute-done.1.pair_ref = bf16[304,128]{1,0:T(8,128)(2,1)S(1)} collective-permute-done((bf16[304,128]{1,0:T(8,128)(2,1)S(1)}, bf16[304,128]{1,0:T(8,128)(2,1)S(1)}, u32[]{:S(2)}, u32[]{:S(2)}) %collective-permute-start.1) | collective-permute-done | bytes 77856 | tf_op jit(solution)/shard_map/ppermute | solution.py:533
  44.1 1.9 %shard_map.123 = (bf16[20,144,128]{2,1,0:T(8,128)(2,1)S(1)}, f32[16,136,128]{2,1,0:T(8,128)S(1)}, f32[144,128]{1,0:T(8,128)S(1)}) custom-call(s32[6]{0:T(128)S(1)} %stack.27.at_ref, bf16[16,128,128]{2,1,0:T(8,128)(2,1)S(1)} %bitcast.18, f32[5,16,128]{2,1,0:T(8,128)S(1)} %get-tuple-element.19.planes_ref, ...), custom_call_target="tpu_custom_call" | custom-call | tf_op jit(solution)/shard_map/pallas_call | solution.py:477
  46.0 0.6 copy-done.3
  46.6 2.0 %all-to-all-done.got_ref = bf16[32,16,128]{2,1,0:T(8,128)(2,1)S(1)} async-done(((bf16[32,16,128]{2,1,0:T(8,128)(2,1)}), bf16[32,16,128]{2,1,0:T(8,128)(2,1)S(1)}, u32[]{:S(2)}, u32[]{:S(2)}) %all-to-all-start) | async-done | bytes 131104 | tf_op jit(solution)/shard_map/all_to_all | solution.py:538
  48.5 0.9 copy-done.4
  49.4 2.9 %shard_map.124 = (bf16[18,144,128]{2,1,0:T(8,128)(2,1)S(1)}, bf16[32,40,128]{2,1,0:T(8,128)(2,1)S(1)}, bf16[20,144,128]{2,1,0:T(8,128)(2,1)S(1)}) custom-call(s32[6]{0:T(128)S(1)} %stack.27.at_ref, bf16[304,128]{1,0:T(8,128)(2,1)S(1)} %collective-permute-done.cross_ref, ...), custom_call_target="tpu_custom_call", output_to_operand_aliasing={{2}: (6, {})} | custom-call | tf_op jit(solution)/shard_map/pallas_call | solution.py:477
  52.3 14.8 %all_to_all.20.got_ref = bf16[32,40,128]{2,1,0:T(8,128)(2,1)S(1)} all-to-all(bf16[32,40,128]{2,1,0:T(8,128)(2,1)S(1)} %get-tuple-element.26), channel_id=1, replica_groups=mesh['dp'=8,'lat_0'=4,'lat_1'=2,'lat_2'=2,'lon'=4] {'lat_0','lat_2','lon'}, dimensions={0} | all-to-all | bytes 655360 | tf_op jit(solution)/shard_map/all_to_all | solution.py:571
  67.2 0.7 shard_map.126
  67.9 13.2 %all-to-all-start.3 = ((bf16[16,24,128]{2,1,0:T(8,128)(2,1)}), bf16[16,24,128]{2,1,0:T(8,128)(2,1)S(1)}, u32[]{:S(2)}, u32[]{:S(2)}) async-start(bf16[16,24,128]{2,1,0:T(8,128)(2,1)} %shard_map.126), calls=%async_computation.3 | async-start | bytes 196608 | tf_op jit(solution)/shard_map/all_to_all | solution.py:573
  81.0 2.1 %shard_map.125 = bf16[16,128,128]{2,1,0:T(8,128)(2,1)} custom-call(bf16[18,144,128]{2,1,0:T(8,128)(2,1)S(1)} %get-tuple-element.25.grad_ref, bf16[3,3,128,128]{3,2,1,0:T(8,128)(2,1)S(1)} %copy-done), custom_call_target="tpu_custom_call" | custom-call | tf_op jit(solution)/shard_map/pallas_call | solution.py:477
  83.1 11.3 %all-to-all-done.3.got_ref = bf16[16,24,128]{2,1,0:T(8,128)(2,1)S(1)} async-done(((bf16[16,24,128]{2,1,0:T(8,128)(2,1)}), bf16[16,24,128]{2,1,0:T(8,128)(2,1)S(1)}, u32[]{:S(2)}, u32[]{:S(2)}) %all-to-all-start.3) | async-done | bytes 98336 | tf_op jit(solution)/shard_map/all_to_all | solution.py:573
  94.4 0.6 shard_map.127
  (16 shorter events, 0.0 us)
Async XLA Ops:
  0.6 43.4 %copy-start = (bf16[3,3,128,128]{3,2,1,0:T(8,128)(2,1)S(1)}, bf16[3,3,128,128]{3,2,1,0:T(8,128)(2,1)}, u32[]{:S(2)}) copy-start(bf16[3,3,128,128]{3,2,1,0:T(8,128)(2,1)} %weight_ref.3) | copy-start | bytes 884740
  0.6 43.4 %copy-start.8 = (f32[6]{0:T(128)S(1)}, f32[6]{0:T(128)}, u32[]{:S(2)}) copy-start(f32[6]{0:T(128)} %beta_ref.1) | copy-start | bytes 76
  0.7 43.4 %copy-start.7 = (f32[6]{0:T(128)S(1)}, f32[6]{0:T(128)}, u32[]{:S(2)}) copy-start(f32[6]{0:T(128)} %alpha_ref.1) | copy-start | bytes 76
  0.7 43.4 %copy-start.6 = (f32[128]{0:T(128)S(1)}, f32[128]{0:T(128)}, u32[]{:S(2)}) copy-start(f32[128]{0:T(128)} %param.12) | copy-start | bytes 1540
  0.7 43.4 %copy-start.5 = (f32[128]{0:T(128)S(1)}, f32[128]{0:T(128)}, u32[]{:S(2)}) copy-start(f32[128]{0:T(128)} %param.11) | copy-start | bytes 1540
  3.1 1.0 %copy-start.1 = (bf16[1,16,128,128]{3,2,1,0:T(8,128)(2,1)S(1)}, bf16[1,16,128,128]{3,2,1,0:T(8,128)(2,1)}, u32[]{:S(2)}) copy-start(bf16[1,16,128,128]{3,2,1,0:T(8,128)(2,1)} %param.9) | copy-start | bytes 1572868
  4.2 39.9 %copy-start.2 = (bf16[1,16,128,128]{3,2,1,0:T(8,128)(2,1)S(1)}, bf16[1,16,128,128]{3,2,1,0:T(8,128)(2,1)}, u32[]{:S(2)}) copy-start(bf16[1,16,128,128]{3,2,1,0:T(8,128)(2,1)} %param.9) | copy-start | bytes 1572868
  5.4 28.9 %all-to-all-start.1 = ((bf16[8,48,128]{2,1,0:T(8,128)(2,1)}), bf16[8,48,128]{2,1,0:T(8,128)(2,1)S(1)}, u32[]{:S(2)}, u32[]{:S(2)}) async-start(bf16[8,48,128]{2,1,0:T(8,128)(2,1)} %get-tuple-element.21), calls=%async_computation.1 | async-start | bytes 196608 | tf_op jit(solution)/shard_map/all_to_all | solution.py:534
  9.7 23.4 %collective-permute-start = (bf16[304,128]{1,0:T(8,128)(2,1)S(1)}, bf16[304,128]{1,0:T(8,128)(2,1)S(1)}, u32[]{:S(2)}, u32[]{:S(2)}) collective-permute-start(bf16[304,128]{1,0:T(8,128)(2,1)S(1)} %get-tuple-element.17), channel_id=1, source_target_pairs={{4,8},{12,16},{20,24},{28,32},{36,40},{44,48},{52,56},{60,0},{8,4}... | collective-permute-start | bytes 233480 | tf_op jit(solution)/shard_map/ppermute | solution.py:525
  34.4 14.2 %all-to-all-start = ((bf16[32,16,128]{2,1,0:T(8,128)(2,1)}), bf16[32,16,128]{2,1,0:T(8,128)(2,1)S(1)}, u32[]{:S(2)}, u32[]{:S(2)}) async-start(bf16[32,16,128]{2,1,0:T(8,128)(2,1)} %shard_map.121), calls=%async_computation | async-start | bytes 262144 | tf_op jit(solution)/shard_map/all_to_all | solution.py:538
  40.9 3.2 %collective-permute-start.1 = (bf16[304,128]{1,0:T(8,128)(2,1)S(1)}, bf16[304,128]{1,0:T(8,128)(2,1)S(1)}, u32[]{:S(2)}, u32[]{:S(2)}) collective-permute-start(bf16[304,128]{1,0:T(8,128)(2,1)S(1)} %get-tuple-element.20), channel_id=1, source_target_pairs={{0,4},{4,0},{1,5},{5,1},{2,6},{6,2},{3,7},{7,3},{8,12},{12,8},{9,1... | collective-permute-start | bytes 233480 | tf_op jit(solution)/shard_map/ppermute | solution.py:533
  45.9 0.6 copy-start.3
  48.5 0.9 copy-start.4
  67.9 26.5 %all-to-all-start.3 = ((bf16[16,24,128]{2,1,0:T(8,128)(2,1)}), bf16[16,24,128]{2,1,0:T(8,128)(2,1)S(1)}, u32[]{:S(2)}, u32[]{:S(2)}) async-start(bf16[16,24,128]{2,1,0:T(8,128)(2,1)} %shard_map.126), calls=%async_computation.3 | async-start | bytes 196608 | tf_op jit(solution)/shard_map/all_to_all | solution.py:573
